TPU v7x, 32 devices: a whole 2x2x4 slice. The times are simulated.
32 devices in a mesh: dp: 8 (over y, x, core), tensor: 4 (over z).
Axes of the slice: x: 2, y: 2, z: 4, core: 2. Of those that a mesh axis runs over, the one named last changes fastest.
Arguments:
- hidden_in: bfloat16 [8, 3072, 768], P('dp', 'tensor'), may hold values from -6 to 6
- segments: int32 [8, 3072], P('dp', 'tensor'), may hold values from 0 to 3, never falling along the last dimension, each value on 1 to 2000 neighbouring positions
- query_weight: bfloat16 [768, 768], P('dp', 'tensor'), may hold values from -0.21875 to 0.21875
- key_weight: bfloat16 [768, 768], P('dp', 'tensor'), may hold values from -0.21875 to 0.21875
- value_weight: bfloat16 [768, 768], P('dp', 'tensor'), may hold values from -0.21875 to 0.21875
- query_bias: float32 [768], P('tensor'), may hold values from -3 to 3
- value_bias: float32 [768], P('tensor'), may hold values from -3 to 3
- mixer_weight: bfloat16 [768, 768], P('tensor', 'dp'), may hold values from -1.75 to 1.75
- mixer_bias: float32 [768], replicated, may hold values from -3 to 3
- first_gain: float32 [768], replicated, may hold values from 0.5 to 1.5
- first_shift: float32 [768], replicated, may hold values from -3 to 3
- inner_weight: bfloat16 [768, 3072], P('dp', 'tensor'), may hold values from -0.21875 to 0.21875
- inner_bias: float32 [3072], P('tensor'), may hold values from -3 to 3
- outer_weight: bfloat16 [3072, 768], P('tensor', 'dp'), may hold values from -0.109375 to 0.109375
- outer_bias: float32 [768], replicated, may hold values from -3 to 3
- second_gain: float32 [768], replicated, may hold values from 0.5 to 1.5
- second_shift: float32 [768], replicated, may hold values from -3 to 3
- cotangent: bfloat16 [8, 3072, 768], P('dp', 'tensor'), may hold values from -6 to 6
Outputs:
- layer_out: bfloat16 [8, 3072, 768], P('dp', 'tensor')
- input_grad: bfloat16 [8, 3072, 768], P('dp', 'tensor')
- grad_query_weight: float32 [768, 768], P('dp', 'tensor')
- grad_key_weight: float32 [768, 768], P('dp', 'tensor')
- grad_value_weight: float32 [768, 768], P('dp', 'tensor')
- grad_query_bias: float32 [768], P('tensor')
- grad_value_bias: float32 [768], P('tensor')
- grad_mixer_weight: float32 [768, 768], P('tensor', 'dp')
- grad_mixer_bias: float32 [768], replicated
- grad_first_gain: float32 [768], replicated
- grad_first_shift: float32 [768], replicated
- grad_inner_weight: float32 [768, 3072], P('dp', 'tensor')
- grad_inner_bias: float32 [3072], P('tensor')
- grad_outer_weight: float32 [3072, 768], P('tensor', 'dp')
- grad_outer_bias: float32 [768], replicated
- grad_second_gain: float32 [768], replicated
- grad_second_shift: float32 [768], replicated
Inputs may be any that keep to these rules, and one draw needn't show every extreme that they name: `segments`: segment numbers never fall along a sequence; a document holds at most 2000 positions, and in every sequence one holds exactly 2000.
All inputs are finite; a program needn't handle non-finite values.
Results may differ from a plain program's by a relative error of at most 0.02.
Values may be sent and summed in bfloat16 or wider, within the bound.
A program may use at most 128 MiB of HBM per device.

v0:
```python
import functools

import jax
import jax.numpy as jnp
from jax import lax
from jax.experimental import pallas as pl
from jax.experimental.pallas import tpu as pltpu
from jax.sharding import PartitionSpec as P


EPS = 1e-12
ROOT_HALF = 0.7071067811865476
INV_ROOT_TWO_PI = 0.3989422804014327
HD=64; SCALE=0.125; APART=-1e30
VM=pltpu.VMEM


def dot(a,b): return jnp.dot(a,b,preferred_element_type=jnp.float32)


def project_body(heads, x_ref, w_ref, b_ref, scol_ref, srow_ref, qt_ref, ka_ref, vt_ref, qn_ref, kt_ref, vn_ref):
    y = dot(x_ref[...], w_ref[...]) + b_ref[...]
    low = y.astype(jnp.bfloat16)
    yt = y.T.astype(jnp.bfloat16)
    rows = y.shape[0]
    apart = jnp.where(lax.broadcasted_iota(jnp.int32,(HD,rows),0)==srow_ref[...],0.0,APART).astype(jnp.bfloat16)
    same = (lax.broadcasted_iota(jnp.int32,(rows,HD),1)==scol_ref[...]).astype(jnp.float32).astype(jnp.bfloat16)
    for h in range(heads):
        at=3*h*HD
        qt_ref[h,:HD,:]=yt[at:at+HD]*jnp.bfloat16(SCALE)
        qt_ref[h,HD:,:]=apart
        qn_ref[h]=low[:,at:at+HD]*jnp.bfloat16(SCALE)
        ka_ref[h]=jnp.concatenate([low[:,at+HD:at+2*HD],same],axis=1)
        kt_ref[h]=yt[at+HD:at+2*HD]
        vt_ref[h]=yt[at+2*HD:at+3*HD]
        vn_ref[h]=low[:,at+2*HD:at+3*HD]


def project(x,w,b,seg,rows=512):
    L,D=x.shape; heads=w.shape[1]//(3*HD)
    bf=jnp.bfloat16
    nat=lambda n: pl.BlockSpec((heads,rows,n),lambda i:(0,i,0))
    tr=lambda n: pl.BlockSpec((heads,n,rows),lambda i:(0,0,i))
    S=jax.ShapeDtypeStruct
    return pl.pallas_call(functools.partial(project_body,heads),grid=(L//rows,),
        in_specs=[pl.BlockSpec((rows,D),lambda i:(i,0)),pl.BlockSpec(w.shape,lambda i:(0,0)),pl.BlockSpec((1,w.shape[1]),lambda i:(0,0)),
                  pl.BlockSpec((rows,1),lambda i:(i,0)),pl.BlockSpec((1,rows),lambda i:(0,i))],
        out_specs=[tr(2*HD),nat(2*HD),tr(HD),nat(HD),tr(HD),nat(HD)],
        out_shape=[S((heads,2*HD,L),bf),S((heads,L,2*HD),bf),S((heads,HD,L),bf),S((heads,L,HD),bf),S((heads,HD,L),bf),S((heads,L,HD),bf)],
        compiler_params=pltpu.CompilerParams(vmem_limit_bytes=48<<20),
        cost_estimate=pl.CostEstimate(flops=2*L*D*w.shape[1],bytes_accessed=L*D*2+w.size*2+L*heads*HD*2*10,transcendentals=0),
        name="project")(x,w,b.reshape(1,-1),seg.reshape(-1,1),seg.reshape(1,-1))


def forward_body(BK, SUB, lo_ref, hi_ref, qt_ref, ka_ref, vt_ref, ctx_ref, ot_ref, lse_ref, m_s, l_s, acc):
    i=pl.program_id(0)
    heads,_,BQ=qt_ref.shape
    chains=[(h,slice(c*SUB,(c+1)*SUB)) for h in range(heads) for c in range(BQ//SUB)]
    m_s[...]=jnp.full(m_s.shape,-jnp.inf,jnp.float32)
    l_s[...]=jnp.zeros(l_s.shape,jnp.float32)
    acc[...]=jnp.zeros(acc.shape,jnp.float32)

    def step(j,_):
        at=pl.multiple_of(j*BK,BK)
        for h,cut in chains:
            s=dot(ka_ref[h,pl.ds(at,BK),:],qt_ref[h,:,cut])
            m_old=m_s[h,:,cut]
            m_new=jnp.maximum(m_old,jnp.max(s,axis=0,keepdims=True))
            p=jnp.exp(s-m_new)
            alpha=jnp.exp(m_old-m_new)
            m_s[h,:,cut]=m_new
            l_s[h,:,cut]=l_s[h,:,cut]*alpha+jnp.sum(p,axis=0,keepdims=True)
            acc[h,:,cut]=acc[h,:,cut]*alpha+dot(vt_ref[h,:,pl.ds(at,BK)],p.astype(jnp.bfloat16))
        return 0

    lax.fori_loop(lo_ref[i],hi_ref[i],step,0)
    for h in range(heads):
        o=acc[h]/l_s[h]
        lse_ref[h]=m_s[h]+jnp.log(l_s[h])
        ot_ref[h]=o
        ctx_ref[0,h*HD:(h+1)*HD,:]=o.astype(jnp.bfloat16)


def attend_forward(first,heads,parts,qt,ka,vt,lo,hi,BQ=384,BK=512,SUB=384):
    L=qt.shape[2]
    S=jax.ShapeDtypeStruct
    per=L//parts//BQ
    return pl.pallas_call(functools.partial(forward_body,BK,SUB),
        grid_spec=pltpu.PrefetchScalarGridSpec(num_scalar_prefetch=2,grid=(L//BQ,),
        in_specs=[pl.BlockSpec((heads,2*HD,BQ),lambda i,*_:(first//heads,0,i)),pl.BlockSpec((heads,L,2*HD),lambda i,*_:(first//heads,0,0)),pl.BlockSpec((heads,HD,L),lambda i,*_:(first//heads,0,0))],
        out_specs=[pl.BlockSpec((1,heads*HD,BQ),lambda i,*_:(i//per,0,i%per)),pl.BlockSpec((heads,HD,BQ),lambda i,*_:(0,0,i)),pl.BlockSpec((heads,1,BQ),lambda i,*_:(0,0,i))],
        scratch_shapes=[VM((heads,1,BQ),jnp.float32),VM((heads,1,BQ),jnp.float32),VM((heads,HD,BQ),jnp.float32)]),
        out_shape=[S((parts,heads*HD,L//parts),jnp.bfloat16),S((heads,HD,L),jnp.float32),S((heads,1,L),jnp.float32)],
        compiler_params=pltpu.CompilerParams(vmem_limit_bytes=56<<20),
        cost_estimate=pl.CostEstimate(flops=2*L*L*HD*2*heads,bytes_accessed=L*heads*HD*2*8,transcendentals=L*L*heads),
        name="attend_forward")(lo,hi,qt,ka,vt)


def backward_body(BQ, BK, SUB, lo_ref, hi_ref, go_ref, ot_ref, lse_ref, qt_ref, ka_ref, qn_ref, kt_ref, vn_ref, out_ref, got, gon, delta, dqt, dkt, dvt, dk_s, dv_s):
    parts,_,rows=go_ref.shape
    heads,_,L=qt_ref.shape
    CH=256
    for h in range(heads):
        for c in range(L//CH):
            p,at=c*CH//rows,c*CH%rows
            gt=go_ref[p,h*HD:(h+1)*HD,at:at+CH]
            wide=gt.astype(jnp.float32)
            got[h,:,c*CH:(c+1)*CH]=gt
            gon[h,c*CH:(c+1)*CH,:]=wide.T.astype(jnp.bfloat16)
            delta[h,:,c*CH:(c+1)*CH]=jnp.sum(wide*ot_ref[h,:,c*CH:(c+1)*CH],axis=0,keepdims=True)
    dqt[...]=jnp.zeros(dqt.shape,jnp.float32)

    def key_block(j,_):
        ka_at=pl.multiple_of(j*BK,BK)
        dk_s[...]=jnp.zeros(dk_s.shape,jnp.float32)
        dv_s[...]=jnp.zeros(dv_s.shape,jnp.float32)

        def query_block(i,_):
            for h,c in [(h,c) for h in range(heads) for c in range(BQ//SUB)]:
                at=pl.multiple_of(i*BQ+c*SUB,SUB)
                s=dot(ka_ref[h,pl.ds(ka_at,BK),:],qt_ref[h,:,pl.ds(at,SUB)])
                p=jnp.exp(s-lse_ref[h,:,pl.ds(at,SUB)])
                dp=dot(vn_ref[h,pl.ds(ka_at,BK),:],got[h,:,pl.ds(at,SUB)])
                ds=(p*(dp-delta[h,:,pl.ds(at,SUB)])).astype(jnp.bfloat16)
                dv_s[h]+=dot(p.astype(jnp.bfloat16),gon[h,pl.ds(at,SUB),:])
                dk_s[h]+=dot(ds,qn_ref[h,pl.ds(at,SUB),:])
                dqt[h,:,pl.ds(at,SUB)]+=dot(kt_ref[h,:,pl.ds(ka_at,BK)],ds)
            return 0

        lax.fori_loop(lo_ref[j],hi_ref[j],query_block,0)
        for h in range(heads):
            dkt[h,:,pl.ds(ka_at,BK)]=dk_s[h].T.astype(jnp.bfloat16)
            dvt[h,:,pl.ds(ka_at,BK)]=dv_s[h].T.astype(jnp.bfloat16)
        return 0

    lax.fori_loop(0,L//BK,key_block,0)
    for h in range(heads):
        for p in range(parts):
            cut=slice(p*rows,(p+1)*rows)
            out_ref[p,3*h*HD:(3*h+1)*HD,:]=(dqt[h,:,cut]*SCALE).astype(jnp.bfloat16)
            out_ref[p,(3*h+1)*HD:(3*h+2)*HD,:]=dkt[h,:,cut]
            out_ref[p,(3*h+2)*HD:(3*h+3)*HD,:]=dvt[h,:,cut]


def attend_backward(first,heads,go,go_first,ot,lse,qt,ka,qn,kt,vn,lo,hi,BQ=512,BK=512,SUB=512):
    parts,_,rows=go.shape; L=parts*rows
    S=jax.ShapeDtypeStruct; f32=jnp.float32; bf=jnp.bfloat16
    some=lambda a: pl.BlockSpec((heads,)+a.shape[1:],lambda i,*_:(first//heads,0,0),pipeline_mode=pl.Buffered(1))
    return pl.pallas_call(functools.partial(backward_body,BQ,BK,SUB),
        grid_spec=pltpu.PrefetchScalarGridSpec(num_scalar_prefetch=2,grid=(1,),
        in_specs=[pl.BlockSpec((parts,heads*HD,rows),lambda i,*_:(0,go_first,0),pipeline_mode=pl.Buffered(1))]+[some(a) for a in (ot,lse,qt,ka,qn,kt,vn)],
        out_specs=pl.BlockSpec((parts,3*heads*HD,rows),lambda i,*_:(0,0,0),pipeline_mode=pl.Buffered(1)),
        scratch_shapes=[VM((heads,HD,L),bf),VM((heads,L,HD),bf),VM((heads,1,L),f32),VM((heads,HD,L),f32),VM((heads,HD,L),bf),VM((heads,HD,L),bf),VM((heads,BK,HD),f32),VM((heads,BK,HD),f32)]),
        out_shape=S((parts,3*heads*HD,rows),bf),
        compiler_params=pltpu.CompilerParams(vmem_limit_bytes=60<<20),
        cost_estimate=pl.CostEstimate(flops=2*L*L*HD*5*heads,bytes_accessed=L*heads*HD*2*14,transcendentals=L*L*heads),
        name="attend_backward")(lo,hi,go,ot,lse,qt,ka,qn,kt,vn)


def ranges(seg,BQ,BK):
    first=seg.reshape(-1,BQ)[:,0]; last=seg.reshape(-1,BQ)[:,-1]
    kf=seg.reshape(-1,BK)[:,0]; kl=seg.reshape(-1,BK)[:,-1]
    lo=jnp.sum((kl[None,:]<first[:,None]).astype(jnp.int32),1)
    hi=jnp.sum((kf[None,:]<=last[:,None]).astype(jnp.int32),1)
    return lo,hi


def dot_right_t(left, right):
    return lax.dot_general(
        left, right, (((1,), (1,)), ((), ())), preferred_element_type=jnp.float32
    )


def layer_norm(values_in, gain, shift):
    mean_row = jnp.mean(values_in, -1, keepdims=True)
    centered = values_in - mean_row
    inverse = lax.rsqrt(jnp.mean(centered * centered, -1, keepdims=True) + EPS)
    normed = centered * inverse
    return (normed * gain + shift, normed, inverse)


def norm_back(grad_in, normed, inverse, gain):
    scaled = grad_in * gain
    return inverse * (
        scaled
        - jnp.mean(scaled, -1, keepdims=True)
        - normed * jnp.mean(scaled * normed, -1, keepdims=True)
    )


def gelu_value(inner):
    return 0.5 * inner * (1.0 + jax.scipy.special.erf(inner * ROOT_HALF))


def gelu_slope(inner):
    return (
        0.5 * (1.0 + jax.scipy.special.erf(inner * ROOT_HALF))
        + inner * jnp.exp(-0.5 * inner * inner) * INV_ROOT_TWO_PI
    )


MESH = pl.DeviceIdType.MESH


def chain_body(n, x_ref, out_ref, send_sem, recv_sem, keep_sem):
    me = lax.axis_index("tensor")
    barrier = pltpu.get_barrier_semaphore()

    @pl.when(me > 0)
    def _():
        pl.semaphore_signal(barrier, inc=1, device_id={"tensor": me - 1}, device_id_type=MESH)

    @pl.when(me < n - 1)
    def _():
        pl.semaphore_signal(barrier, inc=1, device_id={"tensor": me + 1}, device_id_type=MESH)

    pl.semaphore_wait(barrier, jnp.where(me > 0, 1, 0) + jnp.where(me < n - 1, 1, 0))

    keep = pltpu.make_async_copy(x_ref, out_ref.at[me], keep_sem)
    keep.start()

    def hop(side, step):
        block = me - (step - 1) if side else me + (step - 1)
        to = me + 1 if side else me - 1
        return pltpu.make_async_remote_copy(
            src_ref=x_ref if step == 1 else out_ref.at[block],
            dst_ref=out_ref.at[block],
            send_sem=send_sem.at[side, step - 1],
            recv_sem=recv_sem.at[side, step - 1],
            device_id={"tensor": to},
            device_id_type=MESH,
        )

    def sends(side, step):
        if side:
            return (me < n - 1) & (me >= step - 1)
        return (me > 0) & (me + step - 1 <= n - 1)

    def receives(side, step):
        return me >= step if side else me + step <= n - 1

    for step in range(1, n):
        for side in (0, 1):
            if step > 1:

                @pl.when(receives(side, step - 1))
                def _():
                    hop(side, step - 1).wait_recv()

            @pl.when(sends(side, step))
            def _():
                hop(side, step).start()

    for side in (0, 1):

        @pl.when(receives(side, n - 1))
        def _():
            hop(side, n - 1).wait_recv()

        for step in range(1, n):

            @pl.when(sends(side, step))
            def _():
                hop(side, step).wait_send()

    keep.wait()


def chain_gather(x):
    n = lax.axis_size("tensor")
    return pl.pallas_call(
        functools.partial(chain_body, n),
        in_specs=[pl.BlockSpec(memory_space=pltpu.VMEM)],
        out_specs=pl.BlockSpec(memory_space=pl.ANY),
        out_shape=jax.ShapeDtypeStruct((n,) + x.shape, x.dtype),
        scratch_shapes=[
            pltpu.SemaphoreType.DMA((2, n - 1)),
            pltpu.SemaphoreType.DMA((2, n - 1)),
            pltpu.SemaphoreType.DMA,
        ],
        compiler_params=pltpu.CompilerParams(collective_id=0, has_side_effects=True),
        cost_estimate=pl.CostEstimate(flops=0, bytes_accessed=200 << 20, transcendentals=0),
        name="chain_gather",
    )(x)


def weight_grads_body(parts, first_ref, second_ref, attn_ref, inner_ref, active_ref, context_ref, out_ref, ft, st):
    j = pl.program_id(0)

    @pl.when(j == 0)
    def _():
        ft[...] = first_ref[...].T
        st[...] = second_ref[...].T

    @pl.when((j < 2 * parts) & (j % 2 == 0))
    def _():
        out_ref[...] = dot(ft[...], inner_ref[0]).astype(out_ref.dtype)

    @pl.when((j < 2 * parts) & (j % 2 == 1))
    def _():
        out_ref[...] = dot(st[...], active_ref[0]).astype(out_ref.dtype)

    @pl.when(j == 2 * parts)
    def _():
        out_ref[...] = dot_right_t(attn_ref[...].T, context_ref[...]).astype(out_ref.dtype)


def weight_grads_of(first_low, second_low, attn_low, grad_inner, active, context):
    parts, rows, units = active.shape
    width = first_low.shape[1]
    features = context.shape[0]
    fixed = pl.BlockSpec((rows, width), lambda j: (0, 0))
    moving = lambda shift: pl.BlockSpec((1, rows, units), lambda j: (jnp.clip((j - shift) // 2, 0, parts - 1), 0, 0))
    return pl.pallas_call(
        functools.partial(weight_grads_body, parts),
        grid=(2 * parts + 1,),
        in_specs=[fixed, fixed, fixed, moving(0), moving(1), pl.BlockSpec((features, rows), lambda j: (0, 0))],
        out_specs=pl.BlockSpec((width, units), lambda j: (0, j)),
        out_shape=jax.ShapeDtypeStruct((width, units * 2 * parts + features), jnp.bfloat16),
        scratch_shapes=[VM((width, rows), jnp.bfloat16), VM((width, rows), jnp.bfloat16)],
        compiler_params=pltpu.CompilerParams(vmem_limit_bytes=40 << 20),
        cost_estimate=pl.CostEstimate(flops=2 * rows * width * (2 * parts * units + features), bytes_accessed=rows * units * 2 * parts * 4, transcendentals=0),
        name="weight_grads",
    )(first_low, second_low, attn_low, grad_inner, active, context)


def add_up(value):
    for axis in ("dp", "tensor"):
        size = lax.axis_size(axis)
        span = 1
        while span < size:
            value = value + lax.ppermute(value, axis, [(i, i ^ span) for i in range(size)])
            span *= 2
    return value


def rotate(blocks, axis):
    size = lax.axis_size(axis)
    me = lax.axis_index(axis)
    out = []
    for d in range(size):
        block = lax.dynamic_index_in_dim(blocks, (me + d) % size, 0, keepdims=False)
        if d:
            block = lax.ppermute(block, axis, [(i, (i + d) % size) for i in range(size)])
        out.append(block)
    return out


def body(hidden_in, segments, query_weight, key_weight, value_weight, query_bias, value_bias, mixer_weight, mixer_bias, first_gain, first_shift, inner_weight, inner_bias, outer_weight, outer_bias, second_gain, second_shift, cotangent):
    bf = jnp.bfloat16
    f32 = jnp.float32
    _, rows, width = hidden_in.shape
    parts = lax.axis_size("tensor")
    groups = lax.axis_size("dp")
    rank = lax.axis_index("tensor")
    own = query_weight.shape[1]
    heads = own // HD
    three = 3 * HD
    units = inner_weight.shape[1]
    parts_of = range(parts)
    by_head = lambda q, k, v: jnp.stack([a.reshape(a.shape[:-1] + (heads, HD)) for a in (q, k, v)], -2).reshape(q.shape[:-1] + (3 * own,))
    x_own = hidden_in[0]
    qkv_own = by_head(query_weight, key_weight, value_weight)
    qkv_all = lax.all_gather(qkv_own, "dp", axis=0, tiled=True)
    small = jnp.concatenate([segments[0].astype(f32), inner_bias])
    small = lax.all_gather(small[None], "tensor", axis=0, tiled=True)
    segment_all = small[:, :rows].astype(jnp.int32).reshape(-1)
    inner_bias_all = small[:, rows:]
    x_parts = chain_gather(x_own)
    x_all = x_parts.reshape(parts * rows, width)
    rest_own = jnp.concatenate([inner_weight, outer_weight.T, mixer_weight.T, qkv_own], 1)
    rest = lax.all_gather(rest_own, ("tensor", "dp"), axis=0, tiled=True)
    rest = rest.reshape(parts, width, rest_own.shape[1])
    biases = by_head(query_bias, jnp.zeros_like(query_bias), value_bias)

    qt, ka, vt, qn, kt, vn = project(x_all, qkv_all, biases, segment_all)
    lo, hi = ranges(segment_all, 384, 512)
    context, context_t, lse = attend_forward(0, heads, parts, qt, ka, vt, lo, hi)
    context = lax.all_to_all(context, "tensor", 0, 0, tiled=True)
    w1 = [rest[t, :, :units] for t in parts_of]
    w2t = [rest[t, :, units : 2 * units] for t in parts_of]
    mt = [rest[t, :, 2 * units : 2 * units + own] for t in parts_of]
    contract = lambda a, b, i, j: lax.dot_general(a, b, (((i,), (j,)), ((), ())), preferred_element_type=f32)
    mixed = sum(contract(context[t], mt[t], 0, 1) for t in parts_of)
    attn_in = x_own.astype(f32) + mixed + mixer_bias
    first, first_norm, first_inv = layer_norm(attn_in, first_gain, first_shift)
    first_low = first.astype(bf)
    inner = [dot(first_low, w1[t]) + inner_bias_all[t] for t in parts_of]
    active = [gelu_value(inner[t]).astype(bf) for t in parts_of]
    outer = sum(dot_right_t(active[t], w2t[t]) for t in parts_of)
    second_in = first + outer + outer_bias
    second, second_norm, second_inv = layer_norm(second_in, second_gain, second_shift)
    layer_out = second.astype(bf)
    grad_out = cotangent[0].astype(f32)
    second_gain_grad = jnp.sum(grad_out * second_norm, 0)
    second_shift_grad = jnp.sum(grad_out, 0)
    grad_second = norm_back(grad_out, second_norm, second_inv, second_gain)
    outer_bias_grad = jnp.sum(grad_second, 0)
    second_low = grad_second.astype(bf)
    grad_inner = [(dot(second_low, w2t[t]) * gelu_slope(inner[t])).astype(bf) for t in parts_of]
    inner_bias_grad = jnp.stack([jnp.sum(g, 0, dtype=f32) for g in grad_inner])
    grad_first = grad_second + sum(dot_right_t(grad_inner[t], w1[t]) for t in parts_of)
    first_gain_grad = jnp.sum(grad_first * first_norm, 0)
    first_shift_grad = jnp.sum(grad_first, 0)
    grad_attn = norm_back(grad_first, first_norm, first_inv, first_gain)
    mixer_bias_grad = jnp.sum(grad_attn, 0)
    attn_low = grad_attn.astype(bf)
    grad_context = jnp.stack([contract(mt[t], attn_low, 0, 1).astype(bf) for t in parts_of])
    go0 = lax.all_to_all(grad_context[:, :HD], "tensor", 0, 0, tiled=True)
    go1 = lax.all_to_all(grad_context[:, HD:], "tensor", 0, 0, tiled=True)
    weight_grads = weight_grads_of(
        first_low, second_low, attn_low, jnp.stack(grad_inner), jnp.stack(active), context.reshape(-1, rows)
    )
    weight_grads = lax.psum_scatter(weight_grads, "dp", scatter_dimension=0, tiled=True)
    weight_grads = jnp.concatenate(
        [
            weight_grads[:, : 2 * units * parts].reshape(-1, parts, 2 * units),
            weight_grads[:, 2 * units * parts :].reshape(-1, parts, own),
        ],
        2,
    ).transpose(1, 0, 2)
    weight_grads = rotate(weight_grads, "tensor")
    weight_grads = sum(a.astype(f32) for a in weight_grads)
    early = jnp.concatenate(
        [
            mixer_bias_grad,
            first_gain_grad,
            first_shift_grad,
            outer_bias_grad,
            second_gain_grad,
            second_shift_grad,
            inner_bias_grad.reshape(-1),
        ]
    )
    early = add_up(early)

    lo, hi = ranges(segment_all, 512, 512)
    input_back = grad_attn
    qkv_grad = []
    bias_grad = []
    for h in range(heads):
        grads = attend_backward(h, 1, go1 if h else go0, h - 1 if h else 0, context_t, lse, qt, ka, qn, kt, vn, lo, hi)
        if h < heads - 1:
            back = lax.all_to_all(grads, "tensor", 0, 0, tiled=True)
        else:
            back = rotate(grads, "tensor")
        qkv_grad.append(sum(contract(x_parts[p], grads[p], 0, 1) for p in parts_of))
        bias_grad.append(jnp.sum(grads, (0, 2), dtype=f32))
        at = 2 * units + own + h * three
        if h < heads - 1:
            weights = [rest[t, :, at : at + three] for t in parts_of]
        else:
            weights = [
                lax.dynamic_index_in_dim(rest, (rank - t) % parts, 0, keepdims=False)[:, at : at + three]
                for t in parts_of
            ]
        input_back = input_back + sum(contract(back[t], weights[t], 0, 1) for t in parts_of)
    input_grad = input_back.astype(bf)
    bias_grad = jnp.concatenate(bias_grad)
    high = bias_grad.astype(bf)
    low = (bias_grad - high.astype(f32)).astype(bf)
    each = width // groups
    qkv_grad = jnp.concatenate(qkv_grad, 1).astype(bf).reshape(groups, each, 3 * own)
    extra = jnp.pad(jnp.stack([high, low]), ((0, 14), (0, 0)))
    extra = jnp.broadcast_to(extra[None], (groups, 16, 3 * own))
    qkv_grad = lax.all_to_all(jnp.concatenate([qkv_grad, extra], 1), "dp", 0, 0, tiled=True)
    qkv_grad = jnp.sum(qkv_grad.astype(f32), 0)
    bias_grad = qkv_grad[each] + qkv_grad[each + 1]
    pick = lambda a, n: a.reshape(a.shape[:-1] + (heads, 3, HD))[..., n, :].reshape(a.shape[:-1] + (own,))
    stacked = early[: 6 * width].reshape(6, width)
    inner_bias_out = lax.dynamic_slice_in_dim(early, 6 * width + rank * units, units)
    return (
        layer_out[None],
        input_grad[None],
        pick(qkv_grad[:each], 0),
        pick(qkv_grad[:each], 1),
        pick(qkv_grad[:each], 2),
        pick(bias_grad, 0),
        pick(bias_grad, 2),
        weight_grads[:, 2 * units :].T,
        stacked[0],
        stacked[1],
        stacked[2],
        weight_grads[:, :units],
        inner_bias_out,
        weight_grads[:, units : 2 * units].T,
        stacked[3],
        stacked[4],
        stacked[5],
    )


def solution(mesh):
    placed = (
        P("dp", "tensor", None),
        P("dp", "tensor"),
        P("dp", "tensor"),
        P("dp", "tensor"),
        P("dp", "tensor"),
        P("tensor"),
        P("tensor"),
        P("tensor", "dp"),
        P(),
        P(),
        P(),
        P("dp", "tensor"),
        P("tensor"),
        P("tensor", "dp"),
        P(),
        P(),
        P(),
        P("dp", "tensor", None),
    )

    return jax.shard_map(
        body,
        mesh=mesh,
        in_specs=placed,
        out_specs=(
            P("dp", "tensor", None),
            P("dp", "tensor", None),
            P("dp", "tensor"),
            P("dp", "tensor"),
            P("dp", "tensor"),
            P("tensor"),
            P("tensor"),
            P("tensor", "dp"),
            P(),
            P(),
            P(),
            P("dp", "tensor"),
            P("tensor"),
            P("tensor", "dp"),
            P(),
            P(),
            P(),
        ),
        check_vma=False,
    )
```

profile of v0, /device:TPU:0, one launch (start us, length us, event | category | flops | bytes accessed | tf_op | source)
XLA Modules:
  0.0 655.7 jit_solution(6610782320382840105)
XLA Ops:
  11.1 1.9 concatenate.53
  13.1 14.9 %all-gather.1 = f32[4,1,1536]{2,1,0:T(1,128)S(1)} all-gather(f32[1,1,1536]{2,1,0:T(1,128)S(1)} %reshape.255), channel_id=2, replica_groups=mesh['dp'=8,'tensor'=4] {'tensor'}, dimensions={0}, use_global_device_ids=true | all-gather | bytes 30720 | tf_op jit(solution)/shard_map/all_gather | solution.py:366
  28.1 141.9 %chain_gather.1 = bf16[4,768,768]{2,1,0:T(8,128)(2,1)} custom-call(bf16[768,768]{1,0:T(8,128)(2,1)} %bitcast.377), custom_call_target="tpu_custom_call" | custom-call | bytes 209715200 | tf_op jit(solution)/shard_map/chain_gather/pallas_call | solution.py:271
  172.1 10.8 %all_gather.10.w_ref = bf16[768,576]{1,0:T(8,128)(2,1)S(1)} all-gather(bf16[96,576]{1,0:T(8,128)(2,1)S(1)} %copy.131), channel_id=1, replica_groups=mesh['dp'=8,'tensor'=4] {'dp'}, dimensions={0}, use_global_device_ids=true | all-gather | bytes 995328 | tf_op jit(solution)/shard_map/all_gather | solution.py:364
  182.8 9.9 %project.1 = (bf16[3,128,3072]{2,1,0:T(8,128)(2,1)}, bf16[3,3072,128]{2,1,0:T(8,128)(2,1)}, bf16[3,64,3072]{2,1,0:T(8,128)(2,1)S(1)}, bf16[3,3072,64]{2,1,0:T(8,...) custom-call(bf16[3072,768]{1,0:T(8,128)(2,1)} %bitcast.375, ...), custom_call_target="tpu_custom_call" | custom-call | flops 2717908992 | bytes 17399808 | tf_op jit(solution)/shard_map/project/pallas_call | solution.py:45
  194.8 61.9 %attend_forward.1 = (bf16[4,192,768]{2,1,0:T(8,128)(2,1)}, f32[3,64,3072]{2,1,0:T(8,128)}, f32[3,1,3072]{2,1,0:T(1,128)}) custom-call(s32[8]{0:T(128)} %get-tuple-element.207.lo_ref, s32[8]{0:T(128)} %get-tuple-element.206.hi_ref, bf16[3,128,3072]{2,1,0:T(8,128)(2,1)} %get-tuple-element.26.qt_ref, bf16[3,3072,128]{2,1,0:T(8,128)(2,1)} %get-tuple-element.27.ka_ref, ...), custom_call_target="tpu_custom_call" | custom-call | flops 7247757312 | bytes 9437184 | tf_op jit(solution)/shard_map/attend_forward/pallas_call | solution.py:88
  256.7 3.6 all-to-all-start
  260.3 17.3 %all-to-all-done = bf16[4,192,768]{2,1,0:T(8,128)(2,1)S(1)} async-done(((bf16[4,192,768]{2,1,0:T(8,128)(2,1)}), bf16[4,192,768]{2,1,0:T(8,128)(2,1)S(1)}, u32[]{:S(2)}, u32[]{:S(2)}) %all-to-all-start) | async-done | bytes 1179680 | tf_op jit(solution)/shard_map/all_to_all | solution.py:379
  282.3 2.2 fusion.126
  285.5 2.0 copy-done.2
  289.9 2.9 multiply_convert_fusion.2
  293.9 2.7 multiply_convert_fusion.1
  297.8 2.7 multiply_convert_fusion
  300.5 1.8 fusion.127
  304.7 2.5 fusion.121
  308.9 2.8 convert_reduce_fusion.3
  311.7 2.8 convert_reduce_fusion.4
  314.5 2.8 convert_reduce_fusion.2
  317.2 2.8 convert_reduce_fusion.1
  322.3 2.6 fusion.73
  324.8 4.4 multiply_reduce_fusion
  336.1 11.9 %weight_grads.1 = bf16[768,6912]{1,0:T(8,128)(2,1)} custom-call(bf16[768,768]{1,0:T(8,128)(2,1)S(1)} %fusion.33.first_ref, bf16[768,768]{1,0:T(8,128)(2,1)S(1)} %convert_element_type.172.second_ref, bf16[768,768]{1,0:T(8,128)(2,1)S(1)} %convert_element_type.179.attn_ref, bf16[4,768,768]{2,1,0:T(8,128)(2,1)S(1)} %pad_maximum_fusion.inner_ref, ...), custom_call_target="tpu_custom_call" | custom-call | flops 8153726976 | bytes 18874368 | tf_op jit(solution)/shard_map/weight_grads/pallas_call | solution.py:314
  355.1 3.5 all-to-all-start.1
  361.3 11.3 %all-to-all-done.1.go_ref = bf16[4,64,768]{2,1,0:T(8,128)(2,1)S(1)} async-done(((bf16[4,64,768]{2,1,0:T(8,128)(2,1)}), bf16[4,64,768]{2,1,0:T(8,128)(2,1)S(1)}, u32[]{:S(2)}, u32[]{:S(2)}) %all-to-all-start.1) | async-done | bytes 393248 | tf_op jit(solution)/shard_map/all_to_all | solution.py:409
  372.5 4.2 all-to-all-start.3
  376.8 27.3 %attend_backward.3 = bf16[4,192,768]{2,1,0:T(8,128)(2,1)} custom-call(s32[6]{0:T(128)} %get-tuple-element.155.lo_ref, s32[6]{0:T(128)} %get-tuple-element.154.hi_ref, bf16[4,64,768]{2,1,0:T(8,128)(2,1)} %copy-done.24, f32[3,64,3072]{2,1,0:T(8,128)} %get-tuple-element.30.ot_ref, f32[3,1,3072]{2,1,0:T(1,128)} %get-tuple-element.31.lse_ref, ...), custom_call_target="tpu_custom_call" | custom-call | flops 6039797760 | bytes 5505024 | tf_op jit(solution)/shard_map/attend_backward/pallas_call | solution.py:149
  404.1 1.8 fusion.51
  407.7 1.8 convolution_add_fusion.7
  409.5 1.8 fusion.64
  413.9 27.0 %attend_backward.4 = bf16[4,192,768]{2,1,0:T(8,128)(2,1)} custom-call(s32[6]{0:T(128)} %get-tuple-element.155.lo_ref, s32[6]{0:T(128)} %get-tuple-element.154.hi_ref, bf16[4,128,768]{2,1,0:T(8,128)(2,1)} %copy-done.23, f32[3,64,3072]{2,1,0:T(8,128)} %get-tuple-element.30.ot_ref, f32[3,1,3072]{2,1,0:T(1,128)} %get-tuple-element.31.lse_ref, ...), custom_call_target="tpu_custom_call" | custom-call | flops 6039797760 | bytes 5505024 | tf_op jit(solution)/shard_map/attend_backward/pallas_call | solution.py:149
  444.4 1.8 convolution_add_fusion.4
  446.2 1.8 fusion.61
  448.2 26.9 %attend_backward.5 = bf16[4,192,768]{2,1,0:T(8,128)(2,1)} custom-call(s32[6]{0:T(128)} %get-tuple-element.155.lo_ref, s32[6]{0:T(128)} %get-tuple-element.154.hi_ref, bf16[4,128,768]{2,1,0:T(8,128)(2,1)} %copy-done.23, f32[3,64,3072]{2,1,0:T(8,128)} %get-tuple-element.30.ot_ref, f32[3,1,3072]{2,1,0:T(1,128)} %get-tuple-element.31.lse_ref, ...), custom_call_target="tpu_custom_call" | custom-call | flops 6039797760 | bytes 5505024 | tf_op jit(solution)/shard_map/attend_backward/pallas_call | solution.py:149
  475.1 1.9 fusion.47
  485.5 5.6 all-to-all-start.5
  496.1 1.9 collective-permute-start.7
  497.9 9.4 %collective-permute-done.7 = f32[7680]{0:T(1024)S(1)} collective-permute-done((f32[7680]{0:T(1024)S(1)}, f32[7680]{0:T(1024)S(1)}, u32[]{:S(2)}, u32[]{:S(2)}) %collective-permute-start.7) | collective-permute-done | bytes 30752 | tf_op jit(solution)/shard_map/ppermute | solution.py:332
  508.8 2.4 collective-permute-done.8
  511.3 1.8 collective-permute-start.9
  513.1 2.1 collective-permute-done.9
  515.2 2.9 collective-permute-start.10
  518.1 3.5 all-to-all-start.2
  521.7 7.4 %dynamic-slice_bitcast_fusion = (bf16[768,2304]{1,0:T(8,128)(2,1)}, bf16[768,2304]{1,0:T(8,128)(2,1)S(1)}, bf16[768,2304]{1,0:T(8,128)(2,1)S(1)}, bf16[768,2304]{1,0:T(8,128)(2,1)S(1)}) fusion(bf16[4,768,2304]{2,1,0:T(8,128)(2,1)} %bitcast.350, s32[]{:T(128)S(6)} %select_n.86, s32[]{:T(128)S(6)} %select_n.82, s32[]{:T(128)S(6)} %select_n.78, s32[]{:T(128)S(6)} %select_n.74), kind=kLoop, calls=%fused_computation.2 | loop fusion | bytes 28311568 | tf_op jit(solution)/shard_map/jit(dynamic_index_in_dim)/squeeze | solution.py:454
  530.6 2.0 collective-permute-start
  533.3 2.4 collective-permute-start.1
  537.2 2.1 fusion.99
  539.4 13.2 %collective-permute-done = bf16[192,768]{1,0:T(8,128)(2,1)S(1)} collective-permute-done((bf16[192,768]{1,0:T(8,128)(2,1)S(1)}, bf16[192,768]{1,0:T(8,128)(2,1)S(1)}, u32[]{:S(2)}, u32[]{:S(2)}) %collective-permute-start) | collective-permute-done | bytes 294944 | tf_op jit(solution)/shard_map/ppermute | solution.py:344
  552.5 2.1 fusion.97
  554.6 12.8 %collective-permute-done.1 = bf16[192,768]{1,0:T(8,128)(2,1)S(1)} collective-permute-done((bf16[192,768]{1,0:T(8,128)(2,1)S(1)}, bf16[192,768]{1,0:T(8,128)(2,1)S(1)}, u32[]{:S(2)}, u32[]{:S(2)}) %collective-permute-start.1) | collective-permute-done | bytes 294944 | tf_op jit(solution)/shard_map/ppermute | solution.py:344
  567.4 2.1 fusion.95
  569.5 8.5 %all-to-all-start.4 = ((bf16[4,192,768]{2,1,0:T(8,128)(2,1)}), bf16[4,192,768]{2,1,0:T(8,128)(2,1)S(1)}, u32[]{:S(2)}, u32[]{:S(2)}) async-start(bf16[4,192,768]{2,1,0:T(8,128)(2,1)} %attend_backward.4), calls=%async_computation.4 | async-start | bytes 2359296 | tf_op jit(solution)/shard_map/all_to_all | solution.py:444
  583.4 3.1 fusion.106
  586.6 3.1 fusion.107
  589.7 3.2 fusion.108
  592.9 3.2 fusion.105
  596.1 7.6 %all-to-all-done.4 = bf16[4,192,768]{2,1,0:T(8,128)(2,1)S(1)} async-done(((bf16[4,192,768]{2,1,0:T(8,128)(2,1)}), bf16[4,192,768]{2,1,0:T(8,128)(2,1)S(1)}, u32[]{:S(2)}, u32[]{:S(2)}) %all-to-all-start.4) | async-done | bytes 1179680 | tf_op jit(solution)/shard_map/all_to_all | solution.py:444
  603.7 2.9 fusion.102
  606.6 2.9 fusion.103
  609.5 3.0 fusion.104
  612.5 2.9 fusion.101
  620.2 2.0 collective-permute-start.4
  622.2 1.8 collective-permute-start.5
  624.0 10.9 %fusion.53 = bf16[1,768,768]{2,1,0:T(8,128)(2,1)} fusion(f32[768,768]{1,0:T(8,128)} %fusion.95, f32[768,768]{1,0:T(8,128)S(1)} %copy-done.6, f32[768,768]{1,0:T(8,128)} %fusion.97, f32[768,768]{1,0:T(8,128)} %fusion.101, f32[768,768]{1,0:T(8,128)} %fusion.102, f32[768,768]{1,0:T(8,128)} %fusion.104, f32[768,768]{1,0:T(8,128)} %fusion.103, ...), kind=kOutput, calls=%fused_computation.117 | convolution fusion | flops 234160128 | bytes 30179328 | tf_op jit(solution)/shard_map/dot_general | solution.py:383
  634.9 11.0 %collective-permute-done.4 = bf16[96,1728]{1,0:T(8,128)(2,1)S(1)} collective-permute-done((bf16[96,1728]{1,0:T(8,128)(2,1)S(1)}, bf16[96,1728]{1,0:T(8,128)(2,1)S(1)}, u32[]{:S(2)}, u32[]{:S(2)}) %collective-permute-start.4) | collective-permute-done | bytes 331808 | tf_op jit(solution)/shard_map/ppermute | solution.py:344
  (229 shorter events, 80.6 us)
Async XLA Ops:
  7.2 5.9 copy-start.40
  7.2 5.9 copy-start.38
  7.2 270.4 %all-gather.4.cloned.1.call-start = ((), (), s32[]{:S(2)}) async-start(), calls=%async_computation.7 | async-start | bytes 14598144 | tf_op jit(solution)/shard_map/all_gather | solution.py:372
  28.0 142.5 %copy-start.41 = (f32[192]{0:T(256)S(1)}, f32[192]{0:T(256)}, u32[]{:S(2)}) copy-start(f32[192]{0:T(256)} %param.23) | copy-start | bytes 2308
  28.1 142.6 %copy-start.42 = (f32[192]{0:T(256)S(1)}, f32[192]{0:T(256)}, u32[]{:S(2)}) copy-start(f32[192]{0:T(256)} %param.24) | copy-start | bytes 2308
  171.1 11.7 %copy-start.28 = (s32[6]{0:T(128)}, s32[6]{0:T(128)S(1)}, u32[]{:S(2)}) copy-start(s32[6]{0:T(128)S(1)} %get-tuple-element.148) | copy-start | bytes 76
  171.1 11.7 %copy-start.30 = (s32[6]{0:T(128)}, s32[6]{0:T(128)S(1)}, u32[]{:S(2)}) copy-start(s32[6]{0:T(128)S(1)} %get-tuple-element.149) | copy-start | bytes 76
  192.7 1.0 copy-start
  193.8 1.0 copy-start.1
  256.7 20.9 %all-to-all-start = ((bf16[4,192,768]{2,1,0:T(8,128)(2,1)}), bf16[4,192,768]{2,1,0:T(8,128)(2,1)S(1)}, u32[]{:S(2)}, u32[]{:S(2)}) async-start(bf16[4,192,768]{2,1,0:T(8,128)(2,1)} %get-tuple-element.29), calls=%async_computation | async-start | bytes 2359296 | tf_op jit(solution)/shard_map/all_to_all | solution.py:379
  260.3 355.1 %reduce-scatter.2.cloned.1.call-start = ((), (), s32[]{:S(2)}) async-start(), calls=%async_computation.8 | async-start | bytes 11943936 | tf_op jit(solution)/shard_map/reduce_scatter | solution.py:414
  279.1 3.2 copy-start.8
  279.1 3.2 copy-start.32
  280.8 4.2 copy-start.25
  280.8 4.2 copy-start.27
  282.3 5.1 copy-start.2
  288.7 1.1 copy-start.10
  292.8 1.1 copy-start.12
  296.6 1.1 copy-start.14
  297.8 2.7 copy-start.39
  302.3 1.3 copy-start.5
  302.3 1.3 copy-start.26
  302.7 2.0 copy-start.33
  307.3 1.7 copy-start.45
  311.7 8.3 %copy-start.16 = (bf16[768,768]{1,0:T(8,128)(2,1)}, bf16[768,768]{1,0:T(8,128)(2,1)S(1)}, u32[]{:S(2)}) copy-start(bf16[768,768]{1,0:T(8,128)(2,1)S(1)} %get-tuple-element.203) | copy-start | bytes 3538948
  311.7 2.8 copy-start.44
  314.4 6.7 %copy-start.18 = (bf16[768,768]{1,0:T(8,128)(2,1)}, bf16[768,768]{1,0:T(8,128)(2,1)S(1)}, u32[]{:S(2)}) copy-start(bf16[768,768]{1,0:T(8,128)(2,1)S(1)} %get-tuple-element.205) | copy-start | bytes 3538948
  314.5 2.8 copy-start.43
  317.2 5.0 copy-start.20
  330.6 1.4 copy-start.3
  330.7 2.1 copy-start.11
  330.7 2.5 copy-start.13
  330.7 2.8 copy-start.15
  333.5 1.3 copy-start.17
  333.5 1.6 copy-start.19
  333.5 2.0 copy-start.21
  354.3 4.4 copy-start.29
  354.3 4.4 copy-start.31
  354.3 5.9 copy-start.34
  354.3 5.9 copy-start.35
  354.3 5.9 copy-start.36
  354.3 5.9 copy-start.37
  355.1 17.4 %all-to-all-start.1 = ((bf16[4,64,768]{2,1,0:T(8,128)(2,1)}), bf16[4,64,768]{2,1,0:T(8,128)(2,1)S(1)}, u32[]{:S(2)}, u32[]{:S(2)}) async-start(bf16[4,64,768]{2,1,0:T(8,128)(2,1)} %pad_maximum_fusion.6), calls=%async_computation.1 | async-start | bytes 786432 | tf_op jit(solution)/shard_map/all_to_all | solution.py:409
  372.5 4.3 copy-start.24
  372.5 40.5 %all-to-all-start.3 = ((bf16[4,128,768]{2,1,0:T(8,128)(2,1)}), bf16[4,128,768]{2,1,0:T(8,128)(2,1)S(1)}, u32[]{:S(2)}, u32[]{:S(2)}) async-start(bf16[4,128,768]{2,1,0:T(8,128)(2,1)} %pad_maximum_fusion.3), calls=%async_computation.3 | async-start | bytes 1572864 | tf_op jit(solution)/shard_map/all_to_all | solution.py:410
  475.1 1.9 copy-start.7
  485.5 32.6 %all-to-all-start.5 = ((bf16[8,112,576]{2,1,0:T(8,128)(2,1)}), bf16[8,112,576]{2,1,0:T(8,128)(2,1)S(1)}, u32[]{:S(2)}, u32[]{:S(2)}) async-start(bf16[8,112,576]{2,1,0:T(8,128)(2,1)} %pad_maximum_fusion.2), calls=%async_computation.5 | async-start | bytes 2293760 | tf_op jit(solution)/shard_map/all_to_all | solution.py:466
  494.6 1.4 collective-permute-start.6
  496.1 11.3 %collective-permute-start.7 = (f32[7680]{0:T(1024)S(1)}, f32[7680]{0:T(1024)S(1)}, u32[]{:S(2)}, u32[]{:S(2)}) collective-permute-start(f32[7680]{0:T(1024)S(1)} %add.429), channel_id=1, source_target_pairs={{0,8},{4,12},{8,0},{12,4},{16,24},{20,28},{24,16},{28,20},{1,9},{5... | collective-permute-start | bytes 92168 | tf_op jit(solution)/shard_map/ppermute | solution.py:332
  507.4 3.9 collective-permute-start.8
  511.3 3.9 collective-permute-start.9
  515.2 13.9 %collective-permute-start.10 = (f32[7680]{0:T(1024)S(1)}, f32[7680]{0:T(1024)}, u32[]{:S(2)}, u32[]{:S(2)}) collective-permute-start(f32[7680]{0:T(1024)S(1)} %add.432), channel_id=1, source_target_pairs={{0,2},{1,3},{2,0},{3,1},{4,6},{5,7},{6,4},{7,5},{8,10},{9,11},{10,... | collective-permute-start | bytes 92168 | tf_op jit(solution)/shard_map/ppermute | solution.py:332
  518.1 51.3 %all-to-all-start.2 = ((bf16[4,192,768]{2,1,0:T(8,128)(2,1)}), bf16[4,192,768]{2,1,0:T(8,128)(2,1)S(1)}, u32[]{:S(2)}, u32[]{:S(2)}) async-start(bf16[4,192,768]{2,1,0:T(8,128)(2,1)} %attend_backward.3), calls=%async_computation.2 | async-start | bytes 2359296 | tf_op jit(solution)/shard_map/all_to_all | solution.py:444
  530.6 21.9 %collective-permute-start = (bf16[192,768]{1,0:T(8,128)(2,1)S(1)}, bf16[192,768]{1,0:T(8,128)(2,1)S(1)}, u32[]{:S(2)}, u32[]{:S(2)}) collective-permute-start(bf16[192,768]{1,0:T(8,128)(2,1)S(1)} %get-tuple-element.170), channel_id=1, source_target_pairs={{0,1},{1,2},{2,3},{3,0},{4,5},{5,6},{6,7},{7,4},{8,9},{9,10},{10,1... | collective-permute-start | bytes 884744 | tf_op jit(solution)/shard_map/ppermute | solution.py:344
  533.3 34.1 %collective-permute-start.1 = (bf16[192,768]{1,0:T(8,128)(2,1)S(1)}, bf16[192,768]{1,0:T(8,128)(2,1)S(1)}, u32[]{:S(2)}, u32[]{:S(2)}) collective-permute-start(bf16[192,768]{1,0:T(8,128)(2,1)S(1)} %get-tuple-element.169), channel_id=1, source_target_pairs={{0,2},{1,3},{2,0},{3,1},{4,6},{5,7},{6,4},{7,5},{8,10},{9,11},{10,... | collective-permute-start | bytes 884744 | tf_op jit(solution)/shard_map/ppermute | solution.py:344
  535.6 88.4 %collective-permute-start.2 = (bf16[192,768]{1,0:T(8,128)(2,1)}, bf16[192,768]{1,0:T(8,128)(2,1)}, u32[]{:S(2)}, u32[]{:S(2)}) collective-permute-start(bf16[192,768]{1,0:T(8,128)(2,1)} %get-tuple-element.168), channel_id=1, source_target_pairs={{0,3},{1,0},{2,1},{3,2},{4,7},{5,4},{6,5},{7,6},{8,11},{9,8},{10,9... | collective-permute-start | bytes 884744 | tf_op jit(solution)/shard_map/ppermute | solution.py:344
  569.5 34.2 %all-to-all-start.4 = ((bf16[4,192,768]{2,1,0:T(8,128)(2,1)}), bf16[4,192,768]{2,1,0:T(8,128)(2,1)S(1)}, u32[]{:S(2)}, u32[]{:S(2)}) async-start(bf16[4,192,768]{2,1,0:T(8,128)(2,1)} %attend_backward.4), calls=%async_computation.4 | async-start | bytes 2359296 | tf_op jit(solution)/shard_map/all_to_all | solution.py:444
  615.4 1.3 slice-start
  615.4 2.4 copy-start.9
  616.7 7.3 %copy-start.4 = (f32[768,768]{1,0:T(8,128)S(1)}, f32[768,768]{1,0:T(8,128)}, u32[]{:S(2)}) copy-start(f32[768,768]{1,0:T(8,128)} %copy-done.3) | copy-start | bytes 7077892
  618.1 5.9 copy-start.6
  620.1 14.8 %collective-permute-start.3 = (bf16[96,1728]{1,0:T(8,128)(2,1)S(1)}, bf16[96,1728]{1,0:T(8,128)(2,1)S(1)}, u32[]{:S(2)}, u32[]{:S(2)}) collective-permute-start(bf16[96,1728]{1,0:T(8,128)(2,1)S(1)} %get-tuple-element.165), channel_id=1, source_target_pairs={{0,1},{1,2},{2,3},{3,0},{4,5},{5,6},{6,7},{7,4},{8,9},{9,10},{10,1... | collective-permute-start | bytes 995336 | tf_op jit(solution)/shard_map/ppermute | solution.py:344
  620.2 25.7 %collective-permute-start.4 = (bf16[96,1728]{1,0:T(8,128)(2,1)S(1)}, bf16[96,1728]{1,0:T(8,128)(2,1)S(1)}, u32[]{:S(2)}, u32[]{:S(2)}) collective-permute-start(bf16[96,1728]{1,0:T(8,128)(2,1)S(1)} %get-tuple-element.167), channel_id=1, source_target_pairs={{0,2},{1,3},{2,0},{3,1},{4,6},{5,7},{6,4},{7,5},{8,10},{9,11},{10,... | collective-permute-start | bytes 995336 | tf_op jit(solution)/shard_map/ppermute | solution.py:344
  622.2 23.7 %collective-permute-start.5 = (bf16[96,1728]{1,0:T(8,128)(2,1)S(1)}, bf16[96,1728]{1,0:T(8,128)(2,1)S(1)}, u32[]{:S(2)}, u32[]{:S(2)}) collective-permute-start(bf16[96,1728]{1,0:T(8,128)(2,1)S(1)} %get-tuple-element.166), channel_id=1, source_target_pairs={{0,3},{1,0},{2,1},{3,2},{4,7},{5,4},{6,5},{7,6},{8,11},{9,8},{10,9... | collective-permute-start | bytes 995336 | tf_op jit(solution)/shard_map/ppermute | solution.py:344
  (2 other events, 1.6 us)
Sparse Core Ops, SparseCore 0:
  13.2 134.6 all-gather.3
  348.2 86.6 reduce-scatter.1
where the time goes:
time: 669 us; the launch traced here: 656 us
  Pallas kernels  307 us (46%)
  matrix products  111 us (17%)
  waiting for transfers between devices  88 us (13%)
  starting transfers between devices  47.4 us (7%)
  local copies, waits for them, and re-layouts  42.1 us (6%)
  blocking collectives  25.6 us (4%)
  other arithmetic  19.7 us (3%)
  between operations  15.1 us (2%)
    pallas_call x1, Pallas kernels, chain_gather(): pl.pallas_call(functools.partial(chain_body, n), in_specs=[pl.BlockSpec(m...  142 us
    pallas_call x3, Pallas kernels, attend_backward(): pl.pallas_call(functools.partial(backward_body, BQ, BK, SUB), grid_spec=p...  81.2 us
    dot_general x32, matrix products, body(): lax.dot_general(a, b, (((i,), (j,)), ((), ())), preferred_element_type=f32)  75.8 us
    pallas_call x1, Pallas kernels, attend_forward(): pl.pallas_call(functools.partial(forward_body, BK, SUB), grid_spec=pltpu....  61.9 us
    ppermute x6, waiting for transfers between devices, rotate(): lax.ppermute(block, axis, [(i, (i + d) % size) for i in range(size)])  36.9 us
    unnamed x111, local copies, waits for them, and re-layouts  24 us
    dot_general x8, matrix products, dot(): return jnp.dot(a, b, preferred_element_type=jnp.float32)  20.6 us
    all_to_all x1, waiting for transfers between devices, body(): context = lax.all_to_all(context, 'tensor', 0, 0, tiled=True)  17.3 us
  transfers between devices with their start and end apart: 19, of which 10 were waited for; matrix products, arithmetic and copies ran while one was open for 15% of the time, Pallas kernels for 45%

commit v1 on v0

--- a/solution.py
+++ b/solution.py
@@ -202,8 +202,14 @@
 MESH = pl.DeviceIdType.MESH
 
 
-def chain_body(n, x_ref, out_ref, send_sem, recv_sem, keep_sem):
+def flip(index, bit):
+    span = 1 << bit
+    return index + span * (1 - 2 * ((index // span) % 2))
+
+
+def start_body(n, bits, x_ref, w_ref, s_ref, x_out, w_out, s_out, send_z, recv_z, send_d, recv_d, keep_sem):
     me = lax.axis_index("tensor")
+    mine = lax.axis_index("dp")
     barrier = pltpu.get_barrier_semaphore()
 
     @pl.when(me > 0)
@@ -214,20 +220,31 @@
     def _():
         pl.semaphore_signal(barrier, inc=1, device_id={"tensor": me + 1}, device_id_type=MESH)
 
-    pl.semaphore_wait(barrier, jnp.where(me > 0, 1, 0) + jnp.where(me < n - 1, 1, 0))
-
-    keep = pltpu.make_async_copy(x_ref, out_ref.at[me], keep_sem)
-    keep.start()
-
-    def hop(side, step):
+    for bit in range(bits):
+        pl.semaphore_signal(barrier, inc=1, device_id={"dp": flip(mine, bit)}, device_id_type=MESH)
+    pl.semaphore_wait(barrier, bits + jnp.where(me > 0, 1, 0) + jnp.where(me < n - 1, 1, 0))
+
+    keeps = [
+        pltpu.make_async_copy(x_ref, x_out.at[me], keep_sem.at[0]),
+        pltpu.make_async_copy(w_ref, w_out.at[me, mine], keep_sem.at[1]),
+        pltpu.make_async_copy(s_ref, s_out.at[me], keep_sem.at[2]),
+    ]
+    for keep in keeps:
+        keep.start()
+
+    def hop(kind, side, step):
         block = me - (step - 1) if side else me + (step - 1)
-        to = me + 1 if side else me - 1
+        first, place = (
+            (x_ref, x_out.at[block]),
+            (w_ref, w_out.at[block, mine]),
+            (s_ref, s_out.at[block]),
+        )[kind]
         return pltpu.make_async_remote_copy(
-            src_ref=x_ref if step == 1 else out_ref.at[block],
-            dst_ref=out_ref.at[block],
-            send_sem=send_sem.at[side, step - 1],
-            recv_sem=recv_sem.at[side, step - 1],
-            device_id={"tensor": to},
+            src_ref=first if step == 1 else place,
+            dst_ref=place,
+            send_sem=send_z.at[kind, side, step - 1],
+            recv_sem=recv_z.at[kind, side, step - 1],
+            device_id={"tensor": me + 1 if side else me - 1},
             device_id_type=MESH,
         )
 
@@ -239,49 +256,110 @@
     def receives(side, step):
         return me >= step if side else me + step <= n - 1
 
-    for step in range(1, n):
+    def z_start(kinds, step):
         for side in (0, 1):
-            if step > 1:
-
-                @pl.when(receives(side, step - 1))
-                def _():
-                    hop(side, step - 1).wait_recv()
 
             @pl.when(sends(side, step))
             def _():
-                hop(side, step).start()
-
+                for kind in kinds:
+                    hop(kind, side, step).start()
+
+    def z_arrive(kinds, step):
+        for side in (0, 1):
+
+            @pl.when(receives(side, step))
+            def _():
+                for kind in kinds:
+                    hop(kind, side, step).wait_recv()
+
+    half = w_ref.shape[1] // 2
+    up = list(range(bits - 1, -1, -1))
+    orders = (up, [up[1], up[0]] + up[2:] if bits > 1 else up)
+
+    def doubling(side, step):
+        order = orders[side]
+        held = [mine]
+        for bit in order[:step]:
+            held = held + [flip(d, bit) for d in held]
+        cut = pl.ds(side * half, half)
+        return [
+            pltpu.make_async_remote_copy(
+                src_ref=w_out.at[:, d, :, cut],
+                dst_ref=w_out.at[:, d, :, cut],
+                send_sem=send_d.at[side, (1 << step) - 1 + at],
+                recv_sem=recv_d.at[side, (1 << step) - 1 + at],
+                device_id={"dp": flip(mine, order[step])},
+                device_id_type=MESH,
+            )
+            for at, d in enumerate(held)
+        ]
+
+    def d_start(step):
+        for side in (0, 1):
+            for copy in doubling(side, step):
+                copy.start()
+
+    def d_arrive(step):
+        for side in (0, 1):
+            for copy in doubling(side, step):
+                copy.wait_recv()
+
+    for step in range(1, n):
+        z_start((1, 2), step)
+        z_arrive((1, 2), step)
+    keeps[1].wait()
+    for step in range(max(n - 1, bits)):
+        if step < bits:
+            if step:
+                d_arrive(step - 1)
+            d_start(step)
+        if step < n - 1:
+            if step:
+                z_arrive((0,), step)
+            z_start((0,), step + 1)
+    z_arrive((0,), n - 1)
+    d_arrive(bits - 1)
     for side in (0, 1):
-
-        @pl.when(receives(side, n - 1))
-        def _():
-            hop(side, n - 1).wait_recv()
-
         for step in range(1, n):
 
             @pl.when(sends(side, step))
             def _():
-                hop(side, step).wait_send()
-
-    keep.wait()
-
-
-def chain_gather(x):
+                for kind in (0, 1, 2):
+                    hop(kind, side, step).wait_send()
+
+        for step in range(bits):
+            for copy in doubling(side, step):
+                copy.wait_send()
+    keeps[0].wait()
+    keeps[2].wait()
+
+
+def start(x, w, small):
     n = lax.axis_size("tensor")
+    groups = lax.axis_size("dp")
+    bits = groups.bit_length() - 1
+    S = jax.ShapeDtypeStruct
+    anywhere = pl.BlockSpec(memory_space=pl.ANY)
     return pl.pallas_call(
-        functools.partial(chain_body, n),
-        in_specs=[pl.BlockSpec(memory_space=pltpu.VMEM)],
-        out_specs=pl.BlockSpec(memory_space=pl.ANY),
-        out_shape=jax.ShapeDtypeStruct((n,) + x.shape, x.dtype),
+        functools.partial(start_body, n, bits),
+        in_specs=[pl.BlockSpec(memory_space=pltpu.VMEM)] * 3,
+        out_specs=[anywhere] * 3,
+        out_shape=[
+            S((n,) + x.shape, x.dtype),
+            S((n, groups) + w.shape, w.dtype),
+            S((n,) + small.shape, small.dtype),
+        ],
         scratch_shapes=[
-            pltpu.SemaphoreType.DMA((2, n - 1)),
-            pltpu.SemaphoreType.DMA((2, n - 1)),
-            pltpu.SemaphoreType.DMA,
+            pltpu.SemaphoreType.DMA((3, 2, n - 1)),
+            pltpu.SemaphoreType.DMA((3, 2, n - 1)),
+            pltpu.SemaphoreType.DMA((2, groups - 1)),
+            pltpu.SemaphoreType.DMA((2, groups - 1)),
+            pltpu.SemaphoreType.DMA((3,)),
         ],
         compiler_params=pltpu.CompilerParams(collective_id=0, has_side_effects=True),
         cost_estimate=pl.CostEstimate(flops=0, bytes_accessed=200 << 20, transcendentals=0),
-        name="chain_gather",
-    )(x)
+        name="start",
+    )(x, w, small)
 
 
 def weight_grads_body(parts, first_ref, second_ref, attn_ref, inner_ref, active_ref, context_ref, out_ref, ft, st):
@@ -361,25 +439,24 @@
     by_head = lambda q, k, v: jnp.stack([a.reshape(a.shape[:-1] + (heads, HD)) for a in (q, k, v)], -2).reshape(q.shape[:-1] + (3 * own,))
     x_own = hidden_in[0]
     qkv_own = by_head(query_weight, key_weight, value_weight)
-    qkv_all = lax.all_gather(qkv_own, "dp", axis=0, tiled=True)
-    small = jnp.concatenate([segments[0].astype(f32), inner_bias])
-    small = lax.all_gather(small[None], "tensor", axis=0, tiled=True)
+    small = jnp.concatenate([segments[0].astype(f32), inner_bias]).reshape(-1, 128)
+    rest_own = jnp.concatenate([qkv_own, mixer_weight.T, inner_weight, outer_weight.T], 1)
+    x_parts, rest, small = start(x_own, rest_own, small)
+    x_all = x_parts.reshape(parts * rows, width)
+    rest = rest.reshape(parts, width, rest_own.shape[1])
+    small = small.reshape(parts, -1)
     segment_all = small[:, :rows].astype(jnp.int32).reshape(-1)
     inner_bias_all = small[:, rows:]
-    x_parts = chain_gather(x_own)
-    x_all = x_parts.reshape(parts * rows, width)
-    rest_own = jnp.concatenate([inner_weight, outer_weight.T, mixer_weight.T, qkv_own], 1)
-    rest = lax.all_gather(rest_own, ("tensor", "dp"), axis=0, tiled=True)
-    rest = rest.reshape(parts, width, rest_own.shape[1])
+    qkv_all = lax.dynamic_index_in_dim(rest, rank, 0, keepdims=False)[:, : 3 * own]
     biases = by_head(query_bias, jnp.zeros_like(query_bias), value_bias)
 
     qt, ka, vt, qn, kt, vn = project(x_all, qkv_all, biases, segment_all)
     lo, hi = ranges(segment_all, 384, 512)
     context, context_t, lse = attend_forward(0, heads, parts, qt, ka, vt, lo, hi)
     context = lax.all_to_all(context, "tensor", 0, 0, tiled=True)
-    w1 = [rest[t, :, :units] for t in parts_of]
-    w2t = [rest[t, :, units : 2 * units] for t in parts_of]
-    mt = [rest[t, :, 2 * units : 2 * units + own] for t in parts_of]
+    w1 = [rest[t, :, 4 * own : 4 * own + units] for t in parts_of]
+    w2t = [rest[t, :, 4 * own + units :] for t in parts_of]
+    mt = [rest[t, :, 3 * own : 4 * own] for t in parts_of]
     contract = lambda a, b, i, j: lax.dot_general(a, b, (((i,), (j,)), ((), ())), preferred_element_type=f32)
     mixed = sum(contract(context[t], mt[t], 0, 1) for t in parts_of)
     attn_in = x_own.astype(f32) + mixed + mixer_bias
@@ -446,7 +523,7 @@
             back = rotate(grads, "tensor")
         qkv_grad.append(sum(contract(x_parts[p], grads[p], 0, 1) for p in parts_of))
         bias_grad.append(jnp.sum(grads, (0, 2), dtype=f32))
-        at = 2 * units + own + h * three
+        at = h * three
         if h < heads - 1:
             weights = [rest[t, :, at : at + three] for t in parts_of]
         else:

time: 669 us -> 632 us (0.945)
  the two profiles are of different devices: /device:TPU:0 before, /device:TPU:10 now
where the time goes in v1:
time: 632 us; the launch traced here: 621 us
  Pallas kernels  250 us (40%)
  matrix products  117 us (19%)
  waiting for transfers between devices  95.3 us (15%)
  starting transfers between devices  70 us (11%)
  local copies, waits for them, and re-layouts  52.1 us (8%)
  other arithmetic  21.9 us (3%)
  between operations  15.2 us (2%)
    pallas_call x1, Pallas kernels, start(): pl.pallas_call(functools.partial(start_body, n, bits), in_specs=[pl.Block...  111 us
    dot_general x32, matrix products, body(): lax.dot_general(a, b, (((i,), (j,)), ((), ())), preferred_element_type=f32)  81 us
    pallas_call x3, Pallas kernels, attend_backward(): pl.pallas_call(functools.partial(backward_body, BQ, BK, SUB), grid_spec=p...  67.1 us
    pallas_call x1, Pallas kernels, attend_forward(): pl.pallas_call(functools.partial(forward_body, BK, SUB), grid_spec=pltpu....  49.9 us
    ppermute x6, waiting for transfers between devices, rotate(): lax.ppermute(block, axis, [(i, (i + d) % size) for i in range(size)])  31.1 us
    unnamed x114, local copies, waits for them, and re-layouts  27.5 us
    all_to_all x1, starting transfers between devices, body(): lax.all_to_all(jnp.concatenate([qkv_grad, extra], 1), 'dp', 0, 0, tiled=T...  24 us
    all_to_all x1, waiting for transfers between devices, body(): context = lax.all_to_all(context, 'tensor', 0, 0, tiled=True)  23.5 us
  transfers between devices with their start and end apart: 18, of which 13 were waited for; matrix products, arithmetic and copies ran while one was open for 17% of the time, Pallas kernels for 11%

profile of v1, /device:TPU:10, one launch (start us, length us, event | category | flops | bytes accessed | tf_op | source)
XLA Modules:
  0.0 621.2 jit_solution(9734950661379829934)
XLA Ops:
  13.1 1.8 concatenate.55.w_ref
  15.0 111.2 %start.1 = (bf16[4,768,768]{2,1,0:T(8,128)(2,1)}, bf16[4,8,96,2304]{3,2,1,0:T(8,128)(2,1)}, f32[4,12,128]{2,1,0:T(8,128)}) custom-call(bf16[768,768]{1,0:T(8,128)(2,1)} %bitcast.372, bf16[96,2304]{1,0:T(8,128)(2,1)} %concatenate.55.w_ref, f32[12,128]{1,0:T(8,128)} %pad_maximum_fusion.9.s_ref), custom_call_target="tpu_custom_call" | custom-call | bytes 209715200 | tf_op jit(solution)/shard_map/start/pallas_call | solution.py:343
  127.0 10.9 %dynamic-slice_bitcast_fusion = (bf16[768,2304]{1,0:T(8,128)(2,1)}, bf16[768,2304]{1,0:T(8,128)(2,1)}, bf16[768,2304]{1,0:T(8,128)(2,1)}, bf16[768,2304]{1,0:T(8,128)(2,1)}, bf16[768,2304]{1,0:T(8,128)(2,1)S(1)}) fusion(bf16[4,768,2304]{2,1,0:T(8,128)(2,1)} %bitcast.335, s32[]{:T(128)S(6)} %select_n.90, s32[]{:T(128)S(6)} %select_n.86, s32[]{:T(128)S(6)} %select_n.82, ...), kind=kLoop, calls=%fused_computation.2 | loop fusion | bytes 35389460 | tf_op jit(solution)/shard_map/jit(dynamic_index_in_dim)/squeeze | solution.py:531
  139.3 9.9 %project.1 = (bf16[3,128,3072]{2,1,0:T(8,128)(2,1)}, bf16[3,3072,128]{2,1,0:T(8,128)(2,1)}, bf16[3,64,3072]{2,1,0:T(8,128)(2,1)S(1)}, bf16[3,3072,64]{2,1,0:T(8,...) custom-call(bf16[3072,768]{1,0:T(8,128)(2,1)} %bitcast.370, ...), custom_call_target="tpu_custom_call" | custom-call | flops 2717908992 | bytes 17399808 | tf_op jit(solution)/shard_map/project/pallas_call | solution.py:45
  152.0 49.9 %attend_forward.1 = (bf16[4,192,768]{2,1,0:T(8,128)(2,1)}, f32[3,64,3072]{2,1,0:T(8,128)}, f32[3,1,3072]{2,1,0:T(1,128)}) custom-call(s32[8]{0:T(128)} %get-tuple-element.214.lo_ref, s32[8]{0:T(128)} %get-tuple-element.213.hi_ref, bf16[3,128,3072]{2,1,0:T(8,128)(2,1)} %get-tuple-element.32.qt_ref, bf16[3,3072,128]{2,1,0:T(8,128)(2,1)} %get-tuple-element.33.ka_ref, ...), custom_call_target="tpu_custom_call" | custom-call | flops 7247757312 | bytes 9437184 | tf_op jit(solution)/shard_map/attend_forward/pallas_call | solution.py:88
  201.9 6.2 all-to-all-start
  208.1 23.5 %all-to-all-done = bf16[4,192,768]{2,1,0:T(8,128)(2,1)S(1)} async-done(((bf16[4,192,768]{2,1,0:T(8,128)(2,1)}), bf16[4,192,768]{2,1,0:T(8,128)(2,1)S(1)}, u32[]{:S(2)}, u32[]{:S(2)}) %all-to-all-start) | async-done | bytes 1179680 | tf_op jit(solution)/shard_map/all_to_all | solution.py:456
  233.4 1.9 fusion.100
  237.1 2.4 fusion.117
  240.8 4.0 multiply_convert_fusion.2
  246.0 2.9 multiply_convert_fusion.3
  250.0 2.7 multiply_convert_fusion.1
  255.2 1.8 fusion.118
  259.4 1.9 fusion.112
  263.0 2.8 convert_reduce_fusion.3
  265.8 2.8 convert_reduce_fusion.4
  268.5 2.8 convert_reduce_fusion.2
  271.3 2.8 convert_reduce_fusion.1
  276.3 2.5 fusion.64
  278.9 3.8 multiply_reduce_fusion
  284.3 2.0 copy-done.10
  289.6 11.9 %weight_grads.1 = bf16[768,6912]{1,0:T(8,128)(2,1)} custom-call(bf16[768,768]{1,0:T(8,128)(2,1)S(1)} %fusion.33.first_ref, bf16[768,768]{1,0:T(8,128)(2,1)S(1)} %convert_element_type.173.second_ref, bf16[768,768]{1,0:T(8,128)(2,1)S(1)} %convert_element_type.180.attn_ref, bf16[4,768,768]{2,1,0:T(8,128)(2,1)S(1)} %pad_maximum_fusion.inner_ref, ...), custom_call_target="tpu_custom_call" | custom-call | flops 8153726976 | bytes 18874368 | tf_op jit(solution)/shard_map/weight_grads/pallas_call | solution.py:392
  301.6 1.8 fusion.54
  303.3 1.8 fusion.55
  305.1 1.8 fusion.56
  306.9 1.8 fusion.57
  309.6 6.7 %all-to-all-start.1 = ((bf16[4,64,768]{2,1,0:T(8,128)(2,1)}), bf16[4,64,768]{2,1,0:T(8,128)(2,1)S(1)}, u32[]{:S(2)}, u32[]{:S(2)}) async-start(bf16[4,64,768]{2,1,0:T(8,128)(2,1)} %pad_maximum_fusion.6), calls=%async_computation.1 | async-start | bytes 786432 | tf_op jit(solution)/shard_map/all_to_all | solution.py:486
  317.9 7.1 %all-to-all-done.1.go_ref = bf16[4,64,768]{2,1,0:T(8,128)(2,1)S(1)} async-done(((bf16[4,64,768]{2,1,0:T(8,128)(2,1)}), bf16[4,64,768]{2,1,0:T(8,128)(2,1)S(1)}, u32[]{:S(2)}, u32[]{:S(2)}) %all-to-all-start.1) | async-done | bytes 393248 | tf_op jit(solution)/shard_map/all_to_all | solution.py:486
  325.0 6.4 %all-to-all-start.3 = ((bf16[4,128,768]{2,1,0:T(8,128)(2,1)}), bf16[4,128,768]{2,1,0:T(8,128)(2,1)S(1)}, u32[]{:S(2)}, u32[]{:S(2)}) async-start(bf16[4,128,768]{2,1,0:T(8,128)(2,1)} %pad_maximum_fusion.3), calls=%async_computation.3 | async-start | bytes 1572864 | tf_op jit(solution)/shard_map/all_to_all | solution.py:487
  331.4 22.4 %attend_backward.3 = bf16[4,192,768]{2,1,0:T(8,128)(2,1)} custom-call(s32[6]{0:T(128)} %get-tuple-element.161.lo_ref, s32[6]{0:T(128)} %get-tuple-element.160.hi_ref, bf16[4,64,768]{2,1,0:T(8,128)(2,1)} %copy-done.23, f32[3,64,3072]{2,1,0:T(8,128)} %get-tuple-element.36.ot_ref, f32[3,1,3072]{2,1,0:T(1,128)} %get-tuple-element.37.lse_ref, ...), custom_call_target="tpu_custom_call" | custom-call | flops 6039797760 | bytes 5505024 | tf_op jit(solution)/shard_map/attend_backward/pallas_call | solution.py:149
  353.8 1.9 fusion.47
  357.5 1.8 convolution_add_fusion.7
  361.3 2.1 convert_reduce_fusion.7
  364.3 22.4 %attend_backward.4 = bf16[4,192,768]{2,1,0:T(8,128)(2,1)} custom-call(s32[6]{0:T(128)} %get-tuple-element.161.lo_ref, s32[6]{0:T(128)} %get-tuple-element.160.hi_ref, bf16[4,128,768]{2,1,0:T(8,128)(2,1)} %copy-done.22, f32[3,64,3072]{2,1,0:T(8,128)} %get-tuple-element.36.ot_ref, f32[3,1,3072]{2,1,0:T(1,128)} %get-tuple-element.37.lse_ref, ...), custom_call_target="tpu_custom_call" | custom-call | flops 6039797760 | bytes 5505024 | tf_op jit(solution)/shard_map/attend_backward/pallas_call | solution.py:149
  394.0 22.4 %attend_backward.5 = bf16[4,192,768]{2,1,0:T(8,128)(2,1)} custom-call(s32[6]{0:T(128)} %get-tuple-element.161.lo_ref, s32[6]{0:T(128)} %get-tuple-element.160.hi_ref, bf16[4,128,768]{2,1,0:T(8,128)(2,1)} %copy-done.22, f32[3,64,3072]{2,1,0:T(8,128)} %get-tuple-element.36.ot_ref, f32[3,1,3072]{2,1,0:T(1,128)} %get-tuple-element.37.lse_ref, ...), custom_call_target="tpu_custom_call" | custom-call | flops 6039797760 | bytes 5505024 | tf_op jit(solution)/shard_map/attend_backward/pallas_call | solution.py:149
  416.4 1.9 fusion.51
  421.6 2.4 fusion.36
  428.5 24.0 %all-to-all-start.5 = ((bf16[8,112,576]{2,1,0:T(8,128)(2,1)}), bf16[8,112,576]{2,1,0:T(8,128)(2,1)S(1)}, u32[]{:S(2)}, u32[]{:S(2)}) async-start(bf16[8,112,576]{2,1,0:T(8,128)(2,1)} %pad_maximum_fusion.2), calls=%async_computation.5 | async-start | bytes 2293760 | tf_op jit(solution)/shard_map/all_to_all | solution.py:543
  457.4 10.0 %all-to-all-done.5 = bf16[8,112,576]{2,1,0:T(8,128)(2,1)S(1)} async-done(((bf16[8,112,576]{2,1,0:T(8,128)(2,1)}), bf16[8,112,576]{2,1,0:T(8,128)(2,1)S(1)}, u32[]{:S(2)}, u32[]{:S(2)}) %all-to-all-start.5) | async-done | bytes 1032224 | tf_op jit(solution)/shard_map/all_to_all | solution.py:543
  467.4 5.1 all-to-all-start.2
  481.4 2.4 collective-permute-done.7
  484.5 3.3 collective-permute-done.8
  487.8 5.3 collective-permute-done.9
  494.7 4.6 collective-permute-done.10
  503.0 4.4 collective-permute-start.1
  507.4 3.0 fusion.90
  510.4 1.8 collective-permute-done
  512.2 3.0 fusion.88
  515.1 11.7 %collective-permute-done.1 = bf16[192,768]{1,0:T(8,128)(2,1)S(1)} collective-permute-done((bf16[192,768]{1,0:T(8,128)(2,1)S(1)}, bf16[192,768]{1,0:T(8,128)(2,1)S(1)}, u32[]{:S(2)}, u32[]{:S(2)}) %collective-permute-start.1) | collective-permute-done | bytes 294944 | tf_op jit(solution)/shard_map/ppermute | solution.py:422
  526.8 2.9 fusion.86
  529.8 6.3 %all-to-all-start.4 = ((bf16[4,192,768]{2,1,0:T(8,128)(2,1)}), bf16[4,192,768]{2,1,0:T(8,128)(2,1)S(1)}, u32[]{:S(2)}, u32[]{:S(2)}) async-start(bf16[4,192,768]{2,1,0:T(8,128)(2,1)} %attend_backward.4), calls=%async_computation.4 | async-start | bytes 2359296 | tf_op jit(solution)/shard_map/all_to_all | solution.py:521
  541.5 2.9 fusion.98
  544.5 2.9 fusion.99
  547.4 2.9 fusion.97
  550.3 2.9 fusion.96
  553.2 6.7 %all-to-all-done.4 = bf16[4,192,768]{2,1,0:T(8,128)(2,1)S(1)} async-done(((bf16[4,192,768]{2,1,0:T(8,128)(2,1)}), bf16[4,192,768]{2,1,0:T(8,128)(2,1)S(1)}, u32[]{:S(2)}, u32[]{:S(2)}) %all-to-all-start.4) | async-done | bytes 1179680 | tf_op jit(solution)/shard_map/all_to_all | solution.py:521
  559.9 3.2 fusion.94
  563.1 3.2 fusion.95
  566.2 3.2 fusion.93
  569.5 3.2 fusion.92
  578.8 4.2 collective-permute-start.4
  583.0 10.8 %fusion.53 = bf16[1,768,768]{2,1,0:T(8,128)(2,1)} fusion(f32[768,768]{1,0:T(8,128)} %fusion.86, f32[768,768]{1,0:T(8,128)S(1)} %copy-done.5, f32[768,768]{1,0:T(8,128)} %fusion.88, f32[768,768]{1,0:T(8,128)} %fusion.92, f32[768,768]{1,0:T(8,128)} %fusion.93, f32[768,768]{1,0:T(8,128)} %fusion.95, f32[768,768]{1,0:T(8,128)} %fusion.94, ...), kind=kOutput, calls=%fused_computation.118 | convolution fusion | flops 234160128 | bytes 30179328 | tf_op jit(solution)/shard_map/dot_general | solution.py:460
  593.8 13.7 %collective-permute-done.4 = bf16[96,1728]{1,0:T(8,128)(2,1)S(1)} collective-permute-done((bf16[96,1728]{1,0:T(8,128)(2,1)S(1)}, bf16[96,1728]{1,0:T(8,128)(2,1)S(1)}, u32[]{:S(2)}, u32[]{:S(2)}) %collective-permute-start.4) | collective-permute-done | bytes 331808 | tf_op jit(solution)/shard_map/ppermute | solution.py:422
  607.5 3.9 collective-permute-done.5
  (229 shorter events, 87.9 us)
Async XLA Ops:
  139.1 12.2 %copy-start.29 = (s32[6]{0:T(128)}, s32[6]{0:T(128)S(1)}, u32[]{:S(2)}) copy-start(s32[6]{0:T(128)S(1)} %get-tuple-element.154) | copy-start | bytes 76
  139.1 12.2 %copy-start.31 = (s32[6]{0:T(128)}, s32[6]{0:T(128)S(1)}, u32[]{:S(2)}) copy-start(s32[6]{0:T(128)S(1)} %get-tuple-element.155) | copy-start | bytes 76
  149.2 1.1 copy-start
  150.3 1.0 copy-start.1
  201.9 29.7 %all-to-all-start = ((bf16[4,192,768]{2,1,0:T(8,128)(2,1)}), bf16[4,192,768]{2,1,0:T(8,128)(2,1)S(1)}, u32[]{:S(2)}, u32[]{:S(2)}) async-start(bf16[4,192,768]{2,1,0:T(8,128)(2,1)} %get-tuple-element.35), calls=%async_computation | async-start | bytes 2359296 | tf_op jit(solution)/shard_map/all_to_all | solution.py:456
  208.1 364.5 %reduce-scatter.2.cloned.1.call-start = ((), (), s32[]{:S(2)}) async-start(), calls=%async_computation.7 | async-start | bytes 11943936 | tf_op jit(solution)/shard_map/reduce_scatter | solution.py:491
  233.4 3.6 copy-start.7
  233.4 3.6 copy-start.33
  237.0 7.8 %slice-start = ((s8[14155776]{0:T(1024)(128)(4,1)}), s8[4194304]{0:T(1024)(128)(4,1)S(1)}, s32[]{:S(2)}) async-start(s8[14155776]{0:T(1024)(128)(4,1)} %bitcast.353), calls=%async_computation.8 | async-start | bytes 8388608
  237.0 7.8 %slice-start.1 = ((s8[14155776]{0:T(1024)(128)(4,1)}), s8[4194304]{0:T(1024)(128)(4,1)S(1)}, s32[]{:S(2)}) async-start(s8[14155776]{0:T(1024)(128)(4,1)} %bitcast.353), calls=%async_computation.9 | async-start | bytes 8388608
  239.5 0.9 copy-start.24
  239.5 0.9 copy-start.27
  240.4 4.5 slice-start.2
  240.8 4.1 slice-start.3
  244.9 1.2 copy-start.9
  248.9 1.1 copy-start.11
  252.8 1.1 copy-start.13
  253.9 1.2 copy-start.38
  257.0 1.3 copy-start.4
  257.0 1.3 copy-start.25
  257.4 2.0 copy-start.34
  261.3 1.7 copy-start.43
  263.0 2.8 copy-start.42
  265.8 8.3 %copy-start.15 = (bf16[768,768]{1,0:T(8,128)(2,1)}, bf16[768,768]{1,0:T(8,128)(2,1)S(1)}, u32[]{:S(2)}) copy-start(bf16[768,768]{1,0:T(8,128)(2,1)S(1)} %get-tuple-element.210) | copy-start | bytes 3538948
  265.8 2.8 copy-start.41
  268.5 6.7 %copy-start.17 = (bf16[768,768]{1,0:T(8,128)(2,1)}, bf16[768,768]{1,0:T(8,128)(2,1)S(1)}, u32[]{:S(2)}) copy-start(bf16[768,768]{1,0:T(8,128)(2,1)S(1)} %get-tuple-element.212) | copy-start | bytes 3538948
  271.3 5.0 copy-start.19
  284.1 3.5 copy-start.2
  284.2 2.1 copy-start.10
  284.2 2.5 copy-start.12
  284.2 2.8 copy-start.14
  287.0 1.3 copy-start.16
  287.0 1.6 copy-start.18
  287.0 2.0 copy-start.20
  308.7 7.5 %copy-start.30 = (s32[6]{0:T(128)S(1)}, s32[6]{0:T(128)}, u32[]{:S(2)}) copy-start(s32[6]{0:T(128)} %copy-done.29) | copy-start | bytes 76
  308.7 7.5 %copy-start.32 = (s32[6]{0:T(128)S(1)}, s32[6]{0:T(128)}, u32[]{:S(2)}) copy-start(s32[6]{0:T(128)} %copy-done.31) | copy-start | bytes 76
  309.6 15.5 %all-to-all-start.1 = ((bf16[4,64,768]{2,1,0:T(8,128)(2,1)}), bf16[4,64,768]{2,1,0:T(8,128)(2,1)S(1)}, u32[]{:S(2)}, u32[]{:S(2)}) async-start(bf16[4,64,768]{2,1,0:T(8,128)(2,1)} %pad_maximum_fusion.6), calls=%async_computation.1 | async-start | bytes 786432 | tf_op jit(solution)/shard_map/all_to_all | solution.py:486
  325.0 6.4 %copy-start.23 = (bf16[4,64,768]{2,1,0:T(8,128)(2,1)}, bf16[4,64,768]{2,1,0:T(8,128)(2,1)S(1)}, u32[]{:S(2)}) copy-start(bf16[4,64,768]{2,1,0:T(8,128)(2,1)S(1)} %all-to-all-done.1.go_ref) | copy-start | bytes 1179652
  325.0 38.4 %all-to-all-start.3 = ((bf16[4,128,768]{2,1,0:T(8,128)(2,1)}), bf16[4,128,768]{2,1,0:T(8,128)(2,1)S(1)}, u32[]{:S(2)}, u32[]{:S(2)}) async-start(bf16[4,128,768]{2,1,0:T(8,128)(2,1)} %pad_maximum_fusion.3), calls=%async_computation.3 | async-start | bytes 1572864 | tf_op jit(solution)/shard_map/all_to_all | solution.py:487
  363.4 0.9 copy-start.22
  416.4 1.9 copy-start.6
  425.1 1.8 copy-start.28
  428.5 24.3 %copy-start.35 = (f32[768]{0:T(1024)S(1)}, f32[768]{0:T(1024)}, u32[]{:S(2)}) copy-start(f32[768]{0:T(1024)} %get-tuple-element.209) | copy-start | bytes 9220
  428.5 24.3 %copy-start.36 = (f32[768]{0:T(1024)S(1)}, f32[768]{0:T(1024)}, u32[]{:S(2)}) copy-start(f32[768]{0:T(1024)} %get-tuple-element.211) | copy-start | bytes 9220
  428.5 24.3 %copy-start.37 = (f32[768]{0:T(1024)S(1)}, f32[768]{0:T(1024)}, u32[]{:S(2)}) copy-start(f32[768]{0:T(1024)} %get-tuple-element.207) | copy-start | bytes 9220
  428.5 25.0 %copy-start.26 = (f32[768]{0:T(1024)S(1)}, f32[768]{0:T(1024)}, u32[]{:S(2)}) copy-start(f32[768]{0:T(1024)} %get-tuple-element.164) | copy-start | bytes 9220
  428.5 38.9 %all-to-all-start.5 = ((bf16[8,112,576]{2,1,0:T(8,128)(2,1)}), bf16[8,112,576]{2,1,0:T(8,128)(2,1)S(1)}, u32[]{:S(2)}, u32[]{:S(2)}) async-start(bf16[8,112,576]{2,1,0:T(8,128)(2,1)} %pad_maximum_fusion.2), calls=%async_computation.5 | async-start | bytes 2293760 | tf_op jit(solution)/shard_map/all_to_all | solution.py:543
  467.4 62.3 %all-to-all-start.2 = ((bf16[4,192,768]{2,1,0:T(8,128)(2,1)}), bf16[4,192,768]{2,1,0:T(8,128)(2,1)S(1)}, u32[]{:S(2)}, u32[]{:S(2)}) async-start(bf16[4,192,768]{2,1,0:T(8,128)(2,1)} %attend_backward.3), calls=%async_computation.2 | async-start | bytes 2359296 | tf_op jit(solution)/shard_map/all_to_all | solution.py:521
  477.7 1.4 collective-permute-start.6
  479.9 3.9 collective-permute-start.7
  483.8 3.9 collective-permute-start.8
  487.8 5.3 collective-permute-start.9
  493.1 6.2 %collective-permute-start.10 = (f32[7680]{0:T(1024)S(1)}, f32[7680]{0:T(1024)}, u32[]{:S(2)}, u32[]{:S(2)}) collective-permute-start(f32[7680]{0:T(1024)S(1)} %add.418), channel_id=1, source_target_pairs={{0,2},{1,3},{2,0},{3,1},{4,6},{5,7},{6,4},{7,5},{8,10},{9,11},{10,... | collective-permute-start | bytes 92168 | tf_op jit(solution)/shard_map/ppermute | solution.py:410
  500.8 11.3 %collective-permute-start = (bf16[192,768]{1,0:T(8,128)(2,1)S(1)}, bf16[192,768]{1,0:T(8,128)(2,1)S(1)}, u32[]{:S(2)}, u32[]{:S(2)}) collective-permute-start(bf16[192,768]{1,0:T(8,128)(2,1)S(1)} %get-tuple-element.177), channel_id=1, source_target_pairs={{0,1},{1,2},{2,3},{3,0},{4,5},{5,6},{6,7},{7,4},{8,9},{9,10},{10,1... | collective-permute-start | bytes 884744 | tf_op jit(solution)/shard_map/ppermute | solution.py:422
  503.0 23.8 %collective-permute-start.1 = (bf16[192,768]{1,0:T(8,128)(2,1)S(1)}, bf16[192,768]{1,0:T(8,128)(2,1)S(1)}, u32[]{:S(2)}, u32[]{:S(2)}) collective-permute-start(bf16[192,768]{1,0:T(8,128)(2,1)S(1)} %get-tuple-element.176), channel_id=1, source_target_pairs={{0,2},{1,3},{2,0},{3,1},{4,6},{5,7},{6,4},{7,5},{8,10},{9,11},{10,... | collective-permute-start | bytes 884744 | tf_op jit(solution)/shard_map/ppermute | solution.py:422
  507.4 75.6 %collective-permute-start.2 = (bf16[192,768]{1,0:T(8,128)(2,1)}, bf16[192,768]{1,0:T(8,128)(2,1)}, u32[]{:S(2)}, u32[]{:S(2)}) collective-permute-start(bf16[192,768]{1,0:T(8,128)(2,1)} %get-tuple-element.175), channel_id=1, source_target_pairs={{0,3},{1,0},{2,1},{3,2},{4,7},{5,4},{6,5},{7,6},{8,11},{9,8},{10,9... | collective-permute-start | bytes 884744 | tf_op jit(solution)/shard_map/ppermute | solution.py:422
  529.8 30.2 %all-to-all-start.4 = ((bf16[4,192,768]{2,1,0:T(8,128)(2,1)}), bf16[4,192,768]{2,1,0:T(8,128)(2,1)S(1)}, u32[]{:S(2)}, u32[]{:S(2)}) async-start(bf16[4,192,768]{2,1,0:T(8,128)(2,1)} %attend_backward.4), calls=%async_computation.4 | async-start | bytes 2359296 | tf_op jit(solution)/shard_map/all_to_all | solution.py:521
  572.6 1.3 slice-start.4
  572.6 2.4 copy-start.8
  573.9 9.1 %copy-start.3 = (f32[768,768]{1,0:T(8,128)S(1)}, f32[768,768]{1,0:T(8,128)}, u32[]{:S(2)}) copy-start(f32[768,768]{1,0:T(8,128)} %copy-done.2) | copy-start | bytes 7077892
  575.3 7.8 %copy-start.5 = (f32[768,768]{1,0:T(8,128)S(1)}, f32[768,768]{1,0:T(8,128)}, u32[]{:S(2)}) copy-start(f32[768,768]{1,0:T(8,128)} %fusion.90) | copy-start | bytes 7077892
  577.3 16.5 %collective-permute-start.3 = (bf16[96,1728]{1,0:T(8,128)(2,1)S(1)}, bf16[96,1728]{1,0:T(8,128)(2,1)S(1)}, u32[]{:S(2)}, u32[]{:S(2)}) collective-permute-start(bf16[96,1728]{1,0:T(8,128)(2,1)S(1)} %get-tuple-element.172), channel_id=1, source_target_pairs={{0,1},{1,2},{2,3},{3,0},{4,5},{5,6},{6,7},{7,4},{8,9},{9,10},{10,1... | collective-permute-start | bytes 995336 | tf_op jit(solution)/shard_map/ppermute | solution.py:422
  578.8 28.7 %collective-permute-start.4 = (bf16[96,1728]{1,0:T(8,128)(2,1)S(1)}, bf16[96,1728]{1,0:T(8,128)(2,1)S(1)}, u32[]{:S(2)}, u32[]{:S(2)}) collective-permute-start(bf16[96,1728]{1,0:T(8,128)(2,1)S(1)} %get-tuple-element.174), channel_id=1, source_target_pairs={{0,2},{1,3},{2,0},{3,1},{4,6},{5,7},{6,4},{7,5},{8,10},{9,11},{10,... | collective-permute-start | bytes 995336 | tf_op jit(solution)/shard_map/ppermute | solution.py:422
  583.0 28.4 %collective-permute-start.5 = (bf16[96,1728]{1,0:T(8,128)(2,1)S(1)}, bf16[96,1728]{1,0:T(8,128)(2,1)S(1)}, u32[]{:S(2)}, u32[]{:S(2)}) collective-permute-start(bf16[96,1728]{1,0:T(8,128)(2,1)S(1)} %get-tuple-element.173), channel_id=1, source_target_pairs={{0,3},{1,0},{2,1},{3,2},{4,7},{5,4},{6,5},{7,6},{8,11},{9,8},{10,9... | collective-permute-start | bytes 995336 | tf_op jit(solution)/shard_map/ppermute | solution.py:422
  (3 other events, 2.2 us)
Sparse Core Ops, SparseCore 0:
  301.7 90.3 reduce-scatter.1

commit v2 on v1

--- a/solution.py
+++ b/solution.py
@@ -18,8 +18,8 @@
 def dot(a,b): return jnp.dot(a,b,preferred_element_type=jnp.float32)
 
 
-def project_body(heads, x_ref, w_ref, b_ref, scol_ref, srow_ref, qt_ref, ka_ref, vt_ref, qn_ref, kt_ref, vn_ref):
-    y = dot(x_ref[...], w_ref[...]) + b_ref[...]
+def project_body(heads, part_ref, x_ref, w_ref, b_ref, scol_ref, srow_ref, qt_ref, ka_ref, vt_ref, qn_ref, kt_ref, vn_ref):
+    y = dot(x_ref[...], w_ref[0,:,:b_ref.shape[1]]) + b_ref[...]
     low = y.astype(jnp.bfloat16)
     yt = y.T.astype(jnp.bfloat16)
     rows = y.shape[0]
@@ -36,20 +36,22 @@
         vn_ref[h]=low[:,at+2*HD:at+3*HD]
 
 
-def project(x,w,b,seg,rows=512):
-    L,D=x.shape; heads=w.shape[1]//(3*HD)
+def project(x,rest,part,b,seg,rows=512):
+    L,D=x.shape; heads=b.shape[0]//(3*HD)
     bf=jnp.bfloat16
-    nat=lambda n: pl.BlockSpec((heads,rows,n),lambda i:(0,i,0))
-    tr=lambda n: pl.BlockSpec((heads,n,rows),lambda i:(0,0,i))
+    cols=4*heads*HD
+    nat=lambda n: pl.BlockSpec((heads,rows,n),lambda i,*_:(0,i,0))
+    tr=lambda n: pl.BlockSpec((heads,n,rows),lambda i,*_:(0,0,i))
     S=jax.ShapeDtypeStruct
-    return pl.pallas_call(functools.partial(project_body,heads),grid=(L//rows,),
-        in_specs=[pl.BlockSpec((rows,D),lambda i:(i,0)),pl.BlockSpec(w.shape,lambda i:(0,0)),pl.BlockSpec((1,w.shape[1]),lambda i:(0,0)),
-                  pl.BlockSpec((rows,1),lambda i:(i,0)),pl.BlockSpec((1,rows),lambda i:(0,i))],
-        out_specs=[tr(2*HD),nat(2*HD),tr(HD),nat(HD),tr(HD),nat(HD)],
+    return pl.pallas_call(functools.partial(project_body,heads),
+        grid_spec=pltpu.PrefetchScalarGridSpec(num_scalar_prefetch=1,grid=(L//rows,),
+        in_specs=[pl.BlockSpec((rows,D),lambda i,*_:(i,0)),pl.BlockSpec((1,D,cols),lambda i,p:(p[0],0,0)),pl.BlockSpec((1,b.shape[0]),lambda i,*_:(0,0)),
+                  pl.BlockSpec((rows,1),lambda i,*_:(i,0)),pl.BlockSpec((1,rows),lambda i,*_:(0,i))],
+        out_specs=[tr(2*HD),nat(2*HD),tr(HD),nat(HD),tr(HD),nat(HD)]),
         out_shape=[S((heads,2*HD,L),bf),S((heads,L,2*HD),bf),S((heads,HD,L),bf),S((heads,L,HD),bf),S((heads,HD,L),bf),S((heads,L,HD),bf)],
         compiler_params=pltpu.CompilerParams(vmem_limit_bytes=48<<20),
-        cost_estimate=pl.CostEstimate(flops=2*L*D*w.shape[1],bytes_accessed=L*D*2+w.size*2+L*heads*HD*2*10,transcendentals=0),
-        name="project")(x,w,b.reshape(1,-1),seg.reshape(-1,1),seg.reshape(1,-1))
+        cost_estimate=pl.CostEstimate(flops=2*L*D*b.shape[0],bytes_accessed=L*D*2+D*cols*2+L*heads*HD*2*10,transcendentals=0),
+        name="project")(part.reshape(1),x,rest,b.reshape(1,-1),seg.reshape(-1,1),seg.reshape(1,-1))
 
 
 def forward_body(BK, SUB, lo_ref, hi_ref, qt_ref, ka_ref, vt_ref, ctx_ref, ot_ref, lse_ref, m_s, l_s, acc):
@@ -96,7 +98,9 @@
         name="attend_forward")(lo,hi,qt,ka,vt)
 
 
-def backward_body(BQ, BK, SUB, lo_ref, hi_ref, go_ref, ot_ref, lse_ref, qt_ref, ka_ref, qn_ref, kt_ref, vn_ref, out_ref, got, gon, delta, dqt, dkt, dvt, dk_s, dv_s):
+def backward_body(BQ, BK, SUB, lo_ref, hi_ref, go_ref, ot_ref, lse_ref, qt_ref, ka_ref, qn_ref, kt_ref, vn_ref, x_ref, out_ref, wg_ref, sum_ref, got, gon, delta, dqt, dkt, dvt, dk_s, dv_s, x_s, x_sem):
+    bring=pltpu.make_async_copy(x_ref,x_s,x_sem)
+    bring.start()
     parts,_,rows=go_ref.shape
     heads,_,L=qt_ref.shape
     CH=256
@@ -140,21 +144,31 @@
             out_ref[p,3*h*HD:(3*h+1)*HD,:]=(dqt[h,:,cut]*SCALE).astype(jnp.bfloat16)
             out_ref[p,(3*h+1)*HD:(3*h+2)*HD,:]=dkt[h,:,cut]
             out_ref[p,(3*h+2)*HD:(3*h+3)*HD,:]=dvt[h,:,cut]
-
-
-def attend_backward(first,heads,go,go_first,ot,lse,qt,ka,qn,kt,vn,lo,hi,BQ=512,BK=512,SUB=512):
-    parts,_,rows=go.shape; L=parts*rows
+    bring.wait()
+    wg=jnp.zeros(wg_ref.shape[::-1],jnp.float32)
+    total=jnp.zeros((3*heads*HD,1),jnp.float32)
+    for p in range(parts):
+        part=out_ref[p]
+        wg=wg+dot(part,x_s[p])
+        total=total+jnp.sum(part.astype(jnp.float32),axis=1,keepdims=True)
+    wg_ref[...]=wg.T.astype(wg_ref.dtype)
+    sum_ref[...]=jnp.broadcast_to(total,sum_ref.shape)
+
+
+def attend_backward(first,heads,go,go_first,ot,lse,ot_first,qt,ka,qn,kt,vn,x,lo,hi,BQ=512,BK=512,SUB=512):
+    parts,_,rows=go.shape; L=parts*rows; D=x.shape[2]
     S=jax.ShapeDtypeStruct; f32=jnp.float32; bf=jnp.bfloat16
-    some=lambda a: pl.BlockSpec((heads,)+a.shape[1:],lambda i,*_:(first//heads,0,0),pipeline_mode=pl.Buffered(1))
+    at=lambda a,n: pl.BlockSpec((heads,)+a.shape[1:],lambda i,*_:(n//heads,0,0),pipeline_mode=pl.Buffered(1))
+    out=3*heads*HD
     return pl.pallas_call(functools.partial(backward_body,BQ,BK,SUB),
         grid_spec=pltpu.PrefetchScalarGridSpec(num_scalar_prefetch=2,grid=(1,),
-        in_specs=[pl.BlockSpec((parts,heads*HD,rows),lambda i,*_:(0,go_first,0),pipeline_mode=pl.Buffered(1))]+[some(a) for a in (ot,lse,qt,ka,qn,kt,vn)],
-        out_specs=pl.BlockSpec((parts,3*heads*HD,rows),lambda i,*_:(0,0,0),pipeline_mode=pl.Buffered(1)),
-        scratch_shapes=[VM((heads,HD,L),bf),VM((heads,L,HD),bf),VM((heads,1,L),f32),VM((heads,HD,L),f32),VM((heads,HD,L),bf),VM((heads,HD,L),bf),VM((heads,BK,HD),f32),VM((heads,BK,HD),f32)]),
-        out_shape=S((parts,3*heads*HD,rows),bf),
+        in_specs=[pl.BlockSpec((parts,heads*HD,rows),lambda i,*_:(0,go_first,0),pipeline_mode=pl.Buffered(1)),at(ot,ot_first),at(lse,ot_first)]+[at(a,first) for a in (qt,ka,qn,kt,vn)]+[pl.BlockSpec(memory_space=pl.ANY)],
+        out_specs=[pl.BlockSpec((parts,out,rows),lambda i,*_:(0,0,0),pipeline_mode=pl.Buffered(1)),pl.BlockSpec((D,out),lambda i,*_:(0,0)),pl.BlockSpec((out,128),lambda i,*_:(0,0))],
+        scratch_shapes=[VM((heads,HD,L),bf),VM((heads,L,HD),bf),VM((heads,1,L),f32),VM((heads,HD,L),f32),VM((heads,HD,L),bf),VM((heads,HD,L),bf),VM((heads,BK,HD),f32),VM((heads,BK,HD),f32),VM(x.shape,bf),pltpu.SemaphoreType.DMA]),
+        out_shape=[S((parts,out,rows),bf),S((D,out),bf),S((out,128),f32)],
         compiler_params=pltpu.CompilerParams(vmem_limit_bytes=60<<20),
         cost_estimate=pl.CostEstimate(flops=2*L*L*HD*5*heads,bytes_accessed=L*heads*HD*2*14,transcendentals=L*L*heads),
-        name="attend_backward")(lo,hi,go,ot,lse,qt,ka,qn,kt,vn)
+        name="attend_backward")(lo,hi,go,ot,lse,qt,ka,qn,kt,vn,x)
 
 
 def ranges(seg,BQ,BK):
@@ -402,12 +416,69 @@
     )(first_low, second_low, attn_low, grad_inner, active, context)
 
 
+def early_back_body(w_ref, b0_ref, b1_ref, acc_ref):
+    width = b0_ref.shape[1]
+    total = jnp.zeros(acc_ref.shape, jnp.float32)
+    for t in range(b0_ref.shape[0]):
+        total = total + dot(w_ref[t, :, : 2 * width], jnp.concatenate([b0_ref[t], b1_ref[t]], axis=0))
+    acc_ref[...] = total
+
+
+def late_back_body(cut, part_ref, w_ref, acc_ref, grad_ref, *rest):
+    backs, out_ref = rest[:-1], rest[-1]
+    parts = len(backs)
+    total = acc_ref[...]
+    for d in range(parts):
+        total = total + dot(w_ref[(part_ref[0] + parts - d) % parts, :, cut : cut + backs[d].shape[0]], backs[d][...])
+    out_ref[...] = (total.T + grad_ref[...]).astype(out_ref.dtype)
+
+
+def weight_block(rest, cols):
+    return pl.BlockSpec(rest.shape[:2] + (cols,), lambda i, *_: (0, 0, 0), pipeline_mode=pl.Buffered(1))
+
+
+def whole(a):
+    return pl.BlockSpec(a.shape, lambda i, *_: (0,) * a.ndim, pipeline_mode=pl.Buffered(1))
+
+
+def early_back(rest, cols, b0, b1):
+    width, rows = rest.shape[1], b0.shape[2]
+    return pl.pallas_call(
+        early_back_body,
+        grid=(1,),
+        in_specs=[weight_block(rest, cols), whole(b0), whole(b1)],
+        out_specs=pl.BlockSpec((width, rows), lambda i: (0, 0)),
+        out_shape=jax.ShapeDtypeStruct((width, rows), jnp.float32),
+        compiler_params=pltpu.CompilerParams(vmem_limit_bytes=40 << 20),
+        cost_estimate=pl.CostEstimate(flops=4 * width * rows * b0.shape[0] * b0.shape[1], bytes_accessed=10 << 20, transcendentals=0),
+        name="early_back",
+    )(rest, b0, b1)
+
+
+def late_back(rest, cols, cut, part, acc, grad, backs):
+    rows, width = grad.shape
+    return pl.pallas_call(
+        functools.partial(late_back_body, cut),
+        grid_spec=pltpu.PrefetchScalarGridSpec(
+            num_scalar_prefetch=1,
+            grid=(1,),
+            in_specs=[weight_block(rest, cols), whole(acc), whole(grad)] + [whole(b) for b in backs],
+            out_specs=pl.BlockSpec((rows, width), lambda i, *_: (0, 0)),
+        ),
+        out_shape=jax.ShapeDtypeStruct((rows, width), jnp.bfloat16),
+        compiler_params=pltpu.CompilerParams(vmem_limit_bytes=40 << 20),
+        cost_estimate=pl.CostEstimate(flops=2 * width * rows * backs[0].shape[0] * len(backs), bytes_accessed=10 << 20, transcendentals=0),
+        name="late_back",
+    )(part.reshape(1), rest, acc, grad, *backs)
+
+
 def add_up(value):
     for axis in ("dp", "tensor"):
         size = lax.axis_size(axis)
         span = 1
         while span < size:
-            value = value + lax.ppermute(value, axis, [(i, i ^ span) for i in range(size)])
+            other = lax.ppermute(value, axis, [(i, i ^ span) for i in range(size)])
+            value = value + other
             span *= 2
     return value
 
@@ -447,13 +518,18 @@
     small = small.reshape(parts, -1)
     segment_all = small[:, :rows].astype(jnp.int32).reshape(-1)
     inner_bias_all = small[:, rows:]
-    qkv_all = lax.dynamic_index_in_dim(rest, rank, 0, keepdims=False)[:, : 3 * own]
     biases = by_head(query_bias, jnp.zeros_like(query_bias), value_bias)
 
-    qt, ka, vt, qn, kt, vn = project(x_all, qkv_all, biases, segment_all)
+    qt, ka, vt, qn, kt, vn = project(x_all, rest, rank, biases, segment_all)
     lo, hi = ranges(segment_all, 384, 512)
-    context, context_t, lse = attend_forward(0, heads, parts, qt, ka, vt, lo, hi)
-    context = lax.all_to_all(context, "tensor", 0, 0, tiled=True)
+    lead = heads - 1
+    context_t, lse, exchanged = [], [], []
+    for call, (first, count) in enumerate(((0, lead), (lead, 1))):
+        part, out_t, out_lse = attend_forward(first, count, parts, qt, ka, vt, lo, hi)
+        context_t.append(out_t)
+        lse.append(out_lse)
+        exchanged.append(lax.all_to_all(part, "tensor", 0, 0, tiled=True))
+    context = jnp.concatenate(exchanged, 1)
     w1 = [rest[t, :, 4 * own : 4 * own + units] for t in parts_of]
     w2t = [rest[t, :, 4 * own + units :] for t in parts_of]
     mt = [rest[t, :, 3 * own : 4 * own] for t in parts_of]
@@ -512,32 +588,25 @@
     early = add_up(early)
 
     lo, hi = ranges(segment_all, 512, 512)
-    input_back = grad_attn
-    qkv_grad = []
-    bias_grad = []
+    backs, qkv_grad, bias_grad = [], [], []
     for h in range(heads):
-        grads = attend_backward(h, 1, go1 if h else go0, h - 1 if h else 0, context_t, lse, qt, ka, qn, kt, vn, lo, hi)
+        call = 0 if h < lead else 1
+        grads, weight_part, sums = attend_backward(
+            h, 1, go1 if h else go0, h - 1 if h else 0, context_t[call], lse[call], h - call * lead, qt, ka, qn, kt, vn, x_parts, lo, hi
+        )
         if h < heads - 1:
-            back = lax.all_to_all(grads, "tensor", 0, 0, tiled=True)
+            backs.append(lax.all_to_all(grads, "tensor", 0, 0, tiled=True))
         else:
-            back = rotate(grads, "tensor")
-        qkv_grad.append(sum(contract(x_parts[p], grads[p], 0, 1) for p in parts_of))
-        bias_grad.append(jnp.sum(grads, (0, 2), dtype=f32))
-        at = h * three
-        if h < heads - 1:
-            weights = [rest[t, :, at : at + three] for t in parts_of]
-        else:
-            weights = [
-                lax.dynamic_index_in_dim(rest, (rank - t) % parts, 0, keepdims=False)[:, at : at + three]
-                for t in parts_of
-            ]
-        input_back = input_back + sum(contract(back[t], weights[t], 0, 1) for t in parts_of)
-    input_grad = input_back.astype(bf)
+            backs.append(rotate(grads, "tensor"))
+        qkv_grad.append(weight_part)
+        bias_grad.append(sums[:, 0])
+    input_back = early_back(rest, 4 * own, backs[0], backs[1])
+    input_grad = late_back(rest, 4 * own, 2 * three, rank, input_back, grad_attn, backs[2])
     bias_grad = jnp.concatenate(bias_grad)
     high = bias_grad.astype(bf)
     low = (bias_grad - high.astype(f32)).astype(bf)
     each = width // groups
-    qkv_grad = jnp.concatenate(qkv_grad, 1).astype(bf).reshape(groups, each, 3 * own)
+    qkv_grad = jnp.concatenate(qkv_grad, 1).reshape(groups, each, 3 * own)
     extra = jnp.pad(jnp.stack([high, low]), ((0, 14), (0, 0)))
     extra = jnp.broadcast_to(extra[None], (groups, 16, 3 * own))
     qkv_grad = lax.all_to_all(jnp.concatenate([qkv_grad, extra], 1), "dp", 0, 0, tiled=True)

time: 632 us -> 580 us (0.918)
  the two profiles are of different devices: /device:TPU:10 before, /device:TPU:0 now
where the time goes in v2:
time: 580 us; the launch traced here: 574 us
  Pallas kernels  301 us (52%)
  starting transfers between devices  71.5 us (12%)
  local copies, waits for them, and re-layouts  56.4 us (10%)
  matrix products  47.1 us (8%)
  waiting for transfers between devices  39.6 us (7%)
  other arithmetic  23.5 us (4%)
  blocking collectives  19.5 us (3%)
  between operations  15.4 us (3%)
    pallas_call x1, Pallas kernels, start(): pl.pallas_call(functools.partial(start_body, n, bits), in_specs=[pl.Block...  115 us
    pallas_call x3, Pallas kernels, attend_backward(): pl.pallas_call(functools.partial(backward_body, BQ, BK, SUB), grid_spec=p...  83.7 us
    pallas_call x2, Pallas kernels, attend_forward(): pl.pallas_call(functools.partial(forward_body, BK, SUB), grid_spec=pltpu....  69.9 us
    ppermute x6, starting transfers between devices, rotate(): lax.ppermute(block, axis, [(i, (i + d) % size) for i in range(size)])  39.5 us
    unnamed x105, local copies, waits for them, and re-layouts  31.3 us
    dot_general x8, matrix products, dot(): return jnp.dot(a, b, preferred_element_type=jnp.float32)  19.9 us
    all_to_all x1, blocking collectives, body(): lax.all_to_all(jnp.concatenate([qkv_grad, extra], 1), 'dp', 0, 0, tiled=T...  19.5 us
    dot_general x8, matrix products, body(): lax.dot_general(a, b, (((i,), (j,)), ((), ())), preferred_element_type=f32)  16 us
  transfers between devices with their start and end apart: 18, of which 9 were waited for; matrix products, arithmetic and copies ran while one was open for 9% of the time, Pallas kernels for 21%

profile of v2, /device:TPU:0, one launch (start us, length us, event | category | flops | bytes accessed | tf_op | source)
XLA Modules:
  0.0 574.0 jit_solution(9080144311691520841)
XLA Ops:
  13.1 1.8 concatenate.50.w_ref
  14.9 114.7 %start.1 = (bf16[4,768,768]{2,1,0:T(8,128)(2,1)}, bf16[4,8,96,2304]{3,2,1,0:T(8,128)(2,1)}, f32[4,12,128]{2,1,0:T(8,128)}) custom-call(bf16[768,768]{1,0:T(8,128)(2,1)} %bitcast.237, bf16[96,2304]{1,0:T(8,128)(2,1)} %concatenate.50.w_ref, f32[12,128]{1,0:T(8,128)} %pad_maximum_fusion.10.s_ref), custom_call_target="tpu_custom_call" | custom-call | bytes 209715200 | tf_op jit(solution)/shard_map/start/pallas_call | solution.py:357
  132.5 10.3 %project.1 = (bf16[3,128,3072]{2,1,0:T(8,128)(2,1)}, bf16[3,3072,128]{2,1,0:T(8,128)(2,1)}, bf16[3,64,3072]{2,1,0:T(8,128)(2,1)S(1)}, bf16[3,3072,64]{2,1,0:T(8,...) custom-call(s32[1]{0:T(128)} %bitcast.8.part_ref, bf16[3072,768]{1,0:T(8,128)(2,1)} %bitcast.240, ...), custom_call_target="tpu_custom_call" | custom-call | flops 2717908992 | bytes 17694720 | tf_op jit(solution)/shard_map/project/pallas_call | solution.py:46
  144.8 43.9 %attend_forward.2 = (bf16[4,128,768]{2,1,0:T(8,128)(2,1)}, f32[2,64,3072]{2,1,0:T(8,128)}, f32[2,1,3072]{2,1,0:T(1,128)}) custom-call(s32[8]{0:T(128)} %get-tuple-element.217.lo_ref, s32[8]{0:T(128)} %get-tuple-element.216.hi_ref, bf16[3,128,3072]{2,1,0:T(8,128)(2,1)} %get-tuple-element.44.qt_ref, bf16[3,3072,128]{2,1,0:T(8,128)(2,1)} %get-tuple-element.45.ka_ref, ...), custom_call_target="tpu_custom_call" | custom-call | flops 4831838208 | bytes 6291456 | tf_op jit(solution)/shard_map/attend_forward/pallas_call | solution.py:90
  188.7 3.5 all-to-all-start
  192.2 26.0 %attend_forward.3 = (bf16[4,64,768]{2,1,0:T(8,128)(2,1)}, f32[1,64,3072]{2,1,0:T(8,128)}, f32[1,1,3072]{2,1,0:T(1,128)}) custom-call(s32[8]{0:T(128)} %get-tuple-element.217.lo_ref, s32[8]{0:T(128)} %get-tuple-element.216.hi_ref, bf16[3,128,3072]{2,1,0:T(8,128)(2,1)} %get-tuple-element.44.qt_ref, bf16[3,3072,128]{2,1,0:T(8,128)(2,1)} %get-tuple-element.45.ka_ref, ...), custom_call_target="tpu_custom_call" | custom-call | flops 2415919104 | bytes 3145728 | tf_op jit(solution)/shard_map/attend_forward/pallas_call | solution.py:90
  218.2 5.0 all-to-all-start.1
  223.9 8.3 %all-to-all-done.1 = bf16[4,64,768]{2,1,0:T(8,128)(2,1)S(1)} async-done(((bf16[4,64,768]{2,1,0:T(8,128)(2,1)}), bf16[4,64,768]{2,1,0:T(8,128)(2,1)S(1)}, u32[]{:S(2)}, u32[]{:S(2)}) %all-to-all-start.1) | async-done | bytes 393248 | tf_op jit(solution)/shard_map/all_to_all | solution.py:531
  232.2 2.2 fusion.53
  234.4 1.9 fusion.51
  236.2 1.8 fusion.52
  238.0 2.4 fusion.65
  241.8 4.0 multiply_convert_fusion
  250.5 3.0 multiply_convert_fusion.2
  254.6 1.8 fusion.66
  258.9 2.5 fusion.60
  261.6 1.5 copy-done.38
  263.1 2.2 convert_reduce_fusion.1
  265.3 2.8 convert_reduce_fusion.2
  269.2 2.8 convert_reduce_fusion.4
  274.1 2.8 convert_reduce_fusion.3
  278.0 2.7 multiply_reduce_fusion
  280.7 1.5 fusion.62
  287.1 11.9 %weight_grads.1 = bf16[768,6912]{1,0:T(8,128)(2,1)} custom-call(bf16[768,768]{1,0:T(8,128)(2,1)S(1)} %fusion.33.first_ref, bf16[768,768]{1,0:T(8,128)(2,1)S(1)} %convert_element_type.161.second_ref, bf16[768,768]{1,0:T(8,128)(2,1)S(1)} %convert_element_type.166.attn_ref, bf16[4,768,768]{2,1,0:T(8,128)(2,1)S(1)} %pad_maximum_fusion.inner_ref, ...), custom_call_target="tpu_custom_call" | custom-call | flops 8153726976 | bytes 18874368 | tf_op jit(solution)/shard_map/weight_grads/pallas_call | solution.py:406
  299.0 1.8 fusion.38
  300.8 2.0 fusion.37
  302.9 1.9 fusion.36
  304.8 2.0 fusion.35
  308.3 3.5 all-to-all-start.2
  311.8 2.4 pad_maximum_fusion.4
  314.1 7.9 %all-to-all-done.2.go_ref = bf16[4,64,768]{2,1,0:T(8,128)(2,1)S(1)} async-done(((bf16[4,64,768]{2,1,0:T(8,128)(2,1)}), bf16[4,64,768]{2,1,0:T(8,128)(2,1)S(1)}, u32[]{:S(2)}, u32[]{:S(2)}) %all-to-all-start.2) | async-done | bytes 393248 | tf_op jit(solution)/shard_map/all_to_all | solution.py:562
  322.0 3.8 all-to-all-start.4
  326.5 27.9 %attend_backward.3 = (bf16[4,192,768]{2,1,0:T(8,128)(2,1)}, bf16[768,192]{1,0:T(8,128)(2,1)}, f32[192,128]{1,0:T(8,128)}) custom-call(s32[6]{0:T(128)} %get-tuple-element.168.lo_ref, s32[6]{0:T(128)} %get-tuple-element.167.hi_ref, bf16[4,64,768]{2,1,0:T(8,128)(2,1)} %copy-done.26, f32[2,64,3072]{2,1,0:T(8,128)} %get-tuple-element.49.ot_ref, ...), custom_call_target="tpu_custom_call" | custom-call | flops 6039797760 | bytes 5505024 | tf_op jit(solution)/shard_map/attend_backward/pallas_call | solution.py:163
  356.3 27.9 %attend_backward.5 = (bf16[4,192,768]{2,1,0:T(8,128)(2,1)}, bf16[768,192]{1,0:T(8,128)(2,1)}, f32[192,128]{1,0:T(8,128)}) custom-call(s32[6]{0:T(128)} %get-tuple-element.168.lo_ref, s32[6]{0:T(128)} %get-tuple-element.167.hi_ref, bf16[4,128,768]{2,1,0:T(8,128)(2,1)} %copy-done.24, f32[1,64,3072]{2,1,0:T(8,128)} %get-tuple-element.56.ot_ref, ...), custom_call_target="tpu_custom_call" | custom-call | flops 6039797760 | bytes 5505024 | tf_op jit(solution)/shard_map/attend_backward/pallas_call | solution.py:163
  385.2 28.0 %attend_backward.4 = (bf16[4,192,768]{2,1,0:T(8,128)(2,1)}, bf16[768,192]{1,0:T(8,128)(2,1)}, f32[192,128]{1,0:T(8,128)}) custom-call(s32[6]{0:T(128)} %get-tuple-element.168.lo_ref, s32[6]{0:T(128)} %get-tuple-element.167.hi_ref, bf16[4,128,768]{2,1,0:T(8,128)(2,1)} %copy-done.24, f32[2,64,3072]{2,1,0:T(8,128)} %get-tuple-element.49.ot_ref, ...), custom_call_target="tpu_custom_call" | custom-call | flops 6039797760 | bytes 5505024 | tf_op jit(solution)/shard_map/attend_backward/pallas_call | solution.py:163
  415.9 19.5 %all_to_all.35 = bf16[8,112,576]{2,1,0:T(8,128)(2,1)} all-to-all(bf16[8,112,576]{2,1,0:T(8,128)(2,1)S(1)} %pad_maximum_fusion.2), channel_id=1, replica_groups=mesh['dp'=8,'tensor'=4] {'dp'}, dimensions={0} | all-to-all | bytes 2064384 | tf_op jit(solution)/shard_map/all_to_all | solution.py:612
  435.4 5.1 all-to-all-start.3
  440.4 2.1 convert_reduce_fusion
  455.1 1.4 collective-permute-done.6
  457.8 3.4 collective-permute-done.7
  461.7 3.4 collective-permute-done.8
  465.1 2.0 collective-permute-start.9
  467.1 2.3 collective-permute-done.9
  470.0 2.5 collective-permute-start.10
  472.6 2.6 collective-permute-done.10
  476.6 5.0 all-to-all-start.5
  481.7 2.3 dynamic-slice_bitcast_fusion.3
  484.0 2.0 collective-permute-start
  486.0 2.4 collective-permute-start.1
  488.4 1.5 collective-permute-start.2
  491.5 1.8 copy.109
  493.3 1.7 fusion.63
  495.0 1.6 copy.112
  496.7 1.6 copy.113
  498.3 1.6 copy.114
  500.8 1.6 slice.254
  502.4 1.8 reshape.276
  508.2 1.5 collective-permute-start.4
  509.7 3.0 collective-permute-done.rest_1_
  512.7 31.6 %collective-permute-start.3 = (bf16[96,1728]{1,0:T(8,128)(2,1)}, bf16[96,1728]{1,0:T(8,128)(2,1)}, u32[]{:S(2)}, u32[]{:S(2)}) collective-permute-start(bf16[96,1728]{1,0:T(8,128)(2,1)} %get-tuple-element.174), channel_id=1, source_target_pairs={{0,1},{1,2},{2,3},{3,0},{4,5},{5,6},{6,7},{7,4},{8,9},{9,10},{10,1... | collective-permute-start | bytes 995336 | tf_op jit(solution)/shard_map/ppermute | solution.py:493
  545.6 5.4 early_back.1.acc_ref
  551.0 5.2 late_back.1
  556.3 7.3 %collective-permute-done.4 = bf16[96,1728]{1,0:T(8,128)(2,1)} collective-permute-done((bf16[96,1728]{1,0:T(8,128)(2,1)}, bf16[96,1728]{1,0:T(8,128)(2,1)}, u32[]{:S(2)}, u32[]{:S(2)}) %collective-permute-start.4) | collective-permute-done | bytes 331808 | tf_op jit(solution)/shard_map/ppermute | solution.py:493
  563.6 1.4 fusion.50
  (197 shorter events, 63.9 us)
Async XLA Ops:
  7.2 123.6 %copy-start.35 = (f32[192]{0:T(256)S(1)}, f32[192]{0:T(256)}, u32[]{:S(2)}) copy-start(f32[192]{0:T(256)} %param.24) | copy-start | bytes 2308
  7.2 123.7 %copy-start.36 = (f32[192]{0:T(256)S(1)}, f32[192]{0:T(256)}, u32[]{:S(2)}) copy-start(f32[192]{0:T(256)} %param.23) | copy-start | bytes 2308
  142.7 1.0 copy-start.3
  143.8 1.0 copy-start.4
  188.7 29.6 %all-to-all-start = ((bf16[4,128,768]{2,1,0:T(8,128)(2,1)}), bf16[4,128,768]{2,1,0:T(8,128)(2,1)S(1)}, u32[]{:S(2)}, u32[]{:S(2)}) async-start(bf16[4,128,768]{2,1,0:T(8,128)(2,1)} %get-tuple-element.47), calls=%async_computation | async-start | bytes 1572864 | tf_op jit(solution)/shard_map/all_to_all | solution.py:531
  218.2 13.9 %all-to-all-start.1 = ((bf16[4,64,768]{2,1,0:T(8,128)(2,1)}), bf16[4,64,768]{2,1,0:T(8,128)(2,1)S(1)}, u32[]{:S(2)}, u32[]{:S(2)}) async-start(bf16[4,64,768]{2,1,0:T(8,128)(2,1)} %get-tuple-element.48), calls=%async_computation.1 | async-start | bytes 786432 | tf_op jit(solution)/shard_map/all_to_all | solution.py:531
  223.2 277.6 %reduce-scatter.2.cloned.1.call-start = ((), (), s32[]{:S(2)}) async-start(), calls=%async_computation.8 | async-start | bytes 11943936 | tf_op jit(solution)/shard_map/reduce_scatter | solution.py:567
  232.1 5.8 %copy-start = (bf16[4,192,768]{2,1,0:T(8,128)(2,1)}, bf16[4,192,768]{2,1,0:T(8,128)(2,1)S(1)}, u32[]{:S(2)}) copy-start(bf16[4,192,768]{2,1,0:T(8,128)(2,1)S(1)} %constant_dynamic-update-slice_fusion) | copy-start | bytes 3538948
  234.3 3.7 copy-start.7
  234.4 3.7 copy-start.32
  238.0 7.8 %slice-start = ((s8[14155776]{0:T(1024)(128)(4,1)}), s8[4194304]{0:T(1024)(128)(4,1)S(1)}, s32[]{:S(2)}) async-start(s8[14155776]{0:T(1024)(128)(4,1)} %bitcast.219), calls=%async_computation.9 | async-start | bytes 8388608
  238.0 7.8 %slice-start.1 = ((s8[14155776]{0:T(1024)(128)(4,1)}), s8[4194304]{0:T(1024)(128)(4,1)S(1)}, s32[]{:S(2)}) async-start(s8[14155776]{0:T(1024)(128)(4,1)} %bitcast.219), calls=%async_computation.10 | async-start | bytes 8388608
  240.5 0.9 copy-start.29
  240.5 0.9 copy-start.31
  241.4 4.5 slice-start.2
  241.8 4.0 slice-start.3
  249.4 1.1 copy-start.13
  253.5 1.1 copy-start.15
  253.5 1.1 copy-start.34
  256.5 1.3 copy-start.5
  256.5 1.3 copy-start.30
  256.9 2.0 copy-start.33
  261.5 1.7 copy-start.38
  268.1 1.1 copy-start.17
  272.0 1.1 copy-start.19
  272.0 2.1 copy-start.37
  276.9 1.1 copy-start.21
  282.2 1.3 copy-start.18
  282.2 1.6 copy-start.20
  282.2 2.0 copy-start.22
  284.2 1.3 copy-start.14
  284.2 1.6 copy-start.16
  285.8 1.3 copy-start.1
  300.8 6.0 %copy-start.9 = (bf16[1,192,768]{2,1,0:T(8,128)(2,1)}, bf16[1,192,768]{2,1,0:T(8,128)(2,1)S(1)}, u32[]{:S(2)}) copy-start(bf16[1,192,768]{2,1,0:T(8,128)(2,1)S(1)} %fusion.38) | copy-start | bytes 884740
  302.8 3.9 copy-start.10
  304.8 2.0 copy-start.11
  306.8 0.7 copy-start.12
  308.3 13.7 %all-to-all-start.2 = ((bf16[4,64,768]{2,1,0:T(8,128)(2,1)}), bf16[4,64,768]{2,1,0:T(8,128)(2,1)S(1)}, u32[]{:S(2)}, u32[]{:S(2)}) async-start(bf16[4,64,768]{2,1,0:T(8,128)(2,1)} %pad_maximum_fusion.7), calls=%async_computation.2 | async-start | bytes 786432 | tf_op jit(solution)/shard_map/all_to_all | solution.py:562
  322.0 4.5 copy-start.26
  322.0 33.4 %all-to-all-start.4 = ((bf16[4,128,768]{2,1,0:T(8,128)(2,1)}), bf16[4,128,768]{2,1,0:T(8,128)(2,1)S(1)}, u32[]{:S(2)}, u32[]{:S(2)}) async-start(bf16[4,128,768]{2,1,0:T(8,128)(2,1)} %pad_maximum_fusion.4), calls=%async_computation.4 | async-start | bytes 1572864 | tf_op jit(solution)/shard_map/all_to_all | solution.py:563
  355.4 0.9 copy-start.24
  385.1 29.2 %copy-start.27 = (bf16[768,192]{1,0:T(8,128)(2,1)S(1)}, bf16[768,192]{1,0:T(8,128)(2,1)}, u32[]{:S(2)}) copy-start(bf16[768,192]{1,0:T(8,128)(2,1)} %get-tuple-element.59) | copy-start | bytes 884740
  385.2 29.2 %copy-start.28 = (bf16[768,192]{1,0:T(8,128)(2,1)S(1)}, bf16[768,192]{1,0:T(8,128)(2,1)}, u32[]{:S(2)}) copy-start(bf16[768,192]{1,0:T(8,128)(2,1)} %get-tuple-element.61) | copy-start | bytes 884740
  435.4 41.2 %all-to-all-start.3 = ((bf16[4,192,768]{2,1,0:T(8,128)(2,1)}), bf16[4,192,768]{2,1,0:T(8,128)(2,1)S(1)}, u32[]{:S(2)}, u32[]{:S(2)}) async-start(bf16[4,192,768]{2,1,0:T(8,128)(2,1)} %get-tuple-element.54), calls=%async_computation.3 | async-start | bytes 2359296 | tf_op jit(solution)/shard_map/all_to_all | solution.py:598
  455.1 1.4 collective-permute-start.6
  457.2 3.9 collective-permute-start.7
  461.2 3.9 collective-permute-start.8
  465.1 4.3 collective-permute-start.9
  470.0 5.1 collective-permute-start.10
  476.6 69.0 %all-to-all-start.5 = ((bf16[4,192,768]{2,1,0:T(8,128)(2,1)}), bf16[4,192,768]{2,1,0:T(8,128)(2,1)}, u32[]{:S(2)}, u32[]{:S(2)}) async-start(bf16[4,192,768]{2,1,0:T(8,128)(2,1)} %get-tuple-element.55), calls=%async_computation.5 | async-start | bytes 2359296 | tf_op jit(solution)/shard_map/all_to_all | solution.py:598
  481.7 8.2 %copy-start.8 = (bf16[8,112,576]{2,1,0:T(8,128)(2,1)S(1)}, bf16[8,112,576]{2,1,0:T(8,128)(2,1)}, u32[]{:S(2)}) copy-start(bf16[8,112,576]{2,1,0:T(8,128)(2,1)} %all_to_all.35) | copy-start | bytes 3096580
  484.0 28.7 %collective-permute-start = (bf16[192,768]{1,0:T(8,128)(2,1)}, bf16[192,768]{1,0:T(8,128)(2,1)}, u32[]{:S(2)}, u32[]{:S(2)}) collective-permute-start(bf16[192,768]{1,0:T(8,128)(2,1)} %get-tuple-element.179), channel_id=1, source_target_pairs={{0,1},{1,2},{2,3},{3,0},{4,5},{5,6},{6,7},{7,4},{8,9},{9,10},{10,1... | collective-permute-start | bytes 884744 | tf_op jit(solution)/shard_map/ppermute | solution.py:493
  486.0 65.0 %collective-permute-start.1 = (bf16[192,768]{1,0:T(8,128)(2,1)}, bf16[192,768]{1,0:T(8,128)(2,1)}, u32[]{:S(2)}, u32[]{:S(2)}) collective-permute-start(bf16[192,768]{1,0:T(8,128)(2,1)} %get-tuple-element.178), channel_id=1, source_target_pairs={{0,2},{1,3},{2,0},{3,1},{4,6},{5,7},{6,4},{7,5},{8,10},{9,11},{10,... | collective-permute-start | bytes 884744 | tf_op jit(solution)/shard_map/ppermute | solution.py:493
  488.4 62.6 %collective-permute-start.2 = (bf16[192,768]{1,0:T(8,128)(2,1)}, bf16[192,768]{1,0:T(8,128)(2,1)}, u32[]{:S(2)}, u32[]{:S(2)}) collective-permute-start(bf16[192,768]{1,0:T(8,128)(2,1)} %get-tuple-element.177), channel_id=1, source_target_pairs={{0,3},{1,0},{2,1},{3,2},{4,7},{5,4},{6,5},{7,6},{8,11},{9,8},{10,9... | collective-permute-start | bytes 884744 | tf_op jit(solution)/shard_map/ppermute | solution.py:493
  490.0 0.8 copy-start.23
  504.2 1.3 slice-start.4
  504.2 1.4 copy-start.25
  505.6 1.1 copy-start.6
  507.7 48.6 %collective-permute-start.5 = (bf16[96,1728]{1,0:T(8,128)(2,1)}, bf16[96,1728]{1,0:T(8,128)(2,1)}, u32[]{:S(2)}, u32[]{:S(2)}) collective-permute-start(bf16[96,1728]{1,0:T(8,128)(2,1)} %get-tuple-element.175), channel_id=1, source_target_pairs={{0,3},{1,0},{2,1},{3,2},{4,7},{5,4},{6,5},{7,6},{8,11},{9,8},{10,9... | collective-permute-start | bytes 995336 | tf_op jit(solution)/shard_map/ppermute | solution.py:493
  508.2 55.4 %collective-permute-start.4 = (bf16[96,1728]{1,0:T(8,128)(2,1)}, bf16[96,1728]{1,0:T(8,128)(2,1)}, u32[]{:S(2)}, u32[]{:S(2)}) collective-permute-start(bf16[96,1728]{1,0:T(8,128)(2,1)} %get-tuple-element.176), channel_id=1, source_target_pairs={{0,2},{1,3},{2,0},{3,1},{4,6},{5,7},{6,4},{7,5},{8,10},{9,11},{10,... | collective-permute-start | bytes 995336 | tf_op jit(solution)/shard_map/ppermute | solution.py:493
  512.7 50.9 %collective-permute-start.3 = (bf16[96,1728]{1,0:T(8,128)(2,1)}, bf16[96,1728]{1,0:T(8,128)(2,1)}, u32[]{:S(2)}, u32[]{:S(2)}) collective-permute-start(bf16[96,1728]{1,0:T(8,128)(2,1)} %get-tuple-element.174), channel_id=1, source_target_pairs={{0,1},{1,2},{2,3},{3,0},{4,5},{5,6},{6,7},{7,4},{8,9},{9,10},{10,1... | collective-permute-start | bytes 995336 | tf_op jit(solution)/shard_map/ppermute | solution.py:493
  545.6 5.4 copy-start.2
Sparse Core Ops, SparseCore 0:
  299.1 79.8 reduce-scatter.1

commit v3 on v2

--- a/solution.py
+++ b/solution.py
@@ -199,17 +199,6 @@
         scaled
         - jnp.mean(scaled, -1, keepdims=True)
         - normed * jnp.mean(scaled * normed, -1, keepdims=True)
-    )
-
-
-def gelu_value(inner):
-    return 0.5 * inner * (1.0 + jax.scipy.special.erf(inner * ROOT_HALF))
-
-
-def gelu_slope(inner):
-    return (
-        0.5 * (1.0 + jax.scipy.special.erf(inner * ROOT_HALF))
-        + inner * jnp.exp(-0.5 * inner * inner) * INV_ROOT_TWO_PI
     )
 
 
@@ -416,6 +405,119 @@
     )(first_low, second_low, attn_low, grad_inner, active, context)
 
 
+def erf(x):
+    x = jnp.clip(x, -3.7439211627767994, 3.7439211627767994)
+    y = x * x
+    top = jnp.float32(0.00022905065861350646)
+    for c in (0.0034082910107109506, 0.050955695062380861, 0.18520832239976145, 1.128379143519084):
+        top = top * y + c
+    low = jnp.float32(-1.1791602954361697e-7)
+    for c in (0.000023547966471313185, 0.0010179625278914885, 0.014070470171167667, 0.11098505178285362, 0.49746925110067538, 1.0):
+        low = low * y + c
+    return x * top / low
+
+
+def dense_body(own, x_ref, cot_ref, ctx0_ref, ctx1_ref, vec_ref, bias_ref, rest_ref, out_ref, first_ref, second_ref, attn_ref, grad_ref, active_ref, inner_ref, ctx_ref, go0_ref, go1_ref, sum_ref, w_s, mt_s, slope_s, first_s, acc_s, w_sem):
+    i = pl.program_id(0)
+    parts, _, _ = rest_ref.shape
+    f32, bf = jnp.float32, jnp.bfloat16
+    units = active_ref.shape[2]
+    cuts = (slice(0, 4 * own), slice(4 * own, 4 * own + units), slice(4 * own + units, 4 * own + 2 * units))
+    copies = [pltpu.make_async_copy(rest_ref.at[:, :, cut], w_s.at[:, :, cut], w_sem.at[c]) for c, cut in enumerate(cuts)]
+
+    @pl.when(i == 0)
+    def _():
+        for copy in copies:
+            copy.start()
+        sum_ref[...] = jnp.zeros(sum_ref.shape, f32)
+        copies[0].wait()
+        for t in range(parts):
+            mt_s[:, t * own : (t + 1) * own] = w_s[t, :, 3 * own : 4 * own]
+
+    def add_sum(row, value):
+        sum_ref[row : row + 1, :] += jnp.sum(value, axis=0, keepdims=True)
+
+    for t in range(parts):
+        lead = ctx0_ref.shape[1]
+        ctx_ref[t * own : t * own + lead, :] = ctx0_ref[t]
+        ctx_ref[t * own + lead : (t + 1) * own, :] = ctx1_ref[t]
+    mixed = dot(mt_s[...], ctx_ref[...]).T
+    attn_in = x_ref[...].astype(f32) + mixed + vec_ref[0:1]
+    first, first_norm, first_inv = layer_norm(attn_in, vec_ref[1:2], vec_ref[2:3])
+    first_ref[...] = first.astype(bf)
+    first_s[...] = first_norm
+    acc_s[...] = first + vec_ref[3:4]
+
+    @pl.when(i == 0)
+    def _():
+        copies[1].wait()
+        copies[2].wait()
+
+    def ahead(t, _):
+        inner = dot(first_ref[...], w_s[t, :, cuts[1]]) + bias_ref[t]
+        half = 0.5 * (1.0 + erf(inner * ROOT_HALF))
+        slope_s[t] = half + inner * jnp.exp(-0.5 * inner * inner) * INV_ROOT_TWO_PI
+        active_ref[t] = (inner * half).astype(bf)
+        acc_s[...] += dot_right_t(active_ref[t], w_s[t, :, cuts[2]])
+        return 0
+
+    lax.fori_loop(0, parts, ahead, 0)
+    second, second_norm, second_inv = layer_norm(acc_s[...], vec_ref[4:5], vec_ref[5:6])
+    out_ref[...] = second.astype(bf)
+    grad_out = cot_ref[...].astype(f32)
+    add_sum(4, grad_out * second_norm)
+    add_sum(5, grad_out)
+    grad_second = norm_back(grad_out, second_norm, second_inv, vec_ref[4:5])
+    add_sum(3, grad_second)
+    second_ref[...] = grad_second.astype(bf)
+    acc_s[...] = grad_second
+
+    def back(t, _):
+        grad_inner = (dot(second_ref[...], w_s[t, :, cuts[2]]) * slope_s[t]).astype(bf)
+        inner_ref[t] = grad_inner
+        sum_ref[pl.ds(6 + t, 1), :] += jnp.sum(grad_inner.astype(f32), axis=0, keepdims=True)
+        acc_s[...] += dot_right_t(grad_inner, w_s[t, :, cuts[1]])
+        return 0
+
+    lax.fori_loop(0, parts, back, 0)
+    grad_first = acc_s[...]
+    first_norm = first_s[...]
+    add_sum(1, grad_first * first_norm)
+    add_sum(2, grad_first)
+    grad_attn = norm_back(grad_first, first_norm, first_inv, vec_ref[1:2])
+    add_sum(0, grad_attn)
+    grad_ref[...] = grad_attn
+    attn_ref[...] = grad_attn.astype(bf)
+    grad_context = dot(attn_ref[...], mt_s[...]).T.astype(bf)
+    for t in range(parts):
+        go0_ref[t] = grad_context[t * own : t * own + HD]
+        go1_ref[t] = grad_context[t * own + HD : (t + 1) * own]
+
+
+def dense(own, x, cot, ctx0, ctx1, vectors, inner_bias, rest, block=384):
+    rows, width = x.shape
+    parts, _, cols = rest.shape
+    units = (cols - 4 * own) // 2
+    f32, bf = jnp.float32, jnp.bfloat16
+    S = jax.ShapeDtypeStruct
+    tok = pl.BlockSpec((block, width), lambda i: (i, 0))
+    part_tok = pl.BlockSpec((parts, block, units), lambda i: (0, i, 0))
+    lanes = lambda n: pl.BlockSpec((parts, n, block), lambda i: (0, 0, i))
+    fixed = lambda a: pl.BlockSpec(a.shape, lambda i: (0,) * a.ndim)
+    inner_bias = inner_bias.reshape(parts, 1, units)
+    return pl.pallas_call(
+        functools.partial(dense_body, own),
+        grid=(rows // block,),
+        in_specs=[tok, tok, lanes(ctx0.shape[1]), lanes(ctx1.shape[1]), fixed(vectors), fixed(inner_bias), pl.BlockSpec(memory_space=pl.ANY)],
+        out_specs=[tok] * 5 + [part_tok] * 2 + [pl.BlockSpec((parts * own, block), lambda i: (0, i)), lanes(HD), lanes(own - HD), pl.BlockSpec((16, width), lambda i: (0, 0))],
+        out_shape=[S((rows, width), bf)] * 4 + [S((rows, width), f32)] + [S((parts, rows, units), bf)] * 2 + [S((parts * own, rows), bf), S((parts, HD, rows), bf), S((parts, own - HD, rows), bf), S((16, width), f32)],
+        scratch_shapes=[VM((parts, width, cols), bf), VM((width, parts * own), bf), VM((parts, block, units), f32), VM((block, width), f32), VM((block, width), f32), pltpu.SemaphoreType.DMA((3,))],
+        compiler_params=pltpu.CompilerParams(vmem_limit_bytes=62 << 20),
+        cost_estimate=pl.CostEstimate(flops=4 * rows * width * (2 * parts * units + parts * own), bytes_accessed=40 << 20, transcendentals=rows * units * parts),
+        name="dense",
+    )(x, cot, ctx0, ctx1, vectors, inner_bias, rest)
+
+
 def early_back_body(w_ref, b0_ref, b1_ref, acc_ref):
     width = b0_ref.shape[1]
     total = jnp.zeros(acc_ref.shape, jnp.float32)
@@ -506,7 +608,6 @@
     heads = own // HD
     three = 3 * HD
     units = inner_weight.shape[1]
-    parts_of = range(parts)
     by_head = lambda q, k, v: jnp.stack([a.reshape(a.shape[:-1] + (heads, HD)) for a in (q, k, v)], -2).reshape(q.shape[:-1] + (3 * own,))
     x_own = hidden_in[0]
     qkv_own = by_head(query_weight, key_weight, value_weight)
@@ -528,41 +629,18 @@
         part, out_t, out_lse = attend_forward(first, count, parts, qt, ka, vt, lo, hi)
         context_t.append(out_t)
         lse.append(out_lse)
+        if exchanged:
+            part, exchanged[-1] = lax.optimization_barrier((part, exchanged[-1]))
         exchanged.append(lax.all_to_all(part, "tensor", 0, 0, tiled=True))
-    context = jnp.concatenate(exchanged, 1)
-    w1 = [rest[t, :, 4 * own : 4 * own + units] for t in parts_of]
-    w2t = [rest[t, :, 4 * own + units :] for t in parts_of]
-    mt = [rest[t, :, 3 * own : 4 * own] for t in parts_of]
-    contract = lambda a, b, i, j: lax.dot_general(a, b, (((i,), (j,)), ((), ())), preferred_element_type=f32)
-    mixed = sum(contract(context[t], mt[t], 0, 1) for t in parts_of)
-    attn_in = x_own.astype(f32) + mixed + mixer_bias
-    first, first_norm, first_inv = layer_norm(attn_in, first_gain, first_shift)
-    first_low = first.astype(bf)
-    inner = [dot(first_low, w1[t]) + inner_bias_all[t] for t in parts_of]
-    active = [gelu_value(inner[t]).astype(bf) for t in parts_of]
-    outer = sum(dot_right_t(active[t], w2t[t]) for t in parts_of)
-    second_in = first + outer + outer_bias
-    second, second_norm, second_inv = layer_norm(second_in, second_gain, second_shift)
-    layer_out = second.astype(bf)
-    grad_out = cotangent[0].astype(f32)
-    second_gain_grad = jnp.sum(grad_out * second_norm, 0)
-    second_shift_grad = jnp.sum(grad_out, 0)
-    grad_second = norm_back(grad_out, second_norm, second_inv, second_gain)
-    outer_bias_grad = jnp.sum(grad_second, 0)
-    second_low = grad_second.astype(bf)
-    grad_inner = [(dot(second_low, w2t[t]) * gelu_slope(inner[t])).astype(bf) for t in parts_of]
-    inner_bias_grad = jnp.stack([jnp.sum(g, 0, dtype=f32) for g in grad_inner])
-    grad_first = grad_second + sum(dot_right_t(grad_inner[t], w1[t]) for t in parts_of)
-    first_gain_grad = jnp.sum(grad_first * first_norm, 0)
-    first_shift_grad = jnp.sum(grad_first, 0)
-    grad_attn = norm_back(grad_first, first_norm, first_inv, first_gain)
-    mixer_bias_grad = jnp.sum(grad_attn, 0)
-    attn_low = grad_attn.astype(bf)
-    grad_context = jnp.stack([contract(mt[t], attn_low, 0, 1).astype(bf) for t in parts_of])
-    go0 = lax.all_to_all(grad_context[:, :HD], "tensor", 0, 0, tiled=True)
-    go1 = lax.all_to_all(grad_context[:, HD:], "tensor", 0, 0, tiled=True)
+    vectors = jnp.stack([mixer_bias, first_gain, first_shift, outer_bias, second_gain, second_shift])
+    vectors = jnp.pad(vectors, ((0, 2), (0, 0)))
+    layer_out, first_low, second_low, attn_low, grad_attn, active, grad_inner, context, go0, go1, early = dense(
+        own, x_own, cotangent[0], exchanged[0], exchanged[1], vectors, inner_bias_all, rest, block=rows
+    )
+    go0 = lax.all_to_all(go0, "tensor", 0, 0, tiled=True)
+    go1 = lax.all_to_all(go1, "tensor", 0, 0, tiled=True)
     weight_grads = weight_grads_of(
-        first_low, second_low, attn_low, jnp.stack(grad_inner), jnp.stack(active), context.reshape(-1, rows)
+        first_low, second_low, attn_low, grad_inner, active, context
     )
     weight_grads = lax.psum_scatter(weight_grads, "dp", scatter_dimension=0, tiled=True)
     weight_grads = jnp.concatenate(
@@ -574,17 +652,6 @@
     ).transpose(1, 0, 2)
     weight_grads = rotate(weight_grads, "tensor")
     weight_grads = sum(a.astype(f32) for a in weight_grads)
-    early = jnp.concatenate(
-        [
-            mixer_bias_grad,
-            first_gain_grad,
-            first_shift_grad,
-            outer_bias_grad,
-            second_gain_grad,
-            second_shift_grad,
-            inner_bias_grad.reshape(-1),
-        ]
-    )
     early = add_up(early)
 
     lo, hi = ranges(segment_all, 512, 512)
@@ -613,8 +680,7 @@
     qkv_grad = jnp.sum(qkv_grad.astype(f32), 0)
     bias_grad = qkv_grad[each] + qkv_grad[each + 1]
     pick = lambda a, n: a.reshape(a.shape[:-1] + (heads, 3, HD))[..., n, :].reshape(a.shape[:-1] + (own,))
-    stacked = early[: 6 * width].reshape(6, width)
-    inner_bias_out = lax.dynamic_slice_in_dim(early, 6 * width + rank * units, units)
+    inner_bias_out = lax.dynamic_index_in_dim(early, 6 + rank, 0, keepdims=False)
     return (
         layer_out[None],
         input_grad[None],
@@ -624,15 +690,15 @@
         pick(bias_grad, 0),
         pick(bias_grad, 2),
         weight_grads[:, 2 * units :].T,
-        stacked[0],
-        stacked[1],
-        stacked[2],
+        early[0],
+        early[1],
+        early[2],
         weight_grads[:, :units],
         inner_bias_out,
         weight_grads[:, units : 2 * units].T,
-        stacked[3],
-        stacked[4],
-        stacked[5],
+        early[3],
+        early[4],
+        early[5],
     )
 
 

time: 580 us -> 557 us (0.960)
  matrix products: 47.1 us -> 0 us
  Pallas kernels: 301 us -> 342 us
  other arithmetic: 23.5 us -> 6.93 us
  blocking collectives: 19.5 us -> 32.9 us
  local copies, waits for them, and re-layouts: 56.4 us -> 46.4 us
  waiting for transfers between devices: 39.6 us -> 47.9 us
  starting transfers between devices: 71.5 us -> 64.8 us
    dot_general x24 -> x0, matrix products: 47.1 us -> none  [the longest x8 19.9 us: dot(): return jnp.dot(a, b, preferred_element_type=jnp.float32)]
    pallas_call x0 -> x1, Pallas kernels: none -> 40.8 us  [dense(): pl.pallas_call(functools.partial(dense_body, own), grid=(rows // block,),...]
    all_to_all x0 -> x1, blocking collectives: none -> 13.4 us  [body(): go0 = lax.all_to_all(go0, 'tensor', 0, 0, tiled=True)]
    ppermute x5, waiting for transfers between devices: 13 us -> 22.4 us  [add_up(): other = lax.ppermute(value, axis, [(i, i ^ span) for i in range(size)])]
    reduce_sum x6 -> x0, other arithmetic: 8.03 us -> none  [the longest x1 2.54 us: body(): outer_bias_grad = jnp.sum(grad_second, 0)]
    all_to_all x2 -> x1, waiting for transfers between devices: 7.89 us -> 0.01 us  [body(): go1 = lax.all_to_all(go1, 'tensor', 0, 0, tiled=True)]
    ppermute x6, waiting for transfers between devices: 10.4 us -> 18 us  [rotate(): lax.ppermute(block, axis, [(i, (i + d) % size) for i in range(size)])]
    unnamed x105 -> x74, local copies, waits for them, and re-layouts: 31.3 us -> 25.4 us
  transfers between devices with their start and end apart: 18 -> 17, of which waited for: 9 -> 9; matrix products, arithmetic and copies ran while one was open for 9% -> 4% of each run, Pallas kernels for 21% -> 22%
where the time goes in v3:
time: 557 us; the launch traced here: 555 us
  Pallas kernels  342 us (61%)
  starting transfers between devices  64.8 us (12%)
  waiting for transfers between devices  47.9 us (9%)
  local copies, waits for them, and re-layouts  46.4 us (8%)
  blocking collectives  32.9 us (6%)
  between operations  14.6 us (3%)
  other arithmetic  6.93 us (1%)
    pallas_call x1, Pallas kernels, start(): pl.pallas_call(functools.partial(start_body, n, bits), in_specs=[pl.Block...  115 us
    pallas_call x3, Pallas kernels, attend_backward(): pl.pallas_call(functools.partial(backward_body, BQ, BK, SUB), grid_spec=p...  83.9 us
    pallas_call x2, Pallas kernels, attend_forward(): pl.pallas_call(functools.partial(forward_body, BK, SUB), grid_spec=pltpu....  70 us
    pallas_call x1, Pallas kernels, dense(): pl.pallas_call(functools.partial(dense_body, own), grid=(rows // block,),...  40.8 us
    ppermute x6, starting transfers between devices, rotate(): lax.ppermute(block, axis, [(i, (i + d) % size) for i in range(size)])  36 us
    unnamed x74, local copies, waits for them, and re-layouts  25.4 us
    ppermute x5, waiting for transfers between devices, add_up(): other = lax.ppermute(value, axis, [(i, i ^ span) for i in range(size)])  22.4 us
    all_to_all x1, blocking collectives, body(): lax.all_to_all(jnp.concatenate([qkv_grad, extra], 1), 'dp', 0, 0, tiled=T...  19.5 us
  transfers between devices with their start and end apart: 17, of which 9 were waited for; matrix products, arithmetic and copies ran while one was open for 4% of the time, Pallas kernels for 22%

profile of v3, /device:TPU:0, one launch (start us, length us, event | category | flops | bytes accessed | tf_op | source)
XLA Modules:
  0.0 555.1 jit_solution(17767934746639103892)
XLA Ops:
  8.0 0.9 copy.98
  8.9 0.9 copy.99
  9.8 0.9 copy.100
  10.9 0.9 copy.102
  11.8 1.3 pad_maximum_fusion.3.s_ref
  14.0 114.7 %start.1 = (bf16[4,768,768]{2,1,0:T(8,128)(2,1)}, bf16[4,8,96,2304]{3,2,1,0:T(8,128)(2,1)}, f32[4,12,128]{2,1,0:T(8,128)}) custom-call(bf16[768,768]{1,0:T(8,128)(2,1)} %bitcast.75, bf16[96,2304]{1,0:T(8,128)(2,1)} %concatenate.44.w_ref, f32[12,128]{1,0:T(8,128)} %pad_maximum_fusion.3.s_ref), custom_call_target="tpu_custom_call" | custom-call | bytes 209715200 | tf_op jit(solution)/shard_map/start/pallas_call | solution.py:346
  131.7 10.3 %project.1 = (bf16[3,128,3072]{2,1,0:T(8,128)(2,1)}, bf16[3,3072,128]{2,1,0:T(8,128)(2,1)}, bf16[3,64,3072]{2,1,0:T(8,128)(2,1)S(1)}, bf16[3,3072,64]{2,1,0:T(8,...) custom-call(s32[1]{0:T(128)} %bitcast.13.part_ref, bf16[3072,768]{1,0:T(8,128)(2,1)} %bitcast.72, ...), custom_call_target="tpu_custom_call" | custom-call | flops 2717908992 | bytes 17694720 | tf_op jit(solution)/shard_map/project/pallas_call | solution.py:46
  142.0 1.0 copy-done.1
  143.0 1.0 copy-done.2
  144.0 43.9 %attend_forward.3 = (bf16[4,128,768]{2,1,0:T(8,128)(2,1)}, f32[2,64,3072]{2,1,0:T(8,128)}, f32[2,1,3072]{2,1,0:T(1,128)}) custom-call(s32[8]{0:T(128)} %get-tuple-element.207.lo_ref, s32[8]{0:T(128)} %get-tuple-element.206.hi_ref, bf16[3,128,3072]{2,1,0:T(8,128)(2,1)} %get-tuple-element.57.qt_ref, bf16[3,3072,128]{2,1,0:T(8,128)(2,1)} %get-tuple-element.58.ka_ref, ...), custom_call_target="tpu_custom_call" | custom-call | flops 4831838208 | bytes 6291456 | tf_op jit(solution)/shard_map/attend_forward/pallas_call | solution.py:90
  187.9 3.5 all-to-all-start
  191.4 26.1 %attend_forward.2 = (bf16[4,64,768]{2,1,0:T(8,128)(2,1)}, f32[1,64,3072]{2,1,0:T(8,128)}, f32[1,1,3072]{2,1,0:T(1,128)}) custom-call(s32[8]{0:T(128)} %get-tuple-element.207.lo_ref, s32[8]{0:T(128)} %get-tuple-element.206.hi_ref, bf16[3,128,3072]{2,1,0:T(8,128)(2,1)} %get-tuple-element.57.qt_ref, bf16[3,3072,128]{2,1,0:T(8,128)(2,1)} %get-tuple-element.58.ka_ref, ...), custom_call_target="tpu_custom_call" | custom-call | flops 2415919104 | bytes 3145728 | tf_op jit(solution)/shard_map/attend_forward/pallas_call | solution.py:90
  217.6 5.1 all-to-all-start.1
  224.1 7.5 %all-to-all-done.1.ctx1_ref = bf16[4,64,768]{2,1,0:T(8,128)(2,1)S(1)} async-done(((bf16[4,64,768]{2,1,0:T(8,128)(2,1)}), bf16[4,64,768]{2,1,0:T(8,128)(2,1)S(1)}, u32[]{:S(2)}, u32[]{:S(2)}) %all-to-all-start.1) | async-done | bytes 393248 | tf_op jit(solution)/shard_map/all_to_all | solution.py:634
  232.3 40.8 %dense.1 = (bf16[768,768]{1,0:T(8,128)(2,1)}, bf16[768,768]{1,0:T(8,128)(2,1)}, bf16[768,768]{1,0:T(8,128)(2,1)}, bf16[768,768]{1,0:T(8,128)(2,1)}, f32[768,768]...) custom-call(bf16[768,768]{1,0:T(8,128)(2,1)} %bitcast.76, ...), custom_call_target="tpu_custom_call" | custom-call | flops 16307453952 | bytes 41943040 | tf_op jit(solution)/shard_map/dense/pallas_call | solution.py:508
  273.1 2.3 copy-done.3
  275.4 2.3 copy-done.4
  277.8 1.3 copy-done.5
  279.0 1.3 copy-done.6
  280.3 1.3 copy-done.7
  281.6 1.3 copy-done.8
  282.9 11.9 %weight_grads.1 = bf16[768,6912]{1,0:T(8,128)(2,1)} custom-call(bf16[768,768]{1,0:T(8,128)(2,1)S(1)} %copy-done.5, bf16[768,768]{1,0:T(8,128)(2,1)S(1)} %copy-done.6, bf16[768,768]{1,0:T(8,128)(2,1)S(1)} %copy-done.7, bf16[4,768,768]{2,1,0:T(8,128)(2,1)S(1)} %copy-done.4, bf16[4,768,768]{2,1,0:T(8,128)(2,1)S(1)} %copy-done.3, bf16[768,768]{1,0:T(8,128)(2,1)S(1)} %copy-done.8), custom_call_target="tpu_custom_call" | custom-call | flops 8153726976 | bytes 18874368 | tf_op jit(solution)/shard_map/weight_grads/pallas_call | solution.py:395
  294.8 1.0 copy-done.15
  295.8 13.4 %all_to_all.35.go_ref = bf16[4,64,768]{2,1,0:T(8,128)(2,1)} all-to-all(bf16[4,64,768]{2,1,0:T(8,128)(2,1)S(1)} %copy-done.15), channel_id=1, replica_groups=mesh['dp'=8,'tensor'=4] {'tensor'}, dimensions={0} | all-to-all | bytes 786432 | tf_op jit(solution)/shard_map/all_to_all | solution.py:640
  309.2 3.5 all-to-all-start.4
  313.4 27.8 %attend_backward.3 = (bf16[4,192,768]{2,1,0:T(8,128)(2,1)}, bf16[768,192]{1,0:T(8,128)(2,1)}, f32[192,128]{1,0:T(8,128)}) custom-call(s32[6]{0:T(128)} %get-tuple-element.186.lo_ref, s32[6]{0:T(128)} %get-tuple-element.185.hi_ref, bf16[4,64,768]{2,1,0:T(8,128)(2,1)} %all_to_all.35.go_ref, f32[2,64,3072]{2,1,0:T(8,128)} %get-tuple-element.66.ot_ref, ...), custom_call_target="tpu_custom_call" | custom-call | flops 6039797760 | bytes 5505024 | tf_op jit(solution)/shard_map/attend_backward/pallas_call | solution.py:163
  341.3 1.0 slice_reduce_fusion.2
  342.3 0.9 copy-done.12
  343.2 27.9 %attend_backward.5 = (bf16[4,192,768]{2,1,0:T(8,128)(2,1)}, bf16[768,192]{1,0:T(8,128)(2,1)}, f32[192,128]{1,0:T(8,128)}) custom-call(s32[6]{0:T(128)} %get-tuple-element.186.lo_ref, s32[6]{0:T(128)} %get-tuple-element.185.hi_ref, bf16[4,128,768]{2,1,0:T(8,128)(2,1)} %copy-done.12, f32[1,64,3072]{2,1,0:T(8,128)} %get-tuple-element.75.ot_ref, ...), custom_call_target="tpu_custom_call" | custom-call | flops 6039797760 | bytes 5505024 | tf_op jit(solution)/shard_map/attend_backward/pallas_call | solution.py:163
  371.1 1.0 slice_reduce_fusion
  372.2 28.1 %attend_backward.4 = (bf16[4,192,768]{2,1,0:T(8,128)(2,1)}, bf16[768,192]{1,0:T(8,128)(2,1)}, f32[192,128]{1,0:T(8,128)}) custom-call(s32[6]{0:T(128)} %get-tuple-element.186.lo_ref, s32[6]{0:T(128)} %get-tuple-element.185.hi_ref, bf16[4,128,768]{2,1,0:T(8,128)(2,1)} %copy-done.12, f32[2,64,3072]{2,1,0:T(8,128)} %get-tuple-element.66.ot_ref, ...), custom_call_target="tpu_custom_call" | custom-call | flops 6039797760 | bytes 5505024 | tf_op jit(solution)/shard_map/attend_backward/pallas_call | solution.py:163
  400.3 1.0 slice_reduce_fusion.1
  401.5 1.3 pad_maximum_fusion.1
  403.0 19.5 %all_to_all.36 = bf16[8,112,576]{2,1,0:T(8,128)(2,1)} all-to-all(bf16[8,112,576]{2,1,0:T(8,128)(2,1)S(1)} %pad_maximum_fusion), channel_id=1, replica_groups=mesh['dp'=8,'tensor'=4] {'dp'}, dimensions={0} | all-to-all | bytes 2064384 | tf_op jit(solution)/shard_map/all_to_all | solution.py:679
  422.5 5.1 all-to-all-start.3
  427.6 1.2 collective-permute-done.6
  429.5 3.5 collective-permute-done.7
  433.6 3.5 collective-permute-done.8
  437.2 2.1 collective-permute-start.9
  439.3 8.3 %collective-permute-done.9 = f32[16,768]{1,0:T(8,128)S(1)} collective-permute-done((f32[16,768]{1,0:T(8,128)S(1)}, f32[16,768]{1,0:T(8,128)S(1)}, u32[]{:S(2)}, u32[]{:S(2)}) %collective-permute-start.9) | collective-permute-done | bytes 49184 | tf_op jit(solution)/shard_map/ppermute | solution.py:582
  447.6 4.7 collective-permute-start.10
  452.3 5.8 %collective-permute-done.10 = f32[16,768]{1,0:T(8,128)S(1)} collective-permute-done((f32[16,768]{1,0:T(8,128)S(1)}, f32[16,768]{1,0:T(8,128)S(1)}, u32[]{:S(2)}, u32[]{:S(2)}) %collective-permute-start.10) | collective-permute-done | bytes 49184 | tf_op jit(solution)/shard_map/ppermute | solution.py:582
  458.7 3.5 all-to-all-start.5
  462.2 2.3 dynamic-slice_bitcast_fusion.3
  464.5 3.8 collective-permute-start.2
  468.3 1.1 collective-permute-start
  470.4 1.8 copy.109
  472.2 1.7 fusion.8
  473.9 1.6 slice.133
  475.5 1.8 reshape.213
  477.3 1.3 slice-done
  478.7 1.1 dynamic-slice_bitcast_fusion.2
  479.8 2.4 collective-permute-start.3
  482.1 1.5 collective-permute-start.5
  483.6 6.4 %collective-permute-done.2.rest_3_ = bf16[192,768]{1,0:T(8,128)(2,1)S(1)} collective-permute-done((bf16[192,768]{1,0:T(8,128)(2,1)}, bf16[192,768]{1,0:T(8,128)(2,1)S(1)}, u32[]{:S(2)}, u32[]{:S(2)}) %collective-permute-start.2) | collective-permute-done | bytes 294944 | tf_op jit(solution)/shard_map/ppermute | solution.py:595
  490.0 27.3 %collective-permute-start.4 = (bf16[96,1728]{1,0:T(8,128)(2,1)}, bf16[96,1728]{1,0:T(8,128)(2,1)}, u32[]{:S(2)}, u32[]{:S(2)}) collective-permute-start(bf16[96,1728]{1,0:T(8,128)(2,1)} %get-tuple-element.189), channel_id=1, source_target_pairs={{0,2},{1,3},{2,0},{3,1},{4,6},{5,7},{6,4},{7,5},{8,10},{9,11},{10,... | collective-permute-start | bytes 995336 | tf_op jit(solution)/shard_map/ppermute | solution.py:595
  518.6 1.6 copy.114
  520.2 1.6 copy.113
  521.9 1.6 copy.112
  523.5 5.1 early_back.1.acc_ref
  528.6 2.8 collective-permute-done.1.rest_2_
  531.4 5.0 late_back.1
  536.4 8.8 %collective-permute-done.4 = bf16[96,1728]{1,0:T(8,128)(2,1)} collective-permute-done((bf16[96,1728]{1,0:T(8,128)(2,1)}, bf16[96,1728]{1,0:T(8,128)(2,1)}, u32[]{:S(2)}, u32[]{:S(2)}) %collective-permute-start.4) | collective-permute-done | bytes 331808 | tf_op jit(solution)/shard_map/ppermute | solution.py:595
  545.2 1.4 fusion.1
  (119 shorter events, 13.9 us)
Async XLA Ops:
  7.2 6.0 %copy-start.19 = (bf16[768,96]{0,1:T(8,128)(2,1)S(1)}, bf16[768,96]{0,1:T(8,128)(2,1)}, u32[]{:S(2)}) copy-start(bf16[768,96]{0,1:T(8,128)(2,1)} %param.31) | copy-start | bytes 442372
  7.2 6.0 %copy-start.18 = (bf16[96,768]{1,0:T(8,128)(2,1)S(1)}, bf16[96,768]{1,0:T(8,128)(2,1)}, u32[]{:S(2)}) copy-start(bf16[96,768]{1,0:T(8,128)(2,1)} %param.29) | copy-start | bytes 442372
  11.8 117.7 %copy-start.27 = (f32[192]{0:T(256)S(1)}, f32[192]{0:T(256)}, u32[]{:S(2)}) copy-start(f32[192]{0:T(256)} %param.23) | copy-start | bytes 2308
  11.8 117.8 %copy-start.28 = (f32[192]{0:T(256)S(1)}, f32[192]{0:T(256)}, u32[]{:S(2)}) copy-start(f32[192]{0:T(256)} %param.24) | copy-start | bytes 2308
  142.0 1.0 copy-start.1
  143.0 1.0 copy-start.2
  187.9 29.7 %all-to-all-start = ((bf16[4,128,768]{2,1,0:T(8,128)(2,1)}), bf16[4,128,768]{2,1,0:T(8,128)(2,1)S(1)}, u32[]{:S(2)}, u32[]{:S(2)}) async-start(bf16[4,128,768]{2,1,0:T(8,128)(2,1)} %get-tuple-element.61), calls=%async_computation | async-start | bytes 1572864 | tf_op jit(solution)/shard_map/all_to_all | solution.py:634
  191.4 31.3 %copy-start.21 = (f32[768]{0:T(1024)S(1)}, f32[768]{0:T(1024)}, u32[]{:S(2)}) copy-start(f32[768]{0:T(1024)} %param.26) | copy-start | bytes 9220
  191.4 31.3 %copy-start.22 = (f32[768]{0:T(1024)S(1)}, f32[768]{0:T(1024)}, u32[]{:S(2)}) copy-start(f32[768]{0:T(1024)} %param.27) | copy-start | bytes 9220
  191.4 31.3 %copy-start.23 = (f32[768]{0:T(1024)S(1)}, f32[768]{0:T(1024)}, u32[]{:S(2)}) copy-start(f32[768]{0:T(1024)} %param.28) | copy-start | bytes 9220
  191.4 31.4 %copy-start.24 = (f32[768]{0:T(1024)S(1)}, f32[768]{0:T(1024)}, u32[]{:S(2)}) copy-start(f32[768]{0:T(1024)} %param.32) | copy-start | bytes 9220
  191.4 31.4 %copy-start.25 = (f32[768]{0:T(1024)S(1)}, f32[768]{0:T(1024)}, u32[]{:S(2)}) copy-start(f32[768]{0:T(1024)} %param.33) | copy-start | bytes 9220
  191.4 31.4 %copy-start.26 = (f32[768]{0:T(1024)S(1)}, f32[768]{0:T(1024)}, u32[]{:S(2)}) copy-start(f32[768]{0:T(1024)} %param.34) | copy-start | bytes 9220
  217.6 14.0 %copy-start.11 = (bf16[4,128,768]{2,1,0:T(8,128)(2,1)}, bf16[4,128,768]{2,1,0:T(8,128)(2,1)S(1)}, u32[]{:S(2)}) copy-start(bf16[4,128,768]{2,1,0:T(8,128)(2,1)S(1)} %all-to-all-done.ctx0_ref) | copy-start | bytes 2359300
  217.6 14.0 %all-to-all-start.1 = ((bf16[4,64,768]{2,1,0:T(8,128)(2,1)}), bf16[4,64,768]{2,1,0:T(8,128)(2,1)S(1)}, u32[]{:S(2)}, u32[]{:S(2)}) async-start(bf16[4,64,768]{2,1,0:T(8,128)(2,1)} %get-tuple-element.63), calls=%async_computation.1 | async-start | bytes 786432 | tf_op jit(solution)/shard_map/all_to_all | solution.py:634
  222.7 251.2 %reduce-scatter.2.cloned.1.call-start = ((), (), s32[]{:S(2)}) async-start(), calls=%async_computation.8 | async-start | bytes 11943936 | tf_op jit(solution)/shard_map/reduce_scatter | solution.py:645
  231.6 0.8 copy-start.14
  273.1 2.3 copy-start.3
  275.4 2.3 copy-start.4
  277.8 1.3 copy-start.5
  279.0 1.3 copy-start.6
  280.3 1.3 copy-start.7
  281.6 1.3 copy-start.8
  294.8 1.0 copy-start.15
  309.2 33.1 %all-to-all-start.4 = ((bf16[4,128,768]{2,1,0:T(8,128)(2,1)}), bf16[4,128,768]{2,1,0:T(8,128)(2,1)S(1)}, u32[]{:S(2)}, u32[]{:S(2)}) async-start(bf16[4,128,768]{2,1,0:T(8,128)(2,1)} %get-tuple-element.72), calls=%async_computation.4 | async-start | bytes 1572864 | tf_op jit(solution)/shard_map/all_to_all | solution.py:641
  342.3 0.9 copy-start.12
  372.2 29.3 %copy-start.16 = (bf16[768,192]{1,0:T(8,128)(2,1)S(1)}, bf16[768,192]{1,0:T(8,128)(2,1)}, u32[]{:S(2)}) copy-start(bf16[768,192]{1,0:T(8,128)(2,1)} %get-tuple-element.78) | copy-start | bytes 884740
  372.2 29.3 %copy-start.17 = (bf16[768,192]{1,0:T(8,128)(2,1)S(1)}, bf16[768,192]{1,0:T(8,128)(2,1)}, u32[]{:S(2)}) copy-start(bf16[768,192]{1,0:T(8,128)(2,1)} %get-tuple-element.80) | copy-start | bytes 884740
  422.5 5.2 copy-start.20
  422.5 36.2 %all-to-all-start.3 = ((bf16[4,192,768]{2,1,0:T(8,128)(2,1)}), bf16[4,192,768]{2,1,0:T(8,128)(2,1)S(1)}, u32[]{:S(2)}, u32[]{:S(2)}) async-start(bf16[4,192,768]{2,1,0:T(8,128)(2,1)} %get-tuple-element.71), calls=%async_computation.3 | async-start | bytes 2359296 | tf_op jit(solution)/shard_map/all_to_all | solution.py:665
  427.6 1.2 collective-permute-start.6
  428.9 4.1 collective-permute-start.7
  433.0 4.2 collective-permute-start.8
  437.2 10.4 %collective-permute-start.9 = (f32[16,768]{1,0:T(8,128)S(1)}, f32[16,768]{1,0:T(8,128)S(1)}, u32[]{:S(2)}, u32[]{:S(2)}) collective-permute-start(f32[16,768]{1,0:T(8,128)S(1)} %add.108), channel_id=1, source_target_pairs={{0,1},{1,0},{2,3},{3,2},{4,5},{5,4},{6,7},{7,6},{8,9},{9,8},{10,11... | collective-permute-start | bytes 147464 | tf_op jit(solution)/shard_map/ppermute | solution.py:582
  447.6 10.4 %collective-permute-start.10 = (f32[16,768]{1,0:T(8,128)S(1)}, f32[16,768]{1,0:T(8,128)S(1)}, u32[]{:S(2)}, u32[]{:S(2)}) collective-permute-start(f32[16,768]{1,0:T(8,128)S(1)} %add.109), channel_id=1, source_target_pairs={{0,2},{1,3},{2,0},{3,1},{4,6},{5,7},{6,4},{7,5},{8,10},{9,11},{10,... | collective-permute-start | bytes 147464 | tf_op jit(solution)/shard_map/ppermute | solution.py:582
  458.7 64.8 %all-to-all-start.5 = ((bf16[4,192,768]{2,1,0:T(8,128)(2,1)}), bf16[4,192,768]{2,1,0:T(8,128)(2,1)S(1)}, u32[]{:S(2)}, u32[]{:S(2)}) async-start(bf16[4,192,768]{2,1,0:T(8,128)(2,1)} %get-tuple-element.73), calls=%async_computation.5 | async-start | bytes 2359296 | tf_op jit(solution)/shard_map/all_to_all | solution.py:665
  462.2 7.2 %copy-start.10 = (bf16[8,112,576]{2,1,0:T(8,128)(2,1)S(1)}, bf16[8,112,576]{2,1,0:T(8,128)(2,1)}, u32[]{:S(2)}) copy-start(bf16[8,112,576]{2,1,0:T(8,128)(2,1)} %all_to_all.36) | copy-start | bytes 3096580
  464.5 25.5 %collective-permute-start.2 = (bf16[192,768]{1,0:T(8,128)(2,1)}, bf16[192,768]{1,0:T(8,128)(2,1)S(1)}, u32[]{:S(2)}, u32[]{:S(2)}) collective-permute-start(bf16[192,768]{1,0:T(8,128)(2,1)} %get-tuple-element.190), channel_id=1, source_target_pairs={{0,3},{1,0},{2,1},{3,2},{4,7},{5,4},{6,5},{7,6},{8,11},{9,8},{10,9... | collective-permute-start | bytes 884744 | tf_op jit(solution)/shard_map/ppermute | solution.py:595
  468.3 63.1 %collective-permute-start.1 = (bf16[192,768]{1,0:T(8,128)(2,1)}, bf16[192,768]{1,0:T(8,128)(2,1)S(1)}, u32[]{:S(2)}, u32[]{:S(2)}) collective-permute-start(bf16[192,768]{1,0:T(8,128)(2,1)} %get-tuple-element.191), channel_id=1, source_target_pairs={{0,2},{1,3},{2,0},{3,1},{4,6},{5,7},{6,4},{7,5},{8,10},{9,11},{10,... | collective-permute-start | bytes 884744 | tf_op jit(solution)/shard_map/ppermute | solution.py:595
  468.3 63.1 %collective-permute-start = (bf16[192,768]{1,0:T(8,128)(2,1)}, bf16[192,768]{1,0:T(8,128)(2,1)S(1)}, u32[]{:S(2)}, u32[]{:S(2)}) collective-permute-start(bf16[192,768]{1,0:T(8,128)(2,1)} %get-tuple-element.192), channel_id=1, source_target_pairs={{0,1},{1,2},{2,3},{3,0},{4,5},{5,6},{6,7},{7,4},{8,9},{9,10},{10,1... | collective-permute-start | bytes 884744 | tf_op jit(solution)/shard_map/ppermute | solution.py:595
  477.3 1.3 slice-start
  477.3 1.4 copy-start.13
  478.6 11.4 %copy-start.9 = (bf16[96,4,1728]{2,0,1:T(8,128)(2,1)}, bf16[96,4,1728]{2,0,1:T(8,128)(2,1)S(1)}, u32[]{:S(2)}) copy-start(bf16[96,4,1728]{2,0,1:T(8,128)(2,1)S(1)} %copy_dynamic-update-slice_fusion) | copy-start | bytes 3981316
  479.8 56.6 %collective-permute-start.3 = (bf16[96,1728]{1,0:T(8,128)(2,1)}, bf16[96,1728]{1,0:T(8,128)(2,1)}, u32[]{:S(2)}, u32[]{:S(2)}) collective-permute-start(bf16[96,1728]{1,0:T(8,128)(2,1)} %get-tuple-element.187), channel_id=1, source_target_pairs={{0,1},{1,2},{2,3},{3,0},{4,5},{5,6},{6,7},{7,4},{8,9},{9,10},{10,1... | collective-permute-start | bytes 995336 | tf_op jit(solution)/shard_map/ppermute | solution.py:595
  482.1 54.2 %collective-permute-start.5 = (bf16[96,1728]{1,0:T(8,128)(2,1)}, bf16[96,1728]{1,0:T(8,128)(2,1)}, u32[]{:S(2)}, u32[]{:S(2)}) collective-permute-start(bf16[96,1728]{1,0:T(8,128)(2,1)} %get-tuple-element.188), channel_id=1, source_target_pairs={{0,3},{1,0},{2,1},{3,2},{4,7},{5,4},{6,5},{7,6},{8,11},{9,8},{10,9... | collective-permute-start | bytes 995336 | tf_op jit(solution)/shard_map/ppermute | solution.py:595
  490.0 55.2 %collective-permute-start.4 = (bf16[96,1728]{1,0:T(8,128)(2,1)}, bf16[96,1728]{1,0:T(8,128)(2,1)}, u32[]{:S(2)}, u32[]{:S(2)}) collective-permute-start(bf16[96,1728]{1,0:T(8,128)(2,1)} %get-tuple-element.189), channel_id=1, source_target_pairs={{0,2},{1,3},{2,0},{3,1},{4,6},{5,7},{6,4},{7,5},{8,10},{9,11},{10,... | collective-permute-start | bytes 995336 | tf_op jit(solution)/shard_map/ppermute | solution.py:595
  523.5 7.9 %copy-start = (f32[768,768]{1,0:T(8,128)S(1)}, f32[768,768]{1,0:T(8,128)}, u32[]{:S(2)}) copy-start(f32[768,768]{1,0:T(8,128)} %get-tuple-element.74.grad_ref) | copy-start | bytes 7077892
Sparse Core Ops, SparseCore 0:
  294.9 79.8 reduce-scatter.1

commit v4 on v3

--- a/solution.py
+++ b/solution.py
@@ -49,7 +49,7 @@
                   pl.BlockSpec((rows,1),lambda i,*_:(i,0)),pl.BlockSpec((1,rows),lambda i,*_:(0,i))],
         out_specs=[tr(2*HD),nat(2*HD),tr(HD),nat(HD),tr(HD),nat(HD)]),
         out_shape=[S((heads,2*HD,L),bf),S((heads,L,2*HD),bf),S((heads,HD,L),bf),S((heads,L,HD),bf),S((heads,HD,L),bf),S((heads,L,HD),bf)],
-        compiler_params=pltpu.CompilerParams(vmem_limit_bytes=48<<20),
+        compiler_params=pltpu.CompilerParams(vmem_limit_bytes=62 << 20),
         cost_estimate=pl.CostEstimate(flops=2*L*D*b.shape[0],bytes_accessed=L*D*2+D*cols*2+L*heads*HD*2*10,transcendentals=0),
         name="project")(part.reshape(1),x,rest,b.reshape(1,-1),seg.reshape(-1,1),seg.reshape(1,-1))
 
@@ -93,7 +93,7 @@
         out_specs=[pl.BlockSpec((1,heads*HD,BQ),lambda i,*_:(i//per,0,i%per)),pl.BlockSpec((heads,HD,BQ),lambda i,*_:(0,0,i)),pl.BlockSpec((heads,1,BQ),lambda i,*_:(0,0,i))],
         scratch_shapes=[VM((heads,1,BQ),jnp.float32),VM((heads,1,BQ),jnp.float32),VM((heads,HD,BQ),jnp.float32)]),
         out_shape=[S((parts,heads*HD,L//parts),jnp.bfloat16),S((heads,HD,L),jnp.float32),S((heads,1,L),jnp.float32)],
-        compiler_params=pltpu.CompilerParams(vmem_limit_bytes=56<<20),
+        compiler_params=pltpu.CompilerParams(vmem_limit_bytes=62 << 20),
         cost_estimate=pl.CostEstimate(flops=2*L*L*HD*2*heads,bytes_accessed=L*heads*HD*2*8,transcendentals=L*L*heads),
         name="attend_forward")(lo,hi,qt,ka,vt)
 
@@ -166,7 +166,7 @@
         out_specs=[pl.BlockSpec((parts,out,rows),lambda i,*_:(0,0,0),pipeline_mode=pl.Buffered(1)),pl.BlockSpec((D,out),lambda i,*_:(0,0)),pl.BlockSpec((out,128),lambda i,*_:(0,0))],
         scratch_shapes=[VM((heads,HD,L),bf),VM((heads,L,HD),bf),VM((heads,1,L),f32),VM((heads,HD,L),f32),VM((heads,HD,L),bf),VM((heads,HD,L),bf),VM((heads,BK,HD),f32),VM((heads,BK,HD),f32),VM(x.shape,bf),pltpu.SemaphoreType.DMA]),
         out_shape=[S((parts,out,rows),bf),S((D,out),bf),S((out,128),f32)],
-        compiler_params=pltpu.CompilerParams(vmem_limit_bytes=60<<20),
+        compiler_params=pltpu.CompilerParams(vmem_limit_bytes=62 << 20),
         cost_estimate=pl.CostEstimate(flops=2*L*L*HD*5*heads,bytes_accessed=L*heads*HD*2*14,transcendentals=L*L*heads),
         name="attend_backward")(lo,hi,go,ot,lse,qt,ka,qn,kt,vn,x)
 
@@ -399,7 +399,7 @@
         out_specs=pl.BlockSpec((width, units), lambda j: (0, j)),
         out_shape=jax.ShapeDtypeStruct((width, units * 2 * parts + features), jnp.bfloat16),
         scratch_shapes=[VM((width, rows), jnp.bfloat16), VM((width, rows), jnp.bfloat16)],
-        compiler_params=pltpu.CompilerParams(vmem_limit_bytes=40 << 20),
+        compiler_params=pltpu.CompilerParams(vmem_limit_bytes=62 << 20),
         cost_estimate=pl.CostEstimate(flops=2 * rows * width * (2 * parts * units + features), bytes_accessed=rows * units * 2 * parts * 4, transcendentals=0),
         name="weight_grads",
     )(first_low, second_low, attn_low, grad_inner, active, context)
@@ -417,13 +417,14 @@
     return x * top / low
 
 
-def dense_body(own, x_ref, cot_ref, ctx0_ref, ctx1_ref, vec_ref, bias_ref, rest_ref, out_ref, first_ref, second_ref, attn_ref, grad_ref, active_ref, inner_ref, ctx_ref, go0_ref, go1_ref, sum_ref, w_s, mt_s, slope_s, first_s, acc_s, w_sem):
+def dense_body(own, x_ref, cot_ref, ctx0_ref, ctx1_ref, vec_ref, bias_ref, near_ref, far_ref, out_ref, first_ref, second_ref, attn_ref, grad_ref, active_ref, inner_ref, ctx_ref, go0_ref, go1_ref, sum_ref, w_s, mt_s, slope_s, first_s, acc_s, w_sem):
     i = pl.program_id(0)
-    parts, _, _ = rest_ref.shape
+    parts, _, _ = near_ref.shape
     f32, bf = jnp.float32, jnp.bfloat16
     units = active_ref.shape[2]
     cuts = (slice(0, 4 * own), slice(4 * own, 4 * own + units), slice(4 * own + units, 4 * own + 2 * units))
-    copies = [pltpu.make_async_copy(rest_ref.at[:, :, cut], w_s.at[:, :, cut], w_sem.at[c]) for c, cut in enumerate(cuts)]
+    sources = (near_ref, far_ref.at[:, :, :units], far_ref.at[:, :, units:])
+    copies = [pltpu.make_async_copy(sources[c], w_s.at[:, :, cut], w_sem.at[c]) for c, cut in enumerate(cuts)]
 
     @pl.when(i == 0)
     def _():
@@ -494,10 +495,11 @@
         go1_ref[t] = grad_context[t * own + HD : (t + 1) * own]
 
 
-def dense(own, x, cot, ctx0, ctx1, vectors, inner_bias, rest, block=384):
+def dense(own, x, cot, ctx0, ctx1, vectors, inner_bias, near, far, block):
     rows, width = x.shape
-    parts, _, cols = rest.shape
-    units = (cols - 4 * own) // 2
+    parts = near.shape[0]
+    units = far.shape[2] // 2
+    cols = 4 * own + 2 * units
     f32, bf = jnp.float32, jnp.bfloat16
     S = jax.ShapeDtypeStruct
     tok = pl.BlockSpec((block, width), lambda i: (i, 0))
@@ -508,14 +510,14 @@
     return pl.pallas_call(
         functools.partial(dense_body, own),
         grid=(rows // block,),
-        in_specs=[tok, tok, lanes(ctx0.shape[1]), lanes(ctx1.shape[1]), fixed(vectors), fixed(inner_bias), pl.BlockSpec(memory_space=pl.ANY)],
+        in_specs=[tok, tok, lanes(ctx0.shape[1]), lanes(ctx1.shape[1]), fixed(vectors), fixed(inner_bias), pl.BlockSpec(memory_space=pl.ANY), pl.BlockSpec(memory_space=pl.ANY)],
         out_specs=[tok] * 5 + [part_tok] * 2 + [pl.BlockSpec((parts * own, block), lambda i: (0, i)), lanes(HD), lanes(own - HD), pl.BlockSpec((16, width), lambda i: (0, 0))],
         out_shape=[S((rows, width), bf)] * 4 + [S((rows, width), f32)] + [S((parts, rows, units), bf)] * 2 + [S((parts * own, rows), bf), S((parts, HD, rows), bf), S((parts, own - HD, rows), bf), S((16, width), f32)],
         scratch_shapes=[VM((parts, width, cols), bf), VM((width, parts * own), bf), VM((parts, block, units), f32), VM((block, width), f32), VM((block, width), f32), pltpu.SemaphoreType.DMA((3,))],
         compiler_params=pltpu.CompilerParams(vmem_limit_bytes=62 << 20),
         cost_estimate=pl.CostEstimate(flops=4 * rows * width * (2 * parts * units + parts * own), bytes_accessed=40 << 20, transcendentals=rows * units * parts),
         name="dense",
-    )(x, cot, ctx0, ctx1, vectors, inner_bias, rest)
+    )(x, cot, ctx0, ctx1, vectors, inner_bias, near, far)
 
 
 def early_back_body(w_ref, b0_ref, b1_ref, acc_ref):
@@ -551,7 +553,7 @@
         in_specs=[weight_block(rest, cols), whole(b0), whole(b1)],
         out_specs=pl.BlockSpec((width, rows), lambda i: (0, 0)),
         out_shape=jax.ShapeDtypeStruct((width, rows), jnp.float32),
-        compiler_params=pltpu.CompilerParams(vmem_limit_bytes=40 << 20),
+        compiler_params=pltpu.CompilerParams(vmem_limit_bytes=62 << 20),
         cost_estimate=pl.CostEstimate(flops=4 * width * rows * b0.shape[0] * b0.shape[1], bytes_accessed=10 << 20, transcendentals=0),
         name="early_back",
     )(rest, b0, b1)
@@ -568,7 +570,7 @@
             out_specs=pl.BlockSpec((rows, width), lambda i, *_: (0, 0)),
         ),
         out_shape=jax.ShapeDtypeStruct((rows, width), jnp.bfloat16),
-        compiler_params=pltpu.CompilerParams(vmem_limit_bytes=40 << 20),
+        compiler_params=pltpu.CompilerParams(vmem_limit_bytes=62 << 20),
         cost_estimate=pl.CostEstimate(flops=2 * width * rows * backs[0].shape[0] * len(backs), bytes_accessed=10 << 20, transcendentals=0),
         name="late_back",
     )(part.reshape(1), rest, acc, grad, *backs)
@@ -612,16 +614,19 @@
     x_own = hidden_in[0]
     qkv_own = by_head(query_weight, key_weight, value_weight)
     small = jnp.concatenate([segments[0].astype(f32), inner_bias]).reshape(-1, 128)
-    rest_own = jnp.concatenate([qkv_own, mixer_weight.T, inner_weight, outer_weight.T], 1)
-    x_parts, rest, small = start(x_own, rest_own, small)
+    near_own = jnp.concatenate([qkv_own, mixer_weight.T], 1)
+    x_parts, near, small = start(x_own, near_own, small)
     x_all = x_parts.reshape(parts * rows, width)
-    rest = rest.reshape(parts, width, rest_own.shape[1])
+    near = near.reshape(parts, width, 4 * own)
+    far_own = jnp.concatenate([inner_weight, outer_weight.T], 1)
+    far_own, small = lax.optimization_barrier((far_own, small))
+    far = lax.all_gather(far_own, ("tensor", "dp"), axis=0, tiled=True).reshape(parts, width, 2 * units)
     small = small.reshape(parts, -1)
     segment_all = small[:, :rows].astype(jnp.int32).reshape(-1)
     inner_bias_all = small[:, rows:]
     biases = by_head(query_bias, jnp.zeros_like(query_bias), value_bias)
 
-    qt, ka, vt, qn, kt, vn = project(x_all, rest, rank, biases, segment_all)
+    qt, ka, vt, qn, kt, vn = project(x_all, near, rank, biases, segment_all)
     lo, hi = ranges(segment_all, 384, 512)
     lead = heads - 1
     context_t, lse, exchanged = [], [], []
@@ -635,7 +640,7 @@
     vectors = jnp.stack([mixer_bias, first_gain, first_shift, outer_bias, second_gain, second_shift])
     vectors = jnp.pad(vectors, ((0, 2), (0, 0)))
     layer_out, first_low, second_low, attn_low, grad_attn, active, grad_inner, context, go0, go1, early = dense(
-        own, x_own, cotangent[0], exchanged[0], exchanged[1], vectors, inner_bias_all, rest, block=rows
+        own, x_own, cotangent[0], exchanged[0], exchanged[1], vectors, inner_bias_all, near, far, block=rows
     )
     go0 = lax.all_to_all(go0, "tensor", 0, 0, tiled=True)
     go1 = lax.all_to_all(go1, "tensor", 0, 0, tiled=True)
@@ -667,8 +672,8 @@
             backs.append(rotate(grads, "tensor"))
         qkv_grad.append(weight_part)
         bias_grad.append(sums[:, 0])
-    input_back = early_back(rest, 4 * own, backs[0], backs[1])
-    input_grad = late_back(rest, 4 * own, 2 * three, rank, input_back, grad_attn, backs[2])
+    input_back = early_back(near, 4 * own, backs[0], backs[1])
+    input_grad = late_back(near, 4 * own, 2 * three, rank, input_back, grad_attn, backs[2])
     bias_grad = jnp.concatenate(bias_grad)
     high = bias_grad.astype(bf)
     low = (bias_grad - high.astype(f32)).astype(bf)

time: 557 us -> 538 us (0.966)
  waiting for transfers between devices: 47.9 us -> 81.1 us
  starting transfers between devices: 64.8 us -> 35.2 us
  local copies, waits for them, and re-layouts: 46.4 us -> 25 us
  Pallas kernels: 342 us -> 333 us
    ppermute x6, starting transfers between devices: 36 us -> 6.91 us  [rotate(): lax.ppermute(block, axis, [(i, (i + d) % size) for i in range(size)])]
    pallas_call x1, Pallas kernels: 115 us -> 95.4 us  [start(): pl.pallas_call(functools.partial(start_body, n, bits), in_specs=[pl.Block...]
    ppermute x6, waiting for transfers between devices: 18 us -> 36.1 us  [rotate(): lax.ppermute(block, axis, [(i, (i + d) % size) for i in range(size)])]
    unnamed x74 -> x60, local copies, waits for them, and re-layouts: 25.4 us -> 12.2 us
    all_to_all x2, waiting for transfers between devices: 0.01 us -> 11.4 us  [body(): backs.append(lax.all_to_all(grads, 'tensor', 0, 0, tiled=True))]
  transfers between devices with their start and end apart: 17 -> 18, of which waited for: 9 -> 11; matrix products, arithmetic and copies ran while one was open for 4% -> 4% of each run, Pallas kernels for 22% -> 34%
where the time goes in v4:
time: 538 us; the launch traced here: 533 us
  Pallas kernels  333 us (62%)
  waiting for transfers between devices  81.1 us (15%)
  blocking collectives  35.5 us (7%)
  starting transfers between devices  35.2 us (7%)
  local copies, waits for them, and re-layouts  25 us (5%)
  between operations  14.6 us (3%)
  other arithmetic  8.36 us (2%)
    pallas_call x1, Pallas kernels, start(): pl.pallas_call(functools.partial(start_body, n, bits), in_specs=[pl.Block...  95.4 us
    pallas_call x3, Pallas kernels, attend_backward(): pl.pallas_call(functools.partial(backward_body, BQ, BK, SUB), grid_spec=p...  84.4 us
    pallas_call x2, Pallas kernels, attend_forward(): pl.pallas_call(functools.partial(forward_body, BK, SUB), grid_spec=pltpu....  70.2 us
    pallas_call x1, Pallas kernels, dense(): pl.pallas_call(functools.partial(dense_body, own), grid=(rows // block,),...  40.8 us
    ppermute x6, waiting for transfers between devices, rotate(): lax.ppermute(block, axis, [(i, (i + d) % size) for i in range(size)])  36.1 us
    all_to_all x1, blocking collectives, body(): lax.all_to_all(jnp.concatenate([qkv_grad, extra], 1), 'dp', 0, 0, tiled=T...  23.6 us
    ppermute x5, waiting for transfers between devices, add_up(): other = lax.ppermute(value, axis, [(i, i ^ span) for i in range(size)])  22.5 us
    pallas_call x1, Pallas kernels, weight_grads_of(): pl.pallas_call(functools.partial(weight_grads_body, parts), grid=(2 * par...  17.2 us
  transfers between devices with their start and end apart: 18, of which 11 were waited for; matrix products, arithmetic and copies ran while one was open for 4% of the time, Pallas kernels for 34%

profile of v4, /device:TPU:0, one launch (start us, length us, event | category | flops | bytes accessed | tf_op | source)
XLA Modules:
  0.0 532.6 jit_solution(6708310260461928719)
XLA Ops:
  7.3 1.0 copy.98
  8.3 0.9 copy.99
  9.2 0.9 copy.100
  10.3 0.9 copy.102
  11.2 0.7 convert_reduce_fusion.5
  11.9 0.7 pad_maximum_fusion.4.w_ref
  13.3 0.7 pad_maximum_fusion.2
  14.0 95.4 %start.1 = (bf16[4,768,768]{2,1,0:T(8,128)(2,1)}, bf16[4,8,96,768]{3,2,1,0:T(8,128)(2,1)}, f32[4,12,128]{2,1,0:T(8,128)}) custom-call(bf16[768,768]{1,0:T(8,128)(2,1)} %bitcast.75, bf16[96,768]{1,0:T(8,128)(2,1)} %pad_maximum_fusion.4.w_ref, f32[12,128]{1,0:T(8,128)} %pad_maximum_fusion.5.s_ref), custom_call_target="tpu_custom_call" | custom-call | bytes 209715200 | tf_op jit(solution)/shard_map/start/pallas_call | solution.py:346
  109.5 0.8 copy.128
  110.4 1.7 copy.123
  112.4 0.7 reshape_reshape.23.b_ref
  113.5 0.7 convert_reduce_fusion.3
  114.2 11.0 %project.1 = (bf16[3,128,3072]{2,1,0:T(8,128)(2,1)}, bf16[3,3072,128]{2,1,0:T(8,128)(2,1)}, bf16[3,64,3072]{2,1,0:T(8,128)(2,1)}, bf16[3,3072,64]{2,1,0:T(8,128)...) custom-call(s32[1]{0:T(128)} %bitcast.13.part_ref, bf16[3072,768]{1,0:T(8,128)(2,1)} %bitcast.70, ...), custom_call_target="tpu_custom_call" | custom-call | flops 2717908992 | bytes 17694720 | tf_op jit(solution)/shard_map/project/pallas_call | solution.py:46
  125.3 43.9 %attend_forward.3 = (bf16[4,128,768]{2,1,0:T(8,128)(2,1)}, f32[2,64,3072]{2,1,0:T(8,128)}, f32[2,1,3072]{2,1,0:T(1,128)}) custom-call(s32[8]{0:T(128)} %get-tuple-element.211.lo_ref, s32[8]{0:T(128)} %get-tuple-element.210.hi_ref, bf16[3,128,3072]{2,1,0:T(8,128)(2,1)} %get-tuple-element.60.qt_ref, bf16[3,3072,128]{2,1,0:T(8,128)(2,1)} %get-tuple-element.61.ka_ref, ...), custom_call_target="tpu_custom_call" | custom-call | flops 4831838208 | bytes 6291456 | tf_op jit(solution)/shard_map/attend_forward/pallas_call | solution.py:90
  169.2 3.5 all-to-all-start
  172.8 26.2 %attend_forward.2 = (bf16[4,64,768]{2,1,0:T(8,128)(2,1)}, f32[1,64,3072]{2,1,0:T(8,128)}, f32[1,1,3072]{2,1,0:T(1,128)}) custom-call(s32[8]{0:T(128)} %get-tuple-element.211.lo_ref, s32[8]{0:T(128)} %get-tuple-element.210.hi_ref, bf16[3,128,3072]{2,1,0:T(8,128)(2,1)} %get-tuple-element.60.qt_ref, bf16[3,3072,128]{2,1,0:T(8,128)(2,1)} %get-tuple-element.61.ka_ref, ...), custom_call_target="tpu_custom_call" | custom-call | flops 2415919104 | bytes 3145728 | tf_op jit(solution)/shard_map/attend_forward/pallas_call | solution.py:90
  199.0 3.9 all-to-all-done.ctx0_ref
  202.9 3.5 all-to-all-start.1
  208.0 7.2 %all-to-all-done.1.ctx1_ref = bf16[4,64,768]{2,1,0:T(8,128)(2,1)S(1)} async-done(((bf16[4,64,768]{2,1,0:T(8,128)(2,1)}), bf16[4,64,768]{2,1,0:T(8,128)(2,1)S(1)}, u32[]{:S(2)}, u32[]{:S(2)}) %all-to-all-start.1) | async-done | bytes 393248 | tf_op jit(solution)/shard_map/all_to_all | solution.py:639
  215.2 0.8 copy-done.4
  216.0 40.8 %dense.1 = (bf16[768,768]{1,0:T(8,128)(2,1)}, bf16[768,768]{1,0:T(8,128)(2,1)}, bf16[768,768]{1,0:T(8,128)(2,1)}, bf16[768,768]{1,0:T(8,128)(2,1)}, f32[768,768]...) custom-call(bf16[768,768]{1,0:T(8,128)(2,1)} %bitcast.76, ...), custom_call_target="tpu_custom_call" | custom-call | flops 16307453952 | bytes 41943040 | tf_op jit(solution)/shard_map/dense/pallas_call | solution.py:510
  256.8 17.2 %weight_grads.1 = bf16[768,6912]{1,0:T(8,128)(2,1)} custom-call(bf16[768,768]{1,0:T(8,128)(2,1)} %get-tuple-element.88.first_ref, bf16[768,768]{1,0:T(8,128)(2,1)} %get-tuple-element.89.second_ref, bf16[768,768]{1,0:T(8,128)(2,1)} %get-tuple-element.90.attn_ref, bf16[4,768,768]{2,1,0:T(8,128)(2,1)} %get-tuple-element.91.inner_ref, ...), custom_call_target="tpu_custom_call" | custom-call | flops 8153726976 | bytes 18874368 | tf_op jit(solution)/shard_map/weight_grads/pallas_call | solution.py:395
  274.0 1.0 copy-done.5
  275.0 11.9 %all_to_all.35.go_ref = bf16[4,64,768]{2,1,0:T(8,128)(2,1)} all-to-all(bf16[4,64,768]{2,1,0:T(8,128)(2,1)S(1)} %copy-done.5), channel_id=1, replica_groups=mesh['dp'=8,'tensor'=4] {'tensor'}, dimensions={0} | all-to-all | bytes 786432 | tf_op jit(solution)/shard_map/all_to_all | solution.py:645
  286.9 3.5 all-to-all-start.4
  290.5 0.7 convert_reduce_fusion.1
  291.2 28.4 %attend_backward.3 = (bf16[4,192,768]{2,1,0:T(8,128)(2,1)}, bf16[768,192]{1,0:T(8,128)(2,1)}, f32[192,128]{1,0:T(8,128)}) custom-call(s32[6]{0:T(128)} %get-tuple-element.190.lo_ref, s32[6]{0:T(128)} %get-tuple-element.189.hi_ref, bf16[4,64,768]{2,1,0:T(8,128)(2,1)} %all_to_all.35.go_ref, f32[2,64,3072]{2,1,0:T(8,128)} %get-tuple-element.70.ot_ref, ...), custom_call_target="tpu_custom_call" | custom-call | flops 6039797760 | bytes 5505024 | tf_op jit(solution)/shard_map/attend_backward/pallas_call | solution.py:163
  319.6 1.0 slice_reduce_fusion.2
  320.7 0.9 copy-done.3
  321.5 27.8 %attend_backward.5 = (bf16[4,192,768]{2,1,0:T(8,128)(2,1)}, bf16[768,192]{1,0:T(8,128)(2,1)}, f32[192,128]{1,0:T(8,128)}) custom-call(s32[6]{0:T(128)} %get-tuple-element.190.lo_ref, s32[6]{0:T(128)} %get-tuple-element.189.hi_ref, bf16[4,128,768]{2,1,0:T(8,128)(2,1)} %copy-done.3, f32[1,64,3072]{2,1,0:T(8,128)} %get-tuple-element.79.ot_ref, ...), custom_call_target="tpu_custom_call" | custom-call | flops 6039797760 | bytes 5505024 | tf_op jit(solution)/shard_map/attend_backward/pallas_call | solution.py:163
  349.4 1.0 slice_reduce_fusion
  350.4 28.1 %attend_backward.4 = (bf16[4,192,768]{2,1,0:T(8,128)(2,1)}, bf16[768,192]{1,0:T(8,128)(2,1)}, f32[192,128]{1,0:T(8,128)}) custom-call(s32[6]{0:T(128)} %get-tuple-element.190.lo_ref, s32[6]{0:T(128)} %get-tuple-element.189.hi_ref, bf16[4,128,768]{2,1,0:T(8,128)(2,1)} %copy-done.3, f32[2,64,3072]{2,1,0:T(8,128)} %get-tuple-element.70.ot_ref, ...), custom_call_target="tpu_custom_call" | custom-call | flops 6039797760 | bytes 5505024 | tf_op jit(solution)/shard_map/attend_backward/pallas_call | solution.py:163
  378.5 1.0 slice_reduce_fusion.1
  379.7 1.3 pad_maximum_fusion.1
  381.2 23.6 %all_to_all.36 = bf16[8,112,576]{2,1,0:T(8,128)(2,1)S(1)} all-to-all(bf16[8,112,576]{2,1,0:T(8,128)(2,1)S(1)} %pad_maximum_fusion), channel_id=1, replica_groups=mesh['dp'=8,'tensor'=4] {'dp'}, dimensions={0} | all-to-all | bytes 2064384 | tf_op jit(solution)/shard_map/all_to_all | solution.py:684
  404.8 5.3 all-to-all-start.3
  410.1 1.2 collective-permute-done.6
  411.9 3.5 collective-permute-done.7
  416.1 3.5 collective-permute-done.8
  419.6 2.1 collective-permute-start.9
  421.7 8.3 %collective-permute-done.9 = f32[16,768]{1,0:T(8,128)S(1)} collective-permute-done((f32[16,768]{1,0:T(8,128)S(1)}, f32[16,768]{1,0:T(8,128)S(1)}, u32[]{:S(2)}, u32[]{:S(2)}) %collective-permute-start.9) | collective-permute-done | bytes 49184 | tf_op jit(solution)/shard_map/ppermute | solution.py:584
  430.0 4.7 collective-permute-start.10
  434.7 5.8 %collective-permute-done.10 = f32[16,768]{1,0:T(8,128)} collective-permute-done((f32[16,768]{1,0:T(8,128)S(1)}, f32[16,768]{1,0:T(8,128)}, u32[]{:S(2)}, u32[]{:S(2)}) %collective-permute-start.10) | collective-permute-done | bytes 49184 | tf_op jit(solution)/shard_map/ppermute | solution.py:584
  440.5 0.8 add.110
  442.0 4.3 all-to-all-start.5
  446.3 1.0 dynamic-slice_bitcast_fusion.3
  447.3 2.0 collective-permute-start
  449.3 2.4 collective-permute-start.1
  451.7 1.5 collective-permute-start.2
  453.5 0.7 copy.112
  454.2 0.7 copy.113
  455.0 0.7 copy.114
  455.8 0.9 slice.133
  456.9 1.1 slice-done
  458.1 0.9 dynamic-slice_bitcast_fusion.2
  460.1 17.1 %collective-permute-done.rest_1_ = bf16[192,768]{1,0:T(8,128)(2,1)S(1)} collective-permute-done((bf16[192,768]{1,0:T(8,128)(2,1)}, bf16[192,768]{1,0:T(8,128)(2,1)S(1)}, u32[]{:S(2)}, u32[]{:S(2)}) %collective-permute-start) | collective-permute-done | bytes 294944 | tf_op jit(solution)/shard_map/ppermute | solution.py:597
  478.5 11.4 %all-to-all-done.5.b1_ref = bf16[4,192,768]{2,1,0:T(8,128)(2,1)} async-done(((bf16[4,192,768]{2,1,0:T(8,128)(2,1)}), bf16[4,192,768]{2,1,0:T(8,128)(2,1)}, u32[]{:S(2)}, u32[]{:S(2)}) %all-to-all-start.5) | async-done | bytes 1179680 | tf_op jit(solution)/shard_map/all_to_all | solution.py:670
  489.9 7.0 %early_back.1.acc_ref = f32[768,768]{1,0:T(8,128)} custom-call(bf16[4,768,768]{2,1,0:T(8,128)(2,1)} %bitcast.67, bf16[4,192,768]{2,1,0:T(8,128)(2,1)} %copy-done, bf16[4,192,768]{2,1,0:T(8,128)(2,1)} %all-to-all-done.5.b1_ref), custom_call_target="tpu_custom_call" | custom-call | flops 1811939328 | bytes 10485760 | tf_op jit(solution)/shard_map/early_back/pallas_call | solution.py:550
  496.9 12.2 %collective-permute-done.1.rest_2_ = bf16[192,768]{1,0:T(8,128)(2,1)} collective-permute-done((bf16[192,768]{1,0:T(8,128)(2,1)}, bf16[192,768]{1,0:T(8,128)(2,1)}, u32[]{:S(2)}, u32[]{:S(2)}) %collective-permute-start.1) | collective-permute-done | bytes 294944 | tf_op jit(solution)/shard_map/ppermute | solution.py:597
  509.1 6.9 %late_back.1 = bf16[768,768]{1,0:T(8,128)(2,1)} custom-call(s32[1]{0:T(128)} %bitcast.13.part_ref, bf16[4,768,768]{2,1,0:T(8,128)(2,1)} %bitcast.68, f32[768,768]{1,0:T(8,128)} %early_back.1.acc_ref, f32[768,768]{1,0:T(8,128)} %get-tuple-element.78.grad_ref, bf16[192,768]{1,0:T(8,128)(2,1)} %get-tuple-element.197.rest_0_, bf16[192,768]{1,0:T(8,128)(2,1)} %copy-done.8, ...), custom_call_target="tpu_custom_call" | custom-call | flops 905969664 | bytes 10485760 | tf_op jit(solution)/shard_map/late_back/pallas_call | solution.py:564
  516.0 6.8 %collective-permute-done.4 = bf16[96,1728]{1,0:T(8,128)(2,1)} collective-permute-done((bf16[96,1728]{1,0:T(8,128)(2,1)}, bf16[96,1728]{1,0:T(8,128)(2,1)}, u32[]{:S(2)}, u32[]{:S(2)}) %collective-permute-start.4) | collective-permute-done | bytes 331808 | tf_op jit(solution)/shard_map/ppermute | solution.py:597
  522.8 1.3 fusion.1
  524.1 0.9 slice_bitcast_fusion
  525.0 0.7 copy.115
  (109 shorter events, 8.8 us)
Async XLA Ops:
  7.2 5.5 %copy-start.19 = (f32[768]{0:T(1024)S(1)}, f32[768]{0:T(1024)}, u32[]{:S(2)}) copy-start(f32[768]{0:T(1024)} %param.30) | copy-start | bytes 9220
  7.2 6.1 %copy-start.9 = (bf16[768,96]{0,1:T(8,128)(2,1)S(1)}, bf16[768,96]{0,1:T(8,128)(2,1)}, u32[]{:S(2)}) copy-start(bf16[768,96]{0,1:T(8,128)(2,1)} %param.31) | copy-start | bytes 442372
  7.2 6.1 %copy-start.10 = (bf16[96,768]{1,0:T(8,128)(2,1)S(1)}, bf16[96,768]{1,0:T(8,128)(2,1)}, u32[]{:S(2)}) copy-start(bf16[96,768]{1,0:T(8,128)(2,1)} %param.29) | copy-start | bytes 442372
  7.2 208.0 %all-gather.2.cloned.1.call-start = ((), (), s32[]{:S(2)}) async-start(), calls=%async_computation.8 | async-start | bytes 9732096 | tf_op jit(solution)/shard_map/all_gather | solution.py:623
  109.4 2.6 copy-start.20
  109.5 2.7 copy-start.21
  110.3 3.9 copy-start.11
  169.2 33.7 %all-to-all-start = ((bf16[4,128,768]{2,1,0:T(8,128)(2,1)}), bf16[4,128,768]{2,1,0:T(8,128)(2,1)S(1)}, u32[]{:S(2)}, u32[]{:S(2)}) async-start(bf16[4,128,768]{2,1,0:T(8,128)(2,1)} %get-tuple-element.64), calls=%async_computation | async-start | bytes 1572864 | tf_op jit(solution)/shard_map/all_to_all | solution.py:639
  172.7 34.5 %copy-start.13 = (f32[768]{0:T(1024)S(1)}, f32[768]{0:T(1024)}, u32[]{:S(2)}) copy-start(f32[768]{0:T(1024)} %param.26) | copy-start | bytes 9220
  172.7 34.5 %copy-start.14 = (f32[768]{0:T(1024)S(1)}, f32[768]{0:T(1024)}, u32[]{:S(2)}) copy-start(f32[768]{0:T(1024)} %param.27) | copy-start | bytes 9220
  172.7 34.5 %copy-start.15 = (f32[768]{0:T(1024)S(1)}, f32[768]{0:T(1024)}, u32[]{:S(2)}) copy-start(f32[768]{0:T(1024)} %param.28) | copy-start | bytes 9220
  172.7 34.5 %copy-start.16 = (f32[768]{0:T(1024)S(1)}, f32[768]{0:T(1024)}, u32[]{:S(2)}) copy-start(f32[768]{0:T(1024)} %param.32) | copy-start | bytes 9220
  172.7 34.5 %copy-start.17 = (f32[768]{0:T(1024)S(1)}, f32[768]{0:T(1024)}, u32[]{:S(2)}) copy-start(f32[768]{0:T(1024)} %param.33) | copy-start | bytes 9220
  172.8 34.6 %copy-start.18 = (f32[768]{0:T(1024)S(1)}, f32[768]{0:T(1024)}, u32[]{:S(2)}) copy-start(f32[768]{0:T(1024)} %param.34) | copy-start | bytes 9220
  202.9 12.3 %copy-start.2 = (bf16[4,128,768]{2,1,0:T(8,128)(2,1)}, bf16[4,128,768]{2,1,0:T(8,128)(2,1)S(1)}, u32[]{:S(2)}) copy-start(bf16[4,128,768]{2,1,0:T(8,128)(2,1)S(1)} %all-to-all-done.ctx0_ref) | copy-start | bytes 2359300
  202.9 12.3 %all-to-all-start.1 = ((bf16[4,64,768]{2,1,0:T(8,128)(2,1)}), bf16[4,64,768]{2,1,0:T(8,128)(2,1)S(1)}, u32[]{:S(2)}, u32[]{:S(2)}) async-start(bf16[4,64,768]{2,1,0:T(8,128)(2,1)} %get-tuple-element.66), calls=%async_computation.1 | async-start | bytes 786432 | tf_op jit(solution)/shard_map/all_to_all | solution.py:639
  206.4 249.4 %reduce-scatter.2.cloned.1.call-start = ((), (), s32[]{:S(2)}) async-start(), calls=%async_computation.9 | async-start | bytes 11943936 | tf_op jit(solution)/shard_map/reduce_scatter | solution.py:650
  215.2 0.8 copy-start.4
  274.0 1.0 copy-start.5
  286.9 33.7 %all-to-all-start.4 = ((bf16[4,128,768]{2,1,0:T(8,128)(2,1)}), bf16[4,128,768]{2,1,0:T(8,128)(2,1)S(1)}, u32[]{:S(2)}, u32[]{:S(2)}) async-start(bf16[4,128,768]{2,1,0:T(8,128)(2,1)} %get-tuple-element.76), calls=%async_computation.4 | async-start | bytes 1572864 | tf_op jit(solution)/shard_map/all_to_all | solution.py:646
  320.6 0.9 copy-start.3
  350.4 29.3 %copy-start.6 = (bf16[768,192]{1,0:T(8,128)(2,1)S(1)}, bf16[768,192]{1,0:T(8,128)(2,1)}, u32[]{:S(2)}) copy-start(bf16[768,192]{1,0:T(8,128)(2,1)} %get-tuple-element.82) | copy-start | bytes 884740
  350.4 29.3 %copy-start.7 = (bf16[768,192]{1,0:T(8,128)(2,1)S(1)}, bf16[768,192]{1,0:T(8,128)(2,1)}, u32[]{:S(2)}) copy-start(bf16[768,192]{1,0:T(8,128)(2,1)} %get-tuple-element.84) | copy-start | bytes 884740
  404.8 5.3 copy-start.12
  404.8 37.2 %all-to-all-start.3 = ((bf16[4,192,768]{2,1,0:T(8,128)(2,1)}), bf16[4,192,768]{2,1,0:T(8,128)(2,1)S(1)}, u32[]{:S(2)}, u32[]{:S(2)}) async-start(bf16[4,192,768]{2,1,0:T(8,128)(2,1)} %get-tuple-element.75), calls=%async_computation.3 | async-start | bytes 2359296 | tf_op jit(solution)/shard_map/all_to_all | solution.py:670
  410.0 1.2 collective-permute-start.6
  411.3 4.1 collective-permute-start.7
  415.4 4.2 collective-permute-start.8
  419.6 10.4 %collective-permute-start.9 = (f32[16,768]{1,0:T(8,128)S(1)}, f32[16,768]{1,0:T(8,128)S(1)}, u32[]{:S(2)}, u32[]{:S(2)}) collective-permute-start(f32[16,768]{1,0:T(8,128)S(1)} %add.108), channel_id=1, source_target_pairs={{0,1},{1,0},{2,3},{3,2},{4,5},{5,4},{6,7},{7,6},{8,9},{9,8},{10,11... | collective-permute-start | bytes 147464 | tf_op jit(solution)/shard_map/ppermute | solution.py:584
  430.0 16.3 %copy-start.1 = (bf16[4,192,768]{2,1,0:T(8,128)(2,1)S(1)}, bf16[4,192,768]{2,1,0:T(8,128)(2,1)}, u32[]{:S(2)}) copy-start(bf16[4,192,768]{2,1,0:T(8,128)(2,1)} %get-tuple-element.81) | copy-start | bytes 3538948
  430.0 10.5 %collective-permute-start.10 = (f32[16,768]{1,0:T(8,128)S(1)}, f32[16,768]{1,0:T(8,128)}, u32[]{:S(2)}, u32[]{:S(2)}) collective-permute-start(f32[16,768]{1,0:T(8,128)S(1)} %add.109), channel_id=1, source_target_pairs={{0,2},{1,3},{2,0},{3,1},{4,6},{5,7},{6,4},{7,5},{8,10},{9,11},{10,... | collective-permute-start | bytes 147464 | tf_op jit(solution)/shard_map/ppermute | solution.py:584
  442.0 5.3 copy-start
  442.0 47.9 %all-to-all-start.5 = ((bf16[4,192,768]{2,1,0:T(8,128)(2,1)}), bf16[4,192,768]{2,1,0:T(8,128)(2,1)}, u32[]{:S(2)}, u32[]{:S(2)}) async-start(bf16[4,192,768]{2,1,0:T(8,128)(2,1)} %get-tuple-element.77), calls=%async_computation.5 | async-start | bytes 2359296 | tf_op jit(solution)/shard_map/all_to_all | solution.py:670
  447.3 29.9 %collective-permute-start = (bf16[192,768]{1,0:T(8,128)(2,1)}, bf16[192,768]{1,0:T(8,128)(2,1)S(1)}, u32[]{:S(2)}, u32[]{:S(2)}) collective-permute-start(bf16[192,768]{1,0:T(8,128)(2,1)} %get-tuple-element.196), channel_id=1, source_target_pairs={{0,1},{1,2},{2,3},{3,0},{4,5},{5,6},{6,7},{7,4},{8,9},{9,10},{10,1... | collective-permute-start | bytes 884744 | tf_op jit(solution)/shard_map/ppermute | solution.py:597
  449.3 59.8 %collective-permute-start.1 = (bf16[192,768]{1,0:T(8,128)(2,1)}, bf16[192,768]{1,0:T(8,128)(2,1)}, u32[]{:S(2)}, u32[]{:S(2)}) collective-permute-start(bf16[192,768]{1,0:T(8,128)(2,1)} %get-tuple-element.195), channel_id=1, source_target_pairs={{0,2},{1,3},{2,0},{3,1},{4,6},{5,7},{6,4},{7,5},{8,10},{9,11},{10,... | collective-permute-start | bytes 884744 | tf_op jit(solution)/shard_map/ppermute | solution.py:597
  451.7 57.4 %collective-permute-start.2 = (bf16[192,768]{1,0:T(8,128)(2,1)}, bf16[192,768]{1,0:T(8,128)(2,1)}, u32[]{:S(2)}, u32[]{:S(2)}) collective-permute-start(bf16[192,768]{1,0:T(8,128)(2,1)} %get-tuple-element.194), channel_id=1, source_target_pairs={{0,3},{1,0},{2,1},{3,2},{4,7},{5,4},{6,5},{7,6},{8,11},{9,8},{10,9... | collective-permute-start | bytes 884744 | tf_op jit(solution)/shard_map/ppermute | solution.py:597
  456.7 1.3 slice-start
  459.0 56.9 %collective-permute-start.3 = (bf16[96,1728]{1,0:T(8,128)(2,1)}, bf16[96,1728]{1,0:T(8,128)(2,1)}, u32[]{:S(2)}, u32[]{:S(2)}) collective-permute-start(bf16[96,1728]{1,0:T(8,128)(2,1)} %get-tuple-element.191), channel_id=1, source_target_pairs={{0,1},{1,2},{2,3},{3,0},{4,5},{5,6},{6,7},{7,4},{8,9},{9,10},{10,1... | collective-permute-start | bytes 995336 | tf_op jit(solution)/shard_map/ppermute | solution.py:597
  459.6 63.2 %collective-permute-start.4 = (bf16[96,1728]{1,0:T(8,128)(2,1)}, bf16[96,1728]{1,0:T(8,128)(2,1)}, u32[]{:S(2)}, u32[]{:S(2)}) collective-permute-start(bf16[96,1728]{1,0:T(8,128)(2,1)} %get-tuple-element.193), channel_id=1, source_target_pairs={{0,2},{1,3},{2,0},{3,1},{4,6},{5,7},{6,4},{7,5},{8,10},{9,11},{10,... | collective-permute-start | bytes 995336 | tf_op jit(solution)/shard_map/ppermute | solution.py:597
  477.2 19.7 %copy-start.8 = (bf16[192,768]{1,0:T(8,128)(2,1)}, bf16[192,768]{1,0:T(8,128)(2,1)S(1)}, u32[]{:S(2)}) copy-start(bf16[192,768]{1,0:T(8,128)(2,1)S(1)} %collective-permute-done.rest_1_) | copy-start | bytes 884740
  477.2 45.6 %collective-permute-start.5 = (bf16[96,1728]{1,0:T(8,128)(2,1)S(1)}, bf16[96,1728]{1,0:T(8,128)(2,1)}, u32[]{:S(2)}, u32[]{:S(2)}) collective-permute-start(bf16[96,1728]{1,0:T(8,128)(2,1)S(1)} %get-tuple-element.192), channel_id=1, source_target_pairs={{0,3},{1,0},{2,1},{3,2},{4,7},{5,4},{6,5},{7,6},{8,11},{9,8},{10,9... | collective-permute-start | bytes 995336 | tf_op jit(solution)/shard_map/ppermute | solution.py:597
Sparse Core Ops, SparseCore 0:
  109.6 94.5 all-gather.1
  274.1 84.8 reduce-scatter.1

commit v5 on v4

--- a/solution.py
+++ b/solution.py
@@ -54,25 +54,38 @@
         name="project")(part.reshape(1),x,rest,b.reshape(1,-1),seg.reshape(-1,1),seg.reshape(1,-1))
 
 
-def forward_body(BK, SUB, lo_ref, hi_ref, qt_ref, ka_ref, vt_ref, ctx_ref, ot_ref, lse_ref, m_s, l_s, acc):
+def forward_body(BK, lo_ref, hi_ref, qt_ref, ka_ref, vt_ref, ctx_ref, ot_ref, lse_ref, m_s, l_s, acc, s_even, s_odd):
     i=pl.program_id(0)
-    heads,_,BQ=qt_ref.shape
-    chains=[(h,slice(c*SUB,(c+1)*SUB)) for h in range(heads) for c in range(BQ//SUB)]
+    heads=qt_ref.shape[0]
+    half=BK//2
     m_s[...]=jnp.full(m_s.shape,-jnp.inf,jnp.float32)
     l_s[...]=jnp.zeros(l_s.shape,jnp.float32)
     acc[...]=jnp.zeros(acc.shape,jnp.float32)
 
+    def scores(h,at):
+        return dot(ka_ref[h,pl.ds(pl.multiple_of(at,half),half),:],qt_ref[h])
+
+    def use(h,at,s):
+        m_old=m_s[h]
+        m_new=jnp.maximum(m_old,jnp.max(s,axis=0,keepdims=True))
+        p=jnp.exp(s-m_new)
+        alpha=jnp.exp(m_old-m_new)
+        m_s[h]=m_new
+        l_s[h]=l_s[h]*alpha+jnp.sum(p,axis=0,keepdims=True)
+        acc[h]=acc[h]*alpha+dot(vt_ref[h,:,pl.ds(pl.multiple_of(at,half),half)],p.astype(jnp.bfloat16))
+
+    last=hi_ref[i]-1
+    for h in range(heads):
+        s_even[h]=scores(h,lo_ref[i]*BK)
+
     def step(j,_):
-        at=pl.multiple_of(j*BK,BK)
-        for h,cut in chains:
-            s=dot(ka_ref[h,pl.ds(at,BK),:],qt_ref[h,:,cut])
-            m_old=m_s[h,:,cut]
-            m_new=jnp.maximum(m_old,jnp.max(s,axis=0,keepdims=True))
-            p=jnp.exp(s-m_new)
-            alpha=jnp.exp(m_old-m_new)
-            m_s[h,:,cut]=m_new
-            l_s[h,:,cut]=l_s[h,:,cut]*alpha+jnp.sum(p,axis=0,keepdims=True)
-            acc[h,:,cut]=acc[h,:,cut]*alpha+dot(vt_ref[h,:,pl.ds(at,BK)],p.astype(jnp.bfloat16))
+        at=j*BK
+        for h in range(heads):
+            s_odd[h]=scores(h,at+half)
+            use(h,at,s_even[h])
+        for h in range(heads):
+            s_even[h]=scores(h,jnp.minimum(j+1,last)*BK)
+            use(h,at+half,s_odd[h])
         return 0
 
     lax.fori_loop(lo_ref[i],hi_ref[i],step,0)
@@ -83,15 +96,15 @@
         ctx_ref[0,h*HD:(h+1)*HD,:]=o.astype(jnp.bfloat16)
 
 
-def attend_forward(first,heads,parts,qt,ka,vt,lo,hi,BQ=384,BK=512,SUB=384):
+def attend_forward(first,heads,parts,qt,ka,vt,lo,hi,BQ=384,BK=512):
     L=qt.shape[2]
     S=jax.ShapeDtypeStruct
     per=L//parts//BQ
-    return pl.pallas_call(functools.partial(forward_body,BK,SUB),
+    return pl.pallas_call(functools.partial(forward_body,BK),
         grid_spec=pltpu.PrefetchScalarGridSpec(num_scalar_prefetch=2,grid=(L//BQ,),
         in_specs=[pl.BlockSpec((heads,2*HD,BQ),lambda i,*_:(first//heads,0,i)),pl.BlockSpec((heads,L,2*HD),lambda i,*_:(first//heads,0,0)),pl.BlockSpec((heads,HD,L),lambda i,*_:(first//heads,0,0))],
         out_specs=[pl.BlockSpec((1,heads*HD,BQ),lambda i,*_:(i//per,0,i%per)),pl.BlockSpec((heads,HD,BQ),lambda i,*_:(0,0,i)),pl.BlockSpec((heads,1,BQ),lambda i,*_:(0,0,i))],
-        scratch_shapes=[VM((heads,1,BQ),jnp.float32),VM((heads,1,BQ),jnp.float32),VM((heads,HD,BQ),jnp.float32)]),
+        scratch_shapes=[VM((heads,1,BQ),jnp.float32),VM((heads,1,BQ),jnp.float32),VM((heads,HD,BQ),jnp.float32)]+[VM((heads,BK//2,BQ),jnp.float32)]*2),
         out_shape=[S((parts,heads*HD,L//parts),jnp.bfloat16),S((heads,HD,L),jnp.float32),S((heads,1,L),jnp.float32)],
         compiler_params=pltpu.CompilerParams(vmem_limit_bytes=62 << 20),
         cost_estimate=pl.CostEstimate(flops=2*L*L*HD*2*heads,bytes_accessed=L*heads*HD*2*8,transcendentals=L*L*heads),
@@ -423,7 +436,7 @@
     f32, bf = jnp.float32, jnp.bfloat16
     units = active_ref.shape[2]
     cuts = (slice(0, 4 * own), slice(4 * own, 4 * own + units), slice(4 * own + units, 4 * own + 2 * units))
-    sources = (near_ref, far_ref.at[:, :, :units], far_ref.at[:, :, units:])
+    sources = (near_ref.at[:, :, cuts[0]], near_ref.at[:, :, cuts[1]], far_ref)
     copies = [pltpu.make_async_copy(sources[c], w_s.at[:, :, cut], w_sem.at[c]) for c, cut in enumerate(cuts)]
 
     @pl.when(i == 0)
@@ -498,7 +511,7 @@
 def dense(own, x, cot, ctx0, ctx1, vectors, inner_bias, near, far, block):
     rows, width = x.shape
     parts = near.shape[0]
-    units = far.shape[2] // 2
+    units = far.shape[2]
     cols = 4 * own + 2 * units
     f32, bf = jnp.float32, jnp.bfloat16
     S = jax.ShapeDtypeStruct
@@ -614,24 +627,24 @@
     x_own = hidden_in[0]
     qkv_own = by_head(query_weight, key_weight, value_weight)
     small = jnp.concatenate([segments[0].astype(f32), inner_bias]).reshape(-1, 128)
-    near_own = jnp.concatenate([qkv_own, mixer_weight.T], 1)
+    near_own = jnp.concatenate([qkv_own, mixer_weight.T, inner_weight], 1)
     x_parts, near, small = start(x_own, near_own, small)
     x_all = x_parts.reshape(parts * rows, width)
-    near = near.reshape(parts, width, 4 * own)
-    far_own = jnp.concatenate([inner_weight, outer_weight.T], 1)
+    near = near.reshape(parts, width, 4 * own + units)
+    far_own = outer_weight.T
     far_own, small = lax.optimization_barrier((far_own, small))
-    far = lax.all_gather(far_own, ("tensor", "dp"), axis=0, tiled=True).reshape(parts, width, 2 * units)
+    far = lax.all_gather(far_own, ("tensor", "dp"), axis=0, tiled=True).reshape(parts, width, units)
     small = small.reshape(parts, -1)
     segment_all = small[:, :rows].astype(jnp.int32).reshape(-1)
     inner_bias_all = small[:, rows:]
     biases = by_head(query_bias, jnp.zeros_like(query_bias), value_bias)
 
     qt, ka, vt, qn, kt, vn = project(x_all, near, rank, biases, segment_all)
-    lo, hi = ranges(segment_all, 384, 512)
     lead = heads - 1
     context_t, lse, exchanged = [], [], []
-    for call, (first, count) in enumerate(((0, lead), (lead, 1))):
-        part, out_t, out_lse = attend_forward(first, count, parts, qt, ka, vt, lo, hi)
+    for call, (first, count, block) in enumerate(((0, lead, rows // 2), (lead, 1, rows))):
+        lo, hi = ranges(segment_all, block, 512)
+        part, out_t, out_lse = attend_forward(first, count, parts, qt, ka, vt, lo, hi, BQ=block)
         context_t.append(out_t)
         lse.append(out_lse)
         if exchanged:

time: 538 us -> 533 us (level)
  starting transfers between devices: 35.2 us -> 67.5 us
  waiting for transfers between devices: 81.1 us -> 58.9 us
  Pallas kernels: 333 us -> 321 us
    ppermute x6, starting transfers between devices: 6.91 us -> 39.2 us  [rotate(): lax.ppermute(block, axis, [(i, (i + d) % size) for i in range(size)])]
    pallas_call x2, Pallas kernels: 70.2 us -> 49 us  [attend_forward(): pl.pallas_call(functools.partial(forward_body, BK), grid_spec=pltpu.Prefe...]
    ppermute x6, waiting for transfers between devices: 36.1 us -> 21.7 us  [rotate(): lax.ppermute(block, axis, [(i, (i + d) % size) for i in range(size)])]
    all_to_all x2, waiting for transfers between devices: 11.4 us -> 0.01 us  [body(): backs.append(lax.all_to_all(grads, 'tensor', 0, 0, tiled=True))]
    pallas_call x1, Pallas kernels: 95.4 us -> 105 us  [start(): pl.pallas_call(functools.partial(start_body, n, bits), in_specs=[pl.Block...]
    unnamed x60 -> x56, local copies, waits for them, and re-layouts: 12.2 us -> 12.2 us
  transfers between devices with their start and end apart: 18 -> 18, of which waited for: 11 -> 9; matrix products, arithmetic and copies ran while one was open for 4% -> 4% of each run, Pallas kernels for 34% -> 30%
where the time goes in v5:
time: 533 us; the launch traced here: 531 us
  Pallas kernels  321 us (60%)
  starting transfers between devices  67.5 us (13%)
  waiting for transfers between devices  58.9 us (11%)
  blocking collectives  34.7 us (7%)
  local copies, waits for them, and re-layouts  26 us (5%)
  between operations  14.6 us (3%)
  other arithmetic  8.3 us (2%)
    pallas_call x1, Pallas kernels, start(): pl.pallas_call(functools.partial(start_body, n, bits), in_specs=[pl.Block...  105 us
    pallas_call x3, Pallas kernels, attend_backward(): pl.pallas_call(functools.partial(backward_body, BQ, BK, SUB), grid_spec=p...  84 us
    pallas_call x2, Pallas kernels, attend_forward(): pl.pallas_call(functools.partial(forward_body, BK), grid_spec=pltpu.Prefe...  49 us
    pallas_call x1, Pallas kernels, dense(): pl.pallas_call(functools.partial(dense_body, own), grid=(rows // block,),...  40.7 us
    ppermute x6, starting transfers between devices, rotate(): lax.ppermute(block, axis, [(i, (i + d) % size) for i in range(size)])  39.2 us
    ppermute x5, waiting for transfers between devices, add_up(): other = lax.ppermute(value, axis, [(i, i ^ span) for i in range(size)])  22.5 us
    ppermute x6, waiting for transfers between devices, rotate(): lax.ppermute(block, axis, [(i, (i + d) % size) for i in range(size)])  21.7 us
    all_to_all x1, blocking collectives, body(): lax.all_to_all(jnp.concatenate([qkv_grad, extra], 1), 'dp', 0, 0, tiled=T...  21.5 us
  transfers between devices with their start and end apart: 18, of which 9 were waited for; matrix products, arithmetic and copies ran while one was open for 4% of the time, Pallas kernels for 30%

profile of v5, /device:TPU:0, one launch (start us, length us, event | category | flops | bytes accessed | tf_op | source)
XLA Modules:
  0.0 530.8 jit_solution(9045891205996199063)
XLA Ops:
  7.2 0.9 copy.100
  8.2 0.9 copy.99
  9.1 0.9 copy.98
  10.3 0.9 copy.102
  11.2 0.7 convert_reduce_fusion.5
  11.9 1.3 pad_maximum_fusion.3.s_ref
  13.2 0.8 concatenate.44.w_ref
  14.0 105.2 %start.1 = (bf16[4,768,768]{2,1,0:T(8,128)(2,1)}, bf16[4,8,96,1536]{3,2,1,0:T(8,128)(2,1)}, f32[4,12,128]{2,1,0:T(8,128)}) custom-call(bf16[768,768]{1,0:T(8,128)(2,1)} %bitcast.74, bf16[96,1536]{1,0:T(8,128)(2,1)} %concatenate.44.w_ref, f32[12,128]{1,0:T(8,128)} %pad_maximum_fusion.3.s_ref), custom_call_target="tpu_custom_call" | custom-call | bytes 209715200 | tf_op jit(solution)/shard_map/start/pallas_call | solution.py:359
  119.2 0.8 copy.128
  121.3 1.7 copy.123
  123.2 0.7 convert_reduce_fusion.3
  123.9 11.0 %project.1 = (bf16[3,128,3072]{2,1,0:T(8,128)(2,1)}, bf16[3,3072,128]{2,1,0:T(8,128)(2,1)}, bf16[3,64,3072]{2,1,0:T(8,128)(2,1)}, bf16[3,3072,64]{2,1,0:T(8,128)...) custom-call(s32[1]{0:T(128)} %bitcast.11.part_ref, bf16[3072,768]{1,0:T(8,128)(2,1)} %bitcast.71, ...), custom_call_target="tpu_custom_call" | custom-call | flops 2717908992 | bytes 17694720 | tf_op jit(solution)/shard_map/project/pallas_call | solution.py:46
  134.9 30.1 %attend_forward.3 = (bf16[4,128,768]{2,1,0:T(8,128)(2,1)}, f32[2,64,3072]{2,1,0:T(8,128)}, f32[2,1,3072]{2,1,0:T(1,128)}) custom-call(s32[8]{0:T(128)} %get-tuple-element.215.lo_ref, s32[8]{0:T(128)} %get-tuple-element.214.hi_ref, bf16[3,128,3072]{2,1,0:T(8,128)(2,1)} %get-tuple-element.60.qt_ref, bf16[3,3072,128]{2,1,0:T(8,128)(2,1)} %get-tuple-element.61.ka_ref, ...), custom_call_target="tpu_custom_call" | custom-call | flops 4831838208 | bytes 6291456 | tf_op jit(solution)/shard_map/attend_forward/pallas_call | solution.py:103
  165.0 3.5 all-to-all-start
  168.7 0.7 convert_reduce_fusion.6
  169.5 18.9 %attend_forward.2 = (bf16[4,64,768]{2,1,0:T(8,128)(2,1)}, f32[1,64,3072]{2,1,0:T(8,128)}, f32[1,1,3072]{2,1,0:T(1,128)}) custom-call(s32[4]{0:T(128)} %get-tuple-element.213.lo_ref, s32[4]{0:T(128)} %get-tuple-element.212.hi_ref, bf16[3,128,3072]{2,1,0:T(8,128)(2,1)} %get-tuple-element.60.qt_ref, bf16[3,3072,128]{2,1,0:T(8,128)(2,1)} %get-tuple-element.61.ka_ref, ...), custom_call_target="tpu_custom_call" | custom-call | flops 2415919104 | bytes 3145728 | tf_op jit(solution)/shard_map/attend_forward/pallas_call | solution.py:103
  188.4 5.7 %all-to-all-done.ctx0_ref = bf16[4,128,768]{2,1,0:T(8,128)(2,1)S(1)} async-done(((bf16[4,128,768]{2,1,0:T(8,128)(2,1)}), bf16[4,128,768]{2,1,0:T(8,128)(2,1)S(1)}, u32[]{:S(2)}, u32[]{:S(2)}) %all-to-all-start) | async-done | bytes 786464 | tf_op jit(solution)/shard_map/all_to_all | solution.py:652
  194.2 3.5 all-to-all-start.1
  199.2 8.9 %all-to-all-done.1.ctx1_ref = bf16[4,64,768]{2,1,0:T(8,128)(2,1)S(1)} async-done(((bf16[4,64,768]{2,1,0:T(8,128)(2,1)}), bf16[4,64,768]{2,1,0:T(8,128)(2,1)S(1)}, u32[]{:S(2)}, u32[]{:S(2)}) %all-to-all-start.1) | async-done | bytes 393248 | tf_op jit(solution)/shard_map/all_to_all | solution.py:652
  208.2 0.8 copy-done.4
  208.9 40.7 %dense.1 = (bf16[768,768]{1,0:T(8,128)(2,1)}, bf16[768,768]{1,0:T(8,128)(2,1)}, bf16[768,768]{1,0:T(8,128)(2,1)}, bf16[768,768]{1,0:T(8,128)(2,1)}, f32[768,768]...) custom-call(bf16[768,768]{1,0:T(8,128)(2,1)} %bitcast.75, ...), custom_call_target="tpu_custom_call" | custom-call | flops 16307453952 | bytes 41943040 | tf_op jit(solution)/shard_map/dense/pallas_call | solution.py:523
  249.7 17.2 %weight_grads.1 = bf16[768,6912]{1,0:T(8,128)(2,1)} custom-call(bf16[768,768]{1,0:T(8,128)(2,1)} %get-tuple-element.88.first_ref, bf16[768,768]{1,0:T(8,128)(2,1)} %get-tuple-element.89.second_ref, bf16[768,768]{1,0:T(8,128)(2,1)} %get-tuple-element.90.attn_ref, bf16[4,768,768]{2,1,0:T(8,128)(2,1)} %get-tuple-element.91.inner_ref, ...), custom_call_target="tpu_custom_call" | custom-call | flops 8153726976 | bytes 18874368 | tf_op jit(solution)/shard_map/weight_grads/pallas_call | solution.py:408
  266.9 1.0 copy-done.5
  267.9 13.2 %all_to_all.35.go_ref = bf16[4,64,768]{2,1,0:T(8,128)(2,1)} all-to-all(bf16[4,64,768]{2,1,0:T(8,128)(2,1)S(1)} %copy-done.5), channel_id=1, replica_groups=mesh['dp'=8,'tensor'=4] {'tensor'}, dimensions={0} | all-to-all | bytes 786432 | tf_op jit(solution)/shard_map/all_to_all | solution.py:658
  281.1 3.5 all-to-all-start.4
  284.6 0.7 convert_reduce_fusion.1
  285.4 28.0 %attend_backward.3 = (bf16[4,192,768]{2,1,0:T(8,128)(2,1)}, bf16[768,192]{1,0:T(8,128)(2,1)}, f32[192,128]{1,0:T(8,128)}) custom-call(s32[6]{0:T(128)} %get-tuple-element.192.lo_ref, s32[6]{0:T(128)} %get-tuple-element.191.hi_ref, bf16[4,64,768]{2,1,0:T(8,128)(2,1)} %all_to_all.35.go_ref, f32[2,64,3072]{2,1,0:T(8,128)} %get-tuple-element.70.ot_ref, ...), custom_call_target="tpu_custom_call" | custom-call | flops 6039797760 | bytes 5505024 | tf_op jit(solution)/shard_map/attend_backward/pallas_call | solution.py:176
  313.4 1.0 slice_reduce_fusion.2
  314.4 0.9 copy-done.3
  315.3 28.0 %attend_backward.5 = (bf16[4,192,768]{2,1,0:T(8,128)(2,1)}, bf16[768,192]{1,0:T(8,128)(2,1)}, f32[192,128]{1,0:T(8,128)}) custom-call(s32[6]{0:T(128)} %get-tuple-element.192.lo_ref, s32[6]{0:T(128)} %get-tuple-element.191.hi_ref, bf16[4,128,768]{2,1,0:T(8,128)(2,1)} %copy-done.3, f32[1,64,3072]{2,1,0:T(8,128)} %get-tuple-element.79.ot_ref, ...), custom_call_target="tpu_custom_call" | custom-call | flops 6039797760 | bytes 5505024 | tf_op jit(solution)/shard_map/attend_backward/pallas_call | solution.py:176
  343.3 1.0 slice_reduce_fusion
  344.3 28.0 %attend_backward.4 = (bf16[4,192,768]{2,1,0:T(8,128)(2,1)}, bf16[768,192]{1,0:T(8,128)(2,1)}, f32[192,128]{1,0:T(8,128)}) custom-call(s32[6]{0:T(128)} %get-tuple-element.192.lo_ref, s32[6]{0:T(128)} %get-tuple-element.191.hi_ref, bf16[4,128,768]{2,1,0:T(8,128)(2,1)} %copy-done.3, f32[2,64,3072]{2,1,0:T(8,128)} %get-tuple-element.70.ot_ref, ...), custom_call_target="tpu_custom_call" | custom-call | flops 6039797760 | bytes 5505024 | tf_op jit(solution)/shard_map/attend_backward/pallas_call | solution.py:176
  372.4 1.0 slice_reduce_fusion.1
  373.6 1.3 pad_maximum_fusion.1
  375.1 21.5 %all_to_all.36 = bf16[8,112,576]{2,1,0:T(8,128)(2,1)S(1)} all-to-all(bf16[8,112,576]{2,1,0:T(8,128)(2,1)S(1)} %pad_maximum_fusion), channel_id=1, replica_groups=mesh['dp'=8,'tensor'=4] {'dp'}, dimensions={0} | all-to-all | bytes 2064384 | tf_op jit(solution)/shard_map/all_to_all | solution.py:697
  396.6 5.3 all-to-all-start.3
  401.9 1.2 collective-permute-done.6
  403.7 3.5 collective-permute-done.7
  407.9 3.5 collective-permute-done.8
  411.4 2.1 collective-permute-start.9
  413.5 8.3 %collective-permute-done.9 = f32[16,768]{1,0:T(8,128)S(1)} collective-permute-done((f32[16,768]{1,0:T(8,128)S(1)}, f32[16,768]{1,0:T(8,128)S(1)}, u32[]{:S(2)}, u32[]{:S(2)}) %collective-permute-start.9) | collective-permute-done | bytes 49184 | tf_op jit(solution)/shard_map/ppermute | solution.py:597
  421.9 4.7 collective-permute-start.10
  426.5 5.8 %collective-permute-done.10 = f32[16,768]{1,0:T(8,128)} collective-permute-done((f32[16,768]{1,0:T(8,128)S(1)}, f32[16,768]{1,0:T(8,128)}, u32[]{:S(2)}, u32[]{:S(2)}) %collective-permute-start.10) | collective-permute-done | bytes 49184 | tf_op jit(solution)/shard_map/ppermute | solution.py:597
  432.4 0.8 add.110
  433.8 4.3 all-to-all-start.5
  438.1 1.0 dynamic-slice_bitcast_fusion.3
  439.2 2.0 collective-permute-start
  441.1 2.4 collective-permute-start.1
  443.5 1.5 collective-permute-start.2
  445.3 0.7 copy.112
  446.1 0.7 copy.113
  446.8 0.7 copy.114
  447.6 0.9 slice.145
  448.8 1.1 slice-done
  449.9 0.9 dynamic-slice_bitcast_fusion.2
  451.4 1.5 collective-permute-start.4
  452.9 16.2 %collective-permute-done.rest_1_ = bf16[192,768]{1,0:T(8,128)(2,1)S(1)} collective-permute-done((bf16[192,768]{1,0:T(8,128)(2,1)}, bf16[192,768]{1,0:T(8,128)(2,1)S(1)}, u32[]{:S(2)}, u32[]{:S(2)}) %collective-permute-start) | collective-permute-done | bytes 294944 | tf_op jit(solution)/shard_map/ppermute | solution.py:610
  469.1 31.4 %collective-permute-start.3 = (bf16[96,1728]{1,0:T(8,128)(2,1)S(1)}, bf16[96,1728]{1,0:T(8,128)(2,1)}, u32[]{:S(2)}, u32[]{:S(2)}) collective-permute-start(bf16[96,1728]{1,0:T(8,128)(2,1)S(1)} %get-tuple-element.193), channel_id=1, source_target_pairs={{0,1},{1,2},{2,3},{3,0},{4,5},{5,6},{6,7},{7,4},{8,9},{9,10},{10,1... | collective-permute-start | bytes 995336 | tf_op jit(solution)/shard_map/ppermute | solution.py:610
  501.8 7.0 %early_back.1.acc_ref = f32[768,768]{1,0:T(8,128)} custom-call(bf16[4,768,1536]{2,1,0:T(8,128)(2,1)} %bitcast.67, bf16[4,192,768]{2,1,0:T(8,128)(2,1)} %copy-done, bf16[4,192,768]{2,1,0:T(8,128)(2,1)} %all-to-all-done.5.b1_ref), custom_call_target="tpu_custom_call" | custom-call | flops 1811939328 | bytes 10485760 | tf_op jit(solution)/shard_map/early_back/pallas_call | solution.py:563
  508.8 6.7 %late_back.1 = bf16[768,768]{1,0:T(8,128)(2,1)} custom-call(s32[1]{0:T(128)} %bitcast.11.part_ref, bf16[4,768,1536]{2,1,0:T(8,128)(2,1)} %bitcast.68, f32[768,768]{1,0:T(8,128)} %early_back.1.acc_ref, f32[768,768]{1,0:T(8,128)} %get-tuple-element.78.grad_ref, bf16[192,768]{1,0:T(8,128)(2,1)} %get-tuple-element.199.rest_0_, bf16[192,768]{1,0:T(8,128)(2,1)} %copy-done.8, ...), custom_call_target="tpu_custom_call" | custom-call | flops 905969664 | bytes 10485760 | tf_op jit(solution)/shard_map/late_back/pallas_call | solution.py:577
  515.5 5.5 %collective-permute-done.4 = bf16[96,1728]{1,0:T(8,128)(2,1)} collective-permute-done((bf16[96,1728]{1,0:T(8,128)(2,1)}, bf16[96,1728]{1,0:T(8,128)(2,1)}, u32[]{:S(2)}, u32[]{:S(2)}) %collective-permute-start.4) | collective-permute-done | bytes 331808 | tf_op jit(solution)/shard_map/ppermute | solution.py:610
  521.0 1.3 fusion.1
  522.4 0.9 slice_bitcast_fusion
  523.2 0.7 copy.115
  (106 shorter events, 8.4 us)
Async XLA Ops:
  7.2 6.0 %copy-start.9 = (bf16[96,768]{1,0:T(8,128)(2,1)S(1)}, bf16[96,768]{1,0:T(8,128)(2,1)}, u32[]{:S(2)}) copy-start(bf16[96,768]{1,0:T(8,128)(2,1)} %param.29) | copy-start | bytes 442372
  7.2 201.0 %all-gather.2.cloned.1.call-start = ((), (), s32[]{:S(2)}) async-start(), calls=%async_computation.8 | async-start | bytes 4866048 | tf_op jit(solution)/shard_map/all_gather | solution.py:636
  10.1 110.2 %copy-start.18 = (f32[192]{0:T(256)S(1)}, f32[192]{0:T(256)}, u32[]{:S(2)}) copy-start(f32[192]{0:T(256)} %param.24) | copy-start | bytes 2308
  10.1 110.2 %copy-start.19 = (f32[192]{0:T(256)S(1)}, f32[192]{0:T(256)}, u32[]{:S(2)}) copy-start(f32[192]{0:T(256)} %param.23) | copy-start | bytes 2308
  121.2 2.7 copy-start.10
  165.0 29.1 %all-to-all-start = ((bf16[4,128,768]{2,1,0:T(8,128)(2,1)}), bf16[4,128,768]{2,1,0:T(8,128)(2,1)S(1)}, u32[]{:S(2)}, u32[]{:S(2)}) async-start(bf16[4,128,768]{2,1,0:T(8,128)(2,1)} %get-tuple-element.64), calls=%async_computation | async-start | bytes 1572864 | tf_op jit(solution)/shard_map/all_to_all | solution.py:652
  169.5 28.4 %copy-start.12 = (f32[768]{0:T(1024)S(1)}, f32[768]{0:T(1024)}, u32[]{:S(2)}) copy-start(f32[768]{0:T(1024)} %param.26) | copy-start | bytes 9220
  169.5 28.4 %copy-start.13 = (f32[768]{0:T(1024)S(1)}, f32[768]{0:T(1024)}, u32[]{:S(2)}) copy-start(f32[768]{0:T(1024)} %param.27) | copy-start | bytes 9220
  169.5 28.4 %copy-start.14 = (f32[768]{0:T(1024)S(1)}, f32[768]{0:T(1024)}, u32[]{:S(2)}) copy-start(f32[768]{0:T(1024)} %param.28) | copy-start | bytes 9220
  169.5 28.4 %copy-start.15 = (f32[768]{0:T(1024)S(1)}, f32[768]{0:T(1024)}, u32[]{:S(2)}) copy-start(f32[768]{0:T(1024)} %param.32) | copy-start | bytes 9220
  169.5 28.5 %copy-start.16 = (f32[768]{0:T(1024)S(1)}, f32[768]{0:T(1024)}, u32[]{:S(2)}) copy-start(f32[768]{0:T(1024)} %param.33) | copy-start | bytes 9220
  169.5 28.5 %copy-start.17 = (f32[768]{0:T(1024)S(1)}, f32[768]{0:T(1024)}, u32[]{:S(2)}) copy-start(f32[768]{0:T(1024)} %param.34) | copy-start | bytes 9220
  194.1 14.0 %copy-start.2 = (bf16[4,128,768]{2,1,0:T(8,128)(2,1)}, bf16[4,128,768]{2,1,0:T(8,128)(2,1)S(1)}, u32[]{:S(2)}) copy-start(bf16[4,128,768]{2,1,0:T(8,128)(2,1)S(1)} %all-to-all-done.ctx0_ref) | copy-start | bytes 2359300
  194.2 14.0 %all-to-all-start.1 = ((bf16[4,64,768]{2,1,0:T(8,128)(2,1)}), bf16[4,64,768]{2,1,0:T(8,128)(2,1)S(1)}, u32[]{:S(2)}, u32[]{:S(2)}) async-start(bf16[4,64,768]{2,1,0:T(8,128)(2,1)} %get-tuple-element.66), calls=%async_computation.1 | async-start | bytes 786432 | tf_op jit(solution)/shard_map/all_to_all | solution.py:652
  197.6 250.0 %reduce-scatter.2.cloned.1.call-start = ((), (), s32[]{:S(2)}) async-start(), calls=%async_computation.9 | async-start | bytes 11943936 | tf_op jit(solution)/shard_map/reduce_scatter | solution.py:663
  208.2 0.8 copy-start.4
  266.9 1.0 copy-start.5
  281.1 33.4 %all-to-all-start.4 = ((bf16[4,128,768]{2,1,0:T(8,128)(2,1)}), bf16[4,128,768]{2,1,0:T(8,128)(2,1)S(1)}, u32[]{:S(2)}, u32[]{:S(2)}) async-start(bf16[4,128,768]{2,1,0:T(8,128)(2,1)} %get-tuple-element.76), calls=%async_computation.4 | async-start | bytes 1572864 | tf_op jit(solution)/shard_map/all_to_all | solution.py:659
  314.4 0.9 copy-start.3
  344.3 29.3 %copy-start.6 = (bf16[768,192]{1,0:T(8,128)(2,1)S(1)}, bf16[768,192]{1,0:T(8,128)(2,1)}, u32[]{:S(2)}) copy-start(bf16[768,192]{1,0:T(8,128)(2,1)} %get-tuple-element.82) | copy-start | bytes 884740
  344.3 29.3 %copy-start.7 = (bf16[768,192]{1,0:T(8,128)(2,1)S(1)}, bf16[768,192]{1,0:T(8,128)(2,1)}, u32[]{:S(2)}) copy-start(bf16[768,192]{1,0:T(8,128)(2,1)} %get-tuple-element.84) | copy-start | bytes 884740
  396.6 5.3 copy-start.11
  396.6 37.2 %all-to-all-start.3 = ((bf16[4,192,768]{2,1,0:T(8,128)(2,1)}), bf16[4,192,768]{2,1,0:T(8,128)(2,1)S(1)}, u32[]{:S(2)}, u32[]{:S(2)}) async-start(bf16[4,192,768]{2,1,0:T(8,128)(2,1)} %get-tuple-element.75), calls=%async_computation.3 | async-start | bytes 2359296 | tf_op jit(solution)/shard_map/all_to_all | solution.py:683
  401.9 1.2 collective-permute-start.6
  403.1 4.1 collective-permute-start.7
  407.3 4.2 collective-permute-start.8
  411.4 10.4 %collective-permute-start.9 = (f32[16,768]{1,0:T(8,128)S(1)}, f32[16,768]{1,0:T(8,128)S(1)}, u32[]{:S(2)}, u32[]{:S(2)}) collective-permute-start(f32[16,768]{1,0:T(8,128)S(1)} %add.108), channel_id=1, source_target_pairs={{0,1},{1,0},{2,3},{3,2},{4,5},{5,4},{6,7},{7,6},{8,9},{9,8},{10,11... | collective-permute-start | bytes 147464 | tf_op jit(solution)/shard_map/ppermute | solution.py:597
  421.9 16.3 %copy-start.1 = (bf16[4,192,768]{2,1,0:T(8,128)(2,1)S(1)}, bf16[4,192,768]{2,1,0:T(8,128)(2,1)}, u32[]{:S(2)}) copy-start(bf16[4,192,768]{2,1,0:T(8,128)(2,1)} %get-tuple-element.81) | copy-start | bytes 3538948
  421.9 10.5 %collective-permute-start.10 = (f32[16,768]{1,0:T(8,128)S(1)}, f32[16,768]{1,0:T(8,128)}, u32[]{:S(2)}, u32[]{:S(2)}) collective-permute-start(f32[16,768]{1,0:T(8,128)S(1)} %add.109), channel_id=1, source_target_pairs={{0,2},{1,3},{2,0},{3,1},{4,6},{5,7},{6,4},{7,5},{8,10},{9,11},{10,... | collective-permute-start | bytes 147464 | tf_op jit(solution)/shard_map/ppermute | solution.py:597
  433.8 5.3 %copy-start = (bf16[4,192,768]{2,1,0:T(8,128)(2,1)}, bf16[4,192,768]{2,1,0:T(8,128)(2,1)S(1)}, u32[]{:S(2)}) copy-start(bf16[4,192,768]{2,1,0:T(8,128)(2,1)S(1)} %all-to-all-done.3.b0_ref) | copy-start | bytes 3538948
  433.8 67.9 %all-to-all-start.5 = ((bf16[4,192,768]{2,1,0:T(8,128)(2,1)}), bf16[4,192,768]{2,1,0:T(8,128)(2,1)}, u32[]{:S(2)}, u32[]{:S(2)}) async-start(bf16[4,192,768]{2,1,0:T(8,128)(2,1)} %get-tuple-element.77), calls=%async_computation.5 | async-start | bytes 2359296 | tf_op jit(solution)/shard_map/all_to_all | solution.py:683
  439.2 29.9 %collective-permute-start = (bf16[192,768]{1,0:T(8,128)(2,1)}, bf16[192,768]{1,0:T(8,128)(2,1)S(1)}, u32[]{:S(2)}, u32[]{:S(2)}) collective-permute-start(bf16[192,768]{1,0:T(8,128)(2,1)} %get-tuple-element.198), channel_id=1, source_target_pairs={{0,1},{1,2},{2,3},{3,0},{4,5},{5,6},{6,7},{7,4},{8,9},{9,10},{10,1... | collective-permute-start | bytes 884744 | tf_op jit(solution)/shard_map/ppermute | solution.py:610
  441.1 67.7 %collective-permute-start.1 = (bf16[192,768]{1,0:T(8,128)(2,1)}, bf16[192,768]{1,0:T(8,128)(2,1)}, u32[]{:S(2)}, u32[]{:S(2)}) collective-permute-start(bf16[192,768]{1,0:T(8,128)(2,1)} %get-tuple-element.197), channel_id=1, source_target_pairs={{0,2},{1,3},{2,0},{3,1},{4,6},{5,7},{6,4},{7,5},{8,10},{9,11},{10,... | collective-permute-start | bytes 884744 | tf_op jit(solution)/shard_map/ppermute | solution.py:610
  443.5 65.3 %collective-permute-start.2 = (bf16[192,768]{1,0:T(8,128)(2,1)}, bf16[192,768]{1,0:T(8,128)(2,1)}, u32[]{:S(2)}, u32[]{:S(2)}) collective-permute-start(bf16[192,768]{1,0:T(8,128)(2,1)} %get-tuple-element.196), channel_id=1, source_target_pairs={{0,3},{1,0},{2,1},{3,2},{4,7},{5,4},{6,5},{7,6},{8,11},{9,8},{10,9... | collective-permute-start | bytes 884744 | tf_op jit(solution)/shard_map/ppermute | solution.py:610
  448.5 1.3 slice-start
  450.9 64.6 %collective-permute-start.5 = (bf16[96,1728]{1,0:T(8,128)(2,1)}, bf16[96,1728]{1,0:T(8,128)(2,1)}, u32[]{:S(2)}, u32[]{:S(2)}) collective-permute-start(bf16[96,1728]{1,0:T(8,128)(2,1)} %get-tuple-element.194), channel_id=1, source_target_pairs={{0,3},{1,0},{2,1},{3,2},{4,7},{5,4},{6,5},{7,6},{8,11},{9,8},{10,9... | collective-permute-start | bytes 995336 | tf_op jit(solution)/shard_map/ppermute | solution.py:610
  451.4 69.6 %collective-permute-start.4 = (bf16[96,1728]{1,0:T(8,128)(2,1)}, bf16[96,1728]{1,0:T(8,128)(2,1)}, u32[]{:S(2)}, u32[]{:S(2)}) collective-permute-start(bf16[96,1728]{1,0:T(8,128)(2,1)} %get-tuple-element.195), channel_id=1, source_target_pairs={{0,2},{1,3},{2,0},{3,1},{4,6},{5,7},{6,4},{7,5},{8,10},{9,11},{10,... | collective-permute-start | bytes 995336 | tf_op jit(solution)/shard_map/ppermute | solution.py:610
  469.1 39.7 %copy-start.8 = (bf16[192,768]{1,0:T(8,128)(2,1)}, bf16[192,768]{1,0:T(8,128)(2,1)S(1)}, u32[]{:S(2)}) copy-start(bf16[192,768]{1,0:T(8,128)(2,1)S(1)} %collective-permute-done.rest_1_) | copy-start | bytes 884740
  469.1 52.0 %collective-permute-start.3 = (bf16[96,1728]{1,0:T(8,128)(2,1)S(1)}, bf16[96,1728]{1,0:T(8,128)(2,1)}, u32[]{:S(2)}, u32[]{:S(2)}) collective-permute-start(bf16[96,1728]{1,0:T(8,128)(2,1)S(1)} %get-tuple-element.193), channel_id=1, source_target_pairs={{0,1},{1,2},{2,3},{3,0},{4,5},{5,6},{6,7},{7,4},{8,9},{9,10},{10,1... | collective-permute-start | bytes 995336 | tf_op jit(solution)/shard_map/ppermute | solution.py:610
Sparse Core Ops, SparseCore 0:
  119.3 74.1 all-gather.1
  267.0 83.5 reduce-scatter.1

commit v6 on v5

--- a/solution.py
+++ b/solution.py
@@ -430,7 +430,7 @@
     return x * top / low
 
 
-def dense_body(own, x_ref, cot_ref, ctx0_ref, ctx1_ref, vec_ref, bias_ref, near_ref, far_ref, out_ref, first_ref, second_ref, attn_ref, grad_ref, active_ref, inner_ref, ctx_ref, go0_ref, go1_ref, sum_ref, w_s, mt_s, slope_s, first_s, acc_s, w_sem):
+def dense_body(own, x_ref, cot_ref, ctx0_ref, ctx1_ref, vec_ref, bias_ref, near_ref, far_ref, out_ref, first_ref, second_ref, attn_ref, grad_ref, active_ref, inner_ref, ctx_ref, go0_ref, go1_ref, sum_ref, w_s, mt_s, slope_s, first_s, acc_s, even_s, odd_s, w_sem):
     i = pl.program_id(0)
     parts, _, _ = near_ref.shape
     f32, bf = jnp.float32, jnp.bfloat16
@@ -467,12 +467,27 @@
         copies[1].wait()
         copies[2].wait()
 
+    half_units = units // 2
+    first_cut, second_cut = slice(0, half_units), slice(half_units, units)
+    base = 4 * own
+
+    def before(t, cut):
+        return dot(first_ref[...], w_s[t, :, base + cut.start : base + cut.stop]) + bias_ref[t, :, cut]
+
+    def after(t, cut, inner):
+        half = 0.5 * (1.0 + erf(inner * ROOT_HALF))
+        slope_s[t, :, cut] = half + inner * jnp.exp(-0.5 * inner * inner) * INV_ROOT_TWO_PI
+        active = (inner * half).astype(bf)
+        active_ref[t, :, cut] = active
+        acc_s[...] += dot_right_t(active, w_s[t, :, base + units + cut.start : base + units + cut.stop])
+
+    even_s[...] = before(0, first_cut)
+
     def ahead(t, _):
-        inner = dot(first_ref[...], w_s[t, :, cuts[1]]) + bias_ref[t]
-        half = 0.5 * (1.0 + erf(inner * ROOT_HALF))
-        slope_s[t] = half + inner * jnp.exp(-0.5 * inner * inner) * INV_ROOT_TWO_PI
-        active_ref[t] = (inner * half).astype(bf)
-        acc_s[...] += dot_right_t(active_ref[t], w_s[t, :, cuts[2]])
+        odd_s[...] = before(t, second_cut)
+        after(t, first_cut, even_s[...])
+        even_s[...] = before(jnp.minimum(t + 1, parts - 1), first_cut)
+        after(t, second_cut, odd_s[...])
         return 0
 
     lax.fori_loop(0, parts, ahead, 0)
@@ -526,7 +541,7 @@
         in_specs=[tok, tok, lanes(ctx0.shape[1]), lanes(ctx1.shape[1]), fixed(vectors), fixed(inner_bias), pl.BlockSpec(memory_space=pl.ANY), pl.BlockSpec(memory_space=pl.ANY)],
         out_specs=[tok] * 5 + [part_tok] * 2 + [pl.BlockSpec((parts * own, block), lambda i: (0, i)), lanes(HD), lanes(own - HD), pl.BlockSpec((16, width), lambda i: (0, 0))],
         out_shape=[S((rows, width), bf)] * 4 + [S((rows, width), f32)] + [S((parts, rows, units), bf)] * 2 + [S((parts * own, rows), bf), S((parts, HD, rows), bf), S((parts, own - HD, rows), bf), S((16, width), f32)],
-        scratch_shapes=[VM((parts, width, cols), bf), VM((width, parts * own), bf), VM((parts, block, units), f32), VM((block, width), f32), VM((block, width), f32), pltpu.SemaphoreType.DMA((3,))],
+        scratch_shapes=[VM((parts, width, cols), bf), VM((width, parts * own), bf), VM((parts, block, units), f32), VM((block, width), f32), VM((block, width), f32), VM((block, units // 2), f32), VM((block, units // 2), f32), pltpu.SemaphoreType.DMA((3,))],
         compiler_params=pltpu.CompilerParams(vmem_limit_bytes=62 << 20),
         cost_estimate=pl.CostEstimate(flops=4 * rows * width * (2 * parts * units + parts * own), bytes_accessed=40 << 20, transcendentals=rows * units * parts),
         name="dense",
@@ -535,10 +550,14 @@
 
 def early_back_body(w_ref, b0_ref, b1_ref, acc_ref):
     width = b0_ref.shape[1]
-    total = jnp.zeros(acc_ref.shape, jnp.float32)
-    for t in range(b0_ref.shape[0]):
-        total = total + dot(w_ref[t, :, : 2 * width], jnp.concatenate([b0_ref[t], b1_ref[t]], axis=0))
-    acc_ref[...] = total
+    acc_ref[...] = jnp.zeros(acc_ref.shape, jnp.float32)
+
+    def add(t, _):
+        both = jnp.concatenate([b0_ref[t], b1_ref[t]], axis=0)
+        acc_ref[...] += dot(w_ref[t, :, : 2 * width], both)
+        return 0
+
+    lax.fori_loop(0, b0_ref.shape[0], add, 0)
 
 
 def late_back_body(cut, part_ref, w_ref, acc_ref, grad_ref, *rest):
@@ -653,7 +672,7 @@
     vectors = jnp.stack([mixer_bias, first_gain, first_shift, outer_bias, second_gain, second_shift])
     vectors = jnp.pad(vectors, ((0, 2), (0, 0)))
     layer_out, first_low, second_low, attn_low, grad_attn, active, grad_inner, context, go0, go1, early = dense(
-        own, x_own, cotangent[0], exchanged[0], exchanged[1], vectors, inner_bias_all, near, far, block=rows
+        own, x_own, cotangent[0], exchanged[0], exchanged[1], vectors, inner_bias_all, near, far, block=rows // 2
     )
     go0 = lax.all_to_all(go0, "tensor", 0, 0, tiled=True)
     go1 = lax.all_to_all(go1, "tensor", 0, 0, tiled=True)

time: 533 us -> 534 us (level)
  no operation moved by 1% of the time
where the time goes in v6:
time: 534 us; the launch traced here: 532 us
  Pallas kernels  323 us (60%)
  starting transfers between devices  67.5 us (13%)
  waiting for transfers between devices  58.2 us (11%)
  blocking collectives  34.8 us (7%)
  local copies, waits for them, and re-layouts  26 us (5%)
  between operations  14.6 us (3%)
  other arithmetic  8.3 us (2%)
    pallas_call x1, Pallas kernels, start(): pl.pallas_call(functools.partial(start_body, n, bits), in_specs=[pl.Block...  105 us
    pallas_call x3, Pallas kernels, attend_backward(): pl.pallas_call(functools.partial(backward_body, BQ, BK, SUB), grid_spec=p...  84 us
    pallas_call x2, Pallas kernels, attend_forward(): pl.pallas_call(functools.partial(forward_body, BK), grid_spec=pltpu.Prefe...  49 us
    pallas_call x1, Pallas kernels, dense(): pl.pallas_call(functools.partial(dense_body, own), grid=(rows // block,),...  42.3 us
    ppermute x6, starting transfers between devices, rotate(): lax.ppermute(block, axis, [(i, (i + d) % size) for i in range(size)])  39.2 us
    ppermute x5, waiting for transfers between devices, add_up(): other = lax.ppermute(value, axis, [(i, i ^ span) for i in range(size)])  22.5 us
    all_to_all x1, blocking collectives, body(): lax.all_to_all(jnp.concatenate([qkv_grad, extra], 1), 'dp', 0, 0, tiled=T...  21.6 us
    ppermute x6, waiting for transfers between devices, rotate(): lax.ppermute(block, axis, [(i, (i + d) % size) for i in range(size)])  21.1 us
  transfers between devices with their start and end apart: 18, of which 9 were waited for; matrix products, arithmetic and copies ran while one was open for 4% of the time, Pallas kernels for 30%

profile of v6, /device:TPU:0, one launch (start us, length us, event | category | flops | bytes accessed | tf_op | source)
XLA Modules:
  0.0 532.1 jit_solution(201868005572820029)
XLA Ops:
  7.2 0.9 copy.100
  8.2 0.9 copy.99
  9.1 0.9 copy.98
  10.3 0.9 copy.102
  11.2 0.7 convert_reduce_fusion.5
  11.9 1.3 pad_maximum_fusion.3.s_ref
  13.2 0.8 concatenate.44.w_ref
  14.0 105.2 %start.1 = (bf16[4,768,768]{2,1,0:T(8,128)(2,1)}, bf16[4,8,96,1536]{3,2,1,0:T(8,128)(2,1)}, f32[4,12,128]{2,1,0:T(8,128)}) custom-call(bf16[768,768]{1,0:T(8,128)(2,1)} %bitcast.74, bf16[96,1536]{1,0:T(8,128)(2,1)} %concatenate.44.w_ref, f32[12,128]{1,0:T(8,128)} %pad_maximum_fusion.3.s_ref), custom_call_target="tpu_custom_call" | custom-call | bytes 209715200 | tf_op jit(solution)/shard_map/start/pallas_call | solution.py:359
  119.2 0.8 copy.128
  121.3 1.7 copy.123
  123.2 0.7 convert_reduce_fusion.3
  123.9 11.0 %project.1 = (bf16[3,128,3072]{2,1,0:T(8,128)(2,1)}, bf16[3,3072,128]{2,1,0:T(8,128)(2,1)}, bf16[3,64,3072]{2,1,0:T(8,128)(2,1)}, bf16[3,3072,64]{2,1,0:T(8,128)...) custom-call(s32[1]{0:T(128)} %bitcast.11.part_ref, bf16[3072,768]{1,0:T(8,128)(2,1)} %bitcast.71, ...), custom_call_target="tpu_custom_call" | custom-call | flops 2717908992 | bytes 17694720 | tf_op jit(solution)/shard_map/project/pallas_call | solution.py:46
  134.9 30.1 %attend_forward.3 = (bf16[4,128,768]{2,1,0:T(8,128)(2,1)}, f32[2,64,3072]{2,1,0:T(8,128)}, f32[2,1,3072]{2,1,0:T(1,128)}) custom-call(s32[8]{0:T(128)} %get-tuple-element.215.lo_ref, s32[8]{0:T(128)} %get-tuple-element.214.hi_ref, bf16[3,128,3072]{2,1,0:T(8,128)(2,1)} %get-tuple-element.60.qt_ref, bf16[3,3072,128]{2,1,0:T(8,128)(2,1)} %get-tuple-element.61.ka_ref, ...), custom_call_target="tpu_custom_call" | custom-call | flops 4831838208 | bytes 6291456 | tf_op jit(solution)/shard_map/attend_forward/pallas_call | solution.py:103
  165.0 3.5 all-to-all-start
  168.7 0.7 convert_reduce_fusion.6
  169.5 18.9 %attend_forward.2 = (bf16[4,64,768]{2,1,0:T(8,128)(2,1)}, f32[1,64,3072]{2,1,0:T(8,128)}, f32[1,1,3072]{2,1,0:T(1,128)}) custom-call(s32[4]{0:T(128)} %get-tuple-element.213.lo_ref, s32[4]{0:T(128)} %get-tuple-element.212.hi_ref, bf16[3,128,3072]{2,1,0:T(8,128)(2,1)} %get-tuple-element.60.qt_ref, bf16[3,3072,128]{2,1,0:T(8,128)(2,1)} %get-tuple-element.61.ka_ref, ...), custom_call_target="tpu_custom_call" | custom-call | flops 2415919104 | bytes 3145728 | tf_op jit(solution)/shard_map/attend_forward/pallas_call | solution.py:103
  188.4 5.7 %all-to-all-done.ctx0_ref = bf16[4,128,768]{2,1,0:T(8,128)(2,1)S(1)} async-done(((bf16[4,128,768]{2,1,0:T(8,128)(2,1)}), bf16[4,128,768]{2,1,0:T(8,128)(2,1)S(1)}, u32[]{:S(2)}, u32[]{:S(2)}) %all-to-all-start) | async-done | bytes 786464 | tf_op jit(solution)/shard_map/all_to_all | solution.py:671
  194.2 3.5 all-to-all-start.1
  199.2 8.9 %all-to-all-done.1.ctx1_ref = bf16[4,64,768]{2,1,0:T(8,128)(2,1)S(1)} async-done(((bf16[4,64,768]{2,1,0:T(8,128)(2,1)}), bf16[4,64,768]{2,1,0:T(8,128)(2,1)S(1)}, u32[]{:S(2)}, u32[]{:S(2)}) %all-to-all-start.1) | async-done | bytes 393248 | tf_op jit(solution)/shard_map/all_to_all | solution.py:671
  208.2 0.8 copy-done.4
  208.9 42.3 %dense.1 = (bf16[768,768]{1,0:T(8,128)(2,1)}, bf16[768,768]{1,0:T(8,128)(2,1)}, bf16[768,768]{1,0:T(8,128)(2,1)}, bf16[768,768]{1,0:T(8,128)(2,1)}, f32[768,768]...) custom-call(bf16[768,768]{1,0:T(8,128)(2,1)} %bitcast.75, ...), custom_call_target="tpu_custom_call" | custom-call | flops 16307453952 | bytes 41943040 | tf_op jit(solution)/shard_map/dense/pallas_call | solution.py:538
  251.2 17.0 %weight_grads.1 = bf16[768,6912]{1,0:T(8,128)(2,1)} custom-call(bf16[768,768]{1,0:T(8,128)(2,1)} %get-tuple-element.88.first_ref, bf16[768,768]{1,0:T(8,128)(2,1)} %get-tuple-element.89.second_ref, bf16[768,768]{1,0:T(8,128)(2,1)} %get-tuple-element.90.attn_ref, bf16[4,768,768]{2,1,0:T(8,128)(2,1)} %get-tuple-element.91.inner_ref, ...), custom_call_target="tpu_custom_call" | custom-call | flops 8153726976 | bytes 18874368 | tf_op jit(solution)/shard_map/weight_grads/pallas_call | solution.py:408
  268.2 1.0 copy-done.5
  269.2 13.2 %all_to_all.35.go_ref = bf16[4,64,768]{2,1,0:T(8,128)(2,1)} all-to-all(bf16[4,64,768]{2,1,0:T(8,128)(2,1)S(1)} %copy-done.5), channel_id=1, replica_groups=mesh['dp'=8,'tensor'=4] {'tensor'}, dimensions={0} | all-to-all | bytes 786432 | tf_op jit(solution)/shard_map/all_to_all | solution.py:677
  282.4 3.8 all-to-all-start.4
  286.2 0.7 convert_reduce_fusion.1
  286.9 28.0 %attend_backward.3 = (bf16[4,192,768]{2,1,0:T(8,128)(2,1)}, bf16[768,192]{1,0:T(8,128)(2,1)}, f32[192,128]{1,0:T(8,128)}) custom-call(s32[6]{0:T(128)} %get-tuple-element.192.lo_ref, s32[6]{0:T(128)} %get-tuple-element.191.hi_ref, bf16[4,64,768]{2,1,0:T(8,128)(2,1)} %all_to_all.35.go_ref, f32[2,64,3072]{2,1,0:T(8,128)} %get-tuple-element.70.ot_ref, ...), custom_call_target="tpu_custom_call" | custom-call | flops 6039797760 | bytes 5505024 | tf_op jit(solution)/shard_map/attend_backward/pallas_call | solution.py:176
  314.9 1.0 slice_reduce_fusion.2
  315.9 0.9 copy-done.3
  316.8 27.9 %attend_backward.5 = (bf16[4,192,768]{2,1,0:T(8,128)(2,1)}, bf16[768,192]{1,0:T(8,128)(2,1)}, f32[192,128]{1,0:T(8,128)}) custom-call(s32[6]{0:T(128)} %get-tuple-element.192.lo_ref, s32[6]{0:T(128)} %get-tuple-element.191.hi_ref, bf16[4,128,768]{2,1,0:T(8,128)(2,1)} %copy-done.3, f32[1,64,3072]{2,1,0:T(8,128)} %get-tuple-element.79.ot_ref, ...), custom_call_target="tpu_custom_call" | custom-call | flops 6039797760 | bytes 5505024 | tf_op jit(solution)/shard_map/attend_backward/pallas_call | solution.py:176
  344.8 1.0 slice_reduce_fusion
  345.8 28.1 %attend_backward.4 = (bf16[4,192,768]{2,1,0:T(8,128)(2,1)}, bf16[768,192]{1,0:T(8,128)(2,1)}, f32[192,128]{1,0:T(8,128)}) custom-call(s32[6]{0:T(128)} %get-tuple-element.192.lo_ref, s32[6]{0:T(128)} %get-tuple-element.191.hi_ref, bf16[4,128,768]{2,1,0:T(8,128)(2,1)} %copy-done.3, f32[2,64,3072]{2,1,0:T(8,128)} %get-tuple-element.70.ot_ref, ...), custom_call_target="tpu_custom_call" | custom-call | flops 6039797760 | bytes 5505024 | tf_op jit(solution)/shard_map/attend_backward/pallas_call | solution.py:176
  373.9 1.0 slice_reduce_fusion.1
  375.1 1.3 pad_maximum_fusion.1
  376.5 21.6 %all_to_all.36 = bf16[8,112,576]{2,1,0:T(8,128)(2,1)S(1)} all-to-all(bf16[8,112,576]{2,1,0:T(8,128)(2,1)S(1)} %pad_maximum_fusion), channel_id=1, replica_groups=mesh['dp'=8,'tensor'=4] {'dp'}, dimensions={0} | all-to-all | bytes 2064384 | tf_op jit(solution)/shard_map/all_to_all | solution.py:716
  398.2 5.0 all-to-all-start.3
  403.2 1.2 collective-permute-done.6
  405.0 3.5 collective-permute-done.7
  409.2 3.5 collective-permute-done.8
  412.7 2.1 collective-permute-start.9
  414.8 8.3 %collective-permute-done.9 = f32[16,768]{1,0:T(8,128)S(1)} collective-permute-done((f32[16,768]{1,0:T(8,128)S(1)}, f32[16,768]{1,0:T(8,128)S(1)}, u32[]{:S(2)}, u32[]{:S(2)}) %collective-permute-start.9) | collective-permute-done | bytes 49184 | tf_op jit(solution)/shard_map/ppermute | solution.py:616
  423.1 4.7 collective-permute-start.10
  427.8 5.8 %collective-permute-done.10 = f32[16,768]{1,0:T(8,128)} collective-permute-done((f32[16,768]{1,0:T(8,128)S(1)}, f32[16,768]{1,0:T(8,128)}, u32[]{:S(2)}, u32[]{:S(2)}) %collective-permute-start.10) | collective-permute-done | bytes 49184 | tf_op jit(solution)/shard_map/ppermute | solution.py:616
  433.7 0.8 add.110
  435.1 4.3 all-to-all-start.5
  439.4 1.0 dynamic-slice_bitcast_fusion.3
  440.5 2.0 collective-permute-start
  442.4 2.4 collective-permute-start.1
  444.8 1.5 collective-permute-start.2
  446.6 0.7 copy.112
  447.3 0.7 copy.113
  448.1 0.7 copy.114
  448.9 0.9 slice.145
  450.0 1.1 slice-done
  451.2 0.9 dynamic-slice_bitcast_fusion.2
  452.7 1.5 collective-permute-start.4
  454.2 16.2 %collective-permute-done.rest_1_ = bf16[192,768]{1,0:T(8,128)(2,1)S(1)} collective-permute-done((bf16[192,768]{1,0:T(8,128)(2,1)}, bf16[192,768]{1,0:T(8,128)(2,1)S(1)}, u32[]{:S(2)}, u32[]{:S(2)}) %collective-permute-start) | collective-permute-done | bytes 294944 | tf_op jit(solution)/shard_map/ppermute | solution.py:629
  470.4 31.4 %collective-permute-start.3 = (bf16[96,1728]{1,0:T(8,128)(2,1)S(1)}, bf16[96,1728]{1,0:T(8,128)(2,1)}, u32[]{:S(2)}, u32[]{:S(2)}) collective-permute-start(bf16[96,1728]{1,0:T(8,128)(2,1)S(1)} %get-tuple-element.193), channel_id=1, source_target_pairs={{0,1},{1,2},{2,3},{3,0},{4,5},{5,6},{6,7},{7,4},{8,9},{9,10},{10,1... | collective-permute-start | bytes 995336 | tf_op jit(solution)/shard_map/ppermute | solution.py:629
  503.1 7.7 %early_back.1.acc_ref = f32[768,768]{1,0:T(8,128)} custom-call(bf16[4,768,1536]{2,1,0:T(8,128)(2,1)} %bitcast.67, bf16[4,192,768]{2,1,0:T(8,128)(2,1)} %copy-done, bf16[4,192,768]{2,1,0:T(8,128)(2,1)} %all-to-all-done.5.b1_ref), custom_call_target="tpu_custom_call" | custom-call | flops 1811939328 | bytes 10485760 | tf_op jit(solution)/shard_map/early_back/pallas_call | solution.py:582
  510.8 6.7 %late_back.1 = bf16[768,768]{1,0:T(8,128)(2,1)} custom-call(s32[1]{0:T(128)} %bitcast.11.part_ref, bf16[4,768,1536]{2,1,0:T(8,128)(2,1)} %bitcast.68, f32[768,768]{1,0:T(8,128)} %early_back.1.acc_ref, f32[768,768]{1,0:T(8,128)} %get-tuple-element.78.grad_ref, bf16[192,768]{1,0:T(8,128)(2,1)} %get-tuple-element.199.rest_0_, bf16[192,768]{1,0:T(8,128)(2,1)} %copy-done.8, ...), custom_call_target="tpu_custom_call" | custom-call | flops 905969664 | bytes 10485760 | tf_op jit(solution)/shard_map/late_back/pallas_call | solution.py:596
  517.4 4.9 collective-permute-done.4
  522.3 1.3 fusion.1
  523.7 0.9 slice_bitcast_fusion
  524.5 0.7 copy.115
  (106 shorter events, 8.4 us)
Async XLA Ops:
  7.2 6.0 %copy-start.9 = (bf16[96,768]{1,0:T(8,128)(2,1)S(1)}, bf16[96,768]{1,0:T(8,128)(2,1)}, u32[]{:S(2)}) copy-start(bf16[96,768]{1,0:T(8,128)(2,1)} %param.29) | copy-start | bytes 442372
  7.2 201.0 %all-gather.2.cloned.1.call-start = ((), (), s32[]{:S(2)}) async-start(), calls=%async_computation.8 | async-start | bytes 4866048 | tf_op jit(solution)/shard_map/all_gather | solution.py:655
  10.1 110.2 %copy-start.18 = (f32[192]{0:T(256)S(1)}, f32[192]{0:T(256)}, u32[]{:S(2)}) copy-start(f32[192]{0:T(256)} %param.24) | copy-start | bytes 2308
  10.1 110.2 %copy-start.19 = (f32[192]{0:T(256)S(1)}, f32[192]{0:T(256)}, u32[]{:S(2)}) copy-start(f32[192]{0:T(256)} %param.23) | copy-start | bytes 2308
  121.2 2.7 copy-start.10
  165.0 29.1 %all-to-all-start = ((bf16[4,128,768]{2,1,0:T(8,128)(2,1)}), bf16[4,128,768]{2,1,0:T(8,128)(2,1)S(1)}, u32[]{:S(2)}, u32[]{:S(2)}) async-start(bf16[4,128,768]{2,1,0:T(8,128)(2,1)} %get-tuple-element.64), calls=%async_computation | async-start | bytes 1572864 | tf_op jit(solution)/shard_map/all_to_all | solution.py:671
  169.5 28.4 %copy-start.12 = (f32[768]{0:T(1024)S(1)}, f32[768]{0:T(1024)}, u32[]{:S(2)}) copy-start(f32[768]{0:T(1024)} %param.26) | copy-start | bytes 9220
  169.5 28.4 %copy-start.13 = (f32[768]{0:T(1024)S(1)}, f32[768]{0:T(1024)}, u32[]{:S(2)}) copy-start(f32[768]{0:T(1024)} %param.27) | copy-start | bytes 9220
  169.5 28.4 %copy-start.14 = (f32[768]{0:T(1024)S(1)}, f32[768]{0:T(1024)}, u32[]{:S(2)}) copy-start(f32[768]{0:T(1024)} %param.28) | copy-start | bytes 9220
  169.5 28.4 %copy-start.15 = (f32[768]{0:T(1024)S(1)}, f32[768]{0:T(1024)}, u32[]{:S(2)}) copy-start(f32[768]{0:T(1024)} %param.32) | copy-start | bytes 9220
  169.5 28.5 %copy-start.16 = (f32[768]{0:T(1024)S(1)}, f32[768]{0:T(1024)}, u32[]{:S(2)}) copy-start(f32[768]{0:T(1024)} %param.33) | copy-start | bytes 9220
  169.5 28.5 %copy-start.17 = (f32[768]{0:T(1024)S(1)}, f32[768]{0:T(1024)}, u32[]{:S(2)}) copy-start(f32[768]{0:T(1024)} %param.34) | copy-start | bytes 9220
  194.1 14.0 %copy-start.2 = (bf16[4,128,768]{2,1,0:T(8,128)(2,1)}, bf16[4,128,768]{2,1,0:T(8,128)(2,1)S(1)}, u32[]{:S(2)}) copy-start(bf16[4,128,768]{2,1,0:T(8,128)(2,1)S(1)} %all-to-all-done.ctx0_ref) | copy-start | bytes 2359300
  194.2 14.0 %all-to-all-start.1 = ((bf16[4,64,768]{2,1,0:T(8,128)(2,1)}), bf16[4,64,768]{2,1,0:T(8,128)(2,1)S(1)}, u32[]{:S(2)}, u32[]{:S(2)}) async-start(bf16[4,64,768]{2,1,0:T(8,128)(2,1)} %get-tuple-element.66), calls=%async_computation.1 | async-start | bytes 786432 | tf_op jit(solution)/shard_map/all_to_all | solution.py:671
  197.6 251.3 %reduce-scatter.2.cloned.1.call-start = ((), (), s32[]{:S(2)}) async-start(), calls=%async_computation.9 | async-start | bytes 11943936 | tf_op jit(solution)/shard_map/reduce_scatter | solution.py:682
  208.2 0.8 copy-start.4
  268.2 1.0 copy-start.5
  282.4 33.5 %all-to-all-start.4 = ((bf16[4,128,768]{2,1,0:T(8,128)(2,1)}), bf16[4,128,768]{2,1,0:T(8,128)(2,1)S(1)}, u32[]{:S(2)}, u32[]{:S(2)}) async-start(bf16[4,128,768]{2,1,0:T(8,128)(2,1)} %get-tuple-element.76), calls=%async_computation.4 | async-start | bytes 1572864 | tf_op jit(solution)/shard_map/all_to_all | solution.py:678
  315.9 0.9 copy-start.3
  345.8 29.3 %copy-start.6 = (bf16[768,192]{1,0:T(8,128)(2,1)S(1)}, bf16[768,192]{1,0:T(8,128)(2,1)}, u32[]{:S(2)}) copy-start(bf16[768,192]{1,0:T(8,128)(2,1)} %get-tuple-element.82) | copy-start | bytes 884740
  345.8 29.3 %copy-start.7 = (bf16[768,192]{1,0:T(8,128)(2,1)S(1)}, bf16[768,192]{1,0:T(8,128)(2,1)}, u32[]{:S(2)}) copy-start(bf16[768,192]{1,0:T(8,128)(2,1)} %get-tuple-element.84) | copy-start | bytes 884740
  398.1 5.0 copy-start.11
  398.2 37.0 %all-to-all-start.3 = ((bf16[4,192,768]{2,1,0:T(8,128)(2,1)}), bf16[4,192,768]{2,1,0:T(8,128)(2,1)S(1)}, u32[]{:S(2)}, u32[]{:S(2)}) async-start(bf16[4,192,768]{2,1,0:T(8,128)(2,1)} %get-tuple-element.75), calls=%async_computation.3 | async-start | bytes 2359296 | tf_op jit(solution)/shard_map/all_to_all | solution.py:702
  403.2 1.2 collective-permute-start.6
  404.4 4.1 collective-permute-start.7
  408.6 4.2 collective-permute-start.8
  412.7 10.4 %collective-permute-start.9 = (f32[16,768]{1,0:T(8,128)S(1)}, f32[16,768]{1,0:T(8,128)S(1)}, u32[]{:S(2)}, u32[]{:S(2)}) collective-permute-start(f32[16,768]{1,0:T(8,128)S(1)} %add.108), channel_id=1, source_target_pairs={{0,1},{1,0},{2,3},{3,2},{4,5},{5,4},{6,7},{7,6},{8,9},{9,8},{10,11... | collective-permute-start | bytes 147464 | tf_op jit(solution)/shard_map/ppermute | solution.py:616
  423.1 16.3 %copy-start.1 = (bf16[4,192,768]{2,1,0:T(8,128)(2,1)S(1)}, bf16[4,192,768]{2,1,0:T(8,128)(2,1)}, u32[]{:S(2)}) copy-start(bf16[4,192,768]{2,1,0:T(8,128)(2,1)} %get-tuple-element.81) | copy-start | bytes 3538948
  423.1 10.5 %collective-permute-start.10 = (f32[16,768]{1,0:T(8,128)S(1)}, f32[16,768]{1,0:T(8,128)}, u32[]{:S(2)}, u32[]{:S(2)}) collective-permute-start(f32[16,768]{1,0:T(8,128)S(1)} %add.109), channel_id=1, source_target_pairs={{0,2},{1,3},{2,0},{3,1},{4,6},{5,7},{6,4},{7,5},{8,10},{9,11},{10,... | collective-permute-start | bytes 147464 | tf_op jit(solution)/shard_map/ppermute | solution.py:616
  435.1 5.3 %copy-start = (bf16[4,192,768]{2,1,0:T(8,128)(2,1)}, bf16[4,192,768]{2,1,0:T(8,128)(2,1)S(1)}, u32[]{:S(2)}) copy-start(bf16[4,192,768]{2,1,0:T(8,128)(2,1)S(1)} %all-to-all-done.3.b0_ref) | copy-start | bytes 3538948
  435.1 67.9 %all-to-all-start.5 = ((bf16[4,192,768]{2,1,0:T(8,128)(2,1)}), bf16[4,192,768]{2,1,0:T(8,128)(2,1)}, u32[]{:S(2)}, u32[]{:S(2)}) async-start(bf16[4,192,768]{2,1,0:T(8,128)(2,1)} %get-tuple-element.77), calls=%async_computation.5 | async-start | bytes 2359296 | tf_op jit(solution)/shard_map/all_to_all | solution.py:702
  440.5 29.9 %collective-permute-start = (bf16[192,768]{1,0:T(8,128)(2,1)}, bf16[192,768]{1,0:T(8,128)(2,1)S(1)}, u32[]{:S(2)}, u32[]{:S(2)}) collective-permute-start(bf16[192,768]{1,0:T(8,128)(2,1)} %get-tuple-element.198), channel_id=1, source_target_pairs={{0,1},{1,2},{2,3},{3,0},{4,5},{5,6},{6,7},{7,4},{8,9},{9,10},{10,1... | collective-permute-start | bytes 884744 | tf_op jit(solution)/shard_map/ppermute | solution.py:629
  442.4 68.3 %collective-permute-start.1 = (bf16[192,768]{1,0:T(8,128)(2,1)}, bf16[192,768]{1,0:T(8,128)(2,1)}, u32[]{:S(2)}, u32[]{:S(2)}) collective-permute-start(bf16[192,768]{1,0:T(8,128)(2,1)} %get-tuple-element.197), channel_id=1, source_target_pairs={{0,2},{1,3},{2,0},{3,1},{4,6},{5,7},{6,4},{7,5},{8,10},{9,11},{10,... | collective-permute-start | bytes 884744 | tf_op jit(solution)/shard_map/ppermute | solution.py:629
  444.8 66.0 %collective-permute-start.2 = (bf16[192,768]{1,0:T(8,128)(2,1)}, bf16[192,768]{1,0:T(8,128)(2,1)}, u32[]{:S(2)}, u32[]{:S(2)}) collective-permute-start(bf16[192,768]{1,0:T(8,128)(2,1)} %get-tuple-element.196), channel_id=1, source_target_pairs={{0,3},{1,0},{2,1},{3,2},{4,7},{5,4},{6,5},{7,6},{8,11},{9,8},{10,9... | collective-permute-start | bytes 884744 | tf_op jit(solution)/shard_map/ppermute | solution.py:629
  449.8 1.3 slice-start
  452.2 65.3 %collective-permute-start.5 = (bf16[96,1728]{1,0:T(8,128)(2,1)}, bf16[96,1728]{1,0:T(8,128)(2,1)}, u32[]{:S(2)}, u32[]{:S(2)}) collective-permute-start(bf16[96,1728]{1,0:T(8,128)(2,1)} %get-tuple-element.194), channel_id=1, source_target_pairs={{0,3},{1,0},{2,1},{3,2},{4,7},{5,4},{6,5},{7,6},{8,11},{9,8},{10,9... | collective-permute-start | bytes 995336 | tf_op jit(solution)/shard_map/ppermute | solution.py:629
  452.7 69.6 %collective-permute-start.4 = (bf16[96,1728]{1,0:T(8,128)(2,1)}, bf16[96,1728]{1,0:T(8,128)(2,1)}, u32[]{:S(2)}, u32[]{:S(2)}) collective-permute-start(bf16[96,1728]{1,0:T(8,128)(2,1)} %get-tuple-element.195), channel_id=1, source_target_pairs={{0,2},{1,3},{2,0},{3,1},{4,6},{5,7},{6,4},{7,5},{8,10},{9,11},{10,... | collective-permute-start | bytes 995336 | tf_op jit(solution)/shard_map/ppermute | solution.py:629
  470.4 40.4 %copy-start.8 = (bf16[192,768]{1,0:T(8,128)(2,1)}, bf16[192,768]{1,0:T(8,128)(2,1)S(1)}, u32[]{:S(2)}) copy-start(bf16[192,768]{1,0:T(8,128)(2,1)S(1)} %collective-permute-done.rest_1_) | copy-start | bytes 884740
  470.4 52.0 %collective-permute-start.3 = (bf16[96,1728]{1,0:T(8,128)(2,1)S(1)}, bf16[96,1728]{1,0:T(8,128)(2,1)}, u32[]{:S(2)}, u32[]{:S(2)}) collective-permute-start(bf16[96,1728]{1,0:T(8,128)(2,1)S(1)} %get-tuple-element.193), channel_id=1, source_target_pairs={{0,1},{1,2},{2,3},{3,0},{4,5},{5,6},{6,7},{7,4},{8,9},{9,10},{10,1... | collective-permute-start | bytes 995336 | tf_op jit(solution)/shard_map/ppermute | solution.py:629
Sparse Core Ops, SparseCore 0:
  119.3 74.1 all-gather.1
  268.4 83.5 reduce-scatter.1

commit v7 on v6

--- a/solution.py
+++ b/solution.py
@@ -18,13 +18,14 @@
 def dot(a,b): return jnp.dot(a,b,preferred_element_type=jnp.float32)
 
 
-def project_body(heads, part_ref, x_ref, w_ref, b_ref, scol_ref, srow_ref, qt_ref, ka_ref, vt_ref, qn_ref, kt_ref, vn_ref):
-    y = dot(x_ref[...], w_ref[0,:,:b_ref.shape[1]]) + b_ref[...]
+def project_body(heads, part_ref, x_ref, w_ref, b_ref, srow_ref, qt_ref, ka_ref, vt_ref, qn_ref, kt_ref, vn_ref):
+    y=dot(x_ref[...], w_ref[0,:,:b_ref.shape[1]]) + b_ref[...]
     low = y.astype(jnp.bfloat16)
-    yt = y.T.astype(jnp.bfloat16)
+    yt = low.T
     rows = y.shape[0]
-    apart = jnp.where(lax.broadcasted_iota(jnp.int32,(HD,rows),0)==srow_ref[...],0.0,APART).astype(jnp.bfloat16)
-    same = (lax.broadcasted_iota(jnp.int32,(rows,HD),1)==scol_ref[...]).astype(jnp.float32).astype(jnp.bfloat16)
+    match = lax.broadcasted_iota(jnp.int32,(HD,rows),0)==srow_ref[...]
+    apart = jnp.where(match,0.0,APART).astype(jnp.bfloat16)
+    same = jnp.where(match,1.0,0.0).T.astype(jnp.bfloat16)
     for h in range(heads):
         at=3*h*HD
         qt_ref[h,:HD,:]=yt[at:at+HD]*jnp.bfloat16(SCALE)
@@ -46,12 +47,12 @@
     return pl.pallas_call(functools.partial(project_body,heads),
         grid_spec=pltpu.PrefetchScalarGridSpec(num_scalar_prefetch=1,grid=(L//rows,),
         in_specs=[pl.BlockSpec((rows,D),lambda i,*_:(i,0)),pl.BlockSpec((1,D,cols),lambda i,p:(p[0],0,0)),pl.BlockSpec((1,b.shape[0]),lambda i,*_:(0,0)),
-                  pl.BlockSpec((rows,1),lambda i,*_:(i,0)),pl.BlockSpec((1,rows),lambda i,*_:(0,i))],
+                  pl.BlockSpec((1,rows),lambda i,*_:(0,i))],
         out_specs=[tr(2*HD),nat(2*HD),tr(HD),nat(HD),tr(HD),nat(HD)]),
         out_shape=[S((heads,2*HD,L),bf),S((heads,L,2*HD),bf),S((heads,HD,L),bf),S((heads,L,HD),bf),S((heads,HD,L),bf),S((heads,L,HD),bf)],
         compiler_params=pltpu.CompilerParams(vmem_limit_bytes=62 << 20),
         cost_estimate=pl.CostEstimate(flops=2*L*D*b.shape[0],bytes_accessed=L*D*2+D*cols*2+L*heads*HD*2*10,transcendentals=0),
-        name="project")(part.reshape(1),x,rest,b.reshape(1,-1),seg.reshape(-1,1),seg.reshape(1,-1))
+        name="project")(part.reshape(1),x,rest,b.reshape(1,-1),seg.reshape(1,-1))
 
 
 def forward_body(BK, lo_ref, hi_ref, qt_ref, ka_ref, vt_ref, ctx_ref, ot_ref, lse_ref, m_s, l_s, acc, s_even, s_odd):
@@ -378,44 +379,39 @@
     )(x, w, small)
 
 
-def weight_grads_body(parts, first_ref, second_ref, attn_ref, inner_ref, active_ref, context_ref, out_ref, ft, st):
+def weight_grads_body(parts, first_ref, second_ref, attn_ref, both_ref, context_ref, out_ref, left):
     j = pl.program_id(0)
 
     @pl.when(j == 0)
     def _():
-        ft[...] = first_ref[...].T
-        st[...] = second_ref[...].T
-
-    @pl.when((j < 2 * parts) & (j % 2 == 0))
+        left[0] = first_ref[...].T
+        left[1] = second_ref[...].T
+
+    @pl.when(j < 2 * parts)
     def _():
-        out_ref[...] = dot(ft[...], inner_ref[0]).astype(out_ref.dtype)
-
-    @pl.when((j < 2 * parts) & (j % 2 == 1))
-    def _():
-        out_ref[...] = dot(st[...], active_ref[0]).astype(out_ref.dtype)
+        out_ref[...] = dot(left[j % 2], both_ref[0]).astype(out_ref.dtype)
 
     @pl.when(j == 2 * parts)
     def _():
         out_ref[...] = dot_right_t(attn_ref[...].T, context_ref[...]).astype(out_ref.dtype)
 
 
-def weight_grads_of(first_low, second_low, attn_low, grad_inner, active, context):
-    parts, rows, units = active.shape
+def weight_grads_of(first_low, second_low, attn_low, both, context):
+    steps, rows, units = both.shape
     width = first_low.shape[1]
     features = context.shape[0]
     fixed = pl.BlockSpec((rows, width), lambda j: (0, 0))
-    moving = lambda shift: pl.BlockSpec((1, rows, units), lambda j: (jnp.clip((j - shift) // 2, 0, parts - 1), 0, 0))
     return pl.pallas_call(
-        functools.partial(weight_grads_body, parts),
-        grid=(2 * parts + 1,),
-        in_specs=[fixed, fixed, fixed, moving(0), moving(1), pl.BlockSpec((features, rows), lambda j: (0, 0))],
+        functools.partial(weight_grads_body, steps // 2),
+        grid=(steps + 1,),
+        in_specs=[fixed, fixed, fixed, pl.BlockSpec((1, rows, units), lambda j: (jnp.minimum(j, steps - 1), 0, 0)), pl.BlockSpec((features, rows), lambda j: (0, 0))],
         out_specs=pl.BlockSpec((width, units), lambda j: (0, j)),
-        out_shape=jax.ShapeDtypeStruct((width, units * 2 * parts + features), jnp.bfloat16),
-        scratch_shapes=[VM((width, rows), jnp.bfloat16), VM((width, rows), jnp.bfloat16)],
+        out_shape=jax.ShapeDtypeStruct((width, units * steps + features), jnp.bfloat16),
+        scratch_shapes=[VM((2, width, rows), jnp.bfloat16)],
         compiler_params=pltpu.CompilerParams(vmem_limit_bytes=62 << 20),
-        cost_estimate=pl.CostEstimate(flops=2 * rows * width * (2 * parts * units + features), bytes_accessed=rows * units * 2 * parts * 4, transcendentals=0),
+        cost_estimate=pl.CostEstimate(flops=2 * rows * width * (steps * units + features), bytes_accessed=rows * units * steps * 4, transcendentals=0),
         name="weight_grads",
-    )(first_low, second_low, attn_low, grad_inner, active, context)
+    )(first_low, second_low, attn_low, both, context)
 
 
 def erf(x):
@@ -430,13 +426,13 @@
     return x * top / low
 
 
-def dense_body(own, x_ref, cot_ref, ctx0_ref, ctx1_ref, vec_ref, bias_ref, near_ref, far_ref, out_ref, first_ref, second_ref, attn_ref, grad_ref, active_ref, inner_ref, ctx_ref, go0_ref, go1_ref, sum_ref, w_s, mt_s, slope_s, first_s, acc_s, even_s, odd_s, w_sem):
+def dense_body(own, x_ref, cot_ref, ctx0_ref, ctx1_ref, vec_ref, bias_ref, near_ref, out_ref, first_ref, second_ref, attn_ref, grad_ref, both_ref, ctx_ref, go0_ref, go1_ref, sum_ref, w_s, mt_s, slope_s, first_s, acc_s, even_s, odd_s, w_sem):
     i = pl.program_id(0)
     parts, _, _ = near_ref.shape
     f32, bf = jnp.float32, jnp.bfloat16
-    units = active_ref.shape[2]
+    units = both_ref.shape[2]
     cuts = (slice(0, 4 * own), slice(4 * own, 4 * own + units), slice(4 * own + units, 4 * own + 2 * units))
-    sources = (near_ref.at[:, :, cuts[0]], near_ref.at[:, :, cuts[1]], far_ref)
+    sources = (near_ref.at[:, :, cuts[0]], near_ref.at[:, :, cuts[1]], near_ref.at[:, :, cuts[2]])
     copies = [pltpu.make_async_copy(sources[c], w_s.at[:, :, cut], w_sem.at[c]) for c, cut in enumerate(cuts)]
 
     @pl.when(i == 0)
@@ -478,7 +474,7 @@
         half = 0.5 * (1.0 + erf(inner * ROOT_HALF))
         slope_s[t, :, cut] = half + inner * jnp.exp(-0.5 * inner * inner) * INV_ROOT_TWO_PI
         active = (inner * half).astype(bf)
-        active_ref[t, :, cut] = active
+        both_ref[2 * t + 1, :, cut] = active
         acc_s[...] += dot_right_t(active, w_s[t, :, base + units + cut.start : base + units + cut.stop])
 
     even_s[...] = before(0, first_cut)
@@ -503,7 +499,7 @@
 
     def back(t, _):
         grad_inner = (dot(second_ref[...], w_s[t, :, cuts[2]]) * slope_s[t]).astype(bf)
-        inner_ref[t] = grad_inner
+        both_ref[2 * t] = grad_inner
         sum_ref[pl.ds(6 + t, 1), :] += jnp.sum(grad_inner.astype(f32), axis=0, keepdims=True)
         acc_s[...] += dot_right_t(grad_inner, w_s[t, :, cuts[1]])
         return 0
@@ -523,29 +519,29 @@
         go1_ref[t] = grad_context[t * own + HD : (t + 1) * own]
 
 
-def dense(own, x, cot, ctx0, ctx1, vectors, inner_bias, near, far, block):
+def dense(own, x, cot, ctx0, ctx1, vectors, inner_bias, near, block):
     rows, width = x.shape
     parts = near.shape[0]
-    units = far.shape[2]
-    cols = 4 * own + 2 * units
+    cols = near.shape[2]
+    units = (cols - 4 * own) // 2
     f32, bf = jnp.float32, jnp.bfloat16
     S = jax.ShapeDtypeStruct
     tok = pl.BlockSpec((block, width), lambda i: (i, 0))
-    part_tok = pl.BlockSpec((parts, block, units), lambda i: (0, i, 0))
+    part_tok = pl.BlockSpec((2 * parts, block, units), lambda i: (0, i, 0))
     lanes = lambda n: pl.BlockSpec((parts, n, block), lambda i: (0, 0, i))
     fixed = lambda a: pl.BlockSpec(a.shape, lambda i: (0,) * a.ndim)
     inner_bias = inner_bias.reshape(parts, 1, units)
     return pl.pallas_call(
         functools.partial(dense_body, own),
         grid=(rows // block,),
-        in_specs=[tok, tok, lanes(ctx0.shape[1]), lanes(ctx1.shape[1]), fixed(vectors), fixed(inner_bias), pl.BlockSpec(memory_space=pl.ANY), pl.BlockSpec(memory_space=pl.ANY)],
-        out_specs=[tok] * 5 + [part_tok] * 2 + [pl.BlockSpec((parts * own, block), lambda i: (0, i)), lanes(HD), lanes(own - HD), pl.BlockSpec((16, width), lambda i: (0, 0))],
-        out_shape=[S((rows, width), bf)] * 4 + [S((rows, width), f32)] + [S((parts, rows, units), bf)] * 2 + [S((parts * own, rows), bf), S((parts, HD, rows), bf), S((parts, own - HD, rows), bf), S((16, width), f32)],
+        in_specs=[tok, tok, lanes(ctx0.shape[1]), lanes(ctx1.shape[1]), fixed(vectors), fixed(inner_bias), pl.BlockSpec(memory_space=pl.ANY)],
+        out_specs=[tok] * 5 + [part_tok] + [pl.BlockSpec((parts * own, block), lambda i: (0, i)), lanes(HD), lanes(own - HD), pl.BlockSpec((16, width), lambda i: (0, 0))],
+        out_shape=[S((rows, width), bf)] * 4 + [S((rows, width), f32)] + [S((2 * parts, rows, units), bf)] + [S((parts * own, rows), bf), S((parts, HD, rows), bf), S((parts, own - HD, rows), bf), S((16, width), f32)],
         scratch_shapes=[VM((parts, width, cols), bf), VM((width, parts * own), bf), VM((parts, block, units), f32), VM((block, width), f32), VM((block, width), f32), VM((block, units // 2), f32), VM((block, units // 2), f32), pltpu.SemaphoreType.DMA((3,))],
         compiler_params=pltpu.CompilerParams(vmem_limit_bytes=62 << 20),
         cost_estimate=pl.CostEstimate(flops=4 * rows * width * (2 * parts * units + parts * own), bytes_accessed=40 << 20, transcendentals=rows * units * parts),
         name="dense",
-    )(x, cot, ctx0, ctx1, vectors, inner_bias, near, far)
+    )(x, cot, ctx0, ctx1, vectors, inner_bias, near)
 
 
 def early_back_body(w_ref, b0_ref, b1_ref, acc_ref):
@@ -608,15 +604,20 @@
     )(part.reshape(1), rest, acc, grad, *backs)
 
 
-def add_up(value):
-    for axis in ("dp", "tensor"):
-        size = lax.axis_size(axis)
-        span = 1
-        while span < size:
-            other = lax.ppermute(value, axis, [(i, i ^ span) for i in range(size)])
-            value = value + other
-            span *= 2
+def add_up(value, axis):
+    size = lax.axis_size(axis)
+    span, turn = 1, 0
+    while span < size:
+        other = lax.ppermute(value, axis, [(i, i ^ span) for i in range(size)])
+        value = value + other
+        span *= 2
+        turn += 1
     return value
+
+
+def two_halves(value):
+    high = value.astype(jnp.bfloat16)
+    return high, (value - high.astype(jnp.float32)).astype(jnp.bfloat16)
 
 
 def rotate(blocks, axis):
@@ -632,7 +633,6 @@
 
 
 def body(hidden_in, segments, query_weight, key_weight, value_weight, query_bias, value_bias, mixer_weight, mixer_bias, first_gain, first_shift, inner_weight, inner_bias, outer_weight, outer_bias, second_gain, second_shift, cotangent):
-    bf = jnp.bfloat16
     f32 = jnp.float32
     _, rows, width = hidden_in.shape
     parts = lax.axis_size("tensor")
@@ -646,13 +646,10 @@
     x_own = hidden_in[0]
     qkv_own = by_head(query_weight, key_weight, value_weight)
     small = jnp.concatenate([segments[0].astype(f32), inner_bias]).reshape(-1, 128)
-    near_own = jnp.concatenate([qkv_own, mixer_weight.T, inner_weight], 1)
+    near_own = jnp.concatenate([qkv_own, mixer_weight.T, inner_weight, outer_weight.T], 1)
     x_parts, near, small = start(x_own, near_own, small)
     x_all = x_parts.reshape(parts * rows, width)
-    near = near.reshape(parts, width, 4 * own + units)
-    far_own = outer_weight.T
-    far_own, small = lax.optimization_barrier((far_own, small))
-    far = lax.all_gather(far_own, ("tensor", "dp"), axis=0, tiled=True).reshape(parts, width, units)
+    near = near.reshape(parts, width, 4 * own + 2 * units)
     small = small.reshape(parts, -1)
     segment_all = small[:, :rows].astype(jnp.int32).reshape(-1)
     inner_bias_all = small[:, rows:]
@@ -671,13 +668,13 @@
         exchanged.append(lax.all_to_all(part, "tensor", 0, 0, tiled=True))
     vectors = jnp.stack([mixer_bias, first_gain, first_shift, outer_bias, second_gain, second_shift])
     vectors = jnp.pad(vectors, ((0, 2), (0, 0)))
-    layer_out, first_low, second_low, attn_low, grad_attn, active, grad_inner, context, go0, go1, early = dense(
-        own, x_own, cotangent[0], exchanged[0], exchanged[1], vectors, inner_bias_all, near, far, block=rows // 2
+    layer_out, first_low, second_low, attn_low, grad_attn, both, context, go0, go1, early = dense(
+        own, x_own, cotangent[0], exchanged[0], exchanged[1], vectors, inner_bias_all, near, block=rows // 2
     )
     go0 = lax.all_to_all(go0, "tensor", 0, 0, tiled=True)
     go1 = lax.all_to_all(go1, "tensor", 0, 0, tiled=True)
     weight_grads = weight_grads_of(
-        first_low, second_low, attn_low, grad_inner, active, context
+        first_low, second_low, attn_low, both, context
     )
     weight_grads = lax.psum_scatter(weight_grads, "dp", scatter_dimension=0, tiled=True)
     weight_grads = jnp.concatenate(
@@ -689,7 +686,11 @@
     ).transpose(1, 0, 2)
     weight_grads = rotate(weight_grads, "tensor")
     weight_grads = sum(a.astype(f32) for a in weight_grads)
-    early = add_up(early)
+    early = add_up(early[: 6 + parts], "tensor")
+    count = 6 + parts
+    lines = -(-count * width // (3 * own))
+    early = jnp.pad(early.reshape(-1), (0, lines * 3 * own - count * width)).reshape(lines, 3 * own)
+    early = jnp.concatenate(two_halves(early), 0)
 
     lo, hi = ranges(segment_all, 512, 512)
     backs, qkv_grad, bias_grad = [], [], []
@@ -706,16 +707,19 @@
         bias_grad.append(sums[:, 0])
     input_back = early_back(near, 4 * own, backs[0], backs[1])
     input_grad = late_back(near, 4 * own, 2 * three, rank, input_back, grad_attn, backs[2])
-    bias_grad = jnp.concatenate(bias_grad)
-    high = bias_grad.astype(bf)
-    low = (bias_grad - high.astype(f32)).astype(bf)
     each = width // groups
+    bias_grad = jnp.stack(two_halves(jnp.concatenate(bias_grad)))
+    extra = jnp.concatenate([early, bias_grad], 0)
+    spare = -extra.shape[0] % 16
+    extra = jnp.pad(extra, ((0, spare), (0, 0)))
+    extra = jnp.broadcast_to(extra[None], (groups,) + extra.shape)
     qkv_grad = jnp.concatenate(qkv_grad, 1).reshape(groups, each, 3 * own)
-    extra = jnp.pad(jnp.stack([high, low]), ((0, 14), (0, 0)))
-    extra = jnp.broadcast_to(extra[None], (groups, 16, 3 * own))
-    qkv_grad = lax.all_to_all(jnp.concatenate([qkv_grad, extra], 1), "dp", 0, 0, tiled=True)
+    qkv_grad = jnp.concatenate([qkv_grad, extra], 1)
+    qkv_grad = lax.all_to_all(qkv_grad, "dp", 0, 0, tiled=True)
     qkv_grad = jnp.sum(qkv_grad.astype(f32), 0)
-    bias_grad = qkv_grad[each] + qkv_grad[each + 1]
+    early = qkv_grad[each : each + lines] + qkv_grad[each + lines : each + 2 * lines]
+    early = early.reshape(-1)[: count * width].reshape(count, width)
+    bias_grad = qkv_grad[each + 2 * lines] + qkv_grad[each + 2 * lines + 1]
     pick = lambda a, n: a.reshape(a.shape[:-1] + (heads, 3, HD))[..., n, :].reshape(a.shape[:-1] + (own,))
     inner_bias_out = lax.dynamic_index_in_dim(early, 6 + rank, 0, keepdims=False)
     return (

time: 534 us -> 540 us (1.011)
  waiting for transfers between devices: 58.2 us -> 90.1 us
  starting transfers between devices: 67.5 us -> 49 us
  blocking collectives: 34.8 us -> 19.2 us
  Pallas kernels: 323 us -> 331 us
    all_to_all x2, waiting for transfers between devices: 0.01 us -> 60.1 us  [body(): backs.append(lax.all_to_all(grads, 'tensor', 0, 0, tiled=True))]
    ppermute x6, starting transfers between devices: 39.2 us -> 9.79 us  [rotate(): lax.ppermute(block, axis, [(i, (i + d) % size) for i in range(size)])]
    ppermute x6, waiting for transfers between devices: 21.1 us -> 0.02 us  [rotate(): lax.ppermute(block, axis, [(i, (i + d) % size) for i in range(size)])]
    all_to_all x2 -> x1, blocking collectives: 34.8 us -> 19.2 us  [body(): qkv_grad = lax.all_to_all(qkv_grad, 'dp', 0, 0, tiled=True)]
    all_to_all x0 -> x1, waiting for transfers between devices: none -> 12.1 us  [body(): go0 = lax.all_to_all(go0, 'tensor', 0, 0, tiled=True)]
    ppermute x5 -> x2, waiting for transfers between devices: 22.5 us -> 10.4 us  [add_up(): other = lax.ppermute(value, axis, [(i, i ^ span) for i in range(size)])]
    pallas_call x1, Pallas kernels: 105 us -> 115 us  [start(): pl.pallas_call(functools.partial(start_body, n, bits), in_specs=[pl.Block...]
    all_to_all x2, starting transfers between devices: 9.28 us -> 18.1 us  [body(): backs.append(lax.all_to_all(grads, 'tensor', 0, 0, tiled=True))]
  transfers between devices with their start and end apart: 18 -> 15, of which waited for: 9 -> 5; matrix products, arithmetic and copies ran while one was open for 4% -> 3% of each run, Pallas kernels for 30% -> 22%
where the time goes in v7:
time: 540 us; the launch traced here: 539 us
  Pallas kernels  331 us (61%)
  waiting for transfers between devices  90.1 us (17%)
  starting transfers between devices  49 us (9%)
  local copies, waits for them, and re-layouts  26.6 us (5%)
  blocking collectives  19.2 us (4%)
  between operations  14.7 us (3%)
  other arithmetic  8.13 us (2%)
    pallas_call x1, Pallas kernels, start(): pl.pallas_call(functools.partial(start_body, n, bits), in_specs=[pl.Block...  115 us
    pallas_call x3, Pallas kernels, attend_backward(): pl.pallas_call(functools.partial(backward_body, BQ, BK, SUB), grid_spec=p...  83.7 us
    all_to_all x2, waiting for transfers between devices, body(): backs.append(lax.all_to_all(grads, 'tensor', 0, 0, tiled=True))  60.1 us
    pallas_call x2, Pallas kernels, attend_forward(): pl.pallas_call(functools.partial(forward_body, BK), grid_spec=pltpu.Prefe...  49 us
    pallas_call x1, Pallas kernels, dense(): pl.pallas_call(functools.partial(dense_body, own), grid=(rows // block,),...  42.2 us
    all_to_all x1, blocking collectives, body(): qkv_grad = lax.all_to_all(qkv_grad, 'dp', 0, 0, tiled=True)  19.2 us
    all_to_all x2, starting transfers between devices, body(): backs.append(lax.all_to_all(grads, 'tensor', 0, 0, tiled=True))  18.1 us
    pallas_call x1, Pallas kernels, weight_grads_of(): pl.pallas_call(functools.partial(weight_grads_body, steps // 2), grid=(st...  16.5 us
  transfers between devices with their start and end apart: 15, of which 5 were waited for; matrix products, arithmetic and copies ran while one was open for 3% of the time, Pallas kernels for 22%

profile of v7, /device:TPU:0, one launch (start us, length us, event | category | flops | bytes accessed | tf_op | source)
XLA Modules:
  0.0 538.7 jit_solution(14364730270213063541)
XLA Ops:
  7.2 0.7 convert_reduce_fusion.5
  8.0 0.9 copy.120
  8.9 0.9 copy.121
  9.8 0.9 copy.122
  10.9 0.9 copy.124
  11.8 1.3 pad_maximum_fusion.4.s_ref
  13.1 0.9 concatenate.47.w_ref
  14.0 114.7 %start.1 = (bf16[4,768,768]{2,1,0:T(8,128)(2,1)}, bf16[4,8,96,2304]{3,2,1,0:T(8,128)(2,1)}, f32[4,12,128]{2,1,0:T(8,128)}) custom-call(bf16[768,768]{1,0:T(8,128)(2,1)} %bitcast.72, bf16[96,2304]{1,0:T(8,128)(2,1)} %concatenate.47.w_ref, f32[12,128]{1,0:T(8,128)} %pad_maximum_fusion.4.s_ref), custom_call_target="tpu_custom_call" | custom-call | bytes 209715200 | tf_op jit(solution)/shard_map/start/pallas_call | solution.py:360
  128.7 0.8 copy.157
  129.8 0.7 reshape_reshape.9.b_ref
  131.6 0.7 convert_reduce_fusion.3
  132.3 10.5 %project.1 = (bf16[3,128,3072]{2,1,0:T(8,128)(2,1)}, bf16[3,3072,128]{2,1,0:T(8,128)(2,1)}, bf16[3,64,3072]{2,1,0:T(8,128)(2,1)}, bf16[3,3072,64]{2,1,0:T(8,128)...) custom-call(s32[1]{0:T(128)} %bitcast.11.part_ref, bf16[3072,768]{1,0:T(8,128)(2,1)} %bitcast.69, ...), custom_call_target="tpu_custom_call" | custom-call | flops 2717908992 | bytes 17694720 | tf_op jit(solution)/shard_map/project/pallas_call | solution.py:47
  142.8 30.1 %attend_forward.3 = (bf16[4,128,768]{2,1,0:T(8,128)(2,1)}, f32[2,64,3072]{2,1,0:T(8,128)}, f32[2,1,3072]{2,1,0:T(1,128)}) custom-call(s32[8]{0:T(128)} %get-tuple-element.231.lo_ref, s32[8]{0:T(128)} %get-tuple-element.230.hi_ref, bf16[3,128,3072]{2,1,0:T(8,128)(2,1)} %get-tuple-element.56.qt_ref, bf16[3,3072,128]{2,1,0:T(8,128)(2,1)} %get-tuple-element.57.ka_ref, ...), custom_call_target="tpu_custom_call" | custom-call | flops 4831838208 | bytes 6291456 | tf_op jit(solution)/shard_map/attend_forward/pallas_call | solution.py:104
  172.9 3.5 all-to-all-start
  176.6 0.7 convert_reduce_fusion.6
  177.4 18.9 %attend_forward.2 = (bf16[4,64,768]{2,1,0:T(8,128)(2,1)}, f32[1,64,3072]{2,1,0:T(8,128)}, f32[1,1,3072]{2,1,0:T(1,128)}) custom-call(s32[4]{0:T(128)} %get-tuple-element.229.lo_ref, s32[4]{0:T(128)} %get-tuple-element.228.hi_ref, bf16[3,128,3072]{2,1,0:T(8,128)(2,1)} %get-tuple-element.56.qt_ref, bf16[3,3072,128]{2,1,0:T(8,128)(2,1)} %get-tuple-element.57.ka_ref, ...), custom_call_target="tpu_custom_call" | custom-call | flops 2415919104 | bytes 3145728 | tf_op jit(solution)/shard_map/attend_forward/pallas_call | solution.py:104
  196.3 5.1 all-to-all-start.1
  202.8 7.5 %all-to-all-done.1.ctx1_ref = bf16[4,64,768]{2,1,0:T(8,128)(2,1)S(1)} async-done(((bf16[4,64,768]{2,1,0:T(8,128)(2,1)}), bf16[4,64,768]{2,1,0:T(8,128)(2,1)S(1)}, u32[]{:S(2)}, u32[]{:S(2)}) %all-to-all-start.1) | async-done | bytes 393248 | tf_op jit(solution)/shard_map/all_to_all | solution.py:668
  210.3 0.7 copy-done.5
  211.0 42.2 %dense.1 = (bf16[768,768]{1,0:T(8,128)(2,1)}, bf16[768,768]{1,0:T(8,128)(2,1)}, bf16[768,768]{1,0:T(8,128)(2,1)}, bf16[768,768]{1,0:T(8,128)(2,1)}, f32[768,768]...) custom-call(bf16[768,768]{1,0:T(8,128)(2,1)} %bitcast.73, ...), custom_call_target="tpu_custom_call" | custom-call | flops 16307453952 | bytes 41943040 | tf_op jit(solution)/shard_map/dense/pallas_call | solution.py:534
  253.2 16.5 %weight_grads.1 = bf16[768,6912]{1,0:T(8,128)(2,1)} custom-call(bf16[768,768]{1,0:T(8,128)(2,1)} %get-tuple-element.84.first_ref, bf16[768,768]{1,0:T(8,128)(2,1)} %get-tuple-element.85.second_ref, bf16[768,768]{1,0:T(8,128)(2,1)} %get-tuple-element.86.attn_ref, bf16[8,768,768]{2,1,0:T(8,128)(2,1)} %get-tuple-element.87.both_ref, ...), custom_call_target="tpu_custom_call" | custom-call | flops 8153726976 | bytes 18874368 | tf_op jit(solution)/shard_map/weight_grads/pallas_call | solution.py:404
  269.8 3.5 all-to-all-start.2
  273.3 2.0 collective-permute-start.3
  275.3 12.1 %all-to-all-done.2.go_ref = bf16[4,64,768]{2,1,0:T(8,128)(2,1)S(1)} async-done(((bf16[4,64,768]{2,1,0:T(8,128)(2,1)}), bf16[4,64,768]{2,1,0:T(8,128)(2,1)S(1)}, u32[]{:S(2)}, u32[]{:S(2)}) %all-to-all-start.2) | async-done | bytes 393248 | tf_op jit(solution)/shard_map/all_to_all | solution.py:674
  287.3 4.1 all-to-all-start.4
  291.4 3.0 collective-permute-start.4
  294.4 0.7 convert_reduce_fusion.1
  295.1 10.4 %collective-permute-done.4 = f32[10,768]{1,0:T(8,128)S(1)} collective-permute-done((f32[10,768]{1,0:T(8,128)S(1)}, f32[10,768]{1,0:T(8,128)S(1)}, u32[]{:S(2)}, u32[]{:S(2)}) %collective-permute-start.4) | collective-permute-done | bytes 30752 | tf_op jit(solution)/shard_map/ppermute | solution.py:611
  305.7 27.9 %attend_backward.3 = (bf16[4,192,768]{2,1,0:T(8,128)(2,1)}, bf16[768,192]{1,0:T(8,128)(2,1)}, f32[192,128]{1,0:T(8,128)}) custom-call(s32[6]{0:T(128)} %get-tuple-element.196.lo_ref, s32[6]{0:T(128)} %get-tuple-element.195.hi_ref, bf16[4,64,768]{2,1,0:T(8,128)(2,1)} %copy-done.4, f32[2,64,3072]{2,1,0:T(8,128)} %get-tuple-element.65.ot_ref, ...), custom_call_target="tpu_custom_call" | custom-call | flops 6039797760 | bytes 5505024 | tf_op jit(solution)/shard_map/attend_backward/pallas_call | solution.py:177
  333.6 1.0 slice_reduce_fusion.2
  334.6 0.9 copy-done.2
  335.5 27.9 %attend_backward.5 = (bf16[4,192,768]{2,1,0:T(8,128)(2,1)}, bf16[768,192]{1,0:T(8,128)(2,1)}, f32[192,128]{1,0:T(8,128)}) custom-call(s32[6]{0:T(128)} %get-tuple-element.196.lo_ref, s32[6]{0:T(128)} %get-tuple-element.195.hi_ref, bf16[4,128,768]{2,1,0:T(8,128)(2,1)} %copy-done.2, f32[1,64,3072]{2,1,0:T(8,128)} %get-tuple-element.74.ot_ref, ...), custom_call_target="tpu_custom_call" | custom-call | flops 6039797760 | bytes 5505024 | tf_op jit(solution)/shard_map/attend_backward/pallas_call | solution.py:177
  363.4 1.0 slice_reduce_fusion
  364.4 28.0 %attend_backward.4 = (bf16[4,192,768]{2,1,0:T(8,128)(2,1)}, bf16[768,192]{1,0:T(8,128)(2,1)}, f32[192,128]{1,0:T(8,128)}) custom-call(s32[6]{0:T(128)} %get-tuple-element.196.lo_ref, s32[6]{0:T(128)} %get-tuple-element.195.hi_ref, bf16[4,128,768]{2,1,0:T(8,128)(2,1)} %copy-done.2, f32[2,64,3072]{2,1,0:T(8,128)} %get-tuple-element.65.ot_ref, ...), custom_call_target="tpu_custom_call" | custom-call | flops 6039797760 | bytes 5505024 | tf_op jit(solution)/shard_map/attend_backward/pallas_call | solution.py:177
  392.4 1.0 slice_reduce_fusion.1
  393.8 1.3 pad_maximum_fusion.1
  395.1 0.7 copy.131
  396.1 0.7 pad_maximum_fusion
  396.7 19.2 %all_to_all.35 = bf16[8,128,576]{1,2,0:T(8,128)(2,1)S(1)} all-to-all(bf16[8,128,576]{1,2,0:T(8,128)(2,1)S(1)} %pad_maximum_fusion), channel_id=1, replica_groups=mesh['dp'=8,'tensor'=4] {'dp'}, dimensions={0} | all-to-all | bytes 2359296 | tf_op jit(solution)/shard_map/all_to_all | solution.py:718
  415.9 3.7 all-to-all-start.3
  419.6 1.0 dynamic-slice_bitcast_fusion.3
  420.7 3.7 collective-permute-start.2
  424.4 1.1 collective-permute-start
  425.9 24.6 %all-to-all-done.3.b0_ref = bf16[4,192,768]{2,1,0:T(8,128)(2,1)S(1)} async-done(((bf16[4,192,768]{2,1,0:T(8,128)(2,1)}), bf16[4,192,768]{2,1,0:T(8,128)(2,1)S(1)}, u32[]{:S(2)}, u32[]{:S(2)}) %all-to-all-start.3) | async-done | bytes 1179680 | tf_op jit(solution)/shard_map/all_to_all | solution.py:703
  450.4 14.4 %all-to-all-start.5 = ((bf16[4,192,768]{2,1,0:T(8,128)(2,1)}), bf16[4,192,768]{2,1,0:T(8,128)(2,1)}, u32[]{:S(2)}, u32[]{:S(2)}) async-start(bf16[4,192,768]{2,1,0:T(8,128)(2,1)} %get-tuple-element.72), calls=%async_computation.5 | async-start | bytes 2359296 | tf_op jit(solution)/shard_map/all_to_all | solution.py:703
  464.9 0.7 copy.138
  465.7 0.7 copy.137
  466.4 0.7 copy.136
  468.1 0.6 fusion.7
  468.8 0.9 slice.173
  469.9 1.1 slice-done
  471.1 0.9 dynamic-slice_bitcast_fusion.2
  472.0 2.0 collective-permute-start.5
  474.0 1.8 collective-permute-start.7
  475.9 1.1 collective-permute-start.6
  477.0 0.6 reshape_squeeze.19
  477.6 0.6 reshape_squeeze.18
  478.3 0.6 dynamic-slice_reduce_fusion
  478.9 35.5 %all-to-all-done.5.b1_ref = bf16[4,192,768]{2,1,0:T(8,128)(2,1)} async-done(((bf16[4,192,768]{2,1,0:T(8,128)(2,1)}), bf16[4,192,768]{2,1,0:T(8,128)(2,1)}, u32[]{:S(2)}, u32[]{:S(2)}) %all-to-all-start.5) | async-done | bytes 1179680 | tf_op jit(solution)/shard_map/all_to_all | solution.py:703
  514.5 7.7 %early_back.1.acc_ref = f32[768,768]{1,0:T(8,128)} custom-call(bf16[4,768,2304]{2,1,0:T(8,128)(2,1)} %bitcast.65, bf16[4,192,768]{2,1,0:T(8,128)(2,1)} %copy-done, bf16[4,192,768]{2,1,0:T(8,128)(2,1)} %all-to-all-done.5.b1_ref), custom_call_target="tpu_custom_call" | custom-call | flops 1811939328 | bytes 10485760 | tf_op jit(solution)/shard_map/early_back/pallas_call | solution.py:578
  522.1 6.7 %late_back.1 = bf16[768,768]{1,0:T(8,128)(2,1)} custom-call(s32[1]{0:T(128)} %bitcast.11.part_ref, bf16[4,768,2304]{2,1,0:T(8,128)(2,1)} %bitcast.66, f32[768,768]{1,0:T(8,128)} %early_back.1.acc_ref, f32[768,768]{1,0:T(8,128)} %get-tuple-element.73.grad_ref, bf16[192,768]{1,0:T(8,128)(2,1)} %get-tuple-element.205.rest_0_, ...), custom_call_target="tpu_custom_call" | custom-call | flops 905969664 | bytes 10485760 | tf_op jit(solution)/shard_map/late_back/pallas_call | solution.py:592
  528.9 1.4 fusion.1
  530.3 0.9 slice_bitcast_fusion
  531.1 0.7 copy.139
  (113 shorter events, 5.6 us)
Async XLA Ops:
  7.2 5.9 %copy-start.12 = (bf16[768,96]{0,1:T(8,128)(2,1)S(1)}, bf16[768,96]{0,1:T(8,128)(2,1)}, u32[]{:S(2)}) copy-start(bf16[768,96]{0,1:T(8,128)(2,1)} %param.31) | copy-start | bytes 442372
  7.2 5.9 %copy-start.11 = (bf16[96,768]{1,0:T(8,128)(2,1)S(1)}, bf16[96,768]{1,0:T(8,128)(2,1)}, u32[]{:S(2)}) copy-start(bf16[96,768]{1,0:T(8,128)(2,1)} %param.29) | copy-start | bytes 442372
  13.1 116.4 %copy-start.20 = (f32[192]{0:T(256)S(1)}, f32[192]{0:T(256)}, u32[]{:S(2)}) copy-start(f32[192]{0:T(256)} %param.23) | copy-start | bytes 2308
  13.1 116.5 %copy-start.21 = (f32[192]{0:T(256)S(1)}, f32[192]{0:T(256)}, u32[]{:S(2)}) copy-start(f32[192]{0:T(256)} %param.24) | copy-start | bytes 2308
  172.9 23.4 %all-to-all-start = ((bf16[4,128,768]{2,1,0:T(8,128)(2,1)}), bf16[4,128,768]{2,1,0:T(8,128)(2,1)S(1)}, u32[]{:S(2)}, u32[]{:S(2)}) async-start(bf16[4,128,768]{2,1,0:T(8,128)(2,1)} %get-tuple-element.60), calls=%async_computation | async-start | bytes 1572864 | tf_op jit(solution)/shard_map/all_to_all | solution.py:668
  177.4 24.0 %copy-start.14 = (f32[768]{0:T(1024)S(1)}, f32[768]{0:T(1024)}, u32[]{:S(2)}) copy-start(f32[768]{0:T(1024)} %param.26) | copy-start | bytes 9220
  177.4 24.0 %copy-start.15 = (f32[768]{0:T(1024)S(1)}, f32[768]{0:T(1024)}, u32[]{:S(2)}) copy-start(f32[768]{0:T(1024)} %param.27) | copy-start | bytes 9220
  177.4 24.1 %copy-start.16 = (f32[768]{0:T(1024)S(1)}, f32[768]{0:T(1024)}, u32[]{:S(2)}) copy-start(f32[768]{0:T(1024)} %param.28) | copy-start | bytes 9220
  177.4 24.1 %copy-start.17 = (f32[768]{0:T(1024)S(1)}, f32[768]{0:T(1024)}, u32[]{:S(2)}) copy-start(f32[768]{0:T(1024)} %param.32) | copy-start | bytes 9220
  177.4 24.1 %copy-start.18 = (f32[768]{0:T(1024)S(1)}, f32[768]{0:T(1024)}, u32[]{:S(2)}) copy-start(f32[768]{0:T(1024)} %param.33) | copy-start | bytes 9220
  177.4 24.1 %copy-start.19 = (f32[768]{0:T(1024)S(1)}, f32[768]{0:T(1024)}, u32[]{:S(2)}) copy-start(f32[768]{0:T(1024)} %param.34) | copy-start | bytes 9220
  196.3 14.0 %copy-start.3 = (bf16[4,128,768]{2,1,0:T(8,128)(2,1)}, bf16[4,128,768]{2,1,0:T(8,128)(2,1)S(1)}, u32[]{:S(2)}) copy-start(bf16[4,128,768]{2,1,0:T(8,128)(2,1)S(1)} %all-to-all-done.ctx0_ref) | copy-start | bytes 2359300
  196.3 14.0 %all-to-all-start.1 = ((bf16[4,64,768]{2,1,0:T(8,128)(2,1)}), bf16[4,64,768]{2,1,0:T(8,128)(2,1)S(1)}, u32[]{:S(2)}, u32[]{:S(2)}) async-start(bf16[4,64,768]{2,1,0:T(8,128)(2,1)} %get-tuple-element.62), calls=%async_computation.1 | async-start | bytes 786432 | tf_op jit(solution)/shard_map/all_to_all | solution.py:668
  201.4 267.4 %reduce-scatter.2.cloned.1.call-start = ((), (), s32[]{:S(2)}) async-start(), calls=%async_computation.8 | async-start | bytes 11943936 | tf_op jit(solution)/shard_map/reduce_scatter | solution.py:679
  210.3 0.7 copy-start.5
  269.8 3.6 copy-start.13
  269.8 17.6 %all-to-all-start.2 = ((bf16[4,64,768]{2,1,0:T(8,128)(2,1)}), bf16[4,64,768]{2,1,0:T(8,128)(2,1)S(1)}, u32[]{:S(2)}, u32[]{:S(2)}) async-start(bf16[4,64,768]{2,1,0:T(8,128)(2,1)} %get-tuple-element.64), calls=%async_computation.2 | async-start | bytes 786432 | tf_op jit(solution)/shard_map/all_to_all | solution.py:674
  273.3 18.1 %collective-permute-start.3 = (f32[10,768]{1,0:T(8,128)S(1)}, f32[10,768]{1,0:T(8,128)S(1)}, u32[]{:S(2)}, u32[]{:S(2)}) collective-permute-start(f32[10,768]{1,0:T(8,128)S(1)} %bitcast.85), channel_id=1, source_target_pairs={{0,1},{1,0},{2,3},{3,2},{4,5},{5,4},{6,7},{7,6},{8,9},{9,8},{10,11... | collective-permute-start | bytes 92168 | tf_op jit(solution)/shard_map/ppermute | solution.py:611
  287.3 18.3 %copy-start.4 = (bf16[4,64,768]{2,1,0:T(8,128)(2,1)}, bf16[4,64,768]{2,1,0:T(8,128)(2,1)S(1)}, u32[]{:S(2)}) copy-start(bf16[4,64,768]{2,1,0:T(8,128)(2,1)S(1)} %all-to-all-done.2.go_ref) | copy-start | bytes 1179652
  287.3 47.2 %all-to-all-start.4 = ((bf16[4,128,768]{2,1,0:T(8,128)(2,1)}), bf16[4,128,768]{2,1,0:T(8,128)(2,1)S(1)}, u32[]{:S(2)}, u32[]{:S(2)}) async-start(bf16[4,128,768]{2,1,0:T(8,128)(2,1)} %get-tuple-element.71), calls=%async_computation.4 | async-start | bytes 1572864 | tf_op jit(solution)/shard_map/all_to_all | solution.py:675
  291.4 14.1 %collective-permute-start.4 = (f32[10,768]{1,0:T(8,128)S(1)}, f32[10,768]{1,0:T(8,128)S(1)}, u32[]{:S(2)}, u32[]{:S(2)}) collective-permute-start(f32[10,768]{1,0:T(8,128)S(1)} %slice_add_fusion), channel_id=1, source_target_pairs={{0,2},{1,3},{2,0},{3,1},{4,6},{5,7},{6,4},{7,5},{8,10},{9,11},{10,... | collective-permute-start | bytes 92168 | tf_op jit(solution)/shard_map/ppermute | solution.py:611
  334.6 0.9 copy-start.2
  364.4 29.4 %copy-start.6 = (bf16[768,192]{1,0:T(8,128)(2,1)S(1)}, bf16[768,192]{1,0:T(8,128)(2,1)}, u32[]{:S(2)}) copy-start(bf16[768,192]{1,0:T(8,128)(2,1)} %get-tuple-element.77) | copy-start | bytes 884740
  364.4 29.4 %copy-start.7 = (bf16[768,192]{1,0:T(8,128)(2,1)S(1)}, bf16[768,192]{1,0:T(8,128)(2,1)}, u32[]{:S(2)}) copy-start(bf16[768,192]{1,0:T(8,128)(2,1)} %get-tuple-element.79) | copy-start | bytes 884740
  415.9 3.7 copy-start.1
  415.9 34.5 %all-to-all-start.3 = ((bf16[4,192,768]{2,1,0:T(8,128)(2,1)}), bf16[4,192,768]{2,1,0:T(8,128)(2,1)S(1)}, u32[]{:S(2)}, u32[]{:S(2)}) async-start(bf16[4,192,768]{2,1,0:T(8,128)(2,1)} %get-tuple-element.70), calls=%async_computation.3 | async-start | bytes 2359296 | tf_op jit(solution)/shard_map/all_to_all | solution.py:703
  420.7 55.2 %collective-permute-start.2 = (bf16[192,768]{1,0:T(8,128)(2,1)}, bf16[192,768]{1,0:T(8,128)(2,1)S(1)}, u32[]{:S(2)}, u32[]{:S(2)}) collective-permute-start(bf16[192,768]{1,0:T(8,128)(2,1)} %get-tuple-element.202), channel_id=1, source_target_pairs={{0,3},{1,0},{2,1},{3,2},{4,7},{5,4},{6,5},{7,6},{8,11},{9,8},{10,9... | collective-permute-start | bytes 884744 | tf_op jit(solution)/shard_map/ppermute | solution.py:630
  424.4 97.8 %collective-permute-start.1 = (bf16[192,768]{1,0:T(8,128)(2,1)}, bf16[192,768]{1,0:T(8,128)(2,1)}, u32[]{:S(2)}, u32[]{:S(2)}) collective-permute-start(bf16[192,768]{1,0:T(8,128)(2,1)} %get-tuple-element.203), channel_id=1, source_target_pairs={{0,2},{1,3},{2,0},{3,1},{4,6},{5,7},{6,4},{7,5},{8,10},{9,11},{10,... | collective-permute-start | bytes 884744 | tf_op jit(solution)/shard_map/ppermute | solution.py:630
  424.4 97.8 %collective-permute-start = (bf16[192,768]{1,0:T(8,128)(2,1)}, bf16[192,768]{1,0:T(8,128)(2,1)}, u32[]{:S(2)}, u32[]{:S(2)}) collective-permute-start(bf16[192,768]{1,0:T(8,128)(2,1)} %get-tuple-element.204), channel_id=1, source_target_pairs={{0,1},{1,2},{2,3},{3,0},{4,5},{5,6},{6,7},{7,4},{8,9},{9,10},{10,1... | collective-permute-start | bytes 884744 | tf_op jit(solution)/shard_map/ppermute | solution.py:630
  450.4 14.5 %copy-start = (bf16[4,192,768]{2,1,0:T(8,128)(2,1)}, bf16[4,192,768]{2,1,0:T(8,128)(2,1)S(1)}, u32[]{:S(2)}) copy-start(bf16[4,192,768]{2,1,0:T(8,128)(2,1)S(1)} %all-to-all-done.3.b0_ref) | copy-start | bytes 3538948
  450.4 64.0 %all-to-all-start.5 = ((bf16[4,192,768]{2,1,0:T(8,128)(2,1)}), bf16[4,192,768]{2,1,0:T(8,128)(2,1)}, u32[]{:S(2)}, u32[]{:S(2)}) async-start(bf16[4,192,768]{2,1,0:T(8,128)(2,1)} %get-tuple-element.72), calls=%async_computation.5 | async-start | bytes 2359296 | tf_op jit(solution)/shard_map/all_to_all | solution.py:703
  468.1 0.6 copy-start.9
  469.7 1.3 slice-start
  471.0 7.2 %copy-start.10 = (f32[8064]{0:T(1024)S(1)}, f32[8064]{0:T(1024)}, u32[]{:S(2)}) copy-start(f32[8064]{0:T(1024)} %copy-done.9) | copy-start | bytes 96772
  472.0 56.9 %collective-permute-start.5 = (bf16[96,1728]{1,0:T(8,128)(2,1)}, bf16[96,1728]{1,0:T(8,128)(2,1)}, u32[]{:S(2)}, u32[]{:S(2)}) collective-permute-start(bf16[96,1728]{1,0:T(8,128)(2,1)} %get-tuple-element.199), channel_id=1, source_target_pairs={{0,1},{1,2},{2,3},{3,0},{4,5},{5,6},{6,7},{7,4},{8,9},{9,10},{10,1... | collective-permute-start | bytes 995336 | tf_op jit(solution)/shard_map/ppermute | solution.py:630
  474.0 54.8 %collective-permute-start.7 = (bf16[96,1728]{1,0:T(8,128)(2,1)}, bf16[96,1728]{1,0:T(8,128)(2,1)}, u32[]{:S(2)}, u32[]{:S(2)}) collective-permute-start(bf16[96,1728]{1,0:T(8,128)(2,1)} %get-tuple-element.200), channel_id=1, source_target_pairs={{0,3},{1,0},{2,1},{3,2},{4,7},{5,4},{6,5},{7,6},{8,11},{9,8},{10,9... | collective-permute-start | bytes 995336 | tf_op jit(solution)/shard_map/ppermute | solution.py:630
  475.9 46.3 %copy-start.8 = (bf16[192,768]{1,0:T(8,128)(2,1)}, bf16[192,768]{1,0:T(8,128)(2,1)S(1)}, u32[]{:S(2)}) copy-start(bf16[192,768]{1,0:T(8,128)(2,1)S(1)} %collective-permute-done.2.rest_3_) | copy-start | bytes 884740
  475.9 53.0 %collective-permute-start.6 = (bf16[96,1728]{1,0:T(8,128)(2,1)S(1)}, bf16[96,1728]{1,0:T(8,128)(2,1)}, u32[]{:S(2)}, u32[]{:S(2)}) collective-permute-start(bf16[96,1728]{1,0:T(8,128)(2,1)S(1)} %get-tuple-element.201), channel_id=1, source_target_pairs={{0,2},{1,3},{2,0},{3,1},{4,6},{5,7},{6,4},{7,5},{8,10},{9,11},{10,... | collective-permute-start | bytes 995336 | tf_op jit(solution)/shard_map/ppermute | solution.py:630
Sparse Core Ops, SparseCore 0:
  269.9 79.8 reduce-scatter.1

commit v8 on v7

--- a/solution.py
+++ b/solution.py
@@ -18,7 +18,7 @@
 def dot(a,b): return jnp.dot(a,b,preferred_element_type=jnp.float32)
 
 
-def project_body(heads, part_ref, x_ref, w_ref, b_ref, srow_ref, qt_ref, ka_ref, vt_ref, qn_ref, kt_ref, vn_ref):
+def project_body(heads, part_ref, x_ref, w_ref, b_ref, srow_ref, qt_ref, ka_ref, vt_ref, kt_ref, vn_ref):
     y=dot(x_ref[...], w_ref[0,:,:b_ref.shape[1]]) + b_ref[...]
     low = y.astype(jnp.bfloat16)
     yt = low.T
@@ -26,15 +26,15 @@
     match = lax.broadcasted_iota(jnp.int32,(HD,rows),0)==srow_ref[...]
     apart = jnp.where(match,0.0,APART).astype(jnp.bfloat16)
     same = jnp.where(match,1.0,0.0).T.astype(jnp.bfloat16)
+    width=heads*HD
     for h in range(heads):
-        at=3*h*HD
-        qt_ref[h,:HD,:]=yt[at:at+HD]*jnp.bfloat16(SCALE)
+        q_at,k_at,v_at=h*HD,width+h*HD,2*width+h*HD
+        qt_ref[h,:HD,:]=yt[q_at:q_at+HD]*jnp.bfloat16(SCALE)
         qt_ref[h,HD:,:]=apart
-        qn_ref[h]=low[:,at:at+HD]*jnp.bfloat16(SCALE)
-        ka_ref[h]=jnp.concatenate([low[:,at+HD:at+2*HD],same],axis=1)
-        kt_ref[h]=yt[at+HD:at+2*HD]
-        vt_ref[h]=yt[at+2*HD:at+3*HD]
-        vn_ref[h]=low[:,at+2*HD:at+3*HD]
+        ka_ref[h]=jnp.concatenate([low[:,k_at:k_at+HD],same],axis=1)
+        kt_ref[h]=yt[k_at:k_at+HD]
+        vt_ref[h]=yt[v_at:v_at+HD]
+        vn_ref[h]=low[:,v_at:v_at+HD]
 
 
 def project(x,rest,part,b,seg,rows=512):
@@ -48,8 +48,8 @@
         grid_spec=pltpu.PrefetchScalarGridSpec(num_scalar_prefetch=1,grid=(L//rows,),
         in_specs=[pl.BlockSpec((rows,D),lambda i,*_:(i,0)),pl.BlockSpec((1,D,cols),lambda i,p:(p[0],0,0)),pl.BlockSpec((1,b.shape[0]),lambda i,*_:(0,0)),
                   pl.BlockSpec((1,rows),lambda i,*_:(0,i))],
-        out_specs=[tr(2*HD),nat(2*HD),tr(HD),nat(HD),tr(HD),nat(HD)]),
-        out_shape=[S((heads,2*HD,L),bf),S((heads,L,2*HD),bf),S((heads,HD,L),bf),S((heads,L,HD),bf),S((heads,HD,L),bf),S((heads,L,HD),bf)],
+        out_specs=[tr(2*HD),nat(2*HD),tr(HD),tr(HD),nat(HD)]),
+        out_shape=[S((heads,2*HD,L),bf),S((heads,L,2*HD),bf),S((heads,HD,L),bf),S((heads,HD,L),bf),S((heads,L,HD),bf)],
         compiler_params=pltpu.CompilerParams(vmem_limit_bytes=62 << 20),
         cost_estimate=pl.CostEstimate(flops=2*L*D*b.shape[0],bytes_accessed=L*D*2+D*cols*2+L*heads*HD*2*10,transcendentals=0),
         name="project")(part.reshape(1),x,rest,b.reshape(1,-1),seg.reshape(1,-1))
@@ -112,7 +112,7 @@
         name="attend_forward")(lo,hi,qt,ka,vt)
 
 
-def backward_body(BQ, BK, SUB, lo_ref, hi_ref, go_ref, ot_ref, lse_ref, qt_ref, ka_ref, qn_ref, kt_ref, vn_ref, x_ref, out_ref, wg_ref, sum_ref, got, gon, delta, dqt, dkt, dvt, dk_s, dv_s, x_s, x_sem):
+def backward_body(BQ, BK, lo_ref, hi_ref, go_ref, ot_ref, lse_ref, qt_ref, ka_ref, kt_ref, vn_ref, x_ref, out_ref, wg_ref, sum_ref, got, delta, dqt, dkt, dvt, dk_s, dv_s, x_s, x_sem):
     bring=pltpu.make_async_copy(x_ref,x_s,x_sem)
     bring.start()
     parts,_,rows=go_ref.shape
@@ -124,7 +124,6 @@
             gt=go_ref[p,h*HD:(h+1)*HD,at:at+CH]
             wide=gt.astype(jnp.float32)
             got[h,:,c*CH:(c+1)*CH]=gt
-            gon[h,c*CH:(c+1)*CH,:]=wide.T.astype(jnp.bfloat16)
             delta[h,:,c*CH:(c+1)*CH]=jnp.sum(wide*ot_ref[h,:,c*CH:(c+1)*CH],axis=0,keepdims=True)
     dqt[...]=jnp.zeros(dqt.shape,jnp.float32)
 
@@ -134,21 +133,21 @@
         dv_s[...]=jnp.zeros(dv_s.shape,jnp.float32)
 
         def query_block(i,_):
-            for h,c in [(h,c) for h in range(heads) for c in range(BQ//SUB)]:
-                at=pl.multiple_of(i*BQ+c*SUB,SUB)
-                s=dot(ka_ref[h,pl.ds(ka_at,BK),:],qt_ref[h,:,pl.ds(at,SUB)])
-                p=jnp.exp(s-lse_ref[h,:,pl.ds(at,SUB)])
-                dp=dot(vn_ref[h,pl.ds(ka_at,BK),:],got[h,:,pl.ds(at,SUB)])
-                ds=(p*(dp-delta[h,:,pl.ds(at,SUB)])).astype(jnp.bfloat16)
-                dv_s[h]+=dot(p.astype(jnp.bfloat16),gon[h,pl.ds(at,SUB),:])
-                dk_s[h]+=dot(ds,qn_ref[h,pl.ds(at,SUB),:])
-                dqt[h,:,pl.ds(at,SUB)]+=dot(kt_ref[h,:,pl.ds(ka_at,BK)],ds)
+            for h in range(heads):
+                at=pl.multiple_of(i*BQ,BQ)
+                s=dot(ka_ref[h,pl.ds(ka_at,BK),:],qt_ref[h,:,pl.ds(at,BQ)])
+                p=jnp.exp(s-lse_ref[h,:,pl.ds(at,BQ)])
+                dp=dot(vn_ref[h,pl.ds(ka_at,BK),:],got[h,:,pl.ds(at,BQ)])
+                ds=(p*(dp-delta[h,:,pl.ds(at,BQ)])).astype(jnp.bfloat16)
+                dv_s[h]+=dot_right_t(got[h,:,pl.ds(at,BQ)],p.astype(jnp.bfloat16))
+                dk_s[h]+=dot_right_t(qt_ref[h,:HD,pl.ds(at,BQ)],ds)
+                dqt[h,:,pl.ds(at,BQ)]+=dot(kt_ref[h,:,pl.ds(ka_at,BK)],ds)
             return 0
 
         lax.fori_loop(lo_ref[j],hi_ref[j],query_block,0)
         for h in range(heads):
-            dkt[h,:,pl.ds(ka_at,BK)]=dk_s[h].T.astype(jnp.bfloat16)
-            dvt[h,:,pl.ds(ka_at,BK)]=dv_s[h].T.astype(jnp.bfloat16)
+            dkt[h,:,pl.ds(ka_at,BK)]=dk_s[h].astype(jnp.bfloat16)
+            dvt[h,:,pl.ds(ka_at,BK)]=dv_s[h].astype(jnp.bfloat16)
         return 0
 
     lax.fori_loop(0,L//BK,key_block,0)
@@ -169,20 +168,20 @@
     sum_ref[...]=jnp.broadcast_to(total,sum_ref.shape)
 
 
-def attend_backward(first,heads,go,go_first,ot,lse,ot_first,qt,ka,qn,kt,vn,x,lo,hi,BQ=512,BK=512,SUB=512):
+def attend_backward(first,heads,go,go_first,ot,lse,ot_first,qt,ka,kt,vn,x,lo,hi,BQ=512,BK=512):
     parts,_,rows=go.shape; L=parts*rows; D=x.shape[2]
     S=jax.ShapeDtypeStruct; f32=jnp.float32; bf=jnp.bfloat16
     at=lambda a,n: pl.BlockSpec((heads,)+a.shape[1:],lambda i,*_:(n//heads,0,0),pipeline_mode=pl.Buffered(1))
     out=3*heads*HD
-    return pl.pallas_call(functools.partial(backward_body,BQ,BK,SUB),
+    return pl.pallas_call(functools.partial(backward_body,BQ,BK),
         grid_spec=pltpu.PrefetchScalarGridSpec(num_scalar_prefetch=2,grid=(1,),
-        in_specs=[pl.BlockSpec((parts,heads*HD,rows),lambda i,*_:(0,go_first,0),pipeline_mode=pl.Buffered(1)),at(ot,ot_first),at(lse,ot_first)]+[at(a,first) for a in (qt,ka,qn,kt,vn)]+[pl.BlockSpec(memory_space=pl.ANY)],
+        in_specs=[pl.BlockSpec((parts,heads*HD,rows),lambda i,*_:(0,go_first,0),pipeline_mode=pl.Buffered(1)),at(ot,ot_first),at(lse,ot_first)]+[at(a,first) for a in (qt,ka,kt,vn)]+[pl.BlockSpec(memory_space=pl.ANY)],
         out_specs=[pl.BlockSpec((parts,out,rows),lambda i,*_:(0,0,0),pipeline_mode=pl.Buffered(1)),pl.BlockSpec((D,out),lambda i,*_:(0,0)),pl.BlockSpec((out,128),lambda i,*_:(0,0))],
-        scratch_shapes=[VM((heads,HD,L),bf),VM((heads,L,HD),bf),VM((heads,1,L),f32),VM((heads,HD,L),f32),VM((heads,HD,L),bf),VM((heads,HD,L),bf),VM((heads,BK,HD),f32),VM((heads,BK,HD),f32),VM(x.shape,bf),pltpu.SemaphoreType.DMA]),
+        scratch_shapes=[VM((heads,HD,L),bf),VM((heads,1,L),f32),VM((heads,HD,L),f32),VM((heads,HD,L),bf),VM((heads,HD,L),bf),VM((heads,HD,BK),f32),VM((heads,HD,BK),f32),VM(x.shape,bf),pltpu.SemaphoreType.DMA]),
         out_shape=[S((parts,out,rows),bf),S((D,out),bf),S((out,128),f32)],
         compiler_params=pltpu.CompilerParams(vmem_limit_bytes=62 << 20),
         cost_estimate=pl.CostEstimate(flops=2*L*L*HD*5*heads,bytes_accessed=L*heads*HD*2*14,transcendentals=L*L*heads),
-        name="attend_backward")(lo,hi,go,ot,lse,qt,ka,qn,kt,vn,x)
+        name="attend_backward")(lo,hi,go,ot,lse,qt,ka,kt,vn,x)
 
 
 def ranges(seg,BQ,BK):
@@ -544,24 +543,30 @@
     )(x, cot, ctx0, ctx1, vectors, inner_bias, near)
 
 
-def early_back_body(w_ref, b0_ref, b1_ref, acc_ref):
-    width = b0_ref.shape[1]
+def head_columns(weights, own, head):
+    return [weights[:, kind * own + head * HD : kind * own + (head + 1) * HD] for kind in range(3)]
+
+
+def early_back_body(own, w_ref, b0_ref, b1_ref, acc_ref):
     acc_ref[...] = jnp.zeros(acc_ref.shape, jnp.float32)
 
     def add(t, _):
         both = jnp.concatenate([b0_ref[t], b1_ref[t]], axis=0)
-        acc_ref[...] += dot(w_ref[t, :, : 2 * width], both)
+        weights = w_ref[t]
+        weights = jnp.concatenate(head_columns(weights, own, 0) + head_columns(weights, own, 1), axis=1)
+        acc_ref[...] += dot(weights, both)
         return 0
 
     lax.fori_loop(0, b0_ref.shape[0], add, 0)
 
 
-def late_back_body(cut, part_ref, w_ref, acc_ref, grad_ref, *rest):
+def late_back_body(own, head, part_ref, w_ref, acc_ref, grad_ref, *rest):
     backs, out_ref = rest[:-1], rest[-1]
     parts = len(backs)
     total = acc_ref[...]
     for d in range(parts):
-        total = total + dot(w_ref[(part_ref[0] + parts - d) % parts, :, cut : cut + backs[d].shape[0]], backs[d][...])
+        weights = w_ref[(part_ref[0] + parts - d) % parts]
+        total = total + dot(jnp.concatenate(head_columns(weights, own, head), axis=1), backs[d][...])
     out_ref[...] = (total.T + grad_ref[...]).astype(out_ref.dtype)
 
 
@@ -573,12 +578,12 @@
     return pl.BlockSpec(a.shape, lambda i, *_: (0,) * a.ndim, pipeline_mode=pl.Buffered(1))
 
 
-def early_back(rest, cols, b0, b1):
+def early_back(rest, own, b0, b1):
     width, rows = rest.shape[1], b0.shape[2]
     return pl.pallas_call(
-        early_back_body,
+        functools.partial(early_back_body, own),
         grid=(1,),
-        in_specs=[weight_block(rest, cols), whole(b0), whole(b1)],
+        in_specs=[weight_block(rest, 4 * own), whole(b0), whole(b1)],
         out_specs=pl.BlockSpec((width, rows), lambda i: (0, 0)),
         out_shape=jax.ShapeDtypeStruct((width, rows), jnp.float32),
         compiler_params=pltpu.CompilerParams(vmem_limit_bytes=62 << 20),
@@ -587,14 +592,14 @@
     )(rest, b0, b1)
 
 
-def late_back(rest, cols, cut, part, acc, grad, backs):
+def late_back(rest, own, head, part, acc, grad, backs):
     rows, width = grad.shape
     return pl.pallas_call(
-        functools.partial(late_back_body, cut),
+        functools.partial(late_back_body, own, head),
         grid_spec=pltpu.PrefetchScalarGridSpec(
             num_scalar_prefetch=1,
             grid=(1,),
-            in_specs=[weight_block(rest, cols), whole(acc), whole(grad)] + [whole(b) for b in backs],
+            in_specs=[weight_block(rest, 4 * own), whole(acc), whole(grad)] + [whole(b) for b in backs],
             out_specs=pl.BlockSpec((rows, width), lambda i, *_: (0, 0)),
         ),
         out_shape=jax.ShapeDtypeStruct((rows, width), jnp.bfloat16),
@@ -640,22 +645,19 @@
     rank = lax.axis_index("tensor")
     own = query_weight.shape[1]
     heads = own // HD
-    three = 3 * HD
     units = inner_weight.shape[1]
-    by_head = lambda q, k, v: jnp.stack([a.reshape(a.shape[:-1] + (heads, HD)) for a in (q, k, v)], -2).reshape(q.shape[:-1] + (3 * own,))
     x_own = hidden_in[0]
-    qkv_own = by_head(query_weight, key_weight, value_weight)
     small = jnp.concatenate([segments[0].astype(f32), inner_bias]).reshape(-1, 128)
-    near_own = jnp.concatenate([qkv_own, mixer_weight.T, inner_weight, outer_weight.T], 1)
+    near_own = jnp.concatenate([query_weight, key_weight, value_weight, mixer_weight.T, inner_weight, outer_weight.T], 1)
     x_parts, near, small = start(x_own, near_own, small)
     x_all = x_parts.reshape(parts * rows, width)
     near = near.reshape(parts, width, 4 * own + 2 * units)
     small = small.reshape(parts, -1)
     segment_all = small[:, :rows].astype(jnp.int32).reshape(-1)
     inner_bias_all = small[:, rows:]
-    biases = by_head(query_bias, jnp.zeros_like(query_bias), value_bias)
-
-    qt, ka, vt, qn, kt, vn = project(x_all, near, rank, biases, segment_all)
+    biases = jnp.concatenate([query_bias, jnp.zeros_like(query_bias), value_bias])
+
+    qt, ka, vt, kt, vn = project(x_all, near, rank, biases, segment_all)
     lead = heads - 1
     context_t, lse, exchanged = [], [], []
     for call, (first, count, block) in enumerate(((0, lead, rows // 2), (lead, 1, rows))):
@@ -697,7 +699,7 @@
     for h in range(heads):
         call = 0 if h < lead else 1
         grads, weight_part, sums = attend_backward(
-            h, 1, go1 if h else go0, h - 1 if h else 0, context_t[call], lse[call], h - call * lead, qt, ka, qn, kt, vn, x_parts, lo, hi
+            h, 1, go1 if h else go0, h - 1 if h else 0, context_t[call], lse[call], h - call * lead, qt, ka, kt, vn, x_parts, lo, hi
         )
         if h < heads - 1:
             backs.append(lax.all_to_all(grads, "tensor", 0, 0, tiled=True))
@@ -705,31 +707,31 @@
             backs.append(rotate(grads, "tensor"))
         qkv_grad.append(weight_part)
         bias_grad.append(sums[:, 0])
-    input_back = early_back(near, 4 * own, backs[0], backs[1])
-    input_grad = late_back(near, 4 * own, 2 * three, rank, input_back, grad_attn, backs[2])
+    input_back = early_back(near, own, backs[0], backs[1])
+    input_grad = late_back(near, own, heads - 1, rank, input_back, grad_attn, backs[2])
     each = width // groups
-    bias_grad = jnp.stack(two_halves(jnp.concatenate(bias_grad)))
+    by_kind = lambda per_head: [a[..., n * HD : (n + 1) * HD] for n in range(3) for a in per_head]
+    bias_grad = jnp.stack(two_halves(jnp.concatenate(by_kind(bias_grad))))
     extra = jnp.concatenate([early, bias_grad], 0)
     spare = -extra.shape[0] % 16
     extra = jnp.pad(extra, ((0, spare), (0, 0)))
     extra = jnp.broadcast_to(extra[None], (groups,) + extra.shape)
-    qkv_grad = jnp.concatenate(qkv_grad, 1).reshape(groups, each, 3 * own)
+    qkv_grad = jnp.concatenate(by_kind(qkv_grad), 1).reshape(groups, each, 3 * own)
     qkv_grad = jnp.concatenate([qkv_grad, extra], 1)
     qkv_grad = lax.all_to_all(qkv_grad, "dp", 0, 0, tiled=True)
     qkv_grad = jnp.sum(qkv_grad.astype(f32), 0)
     early = qkv_grad[each : each + lines] + qkv_grad[each + lines : each + 2 * lines]
     early = early.reshape(-1)[: count * width].reshape(count, width)
     bias_grad = qkv_grad[each + 2 * lines] + qkv_grad[each + 2 * lines + 1]
-    pick = lambda a, n: a.reshape(a.shape[:-1] + (heads, 3, HD))[..., n, :].reshape(a.shape[:-1] + (own,))
     inner_bias_out = lax.dynamic_index_in_dim(early, 6 + rank, 0, keepdims=False)
     return (
         layer_out[None],
         input_grad[None],
-        pick(qkv_grad[:each], 0),
-        pick(qkv_grad[:each], 1),
-        pick(qkv_grad[:each], 2),
-        pick(bias_grad, 0),
-        pick(bias_grad, 2),
+        qkv_grad[:each, 0 * own : 1 * own],
+        qkv_grad[:each, 1 * own : 2 * own],
+        qkv_grad[:each, 2 * own : 3 * own],
+        bias_grad[:own],
+        bias_grad[2 * own :],
         weight_grads[:, 2 * units :].T,
         early[0],
         early[1],

time: 540 us -> 524 us (0.970)
  waiting for transfers between devices: 90.1 us -> 73.7 us
    all_to_all x1, waiting for transfers between devices: 12.1 us -> 0.75 us  [body(): go0 = lax.all_to_all(go0, 'tensor', 0, 0, tiled=True)]
    unnamed x64 -> x45, local copies, waits for them, and re-layouts: 10.8 us -> 8.49 us
  transfers between devices with their start and end apart: 15 -> 15, of which waited for: 5 -> 5; matrix products, arithmetic and copies ran while one was open for 3% -> 4% of each run, Pallas kernels for 22% -> 22%
where the time goes in v8:
time: 524 us; the launch traced here: 522 us
  Pallas kernels  328 us (63%)
  waiting for transfers between devices  73.7 us (14%)
  starting transfers between devices  51.8 us (10%)
  local copies, waits for them, and re-layouts  27.4 us (5%)
  blocking collectives  19.1 us (4%)
  between operations  14.5 us (3%)
  other arithmetic  6.93 us (1%)
    pallas_call x1, Pallas kernels, start(): pl.pallas_call(functools.partial(start_body, n, bits), in_specs=[pl.Block...  115 us
    pallas_call x3, Pallas kernels, attend_backward(): pl.pallas_call(functools.partial(backward_body, BQ, BK), grid_spec=pltpu....  81.7 us
    all_to_all x2, waiting for transfers between devices, body(): backs.append(lax.all_to_all(grads, 'tensor', 0, 0, tiled=True))  58.6 us
    pallas_call x2, Pallas kernels, attend_forward(): pl.pallas_call(functools.partial(forward_body, BK), grid_spec=pltpu.Prefe...  49 us
    pallas_call x1, Pallas kernels, dense(): pl.pallas_call(functools.partial(dense_body, own), grid=(rows // block,),...  42.3 us
    all_to_all x2, starting transfers between devices, body(): backs.append(lax.all_to_all(grads, 'tensor', 0, 0, tiled=True))  19.3 us
    all_to_all x1, blocking collectives, body(): qkv_grad = lax.all_to_all(qkv_grad, 'dp', 0, 0, tiled=True)  19.1 us
    pallas_call x1, Pallas kernels, weight_grads_of(): pl.pallas_call(functools.partial(weight_grads_body, steps // 2), grid=(st...  16.5 us
  transfers between devices with their start and end apart: 15, of which 5 were waited for; matrix products, arithmetic and copies ran while one was open for 4% of the time, Pallas kernels for 22%

profile of v8, /device:TPU:0, one launch (start us, length us, event | category | flops | bytes accessed | tf_op | source)
XLA Modules:
  0.0 521.9 jit_solution(7913934234540614005)
XLA Ops:
  7.2 0.7 convert_reduce_fusion.5
  7.9 0.9 copy.99
  8.8 1.3 pad_maximum_fusion.2.s_ref
  10.1 2.0 concatenate.62.w_ref
  12.1 114.7 %start.1 = (bf16[4,768,768]{2,1,0:T(8,128)(2,1)}, bf16[4,8,96,2304]{3,2,1,0:T(8,128)(2,1)}, f32[4,12,128]{2,1,0:T(8,128)}) custom-call(bf16[768,768]{1,0:T(8,128)(2,1)} %bitcast.67, bf16[96,2304]{1,0:T(8,128)(2,1)} %concatenate.62.w_ref, f32[12,128]{1,0:T(8,128)} %pad_maximum_fusion.2.s_ref), custom_call_target="tpu_custom_call" | custom-call | bytes 209715200 | tf_op jit(solution)/shard_map/start/pallas_call | solution.py:359
  126.7 0.8 copy.124
  128.3 0.6 copy.120
  129.4 0.7 convert_reduce_fusion.3
  130.1 9.9 %project.1 = (bf16[3,128,3072]{2,1,0:T(8,128)(2,1)}, bf16[3,3072,128]{2,1,0:T(8,128)(2,1)}, bf16[3,64,3072]{2,1,0:T(8,128)(2,1)}, bf16[3,64,3072]{2,1,0:T(8,128)(2,1)}, bf16[3,3072,64]{2,1,0:T(8,128)(2,1)}) custom-call(s32[1]{0:T(128)} %bitcast.7.part_ref, bf16[3072,768]{1,0:T(8,128)(2,1)} %bitcast.64, bf16[4,768,2304]{2,1,0:T(8,128)(2,1)} %bitcast.59, ...), custom_call_target="tpu_custom_call" | custom-call | flops 2717908992 | bytes 17694720 | tf_op jit(solution)/shard_map/project/pallas_call | solution.py:47
  140.0 30.1 %attend_forward.3 = (bf16[4,128,768]{2,1,0:T(8,128)(2,1)}, f32[2,64,3072]{2,1,0:T(8,128)}, f32[2,1,3072]{2,1,0:T(1,128)}) custom-call(s32[8]{0:T(128)} %get-tuple-element.262.lo_ref, s32[8]{0:T(128)} %get-tuple-element.261.hi_ref, bf16[3,128,3072]{2,1,0:T(8,128)(2,1)} %get-tuple-element.55.qt_ref, bf16[3,3072,128]{2,1,0:T(8,128)(2,1)} %get-tuple-element.56.ka_ref, ...), custom_call_target="tpu_custom_call" | custom-call | flops 4831838208 | bytes 6291456 | tf_op jit(solution)/shard_map/attend_forward/pallas_call | solution.py:104
  170.0 3.5 all-to-all-start
  173.7 0.7 convert_reduce_fusion.6
  174.5 18.9 %attend_forward.2 = (bf16[4,64,768]{2,1,0:T(8,128)(2,1)}, f32[1,64,3072]{2,1,0:T(8,128)}, f32[1,1,3072]{2,1,0:T(1,128)}) custom-call(s32[4]{0:T(128)} %get-tuple-element.260.lo_ref, s32[4]{0:T(128)} %get-tuple-element.259.hi_ref, bf16[3,128,3072]{2,1,0:T(8,128)(2,1)} %get-tuple-element.55.qt_ref, bf16[3,3072,128]{2,1,0:T(8,128)(2,1)} %get-tuple-element.56.ka_ref, ...), custom_call_target="tpu_custom_call" | custom-call | flops 2415919104 | bytes 3145728 | tf_op jit(solution)/shard_map/attend_forward/pallas_call | solution.py:104
  193.4 5.1 all-to-all-start.1
  198.7 0.6 pad.12.vec_ref
  199.3 0.6 reshape.439.bias_ref
  199.9 7.5 %all-to-all-done.1.ctx1_ref = bf16[4,64,768]{2,1,0:T(8,128)(2,1)S(1)} async-done(((bf16[4,64,768]{2,1,0:T(8,128)(2,1)}), bf16[4,64,768]{2,1,0:T(8,128)(2,1)S(1)}, u32[]{:S(2)}, u32[]{:S(2)}) %all-to-all-start.1) | async-done | bytes 393248 | tf_op jit(solution)/shard_map/all_to_all | solution.py:670
  207.4 0.7 copy-done.6
  208.1 42.3 %dense.1 = (bf16[768,768]{1,0:T(8,128)(2,1)}, bf16[768,768]{1,0:T(8,128)(2,1)}, bf16[768,768]{1,0:T(8,128)(2,1)}, bf16[768,768]{1,0:T(8,128)(2,1)}, f32[768,768]...) custom-call(bf16[768,768]{1,0:T(8,128)(2,1)} %bitcast.68, ...), custom_call_target="tpu_custom_call" | custom-call | flops 16307453952 | bytes 41943040 | tf_op jit(solution)/shard_map/dense/pallas_call | solution.py:533
  250.4 16.5 %weight_grads.1 = bf16[768,6912]{1,0:T(8,128)(2,1)} custom-call(bf16[768,768]{1,0:T(8,128)(2,1)} %get-tuple-element.82.first_ref, bf16[768,768]{1,0:T(8,128)(2,1)} %get-tuple-element.83.second_ref, bf16[768,768]{1,0:T(8,128)(2,1)} %get-tuple-element.84.attn_ref, bf16[8,768,768]{2,1,0:T(8,128)(2,1)} %get-tuple-element.85.both_ref, ...), custom_call_target="tpu_custom_call" | custom-call | flops 8153726976 | bytes 18874368 | tf_op jit(solution)/shard_map/weight_grads/pallas_call | solution.py:403
  266.9 3.5 all-to-all-start.2
  270.5 2.0 collective-permute-start.3
  272.4 6.8 %collective-permute-done.3 = f32[10,768]{1,0:T(8,128)S(1)} collective-permute-done((f32[10,768]{1,0:T(8,128)S(1)}, f32[10,768]{1,0:T(8,128)S(1)}, u32[]{:S(2)}, u32[]{:S(2)}) %collective-permute-start.3) | collective-permute-done | bytes 30752 | tf_op jit(solution)/shard_map/ppermute | solution.py:616
  279.2 4.8 collective-permute-start.4
  284.0 0.8 all-to-all-done.2.go_ref
  284.8 3.7 all-to-all-start.4
  288.5 0.7 convert_reduce_fusion.1
  289.4 27.6 %attend_backward.3 = (bf16[4,192,768]{2,1,0:T(8,128)(2,1)}, bf16[768,192]{1,0:T(8,128)(2,1)}, f32[192,128]{1,0:T(8,128)}) custom-call(s32[6]{0:T(128)} %get-tuple-element.220.lo_ref, s32[6]{0:T(128)} %get-tuple-element.219.hi_ref, bf16[4,64,768]{2,1,0:T(8,128)(2,1)} %copy-done.5, f32[2,64,3072]{2,1,0:T(8,128)} %get-tuple-element.64.ot_ref, ...), custom_call_target="tpu_custom_call" | custom-call | flops 6039797760 | bytes 5505024 | tf_op jit(solution)/shard_map/attend_backward/pallas_call | solution.py:176
  317.0 0.9 slice_reduce_fusion.4
  317.9 1.2 fusion.5
  319.2 0.9 copy-done.3
  320.1 27.0 %attend_backward.5 = (bf16[4,192,768]{2,1,0:T(8,128)(2,1)}, bf16[768,192]{1,0:T(8,128)(2,1)}, f32[192,128]{1,0:T(8,128)}) custom-call(s32[6]{0:T(128)} %get-tuple-element.220.lo_ref, s32[6]{0:T(128)} %get-tuple-element.219.hi_ref, bf16[4,128,768]{2,1,0:T(8,128)(2,1)} %copy-done.3, f32[1,64,3072]{2,1,0:T(8,128)} %get-tuple-element.72.ot_ref, ...), custom_call_target="tpu_custom_call" | custom-call | flops 6039797760 | bytes 5505024 | tf_op jit(solution)/shard_map/attend_backward/pallas_call | solution.py:176
  347.1 0.9 slice_reduce_fusion.2
  348.0 27.1 %attend_backward.4 = (bf16[4,192,768]{2,1,0:T(8,128)(2,1)}, bf16[768,192]{1,0:T(8,128)(2,1)}, f32[192,128]{1,0:T(8,128)}) custom-call(s32[6]{0:T(128)} %get-tuple-element.220.lo_ref, s32[6]{0:T(128)} %get-tuple-element.219.hi_ref, bf16[4,128,768]{2,1,0:T(8,128)(2,1)} %copy-done.3, f32[2,64,3072]{2,1,0:T(8,128)} %get-tuple-element.64.ot_ref, ...), custom_call_target="tpu_custom_call" | custom-call | flops 6039797760 | bytes 5505024 | tf_op jit(solution)/shard_map/attend_backward/pallas_call | solution.py:176
  375.2 1.0 slice_reduce_fusion.3
  376.7 0.7 concatenate.66
  377.5 0.7 copy.105
  378.4 0.7 pad_maximum_fusion
  379.1 19.1 %all_to_all.35 = bf16[8,128,576]{1,2,0:T(8,128)(2,1)S(1)} all-to-all(bf16[8,128,576]{1,2,0:T(8,128)(2,1)S(1)} %pad_maximum_fusion), channel_id=1, replica_groups=mesh['dp'=8,'tensor'=4] {'dp'}, dimensions={0} | all-to-all | bytes 2359296 | tf_op jit(solution)/shard_map/all_to_all | solution.py:721
  398.2 4.9 all-to-all-start.3
  403.1 2.2 dynamic-slice_bitcast_fusion.3
  405.2 3.8 collective-permute-start.2
  409.1 1.1 collective-permute-start
  410.8 23.2 %all-to-all-done.3.b0_ref = bf16[4,192,768]{2,1,0:T(8,128)(2,1)S(1)} async-done(((bf16[4,192,768]{2,1,0:T(8,128)(2,1)}), bf16[4,192,768]{2,1,0:T(8,128)(2,1)S(1)}, u32[]{:S(2)}, u32[]{:S(2)}) %all-to-all-start.3) | async-done | bytes 1179680 | tf_op jit(solution)/shard_map/all_to_all | solution.py:705
  434.0 1.0 copy-done
  435.0 14.4 %all-to-all-start.5 = ((bf16[4,192,768]{2,1,0:T(8,128)(2,1)}), bf16[4,192,768]{2,1,0:T(8,128)(2,1)}, u32[]{:S(2)}, u32[]{:S(2)}) async-start(bf16[4,192,768]{2,1,0:T(8,128)(2,1)} %get-tuple-element.70), calls=%async_computation.5 | async-start | bytes 2359296 | tf_op jit(solution)/shard_map/all_to_all | solution.py:705
  449.5 0.7 copy.111
  450.2 0.7 copy.110
  450.9 0.7 copy.109
  451.7 0.6 dynamic-slice_reduce_fusion
  452.3 0.6 fusion.7
  453.1 0.9 slice.255
  454.3 1.3 slice-done
  455.7 0.9 dynamic-slice_bitcast_fusion.2
  456.6 2.0 collective-permute-start.5
  458.6 1.8 collective-permute-start.7
  460.4 1.1 collective-permute-start.6
  461.6 0.7 slice_reduce_fusion
  462.3 35.5 %all-to-all-done.5.b1_ref = bf16[4,192,768]{2,1,0:T(8,128)(2,1)} async-done(((bf16[4,192,768]{2,1,0:T(8,128)(2,1)}), bf16[4,192,768]{2,1,0:T(8,128)(2,1)}, u32[]{:S(2)}, u32[]{:S(2)}) %all-to-all-start.5) | async-done | bytes 1179680 | tf_op jit(solution)/shard_map/all_to_all | solution.py:705
  497.7 7.7 %early_back.1.acc_ref = f32[768,768]{1,0:T(8,128)} custom-call(bf16[4,768,2304]{2,1,0:T(8,128)(2,1)} %bitcast.61, bf16[4,192,768]{2,1,0:T(8,128)(2,1)} %copy-done, bf16[4,192,768]{2,1,0:T(8,128)(2,1)} %all-to-all-done.5.b1_ref), custom_call_target="tpu_custom_call" | custom-call | flops 1811939328 | bytes 10485760 | tf_op jit(solution)/shard_map/early_back/pallas_call | solution.py:583
  505.4 6.7 %late_back.1 = bf16[768,768]{1,0:T(8,128)(2,1)} custom-call(s32[1]{0:T(128)} %bitcast.7.part_ref, bf16[4,768,2304]{2,1,0:T(8,128)(2,1)} %bitcast.62, f32[768,768]{1,0:T(8,128)} %early_back.1.acc_ref, f32[768,768]{1,0:T(8,128)} %get-tuple-element.71.grad_ref, bf16[192,768]{1,0:T(8,128)(2,1)} %get-tuple-element.229.rest_0_, ...), custom_call_target="tpu_custom_call" | custom-call | flops 905969664 | bytes 10485760 | tf_op jit(solution)/shard_map/late_back/pallas_call | solution.py:597
  512.1 1.4 fusion.1
  513.5 0.9 slice_bitcast_fusion
  514.3 0.7 copy.112
  (88 shorter events, 3.6 us)
Async XLA Ops:
  10.1 117.5 %copy-start.14 = (f32[192]{0:T(256)S(1)}, f32[192]{0:T(256)}, u32[]{:S(2)}) copy-start(f32[192]{0:T(256)} %param.24) | copy-start | bytes 2308
  10.1 117.5 %copy-start.15 = (f32[192]{0:T(256)S(1)}, f32[192]{0:T(256)}, u32[]{:S(2)}) copy-start(f32[192]{0:T(256)} %param.23) | copy-start | bytes 2308
  170.0 23.4 %all-to-all-start = ((bf16[4,128,768]{2,1,0:T(8,128)(2,1)}), bf16[4,128,768]{2,1,0:T(8,128)(2,1)S(1)}, u32[]{:S(2)}, u32[]{:S(2)}) async-start(bf16[4,128,768]{2,1,0:T(8,128)(2,1)} %get-tuple-element.59), calls=%async_computation | async-start | bytes 1572864 | tf_op jit(solution)/shard_map/all_to_all | solution.py:670
  174.5 24.0 %copy-start.8 = (f32[768]{0:T(1024)S(1)}, f32[768]{0:T(1024)}, u32[]{:S(2)}) copy-start(f32[768]{0:T(1024)} %param.26) | copy-start | bytes 9220
  174.5 24.0 %copy-start.9 = (f32[768]{0:T(1024)S(1)}, f32[768]{0:T(1024)}, u32[]{:S(2)}) copy-start(f32[768]{0:T(1024)} %param.27) | copy-start | bytes 9220
  174.5 24.1 %copy-start.10 = (f32[768]{0:T(1024)S(1)}, f32[768]{0:T(1024)}, u32[]{:S(2)}) copy-start(f32[768]{0:T(1024)} %param.28) | copy-start | bytes 9220
  174.5 24.1 %copy-start.11 = (f32[768]{0:T(1024)S(1)}, f32[768]{0:T(1024)}, u32[]{:S(2)}) copy-start(f32[768]{0:T(1024)} %param.32) | copy-start | bytes 9220
  174.5 24.1 %copy-start.12 = (f32[768]{0:T(1024)S(1)}, f32[768]{0:T(1024)}, u32[]{:S(2)}) copy-start(f32[768]{0:T(1024)} %param.33) | copy-start | bytes 9220
  174.5 24.1 %copy-start.13 = (f32[768]{0:T(1024)S(1)}, f32[768]{0:T(1024)}, u32[]{:S(2)}) copy-start(f32[768]{0:T(1024)} %param.34) | copy-start | bytes 9220
  193.4 14.0 %copy-start.4 = (bf16[4,128,768]{2,1,0:T(8,128)(2,1)}, bf16[4,128,768]{2,1,0:T(8,128)(2,1)S(1)}, u32[]{:S(2)}) copy-start(bf16[4,128,768]{2,1,0:T(8,128)(2,1)S(1)} %all-to-all-done.ctx0_ref) | copy-start | bytes 2359300
  193.4 14.0 %all-to-all-start.1 = ((bf16[4,64,768]{2,1,0:T(8,128)(2,1)}), bf16[4,64,768]{2,1,0:T(8,128)(2,1)S(1)}, u32[]{:S(2)}, u32[]{:S(2)}) async-start(bf16[4,64,768]{2,1,0:T(8,128)(2,1)} %get-tuple-element.61), calls=%async_computation.1 | async-start | bytes 786432 | tf_op jit(solution)/shard_map/all_to_all | solution.py:670
  198.5 254.7 %reduce-scatter.2.cloned.1.call-start = ((), (), s32[]{:S(2)}) async-start(), calls=%async_computation.8 | async-start | bytes 11943936 | tf_op jit(solution)/shard_map/reduce_scatter | solution.py:681
  207.4 0.7 copy-start.6
  266.9 3.6 copy-start.7
  266.9 17.9 %all-to-all-start.2 = ((bf16[4,64,768]{2,1,0:T(8,128)(2,1)}), bf16[4,64,768]{2,1,0:T(8,128)(2,1)S(1)}, u32[]{:S(2)}, u32[]{:S(2)}) async-start(bf16[4,64,768]{2,1,0:T(8,128)(2,1)} %get-tuple-element.63), calls=%async_computation.2 | async-start | bytes 786432 | tf_op jit(solution)/shard_map/all_to_all | solution.py:676
  270.5 8.7 %collective-permute-start.3 = (f32[10,768]{1,0:T(8,128)S(1)}, f32[10,768]{1,0:T(8,128)S(1)}, u32[]{:S(2)}, u32[]{:S(2)}) collective-permute-start(f32[10,768]{1,0:T(8,128)S(1)} %bitcast.73), channel_id=1, source_target_pairs={{0,1},{1,0},{2,3},{3,2},{4,5},{5,4},{6,7},{7,6},{8,9},{9,8},{10,11... | collective-permute-start | bytes 92168 | tf_op jit(solution)/shard_map/ppermute | solution.py:616
  279.2 10.0 %collective-permute-start.4 = (f32[10,768]{1,0:T(8,128)S(1)}, f32[10,768]{1,0:T(8,128)S(1)}, u32[]{:S(2)}, u32[]{:S(2)}) collective-permute-start(f32[10,768]{1,0:T(8,128)S(1)} %slice_add_fusion.2), channel_id=1, source_target_pairs={{0,2},{1,3},{2,0},{3,1},{4,6},{5,7},{6,4},{7,5},{8,10},{9,11},{10,... | collective-permute-start | bytes 92168 | tf_op jit(solution)/shard_map/ppermute | solution.py:616
  284.8 4.6 copy-start.5
  284.8 34.4 %all-to-all-start.4 = ((bf16[4,128,768]{2,1,0:T(8,128)(2,1)}), bf16[4,128,768]{2,1,0:T(8,128)(2,1)S(1)}, u32[]{:S(2)}, u32[]{:S(2)}) async-start(bf16[4,128,768]{2,1,0:T(8,128)(2,1)} %get-tuple-element.69), calls=%async_computation.4 | async-start | bytes 1572864 | tf_op jit(solution)/shard_map/all_to_all | solution.py:677
  319.2 0.9 copy-start.3
  348.0 28.4 %copy-start.1 = (bf16[768,192]{1,0:T(8,128)(2,1)S(1)}, bf16[768,192]{1,0:T(8,128)(2,1)}, u32[]{:S(2)}) copy-start(bf16[768,192]{1,0:T(8,128)(2,1)} %get-tuple-element.77) | copy-start | bytes 884740
  375.1 1.4 copy-start.2
  398.2 35.8 %all-to-all-start.3 = ((bf16[4,192,768]{2,1,0:T(8,128)(2,1)}), bf16[4,192,768]{2,1,0:T(8,128)(2,1)S(1)}, u32[]{:S(2)}, u32[]{:S(2)}) async-start(bf16[4,192,768]{2,1,0:T(8,128)(2,1)} %get-tuple-element.68), calls=%async_computation.3 | async-start | bytes 2359296 | tf_op jit(solution)/shard_map/all_to_all | solution.py:705
  405.2 55.2 %collective-permute-start.2 = (bf16[192,768]{1,0:T(8,128)(2,1)}, bf16[192,768]{1,0:T(8,128)(2,1)}, u32[]{:S(2)}, u32[]{:S(2)}) collective-permute-start(bf16[192,768]{1,0:T(8,128)(2,1)} %get-tuple-element.226), channel_id=1, source_target_pairs={{0,3},{1,0},{2,1},{3,2},{4,7},{5,4},{6,5},{7,6},{8,11},{9,8},{10,9... | collective-permute-start | bytes 884744 | tf_op jit(solution)/shard_map/ppermute | solution.py:635
  409.0 96.3 %collective-permute-start.1 = (bf16[192,768]{1,0:T(8,128)(2,1)}, bf16[192,768]{1,0:T(8,128)(2,1)}, u32[]{:S(2)}, u32[]{:S(2)}) collective-permute-start(bf16[192,768]{1,0:T(8,128)(2,1)} %get-tuple-element.227), channel_id=1, source_target_pairs={{0,2},{1,3},{2,0},{3,1},{4,6},{5,7},{6,4},{7,5},{8,10},{9,11},{10,... | collective-permute-start | bytes 884744 | tf_op jit(solution)/shard_map/ppermute | solution.py:635
  409.1 96.3 %collective-permute-start = (bf16[192,768]{1,0:T(8,128)(2,1)S(1)}, bf16[192,768]{1,0:T(8,128)(2,1)}, u32[]{:S(2)}, u32[]{:S(2)}) collective-permute-start(bf16[192,768]{1,0:T(8,128)(2,1)S(1)} %get-tuple-element.228), channel_id=1, source_target_pairs={{0,1},{1,2},{2,3},{3,0},{4,5},{5,6},{6,7},{7,4},{8,9},{9,10},{10,1... | collective-permute-start | bytes 884744 | tf_op jit(solution)/shard_map/ppermute | solution.py:635
  434.0 1.0 copy-start
  435.0 62.7 %all-to-all-start.5 = ((bf16[4,192,768]{2,1,0:T(8,128)(2,1)}), bf16[4,192,768]{2,1,0:T(8,128)(2,1)}, u32[]{:S(2)}, u32[]{:S(2)}) async-start(bf16[4,192,768]{2,1,0:T(8,128)(2,1)} %get-tuple-element.70), calls=%async_computation.5 | async-start | bytes 2359296 | tf_op jit(solution)/shard_map/all_to_all | solution.py:705
  454.3 1.3 slice-start
  456.6 55.5 %collective-permute-start.5 = (bf16[96,1728]{1,0:T(8,128)(2,1)}, bf16[96,1728]{1,0:T(8,128)(2,1)}, u32[]{:S(2)}, u32[]{:S(2)}) collective-permute-start(bf16[96,1728]{1,0:T(8,128)(2,1)} %get-tuple-element.223), channel_id=1, source_target_pairs={{0,1},{1,2},{2,3},{3,0},{4,5},{5,6},{6,7},{7,4},{8,9},{9,10},{10,1... | collective-permute-start | bytes 995336 | tf_op jit(solution)/shard_map/ppermute | solution.py:635
  458.6 53.5 %collective-permute-start.7 = (bf16[96,1728]{1,0:T(8,128)(2,1)}, bf16[96,1728]{1,0:T(8,128)(2,1)}, u32[]{:S(2)}, u32[]{:S(2)}) collective-permute-start(bf16[96,1728]{1,0:T(8,128)(2,1)} %get-tuple-element.224), channel_id=1, source_target_pairs={{0,3},{1,0},{2,1},{3,2},{4,7},{5,4},{6,5},{7,6},{8,11},{9,8},{10,9... | collective-permute-start | bytes 995336 | tf_op jit(solution)/shard_map/ppermute | solution.py:635
  460.4 51.7 %collective-permute-start.6 = (bf16[96,1728]{1,0:T(8,128)(2,1)S(1)}, bf16[96,1728]{1,0:T(8,128)(2,1)}, u32[]{:S(2)}, u32[]{:S(2)}) collective-permute-start(bf16[96,1728]{1,0:T(8,128)(2,1)S(1)} %get-tuple-element.225), channel_id=1, source_target_pairs={{0,2},{1,3},{2,0},{3,1},{4,6},{5,7},{6,4},{7,5},{8,10},{9,11},{10,... | collective-permute-start | bytes 995336 | tf_op jit(solution)/shard_map/ppermute | solution.py:635
Sparse Core Ops, SparseCore 0:
  267.0 79.8 reduce-scatter.1

commit v9 on v8

--- a/solution.py
+++ b/solution.py
@@ -607,6 +607,29 @@
         cost_estimate=pl.CostEstimate(flops=2 * width * rows * backs[0].shape[0] * len(backs), bytes_accessed=10 << 20, transcendentals=0),
         name="late_back",
     )(part.reshape(1), rest, acc, grad, *backs)
+
+
+def finish_body(units, *refs):
+    inner_ref, outer_ref, mixer_ref = refs[-3:]
+    total = sum(a[...].astype(jnp.float32) for a in refs[:-3])
+    inner_ref[...] = total[:, :units]
+    outer_ref[...] = total[:, units : 2 * units].T
+    mixer_ref[...] = total[:, 2 * units :].T
+
+
+def finish(shares, units):
+    each, cols = shares[0].shape
+    own = cols - 2 * units
+    shapes = ((each, units), (units, each), (own, each))
+    return pl.pallas_call(
+        functools.partial(finish_body, units),
+        grid=(1,),
+        in_specs=[whole(a) for a in shares],
+        out_specs=[pl.BlockSpec(a, lambda i: (0, 0)) for a in shapes],
+        out_shape=[jax.ShapeDtypeStruct(a, jnp.float32) for a in shapes],
+        compiler_params=pltpu.CompilerParams(vmem_limit_bytes=62 << 20),
+        name="finish",
+    )(*shares)
 
 
 def add_up(value, axis):
@@ -687,7 +710,7 @@
         2,
     ).transpose(1, 0, 2)
     weight_grads = rotate(weight_grads, "tensor")
-    weight_grads = sum(a.astype(f32) for a in weight_grads)
+    inner_grad, outer_grad, mixer_grad = finish(weight_grads, units)
     early = add_up(early[: 6 + parts], "tensor")
     count = 6 + parts
     lines = -(-count * width // (3 * own))
@@ -732,13 +755,13 @@
         qkv_grad[:each, 2 * own : 3 * own],
         bias_grad[:own],
         bias_grad[2 * own :],
-        weight_grads[:, 2 * units :].T,
+        mixer_grad,
         early[0],
         early[1],
         early[2],
-        weight_grads[:, :units],
+        inner_grad,
         inner_bias_out,
-        weight_grads[:, units : 2 * units].T,
+        outer_grad,
         early[3],
         early[4],
         early[5],

time: 524 us -> 526 us (level)
  no operation moved by 1% of the time
where the time goes in v9:
time: 526 us; the launch traced here: 524 us
  Pallas kernels  331 us (63%)
  waiting for transfers between devices  73.8 us (14%)
  starting transfers between devices  51.9 us (10%)
  local copies, waits for them, and re-layouts  28.4 us (5%)
  blocking collectives  19.1 us (4%)
  between operations  14.5 us (3%)
  other arithmetic  5.58 us (1%)
    pallas_call x1, Pallas kernels, start(): pl.pallas_call(functools.partial(start_body, n, bits), in_specs=[pl.Block...  115 us
    pallas_call x3, Pallas kernels, attend_backward(): pl.pallas_call(functools.partial(backward_body, BQ, BK), grid_spec=pltpu....  81.6 us
    all_to_all x2, waiting for transfers between devices, body(): backs.append(lax.all_to_all(grads, 'tensor', 0, 0, tiled=True))  58.7 us
    pallas_call x2, Pallas kernels, attend_forward(): pl.pallas_call(functools.partial(forward_body, BK), grid_spec=pltpu.Prefe...  49 us
    pallas_call x1, Pallas kernels, dense(): pl.pallas_call(functools.partial(dense_body, own), grid=(rows // block,),...  42.2 us
    all_to_all x2, starting transfers between devices, body(): backs.append(lax.all_to_all(grads, 'tensor', 0, 0, tiled=True))  19.4 us
    all_to_all x1, blocking collectives, body(): qkv_grad = lax.all_to_all(qkv_grad, 'dp', 0, 0, tiled=True)  19.1 us
    pallas_call x1, Pallas kernels, weight_grads_of(): pl.pallas_call(functools.partial(weight_grads_body, steps // 2), grid=(st...  16.5 us
  transfers between devices with their start and end apart: 15, of which 5 were waited for; matrix products, arithmetic and copies ran while one was open for 4% of the time, Pallas kernels for 22%

profile of v9, /device:TPU:0, one launch (start us, length us, event | category | flops | bytes accessed | tf_op | source)
XLA Modules:
  0.0 523.9 jit_solution(12048352658276835131)
XLA Ops:
  7.2 0.7 convert_reduce_fusion.5
  7.9 0.9 copy.99
  8.8 1.3 pad_maximum_fusion.2.s_ref
  10.1 2.0 concatenate.62.w_ref
  12.1 114.7 %start.1 = (bf16[4,768,768]{2,1,0:T(8,128)(2,1)}, bf16[4,8,96,2304]{3,2,1,0:T(8,128)(2,1)}, f32[4,12,128]{2,1,0:T(8,128)}) custom-call(bf16[768,768]{1,0:T(8,128)(2,1)} %bitcast.62, bf16[96,2304]{1,0:T(8,128)(2,1)} %concatenate.62.w_ref, f32[12,128]{1,0:T(8,128)} %pad_maximum_fusion.2.s_ref), custom_call_target="tpu_custom_call" | custom-call | bytes 209715200 | tf_op jit(solution)/shard_map/start/pallas_call | solution.py:359
  126.7 0.8 copy.124
  127.7 0.6 reshape.436.b_ref
  128.3 0.6 copy.120
  129.4 0.7 convert_reduce_fusion.3
  130.1 9.8 %project.1 = (bf16[3,128,3072]{2,1,0:T(8,128)(2,1)}, bf16[3,3072,128]{2,1,0:T(8,128)(2,1)}, bf16[3,64,3072]{2,1,0:T(8,128)(2,1)}, bf16[3,64,3072]{2,1,0:T(8,128)(2,1)}, bf16[3,3072,64]{2,1,0:T(8,128)(2,1)}) custom-call(s32[1]{0:T(128)} %bitcast.7.part_ref, bf16[3072,768]{1,0:T(8,128)(2,1)} %bitcast.59, bf16[4,768,2304]{2,1,0:T(8,128)(2,1)} %bitcast.54, ...), custom_call_target="tpu_custom_call" | custom-call | flops 2717908992 | bytes 17694720 | tf_op jit(solution)/shard_map/project/pallas_call | solution.py:47
  139.9 30.1 %attend_forward.3 = (bf16[4,128,768]{2,1,0:T(8,128)(2,1)}, f32[2,64,3072]{2,1,0:T(8,128)}, f32[2,1,3072]{2,1,0:T(1,128)}) custom-call(s32[8]{0:T(128)} %get-tuple-element.267.lo_ref, s32[8]{0:T(128)} %get-tuple-element.266.hi_ref, bf16[3,128,3072]{2,1,0:T(8,128)(2,1)} %get-tuple-element.58.qt_ref, bf16[3,3072,128]{2,1,0:T(8,128)(2,1)} %get-tuple-element.59.ka_ref, ...), custom_call_target="tpu_custom_call" | custom-call | flops 4831838208 | bytes 6291456 | tf_op jit(solution)/shard_map/attend_forward/pallas_call | solution.py:104
  170.0 3.5 all-to-all-start
  173.7 0.7 convert_reduce_fusion.6
  174.5 18.9 %attend_forward.2 = (bf16[4,64,768]{2,1,0:T(8,128)(2,1)}, f32[1,64,3072]{2,1,0:T(8,128)}, f32[1,1,3072]{2,1,0:T(1,128)}) custom-call(s32[4]{0:T(128)} %get-tuple-element.265.lo_ref, s32[4]{0:T(128)} %get-tuple-element.264.hi_ref, bf16[3,128,3072]{2,1,0:T(8,128)(2,1)} %get-tuple-element.58.qt_ref, bf16[3,3072,128]{2,1,0:T(8,128)(2,1)} %get-tuple-element.59.ka_ref, ...), custom_call_target="tpu_custom_call" | custom-call | flops 2415919104 | bytes 3145728 | tf_op jit(solution)/shard_map/attend_forward/pallas_call | solution.py:104
  193.4 5.1 all-to-all-start.1
  198.6 0.6 pad.12.vec_ref
  199.2 0.6 reshape.437.bias_ref
  199.8 7.5 %all-to-all-done.1.ctx1_ref = bf16[4,64,768]{2,1,0:T(8,128)(2,1)S(1)} async-done(((bf16[4,64,768]{2,1,0:T(8,128)(2,1)}), bf16[4,64,768]{2,1,0:T(8,128)(2,1)S(1)}, u32[]{:S(2)}, u32[]{:S(2)}) %all-to-all-start.1) | async-done | bytes 393248 | tf_op jit(solution)/shard_map/all_to_all | solution.py:693
  207.3 0.7 copy-done.6
  208.1 42.2 %dense.1 = (bf16[768,768]{1,0:T(8,128)(2,1)}, bf16[768,768]{1,0:T(8,128)(2,1)}, bf16[768,768]{1,0:T(8,128)(2,1)}, bf16[768,768]{1,0:T(8,128)(2,1)}, f32[768,768]...) custom-call(bf16[768,768]{1,0:T(8,128)(2,1)} %bitcast.63, ...), custom_call_target="tpu_custom_call" | custom-call | flops 16307453952 | bytes 41943040 | tf_op jit(solution)/shard_map/dense/pallas_call | solution.py:533
  250.3 16.5 %weight_grads.1 = bf16[768,6912]{1,0:T(8,128)(2,1)} custom-call(bf16[768,768]{1,0:T(8,128)(2,1)} %get-tuple-element.85.first_ref, bf16[768,768]{1,0:T(8,128)(2,1)} %get-tuple-element.86.second_ref, bf16[768,768]{1,0:T(8,128)(2,1)} %get-tuple-element.87.attn_ref, bf16[8,768,768]{2,1,0:T(8,128)(2,1)} %get-tuple-element.88.both_ref, ...), custom_call_target="tpu_custom_call" | custom-call | flops 8153726976 | bytes 18874368 | tf_op jit(solution)/shard_map/weight_grads/pallas_call | solution.py:403
  266.8 3.5 all-to-all-start.2
  270.4 2.0 collective-permute-start.3
  272.3 6.8 %collective-permute-done.3 = f32[10,768]{1,0:T(8,128)S(1)} collective-permute-done((f32[10,768]{1,0:T(8,128)S(1)}, f32[10,768]{1,0:T(8,128)S(1)}, u32[]{:S(2)}, u32[]{:S(2)}) %collective-permute-start.3) | collective-permute-done | bytes 30752 | tf_op jit(solution)/shard_map/ppermute | solution.py:639
  279.1 4.8 collective-permute-start.4
  283.9 0.8 all-to-all-done.2.go_ref
  284.7 3.7 all-to-all-start.4
  288.4 0.7 convert_reduce_fusion.1
  289.3 27.6 %attend_backward.3 = (bf16[4,192,768]{2,1,0:T(8,128)(2,1)}, bf16[768,192]{1,0:T(8,128)(2,1)}, f32[192,128]{1,0:T(8,128)}) custom-call(s32[6]{0:T(128)} %get-tuple-element.226.lo_ref, s32[6]{0:T(128)} %get-tuple-element.225.hi_ref, bf16[4,64,768]{2,1,0:T(8,128)(2,1)} %copy-done.5, f32[2,64,3072]{2,1,0:T(8,128)} %get-tuple-element.67.ot_ref, ...), custom_call_target="tpu_custom_call" | custom-call | flops 6039797760 | bytes 5505024 | tf_op jit(solution)/shard_map/attend_backward/pallas_call | solution.py:176
  316.9 0.9 slice_reduce_fusion.4
  317.8 1.2 fusion.3
  319.1 0.9 copy-done.3
  320.0 27.0 %attend_backward.5 = (bf16[4,192,768]{2,1,0:T(8,128)(2,1)}, bf16[768,192]{1,0:T(8,128)(2,1)}, f32[192,128]{1,0:T(8,128)}) custom-call(s32[6]{0:T(128)} %get-tuple-element.226.lo_ref, s32[6]{0:T(128)} %get-tuple-element.225.hi_ref, bf16[4,128,768]{2,1,0:T(8,128)(2,1)} %copy-done.3, f32[1,64,3072]{2,1,0:T(8,128)} %get-tuple-element.75.ot_ref, ...), custom_call_target="tpu_custom_call" | custom-call | flops 6039797760 | bytes 5505024 | tf_op jit(solution)/shard_map/attend_backward/pallas_call | solution.py:176
  346.9 0.9 slice_reduce_fusion.2
  347.9 27.1 %attend_backward.4 = (bf16[4,192,768]{2,1,0:T(8,128)(2,1)}, bf16[768,192]{1,0:T(8,128)(2,1)}, f32[192,128]{1,0:T(8,128)}) custom-call(s32[6]{0:T(128)} %get-tuple-element.226.lo_ref, s32[6]{0:T(128)} %get-tuple-element.225.hi_ref, bf16[4,128,768]{2,1,0:T(8,128)(2,1)} %copy-done.3, f32[2,64,3072]{2,1,0:T(8,128)} %get-tuple-element.67.ot_ref, ...), custom_call_target="tpu_custom_call" | custom-call | flops 6039797760 | bytes 5505024 | tf_op jit(solution)/shard_map/attend_backward/pallas_call | solution.py:176
  375.0 1.0 slice_reduce_fusion.3
  376.6 0.7 concatenate.66
  377.3 0.7 copy.105
  378.3 0.7 pad_maximum_fusion
  378.9 19.1 %all_to_all.35 = bf16[8,128,576]{1,2,0:T(8,128)(2,1)S(1)} all-to-all(bf16[8,128,576]{1,2,0:T(8,128)(2,1)S(1)} %pad_maximum_fusion), channel_id=1, replica_groups=mesh['dp'=8,'tensor'=4] {'dp'}, dimensions={0} | all-to-all | bytes 2359296 | tf_op jit(solution)/shard_map/all_to_all | solution.py:744
  398.1 4.9 all-to-all-start.3
  403.0 2.2 dynamic-slice_bitcast_fusion.4
  405.1 3.8 collective-permute-start.2
  409.0 1.1 collective-permute-start
  410.7 23.2 %all-to-all-done.3.b0_ref = bf16[4,192,768]{2,1,0:T(8,128)(2,1)S(1)} async-done(((bf16[4,192,768]{2,1,0:T(8,128)(2,1)}), bf16[4,192,768]{2,1,0:T(8,128)(2,1)S(1)}, u32[]{:S(2)}, u32[]{:S(2)}) %all-to-all-start.3) | async-done | bytes 1179680 | tf_op jit(solution)/shard_map/all_to_all | solution.py:728
  433.9 1.0 copy-done
  434.9 14.4 %all-to-all-start.5 = ((bf16[4,192,768]{2,1,0:T(8,128)(2,1)}), bf16[4,192,768]{2,1,0:T(8,128)(2,1)}, u32[]{:S(2)}, u32[]{:S(2)}) async-start(bf16[4,192,768]{2,1,0:T(8,128)(2,1)} %get-tuple-element.73), calls=%async_computation.5 | async-start | bytes 2359296 | tf_op jit(solution)/shard_map/all_to_all | solution.py:728
  449.4 0.7 copy.111
  450.1 0.7 copy.110
  450.8 0.7 copy.109
  451.6 0.6 dynamic-slice_reduce_fusion
  452.2 0.6 fusion.5
  453.0 0.9 slice.243
  454.2 1.3 slice-done
  455.6 0.8 dynamic-slice_bitcast_fusion
  456.4 3.8 collective-permute-start.7
  460.2 1.1 collective-permute-start.5
  461.4 0.7 slice_reduce_fusion
  462.1 35.5 %all-to-all-done.5.b1_ref = bf16[4,192,768]{2,1,0:T(8,128)(2,1)} async-done(((bf16[4,192,768]{2,1,0:T(8,128)(2,1)}), bf16[4,192,768]{2,1,0:T(8,128)(2,1)}, u32[]{:S(2)}, u32[]{:S(2)}) %all-to-all-start.5) | async-done | bytes 1179680 | tf_op jit(solution)/shard_map/all_to_all | solution.py:728
  497.6 7.6 %early_back.1.acc_ref = f32[768,768]{1,0:T(8,128)} custom-call(bf16[4,768,2304]{2,1,0:T(8,128)(2,1)} %bitcast.56, bf16[4,192,768]{2,1,0:T(8,128)(2,1)} %copy-done, bf16[4,192,768]{2,1,0:T(8,128)(2,1)} %all-to-all-done.5.b1_ref), custom_call_target="tpu_custom_call" | custom-call | flops 1811939328 | bytes 10485760 | tf_op jit(solution)/shard_map/early_back/pallas_call | solution.py:583
  505.3 6.7 %late_back.1 = bf16[768,768]{1,0:T(8,128)(2,1)} custom-call(s32[1]{0:T(128)} %bitcast.7.part_ref, bf16[4,768,2304]{2,1,0:T(8,128)(2,1)} %bitcast.57, f32[768,768]{1,0:T(8,128)} %early_back.1.acc_ref, f32[768,768]{1,0:T(8,128)} %get-tuple-element.74.grad_ref, bf16[192,768]{1,0:T(8,128)(2,1)} %get-tuple-element.236.rest_0_, ...), custom_call_target="tpu_custom_call" | custom-call | flops 905969664 | bytes 10485760 | tf_op jit(solution)/shard_map/late_back/pallas_call | solution.py:597
  512.0 0.7 copy-done.7
  512.8 2.4 finish.1
  515.2 1.9 copy.112
  (90 shorter events, 3.1 us)
Async XLA Ops:
  10.1 117.5 %copy-start.16 = (f32[192]{0:T(256)S(1)}, f32[192]{0:T(256)}, u32[]{:S(2)}) copy-start(f32[192]{0:T(256)} %param.24) | copy-start | bytes 2308
  10.1 117.5 %copy-start.17 = (f32[192]{0:T(256)S(1)}, f32[192]{0:T(256)}, u32[]{:S(2)}) copy-start(f32[192]{0:T(256)} %param.23) | copy-start | bytes 2308
  170.0 23.4 %all-to-all-start = ((bf16[4,128,768]{2,1,0:T(8,128)(2,1)}), bf16[4,128,768]{2,1,0:T(8,128)(2,1)S(1)}, u32[]{:S(2)}, u32[]{:S(2)}) async-start(bf16[4,128,768]{2,1,0:T(8,128)(2,1)} %get-tuple-element.62), calls=%async_computation | async-start | bytes 1572864 | tf_op jit(solution)/shard_map/all_to_all | solution.py:693
  174.4 24.0 %copy-start.10 = (f32[768]{0:T(1024)S(1)}, f32[768]{0:T(1024)}, u32[]{:S(2)}) copy-start(f32[768]{0:T(1024)} %param.26) | copy-start | bytes 9220
  174.4 24.0 %copy-start.11 = (f32[768]{0:T(1024)S(1)}, f32[768]{0:T(1024)}, u32[]{:S(2)}) copy-start(f32[768]{0:T(1024)} %param.27) | copy-start | bytes 9220
  174.4 24.1 %copy-start.12 = (f32[768]{0:T(1024)S(1)}, f32[768]{0:T(1024)}, u32[]{:S(2)}) copy-start(f32[768]{0:T(1024)} %param.28) | copy-start | bytes 9220
  174.4 24.1 %copy-start.13 = (f32[768]{0:T(1024)S(1)}, f32[768]{0:T(1024)}, u32[]{:S(2)}) copy-start(f32[768]{0:T(1024)} %param.32) | copy-start | bytes 9220
  174.4 24.1 %copy-start.14 = (f32[768]{0:T(1024)S(1)}, f32[768]{0:T(1024)}, u32[]{:S(2)}) copy-start(f32[768]{0:T(1024)} %param.33) | copy-start | bytes 9220
  174.4 24.1 %copy-start.15 = (f32[768]{0:T(1024)S(1)}, f32[768]{0:T(1024)}, u32[]{:S(2)}) copy-start(f32[768]{0:T(1024)} %param.34) | copy-start | bytes 9220
  193.4 14.0 %copy-start.4 = (bf16[4,128,768]{2,1,0:T(8,128)(2,1)}, bf16[4,128,768]{2,1,0:T(8,128)(2,1)S(1)}, u32[]{:S(2)}) copy-start(bf16[4,128,768]{2,1,0:T(8,128)(2,1)S(1)} %all-to-all-done.ctx0_ref) | copy-start | bytes 2359300
  193.4 14.0 %all-to-all-start.1 = ((bf16[4,64,768]{2,1,0:T(8,128)(2,1)}), bf16[4,64,768]{2,1,0:T(8,128)(2,1)S(1)}, u32[]{:S(2)}, u32[]{:S(2)}) async-start(bf16[4,64,768]{2,1,0:T(8,128)(2,1)} %get-tuple-element.64), calls=%async_computation.1 | async-start | bytes 786432 | tf_op jit(solution)/shard_map/all_to_all | solution.py:693
  198.4 254.6 %reduce-scatter.2.cloned.1.call-start = ((), (), s32[]{:S(2)}) async-start(), calls=%async_computation.8 | async-start | bytes 11943936 | tf_op jit(solution)/shard_map/reduce_scatter | solution.py:704
  207.3 0.7 copy-start.6
  266.8 3.6 copy-start.9
  266.8 17.9 %all-to-all-start.2 = ((bf16[4,64,768]{2,1,0:T(8,128)(2,1)}), bf16[4,64,768]{2,1,0:T(8,128)(2,1)S(1)}, u32[]{:S(2)}, u32[]{:S(2)}) async-start(bf16[4,64,768]{2,1,0:T(8,128)(2,1)} %get-tuple-element.66), calls=%async_computation.2 | async-start | bytes 786432 | tf_op jit(solution)/shard_map/all_to_all | solution.py:699
  270.4 8.7 %collective-permute-start.3 = (f32[10,768]{1,0:T(8,128)S(1)}, f32[10,768]{1,0:T(8,128)S(1)}, u32[]{:S(2)}, u32[]{:S(2)}) collective-permute-start(f32[10,768]{1,0:T(8,128)S(1)} %bitcast.68), channel_id=1, source_target_pairs={{0,1},{1,0},{2,3},{3,2},{4,5},{5,4},{6,7},{7,6},{8,9},{9,8},{10,11... | collective-permute-start | bytes 92168 | tf_op jit(solution)/shard_map/ppermute | solution.py:639
  279.1 10.0 %collective-permute-start.4 = (f32[10,768]{1,0:T(8,128)S(1)}, f32[10,768]{1,0:T(8,128)S(1)}, u32[]{:S(2)}, u32[]{:S(2)}) collective-permute-start(f32[10,768]{1,0:T(8,128)S(1)} %slice_add_fusion.2), channel_id=1, source_target_pairs={{0,2},{1,3},{2,0},{3,1},{4,6},{5,7},{6,4},{7,5},{8,10},{9,11},{10,... | collective-permute-start | bytes 92168 | tf_op jit(solution)/shard_map/ppermute | solution.py:639
  284.7 4.6 copy-start.5
  284.7 34.4 %all-to-all-start.4 = ((bf16[4,128,768]{2,1,0:T(8,128)(2,1)}), bf16[4,128,768]{2,1,0:T(8,128)(2,1)S(1)}, u32[]{:S(2)}, u32[]{:S(2)}) async-start(bf16[4,128,768]{2,1,0:T(8,128)(2,1)} %get-tuple-element.72), calls=%async_computation.4 | async-start | bytes 1572864 | tf_op jit(solution)/shard_map/all_to_all | solution.py:700
  319.1 0.9 copy-start.3
  347.9 28.4 %copy-start.1 = (bf16[768,192]{1,0:T(8,128)(2,1)S(1)}, bf16[768,192]{1,0:T(8,128)(2,1)}, u32[]{:S(2)}) copy-start(bf16[768,192]{1,0:T(8,128)(2,1)} %get-tuple-element.80) | copy-start | bytes 884740
  375.0 1.4 copy-start.2
  398.1 35.8 %all-to-all-start.3 = ((bf16[4,192,768]{2,1,0:T(8,128)(2,1)}), bf16[4,192,768]{2,1,0:T(8,128)(2,1)S(1)}, u32[]{:S(2)}, u32[]{:S(2)}) async-start(bf16[4,192,768]{2,1,0:T(8,128)(2,1)} %get-tuple-element.71), calls=%async_computation.3 | async-start | bytes 2359296 | tf_op jit(solution)/shard_map/all_to_all | solution.py:728
  405.1 55.1 %collective-permute-start.2 = (bf16[192,768]{1,0:T(8,128)(2,1)}, bf16[192,768]{1,0:T(8,128)(2,1)}, u32[]{:S(2)}, u32[]{:S(2)}) collective-permute-start(bf16[192,768]{1,0:T(8,128)(2,1)} %get-tuple-element.233), channel_id=1, source_target_pairs={{0,3},{1,0},{2,1},{3,2},{4,7},{5,4},{6,5},{7,6},{8,11},{9,8},{10,9... | collective-permute-start | bytes 884744 | tf_op jit(solution)/shard_map/ppermute | solution.py:658
  408.9 96.3 %collective-permute-start.1 = (bf16[192,768]{1,0:T(8,128)(2,1)}, bf16[192,768]{1,0:T(8,128)(2,1)}, u32[]{:S(2)}, u32[]{:S(2)}) collective-permute-start(bf16[192,768]{1,0:T(8,128)(2,1)} %get-tuple-element.234), channel_id=1, source_target_pairs={{0,2},{1,3},{2,0},{3,1},{4,6},{5,7},{6,4},{7,5},{8,10},{9,11},{10,... | collective-permute-start | bytes 884744 | tf_op jit(solution)/shard_map/ppermute | solution.py:658
  409.0 96.3 %collective-permute-start = (bf16[192,768]{1,0:T(8,128)(2,1)S(1)}, bf16[192,768]{1,0:T(8,128)(2,1)}, u32[]{:S(2)}, u32[]{:S(2)}) collective-permute-start(bf16[192,768]{1,0:T(8,128)(2,1)S(1)} %get-tuple-element.235), channel_id=1, source_target_pairs={{0,1},{1,2},{2,3},{3,0},{4,5},{5,6},{6,7},{7,4},{8,9},{9,10},{10,1... | collective-permute-start | bytes 884744 | tf_op jit(solution)/shard_map/ppermute | solution.py:658
  433.9 1.0 copy-start
  434.9 62.7 %all-to-all-start.5 = ((bf16[4,192,768]{2,1,0:T(8,128)(2,1)}), bf16[4,192,768]{2,1,0:T(8,128)(2,1)}, u32[]{:S(2)}, u32[]{:S(2)}) async-start(bf16[4,192,768]{2,1,0:T(8,128)(2,1)} %get-tuple-element.73), calls=%async_computation.5 | async-start | bytes 2359296 | tf_op jit(solution)/shard_map/all_to_all | solution.py:728
  454.2 1.3 slice-start
  456.4 55.5 %collective-permute-start.7 = (bf16[96,1728]{1,0:T(8,128)(2,1)S(1)}, bf16[96,1728]{1,0:T(8,128)(2,1)S(1)}, u32[]{:S(2)}, u32[]{:S(2)}) collective-permute-start(bf16[96,1728]{1,0:T(8,128)(2,1)S(1)} %get-tuple-element.229), channel_id=1, source_target_pairs={{0,3},{1,0},{2,1},{3,2},{4,7},{5,4},{6,5},{7,6},{8,11},{9,8},{10,9... | collective-permute-start | bytes 995336 | tf_op jit(solution)/shard_map/ppermute | solution.py:658
  460.2 51.7 %collective-permute-start.6 = (bf16[96,1728]{1,0:T(8,128)(2,1)S(1)}, bf16[96,1728]{1,0:T(8,128)(2,1)S(1)}, u32[]{:S(2)}, u32[]{:S(2)}) collective-permute-start(bf16[96,1728]{1,0:T(8,128)(2,1)S(1)} %get-tuple-element.230), channel_id=1, source_target_pairs={{0,2},{1,3},{2,0},{3,1},{4,6},{5,7},{6,4},{7,5},{8,10},{9,11},{10,... | collective-permute-start | bytes 995336 | tf_op jit(solution)/shard_map/ppermute | solution.py:658
  460.2 51.7 %collective-permute-start.5 = (bf16[96,1728]{1,0:T(8,128)(2,1)S(1)}, bf16[96,1728]{1,0:T(8,128)(2,1)}, u32[]{:S(2)}, u32[]{:S(2)}) collective-permute-start(bf16[96,1728]{1,0:T(8,128)(2,1)S(1)} %get-tuple-element.231), channel_id=1, source_target_pairs={{0,1},{1,2},{2,3},{3,0},{4,5},{5,6},{6,7},{7,4},{8,9},{9,10},{10,1... | collective-permute-start | bytes 995336 | tf_op jit(solution)/shard_map/ppermute | solution.py:658
  511.9 0.7 copy-start.7
  512.0 0.8 copy-start.8
Sparse Core Ops, SparseCore 0:
  267.0 79.8 reduce-scatter.1
